TPU v7x, 32 devices: a whole 2x2x4 slice. The times are simulated.
32 devices in a mesh: fsdp: 8 (over z, x), dp: 4 (over y, core).
Axes of the slice: x: 2, y: 2, z: 4, core: 2. Of those that a mesh axis runs over, the one named last changes fastest.
Arguments:
- tokens: bfloat16 [128, 96, 768], P(('fsdp', 'dp')), may hold values from -6 to 6
- memory: bfloat16 [128, 196, 768], P(('fsdp', 'dp')), may hold values from -6 to 6
- suffix_len: int32 [128], P(('fsdp', 'dp')), may hold values from 1 to 64, as said below
- cotangent: bfloat16 [128, 96, 768], P(('fsdp', 'dp')), may hold values from -6 to 6
- attn_in: bfloat16 [768, 2304], P(('fsdp', 'dp')), may hold values from -0.21875 to 0.21875
- attn_out: bfloat16 [768, 768], P(('fsdp', 'dp')), may hold values from -0.625 to 0.625
- cross_query: bfloat16 [768, 768], P(('fsdp', 'dp')), may hold values from -0.21875 to 0.21875
- cross_kv: bfloat16 [768, 1536], P(('fsdp', 'dp')), may hold values from -0.21875 to 0.21875
- cross_out: bfloat16 [768, 768], P(('fsdp', 'dp')), may hold values from -0.875 to 0.875
- mlp_in: bfloat16 [768, 3072], P(('fsdp', 'dp')), may hold values from -0.21875 to 0.21875
- mlp_out: bfloat16 [3072, 768], P(('fsdp', 'dp')), may hold values from -0.109375 to 0.109375
- ln_gain: bfloat16 [768, 3], P(('fsdp', 'dp')), may hold values from 0.25 to 1.75
- shifts: bfloat16 [768, 4], P(('fsdp', 'dp')), may hold values from -1.75 to 1.75
- mlp_bias: bfloat16 [3072], P(('fsdp', 'dp')), may hold values from -1.75 to 1.75
Outputs:
- layer_out: bfloat16 [128, 96, 768], P(('fsdp', 'dp'))
- input_grad: float32 [128, 96, 768], P(('fsdp', 'dp'))
- memory_grad: float32 [128, 196, 768], P(('fsdp', 'dp'))
- attn_in_grad: float32 [768, 2304], P(('fsdp', 'dp'))
- attn_out_grad: float32 [768, 768], P(('fsdp', 'dp'))
- cross_query_grad: float32 [768, 768], P(('fsdp', 'dp'))
- cross_kv_grad: float32 [768, 1536], P(('fsdp', 'dp'))
- cross_out_grad: float32 [768, 768], P(('fsdp', 'dp'))
- mlp_in_grad: float32 [768, 3072], P(('fsdp', 'dp'))
- mlp_out_grad: float32 [3072, 768], P(('fsdp', 'dp'))
- ln_gain_grad: float32 [768, 3], P(('fsdp', 'dp'))
- shifts_grad: float32 [768, 4], P(('fsdp', 'dp'))
- mlp_bias_grad: float32 [3072], P(('fsdp', 'dp'))
Inputs may be any that keep to these rules, and one draw needn't show every extreme that they name: `suffix_len`: the number of live suffix tokens of each sequence, mostly under 10; some sequence has 64.
All inputs are finite; a program needn't handle non-finite values.
Results may differ from a plain program's by a relative error of at most 0.017.
Values may be sent and summed in bfloat16 or wider, within the bound.
No kernel may reach another device: no remote copies, remote signals or barrier semaphores. Data moves between devices by JAX's collectives and lax.ppermute only.
A program may use at most 192 MiB of HBM per device.

v0:
```python
import jax
import jax.numpy as jnp
from jax import lax
from jax.sharding import PartitionSpec as P

D = 768
HEADS = 12
HEAD_DIM = 64
PREFIX = 32


EPS = 1e-05


def norm_forward(value_tensor, gain, shift):
    mean = jnp.mean(value_tensor, axis=-1, keepdims=True)
    centred = value_tensor - mean
    spread = jnp.mean(centred * centred, axis=-1, keepdims=True)
    scale_inv = lax.rsqrt(spread + EPS)
    standard = centred * scale_inv
    return (standard * gain + shift, standard, scale_inv)


def norm_backward(upstream_gradient, standard, scale_inv, gain):
    grad_gain = jnp.sum(upstream_gradient * standard, axis=(0, 1))
    grad_shift = jnp.sum(upstream_gradient, axis=(0, 1))
    inner = upstream_gradient * gain
    first = jnp.mean(inner, axis=-1, keepdims=True)
    second = jnp.mean(inner * standard, axis=-1, keepdims=True)
    return (scale_inv * (inner - first - standard * second), grad_gain, grad_shift)


def project(value_tensor, weight_matrix):
    return jnp.einsum(
        "owh,ht->owt", value_tensor, weight_matrix, preferred_element_type=jnp.float32
    )


def back_project(upstream_gradient, weight_matrix):
    return jnp.einsum(
        "rmj,aj->rma", upstream_gradient, weight_matrix, preferred_element_type=jnp.float32
    )


def contract(value_tensor, upstream_gradient):
    return jnp.einsum(
        "xhq,xhg->qg", value_tensor, upstream_gradient, preferred_element_type=jnp.float32
    )


def scores_of(query, key, allowed):
    raw = jnp.einsum("sqhe,skhe->shqk", query, key, preferred_element_type=jnp.float32)
    scaled = raw * query.shape[-1] ** (-0.5)
    if allowed is None:
        return scaled
    return jnp.where(allowed, scaled, -1e30)


def attend_forward(query, key, value, allowed):
    scores = scores_of(query, key, allowed)
    top = jnp.max(scores, axis=-1, keepdims=True)
    weights = jnp.exp(scores - top)
    total = jnp.sum(weights, axis=-1, keepdims=True)
    probs = (weights / total).astype(jnp.bfloat16)
    context = jnp.einsum("shqk,skhe->sqhe", probs, value, preferred_element_type=jnp.float32)
    return (context.astype(jnp.bfloat16), top + jnp.log(total))


def attend_backward(query, key, value, allowed, summary, grad_context):
    probs = jnp.exp(scores_of(query, key, allowed) - summary)
    grad_probs = jnp.einsum(
        "sqhe,skhe->shqk", grad_context, value, preferred_element_type=jnp.float32
    )
    delta = jnp.sum(grad_probs * probs, axis=-1, keepdims=True)
    grad_scores = (probs * (grad_probs - delta) * query.shape[-1] ** (-0.5)).astype(jnp.bfloat16)
    grad_query = jnp.einsum("shqk,skhe->sqhe", grad_scores, key, preferred_element_type=jnp.float32)
    grad_key = jnp.einsum("shqk,sqhe->skhe", grad_scores, query, preferred_element_type=jnp.float32)
    grad_value = jnp.einsum(
        "shqk,sqhe->skhe",
        probs.astype(jnp.bfloat16),
        grad_context,
        preferred_element_type=jnp.float32,
    )
    return (grad_query, grad_key, grad_value)


def pack_terms(terms, owners):
    return jnp.concatenate([t.reshape(owners, -1) for t in terms], axis=1)


def unpack_terms(packed_row, terms, owners):
    results = []
    offset = 0
    for t in terms:
        owned_shape = (t.shape[0] // owners,) + t.shape[1:]
        length = 1
        for extent in owned_shape:
            length = length * extent
        results.append(packed_row[offset : offset + length].reshape(owned_shape))
        offset = offset + length
    return results


def local(
    tokens,
    memory,
    suffix_len,
    cotangent,
    attn_in,
    attn_out,
    cross_query,
    cross_kv,
    cross_out,
    mlp_in,
    mlp_out,
    ln_gain,
    shifts,
    mlp_bias,
):
    whole = (
        lax.all_gather(attn_in, ("fsdp", "dp"), axis=0, tiled=True),
        lax.all_gather(attn_out, ("fsdp", "dp"), axis=0, tiled=True),
        lax.all_gather(cross_query, ("fsdp", "dp"), axis=0, tiled=True),
        lax.all_gather(cross_kv, ("fsdp", "dp"), axis=0, tiled=True),
        lax.all_gather(cross_out, ("fsdp", "dp"), axis=0, tiled=True),
        lax.all_gather(mlp_in, ("fsdp", "dp"), axis=0, tiled=True),
        lax.all_gather(mlp_out, ("fsdp", "dp"), axis=0, tiled=True),
        lax.all_gather(ln_gain, ("fsdp", "dp"), axis=0, tiled=True),
        lax.all_gather(shifts, ("fsdp", "dp"), axis=0, tiled=True),
        lax.all_gather(mlp_bias, ("fsdp", "dp"), axis=0, tiled=True),
    )
    w_qkv, w_out, w_cquery, w_ckv, w_cout, w_in, w_down, gains, biases, hidden_bias = whole
    seqs, rows, width = tokens.shape
    position = jnp.arange(rows)
    live = position[None, :] < (PREFIX + suffix_len)[:, None]
    allowed = (position[None, :] <= position[:, None])[None, None, :, :] & live[:, None, None, :]
    gain_vals = gains.astype(jnp.float32)
    bias_vals = biases.astype(jnp.float32)
    stream0 = tokens.astype(jnp.float32)
    normed1, standard1, inverse1 = norm_forward(stream0, gain_vals[:, 0], bias_vals[:, 0])
    normed1 = normed1.astype(jnp.bfloat16)
    qkv = project(normed1, w_qkv).astype(jnp.bfloat16)
    query = qkv[..., :D].reshape(seqs, rows, HEADS, HEAD_DIM)
    key = qkv[..., D : 2 * D].reshape(seqs, rows, HEADS, HEAD_DIM)
    value = qkv[..., 2 * D :].reshape(seqs, rows, HEADS, HEAD_DIM)
    context, first_statistics = attend_forward(query, key, value, allowed)
    joined = context.reshape(seqs, rows, D)
    stream1 = stream0 + project(joined, w_out)
    normed2, standard2, inverse2 = norm_forward(stream1, gain_vals[:, 1], bias_vals[:, 1])
    normed2 = normed2.astype(jnp.bfloat16)
    cquery = project(normed2, w_cquery).astype(jnp.bfloat16).reshape(seqs, rows, HEADS, HEAD_DIM)
    ckv = project(memory, w_ckv).astype(jnp.bfloat16)
    mem_rows = memory.shape[1]
    ckey = ckv[..., :D].reshape(seqs, mem_rows, HEADS, HEAD_DIM)
    cvalue = ckv[..., D:].reshape(seqs, mem_rows, HEADS, HEAD_DIM)
    ccontext, summary2 = attend_forward(cquery, ckey, cvalue, None)
    cjoined = ccontext.reshape(seqs, rows, D)
    stream2 = stream1 + project(cjoined, w_cout)
    third_normalized, standard3, inverse3 = norm_forward(stream2, gain_vals[:, 2], bias_vals[:, 2])
    third_normalized = third_normalized.astype(jnp.bfloat16)
    pre = project(third_normalized, w_in) + hidden_bias.astype(jnp.float32)
    activated = jax.nn.gelu(pre, approximate=True).astype(jnp.bfloat16)
    layer_out = (stream2 + project(activated, w_down) + bias_vals[:, 3]).astype(jnp.bfloat16)
    w_qkv, w_out, w_cquery, w_ckv, w_cout, w_in, w_down, gains, biases, hidden_bias = (
        lax.all_gather(attn_in, ("fsdp", "dp"), axis=0, tiled=True),
        lax.all_gather(attn_out, ("fsdp", "dp"), axis=0, tiled=True),
        lax.all_gather(cross_query, ("fsdp", "dp"), axis=0, tiled=True),
        lax.all_gather(cross_kv, ("fsdp", "dp"), axis=0, tiled=True),
        lax.all_gather(cross_out, ("fsdp", "dp"), axis=0, tiled=True),
        lax.all_gather(mlp_in, ("fsdp", "dp"), axis=0, tiled=True),
        lax.all_gather(mlp_out, ("fsdp", "dp"), axis=0, tiled=True),
        lax.all_gather(ln_gain, ("fsdp", "dp"), axis=0, tiled=True),
        lax.all_gather(shifts, ("fsdp", "dp"), axis=0, tiled=True),
        lax.all_gather(mlp_bias, ("fsdp", "dp"), axis=0, tiled=True),
    )
    upstream_gradient = cotangent.astype(jnp.float32) * live[..., None].astype(jnp.float32)
    grad_low = upstream_gradient.astype(jnp.bfloat16)
    down_weight_grad = contract(activated, grad_low)
    g_out_bias = jnp.sum(grad_low, axis=(0, 1), dtype=jnp.float32)
    grad_act = back_project(grad_low, w_down)
    _, gelu_back = jax.vjp(lambda v: jax.nn.gelu(v, approximate=True), pre)
    grad_pre = gelu_back(grad_act)[0].astype(jnp.bfloat16)
    g_hidden_bias = jnp.sum(grad_pre, axis=(0, 1), dtype=jnp.float32)
    g_in = contract(third_normalized, grad_pre)
    grad_back, g_gain3, g_shift3 = norm_backward(
        back_project(grad_pre, w_in), standard3, inverse3, gain_vals[:, 2]
    )
    upstream_gradient = upstream_gradient + grad_back
    grad_low = upstream_gradient.astype(jnp.bfloat16)
    g_cout = contract(cjoined, grad_low)
    grad_cctx = (
        back_project(grad_low, w_cout).astype(jnp.bfloat16).reshape(seqs, rows, HEADS, HEAD_DIM)
    )
    grad_cq, grad_ck, grad_cv = attend_backward(cquery, ckey, cvalue, None, summary2, grad_cctx)
    grad_cq = grad_cq.astype(jnp.bfloat16).reshape(seqs, rows, D)
    grad_ckv = jnp.concatenate(
        (grad_ck.reshape(seqs, mem_rows, D), grad_cv.reshape(seqs, mem_rows, D)), axis=-1
    ).astype(jnp.bfloat16)
    g_cquery = contract(normed2, grad_cq)
    g_ckv = contract(memory, grad_ckv)
    memory_grad = back_project(grad_ckv, w_ckv)
    grad_back, g_gain2, g_shift2 = norm_backward(
        back_project(grad_cq, w_cquery), standard2, inverse2, gain_vals[:, 1]
    )
    upstream_gradient = upstream_gradient + grad_back
    grad_low = upstream_gradient.astype(jnp.bfloat16)
    g_out = contract(joined, grad_low)
    grad_ctx = (
        back_project(grad_low, w_out).astype(jnp.bfloat16).reshape(seqs, rows, HEADS, HEAD_DIM)
    )
    grad_q, grad_k, grad_v = attend_backward(query, key, value, allowed, first_statistics, grad_ctx)
    grad_qkv = jnp.concatenate(
        (
            grad_q.reshape(seqs, rows, D),
            grad_k.reshape(seqs, rows, D),
            grad_v.reshape(seqs, rows, D),
        ),
        axis=-1,
    ).astype(jnp.bfloat16)
    g_qkv = contract(normed1, grad_qkv)
    grad_back, g_gain1, g_shift1 = norm_backward(
        back_project(grad_qkv, w_qkv), standard1, inverse1, gain_vals[:, 0]
    )
    input_grad = upstream_gradient + grad_back
    g_gains = jnp.stack((g_gain1, g_gain2, g_gain3), axis=1)
    g_shifts = jnp.stack((g_shift1, g_shift2, g_shift3, g_out_bias), axis=1)
    terms = [
        g_qkv,
        g_out,
        g_cquery,
        g_ckv,
        g_cout,
        g_in,
        down_weight_grad,
        g_gains,
        g_shifts,
        g_hidden_bias,
    ]
    outer = lax.axis_size("fsdp")
    inner = lax.axis_size("dp")
    owners = outer * inner
    packed = pack_terms(terms, owners)
    summed = lax.psum_scatter(packed, ("fsdp", "dp"), scatter_dimension=0, tiled=True)
    packed_row = summed[0]
    owned = unpack_terms(packed_row, terms, owners)
    return (
        layer_out,
        input_grad,
        memory_grad,
        owned[0],
        owned[1],
        owned[2],
        owned[3],
        owned[4],
        owned[5],
        owned[6],
        owned[7],
        owned[8],
        owned[9],
    )


def solution(mesh):
    in_specs = (
        P(("fsdp", "dp"), None, None),
        P(("fsdp", "dp"), None, None),
        P(("fsdp", "dp")),
        P(("fsdp", "dp"), None, None),
        P(("fsdp", "dp"), None),
        P(("fsdp", "dp"), None),
        P(("fsdp", "dp"), None),
        P(("fsdp", "dp"), None),
        P(("fsdp", "dp"), None),
        P(("fsdp", "dp"), None),
        P(("fsdp", "dp"), None),
        P(("fsdp", "dp"), None),
        P(("fsdp", "dp"), None),
        P(("fsdp", "dp")),
    )
    out_specs = (
        P(("fsdp", "dp"), None, None),
        P(("fsdp", "dp"), None, None),
        P(("fsdp", "dp"), None, None),
        P(("fsdp", "dp"), None),
        P(("fsdp", "dp"), None),
        P(("fsdp", "dp"), None),
        P(("fsdp", "dp"), None),
        P(("fsdp", "dp"), None),
        P(("fsdp", "dp"), None),
        P(("fsdp", "dp"), None),
        P(("fsdp", "dp"), None),
        P(("fsdp", "dp"), None),
        P(("fsdp", "dp")),
    )
    return jax.shard_map(local, mesh=mesh, in_specs=in_specs, out_specs=out_specs, check_vma=False)
```

profile of v0, /device:TPU:0, one launch (start us, length us, event | category | flops | bytes accessed | tf_op | source)
XLA Modules:
  0.0 1251.4 jit_solution(116355494036843963)
XLA Ops:
  12.0 43.6 %all-gather.1 = bf16[32,24,4]{1,2,0:T(4,128)(2,1)S(1)} all-gather(bf16[1,24,4]{1,2,0:T(4,128)(2,1)} %bitcast.166), channel_id=1, replica_groups=mesh['fsdp'=8,'dp'=4] {'fsdp','dp'}, dimensions={0}, use_global_device_ids=true | all-gather | bytes 6336 | tf_op jit(solution)/shard_map/all_gather | solution.py:129
  55.8 37.0 %all-gather = bf16[32,24,3]{1,2,0:T(4,128)(2,1)S(1)} all-gather(bf16[1,24,3]{1,2,0:T(4,128)(2,1)} %bitcast.167), channel_id=1, replica_groups=mesh['fsdp'=8,'dp'=4] {'fsdp','dp'}, dimensions={0}, use_global_device_ids=true | all-gather | bytes 4752 | tf_op jit(solution)/shard_map/all_gather | solution.py:128
  94.0 37.7 %all-reduce = bf16[3072]{0:T(1024)(128)(2,1)S(1)} all-reduce(bf16[3072]{0:T(1024)(128)(2,1)S(1)} %dynamic-update-slice), channel_id=1, replica_groups=mesh['fsdp'=8,'dp'=4] {'fsdp','dp'}, use_global_device_ids=true, to_apply=%add | all-reduce | flops 3072 | bytes 12288
  137.0 3.7 convolution_convert_fusion.1
  144.1 3.7 convolution_convert_fusion
  154.6 33.8 %all-gather.12.cloned.1.call-done = bf16[768,768]{1,0:T(8,128)(2,1)} async-done(((bf16[24,768]{1,0:T(8,128)(2,1)}), bf16[768,768]{1,0:T(8,128)(2,1)}) %all-gather.12.cloned.1.call-update) | async-done | bytes 1179664 | tf_op jit(solution)/shard_map/all_gather | solution.py:122
  192.2 51.8 %all-gather.16.cloned.1.call-done = bf16[768,768]{1,0:T(8,128)(2,1)} async-done(((bf16[24,768]{1,0:T(8,128)(2,1)}), bf16[768,768]{1,0:T(8,128)(2,1)}) %all-gather.16.cloned.1.call-update) | async-done | bytes 1179664 | tf_op jit(solution)/shard_map/all_gather | solution.py:123
  244.0 2.8 convolution_convert_fusion.6
  249.1 3.0 multiply_reduce_fusion.1
  254.7 3.3 fusion.81
  258.0 41.7 %all-gather.18.cloned.1.call-done = bf16[768,768]{1,0:T(8,128)(2,1)} async-done(((bf16[24,768]{1,0:T(8,128)(2,1)}), bf16[768,768]{1,0:T(8,128)(2,1)}) %all-gather.18.cloned.1.call-update) | async-done | bytes 1179664 | tf_op jit(solution)/shard_map/all_gather | solution.py:125
  305.2 59.8 %all-gather.20.cloned.1.call-done = bf16[768,3072]{1,0:T(8,128)(2,1)} async-done(((bf16[24,3072]{1,0:T(8,128)(2,1)}), bf16[768,3072]{1,0:T(8,128)(2,1)}) %all-gather.20.cloned.1.call-update) | async-done | bytes 4718608 | tf_op jit(solution)/shard_map/all_gather | solution.py:126
  365.0 6.9 fusion.18
  371.9 57.9 %all-gather.22.cloned.1.call-done = bf16[3072,768]{1,0:T(8,128)(2,1)} async-done(((bf16[96,768]{1,0:T(8,128)(2,1)}), bf16[3072,768]{1,0:T(8,128)(2,1)}) %all-gather.22.cloned.1.call-update) | async-done | bytes 4718608 | tf_op jit(solution)/shard_map/all_gather | solution.py:127
  429.8 7.8 convert_reduce_fusion
  437.7 2.9 multiply_reduce_fusion.3
  446.4 4.6 fusion.150
  451.0 33.6 %fusion.82 = bf16[4,12,64,96]{3,2,1,0:T(8,128)(2,1)} fusion(bf16[4,196,12,64]{1,3,2,0:T(8,128)(2,1)} %bitcast.148, f32[4,12,96,196]{3,2,1,0:T(8,128)} %fusion.150, f32[4,12,96,196]{3,2,1,0:T(8,128)} %copy-done, f32[4,12,96]{2,1,0:T(8,128)} %log_add_fusion.1), kind=kOutput, calls=%fused_computation.86 | convolution fusion | flops 124033728 | bytes 9037824 | tf_op jit(solution)/shard_map/shqk,skhe->sqhe/dot_general | solution.py:76
  484.7 3.4 multiply_reduce_fusion.4
  493.3 3.4 fusion.151
  498.5 4.6 fusion.78
  503.1 4.7 fusion.75
  507.8 5.0 fusion.66
  512.8 32.9 %fusion.63 = bf16[4,12,64,196]{3,2,1,0:T(8,128)(2,1)} fusion(bf16[4,96,12,64]{1,3,2,0:T(8,128)(2,1)S(1)} %bitcast.151, f32[4,12,96,196]{3,2,1,0:T(8,128)} %fusion.150, f32[4,12,96,196]{3,2,1,0:T(8,128)} %copy-done, f32[4,12,96]{2,1,0:T(8,128)S(1)} %copy-done.36), kind=kOutput, calls=%fused_computation.72 | convolution fusion | flops 124340928 | bytes 9037824 | tf_op jit(solution)/shard_map/shqk,sqhe->skhe/dot_general | solution.py:77
  545.7 3.4 convolution_bitcast_fusion.6
  549.2 2.4 convolution_bitcast_fusion.5
  554.0 5.4 convolution_bitcast_fusion.2
  559.4 5.5 convolution_bitcast_fusion.1
  570.7 2.8 copy.152
  573.5 5.1 convolution_bitcast_fusion
  578.7 6.6 reshape.317
  585.3 6.3 constant_dynamic-update-slice_fusion.6
  593.4 2.9 reshape.319
  596.3 6.8 convolution_bitcast_fusion.3
  603.1 6.0 copy.157
  609.2 5.3 reshape.320
  614.5 2.9 reshape.321
  617.4 8.2 reshape.322
  625.5 8.1 reshape.323
  634.3 5.7 fusion.100
  645.2 3.8 constant_dynamic-update-slice_fusion.4
  649.0 4.9 constant_dynamic-update-slice_fusion.3
  655.5 5.4 constant_dynamic-update-slice_fusion.1
  662.0 4.3 constant_dynamic-update-slice_fusion
  672.5 3.8 fusion.38
  680.2 7.7 fusion.91
  687.9 537.6 %all-reduce.4.cloned.1.call-done = f32[32,295176]{1,0:T(8,128)} async-done(((f32[32,295176]{1,0:T(8,128)}), f32[32,295176]{1,0:T(8,128)}) %all-reduce.4.cloned.1.call-update) | async-done | bytes 37782544
  1234.8 4.1 dynamic-slice_reduce_fusion
  (275 shorter events, 91.3 us)
Async XLA Ops:
  7.2 129.0 %copy-start.67 = (s32[4]{0:T(128)S(1)}, s32[4]{0:T(128)}, u32[]{:S(2)}) copy-start(s32[4]{0:T(128)} %param.16) | copy-start | bytes 52
  7.2 129.8 %copy-start.66 = (bf16[4,196,768]{2,0,1:T(4,128)(2,1)S(1)}, bf16[4,196,768]{2,0,1:T(4,128)(2,1)}, u32[]{:S(2)}) copy-start(bf16[4,196,768]{2,0,1:T(4,128)(2,1)} %param.15) | copy-start | bytes 3612676
  7.2 129.8 %all-gather.14.cloned.1.call-start = ((), (), s32[]{:S(2)}) async-start(), calls=%async_computation.2 | async-start | bytes 2433024 | tf_op jit(solution)/shard_map/all_gather | solution.py:124
  7.9 136.2 %all-gather.10.cloned.1.call-start = ((), (), s32[]{:S(2)}) async-start(), calls=%async_computation | async-start | bytes 3649536 | tf_op jit(solution)/shard_map/all_gather | solution.py:121
  8.7 179.6 %all-gather.12.cloned.1.call-start = ((), (), s32[]{:S(2)}) async-start(), calls=%async_computation.1 | async-start | bytes 1216512 | tf_op jit(solution)/shard_map/all_gather | solution.py:122
  9.4 234.6 %all-gather.16.cloned.1.call-start = ((), (), s32[]{:S(2)}) async-start(), calls=%async_computation.3 | async-start | bytes 1216512 | tf_op jit(solution)/shard_map/all_gather | solution.py:123
  10.0 289.7 %all-gather.18.cloned.1.call-start = ((), (), s32[]{:S(2)}) async-start(), calls=%async_computation.4 | async-start | bytes 1216512 | tf_op jit(solution)/shard_map/all_gather | solution.py:125
  10.6 354.4 %all-gather.20.cloned.1.call-start = ((), (), s32[]{:S(2)}) async-start(), calls=%async_computation.5 | async-start | bytes 4866048 | tf_op jit(solution)/shard_map/all_gather | solution.py:126
  11.2 418.6 %all-gather.22.cloned.1.call-start = ((), (), s32[]{:S(2)}) async-start(), calls=%async_computation.6 | async-start | bytes 4866048 | tf_op jit(solution)/shard_map/all_gather | solution.py:127
  11.9 1213.6 %all-reduce.4.cloned.1.call-start = ((), (), s32[]{:S(2)}) async-start(), calls=%async_computation.7 | async-start | bytes 75595776
  299.7 4.2 copy-start.35
  299.7 4.2 copy-start.41
  299.7 4.8 copy-start.33
  299.7 4.8 copy-start.39
  429.8 7.8 copy-start.11
  429.8 7.9 copy-start.43
  429.8 7.9 copy-start.49
  429.8 7.9 copy-start.55
  429.8 7.9 copy-start.65
  484.6 3.5 copy-start.46
  484.6 3.5 copy-start.51
  484.6 3.5 copy-start.57
  507.8 5.0 copy-start.20
  507.8 5.0 copy-start.36
  512.7 32.9 %copy-start.2 = (f32[4,96,768]{2,1,0:T(8,128)S(1)}, f32[4,96,768]{2,1,0:T(8,128)}, u32[]{:S(2)}) copy-start(f32[4,96,768]{2,1,0:T(8,128)} %copy-done.1) | copy-start | bytes 3538948
  545.7 3.5 copy-start.47
  545.7 3.5 copy-start.52
  545.7 3.5 copy-start.58
  545.7 3.5 copy-start.61
  545.7 3.5 copy-start.68
  549.2 4.8 copy-start.70
  551.7 7.7 slice-start.6
  554.0 5.4 copy-start.31
  554.0 5.4 copy-start.54
  554.0 5.4 slice-start.7
  559.4 5.5 copy-start.23
  564.9 4.3 copy-start.17
  566.8 6.8 copy-start.25
  569.2 4.3 copy-start.8
  625.5 8.1 copy-start.62
  634.3 6.1 copy-start.48
  643.6 11.8 slice-start.3
  645.2 10.3 slice-start.4
  648.9 5.0 copy-start.14
  648.9 6.5 slice-start.5
  653.9 7.0 slice-start
  655.5 5.7 slice-start.1
  655.5 6.5 slice-start.2
  (39 other events, 84.4 us)
Sparse Core Ops, SparseCore 0:
  10.9 59.7 all-gather.13
  73.6 58.9 all-gather.9
  135.5 52.7 all-gather.11
  191.1 52.8 all-gather.15
  246.8 52.8 all-gather.17
  302.5 62.4 all-gather.19
  367.9 61.8 all-gather.21
  671.0 554.4 all-reduce.3
where the time goes:
time: 1260 us; the launch traced here: 1250 us
  waiting for transfers between devices  787 us (62%)
  matrix products  187 us (15%)
  local copies, waits for them, and re-layouts  131 us (10%)
  blocking collectives  118 us (9%)
  between operations  15.5 us (1%)
    unnamed x9, waiting for transfers between devices  542 us
    all_gather x1, waiting for transfers between devices, local(): lax.all_gather(mlp_in, ('fsdp', 'dp'), axis=0, tiled=True)  59.8 us
    all_gather x1, waiting for transfers between devices, local(): lax.all_gather(mlp_out, ('fsdp', 'dp'), axis=0, tiled=True)  57.9 us
    all_gather x1, waiting for transfers between devices, local(): lax.all_gather(cross_query, ('fsdp', 'dp'), axis=0, tiled=True)  51.8 us
    all_gather x1, blocking collectives, local(): lax.all_gather(shifts, ('fsdp', 'dp'), axis=0, tiled=True)  43.6 us
    unnamed x172, local copies, waits for them, and re-layouts  42.8 us
    all_gather x1, waiting for transfers between devices, local(): lax.all_gather(cross_out, ('fsdp', 'dp'), axis=0, tiled=True)  41.7 us
    dot_general x2, matrix products, attend_backward(): jnp.einsum('shqk,skhe->sqhe', grad_scores, key, preferred_element_type=jn...  38.3 us
  transfers between devices with their start and end apart: 8, of which 6 were waited for; matrix products, arithmetic and copies ran while one was open for 5% of the time, Pallas kernels for 0%

commit v1 on v0

--- a/solution.py
+++ b/solution.py
@@ -1,6 +1,10 @@
+import functools
+
 import jax
 import jax.numpy as jnp
 from jax import lax
+from jax.experimental import pallas as pl
+from jax.experimental.pallas import tpu as pltpu
 from jax.sharding import PartitionSpec as P
 
 D = 768
@@ -84,24 +88,231 @@
     return (grad_query, grad_key, grad_value)
 
 
-def pack_terms(terms, owners):
-    return jnp.concatenate([t.reshape(owners, -1) for t in terms], axis=1)
-
-
-def unpack_terms(packed_row, terms, owners):
+AXES = ("fsdp", "dp")
+
+
+def grid_rank(z, x, y, core):
+    return ((z * 2 + x) * 2 + y) * 2 + core
+
+
+def grid_perm(move):
+    return [
+        (grid_rank(z, x, y, core), grid_rank(*move(z, x, y, core)))
+        for z in range(4)
+        for x in range(2)
+        for y in range(2)
+        for core in range(2)
+    ]
+
+
+CORE = grid_perm(lambda z, x, y, core: (z, x, y, core ^ 1))
+ZSHIFT = [
+    grid_perm(lambda z, x, y, core, k=k: ((z + k) % 4, x, y, core)) for k in range(4)
+]
+FIRST = grid_perm(lambda z, x, y, core: (z, x ^ (1 - core), y ^ core, core))
+SECOND = grid_perm(lambda z, x, y, core: (z, x ^ core, y ^ (1 - core), core))
+
+
+def move(value, perm):
+    return lax.ppermute(value, AXES, perm)
+
+
+def place():
+    outer, inner = lax.axis_index("fsdp"), lax.axis_index("dp")
+    return outer // 2, outer % 2, inner // 2, inner % 2
+
+
+def half_of(value, side):
+    width = value.shape[1] // 2
+    return lax.dynamic_slice_in_dim(value, side * width, width, axis=1)
+
+
+def assemble_body(rows, widths, *refs):
+    parts, outs, sem = refs[:8], refs[8:-1], refs[-1]
+    z, x, y, core = place()
+    copies = []
+    for theirs in range(2):
+        side = 1 - core if theirs else core
+        for j in range(4):
+            flip_x = (0, 1 - side, side, 1)[j]
+            flip_y = (0, side, 1 - side, 1)[j]
+            at_x = lax.rem(x + flip_x, 2)
+            at_y = lax.rem(y + flip_y, 2)
+            for k in range(4):
+                at_z = lax.rem(z + 4 - k, 4)
+                offset = 0
+                for width, out in zip(widths, outs):
+                    part = width // 2
+                    target = pl.ds(pl.multiple_of(side * part, 128), part)
+                    copies.append(
+                        pltpu.make_async_copy(
+                            parts[theirs * 4 + j].at[k, :, pl.ds(offset, part)],
+                            out.at[at_z, at_x, at_y, :, target],
+                            sem,
+                        )
+                    )
+                    offset += part
+    for copy in copies:
+        copy.start()
+    for copy in copies:
+        copy.wait()
+
+
+def assemble(parts, rows, widths):
+    outs = pl.pallas_call(
+        functools.partial(assemble_body, rows, widths),
+        out_shape=[jax.ShapeDtypeStruct((4, 2, 2, 2 * rows, w), jnp.bfloat16) for w in widths],
+        in_specs=[pl.BlockSpec(memory_space=pl.ANY)] * 8,
+        out_specs=[pl.BlockSpec(memory_space=pl.ANY)] * len(widths),
+        scratch_shapes=[pltpu.SemaphoreType.DMA],
+        name="assemble",
+    )(*parts)
+    return [o.reshape(32 * rows, w) for o, w in zip(outs, widths)]
+
+
+def gather_grid(shards):
+    rows = shards[0].shape[0]
+    core = place()[3]
+    widths = [s.shape[1] for s in shards]
+    left = jnp.concatenate([s[:, : w // 2] for s, w in zip(shards, widths)], axis=1)
+    right = jnp.concatenate([s[:, w // 2 :] for s, w in zip(shards, widths)], axis=1)
+    mine = jnp.where(core == 0, left, right)
+    got = move(jnp.where(core == 0, right, left), CORE)
+    pair = jnp.where(core == 0, jnp.concatenate([mine, got]), jnp.concatenate([got, mine]))
+    line = jnp.stack([pair] + [move(pair, ZSHIFT[k]) for k in (1, 2, 3)])
+    one = move(line, FIRST)
+    two = move(line, SECOND)
+    both = move(one, SECOND)
+    parts = [line, one, two, both]
+    parts = parts + [move(p, CORE) for p in parts]
+    return assemble(parts, rows, widths)
+
+
+def split_body(count, which, *refs):
+    del which
+    keeps, sends, outs = refs[: 2 * count], refs[2 * count : 4 * count], refs[4 * count :]
+    for source, out in ((keeps, outs[0]), (sends, outs[1])):
+        offset = 0
+        for i in range(count):
+            width = source[2 * i].shape[-1]
+            total = source[2 * i][...].astype(jnp.float32) + source[2 * i + 1][...].astype(
+                jnp.float32
+            )
+            out[:, :, :, offset : offset + width] = total.astype(jnp.bfloat16)
+            offset += width
+
+
+def split_add(pairs, rows):
+    z, x, y, core = place()
+    first = jnp.where(core == 0, x, y)
+    second = jnp.where(core == 0, y, x)
+    first_weight = jnp.where(core == 0, 2, 1)
+    second_weight = 3 - first_weight
+    which = jnp.stack(
+        [
+            (first ^ f) * first_weight + (second ^ s) * second_weight
+            for s in range(2)
+            for f in range(2)
+        ]
+    ).astype(jnp.int32)
+    views, keep_specs, send_specs = [], [], []
+    for keep, got in pairs:
+        width = keep.shape[1]
+        block = (4, 1, 2 * rows, width)
+        for value in (keep, got):
+            views.append(value.reshape(4, 4, 2 * rows, width))
+            keep_specs.append(pl.BlockSpec(block, lambda f, which: (0, which[f], 0, 0)))
+            send_specs.append(pl.BlockSpec(block, lambda f, which: (0, which[2 + f], 0, 0)))
+    total = sum(keep.shape[1] for keep, _ in pairs)
+    shape = jax.ShapeDtypeStruct((4, 2, 2 * rows, total), jnp.bfloat16)
+    out_spec = pl.BlockSpec((4, 1, 2 * rows, total), lambda f, which: (0, f, 0, 0))
+    return pl.pallas_call(
+        functools.partial(split_body, len(pairs)),
+        out_shape=[shape, shape],
+        grid_spec=pltpu.PrefetchScalarGridSpec(
+            num_scalar_prefetch=1,
+            grid=(2,),
+            in_specs=keep_specs + send_specs,
+            out_specs=[out_spec, out_spec],
+        ),
+        name="split_add",
+    )(which, *views, *views)
+
+
+def reduce_grid(factors):
+    z, x, y, core = place()
+    pairs = []
+    rows = factors[0][0].shape[1] // 32
+    for value, upstream in factors:
+        send = contract_low(value, half_of(upstream, 1 - core))
+        got = move(send, CORE)
+        keep = contract_low(value, half_of(upstream, core))
+        pairs.append((keep, got))
+    keep, send = split_add(pairs, rows)
+    got = move(send, SECOND)
+    f32 = jnp.float32
+    got_first = move(
+        (keep[:, 1].astype(f32) + got[:, 1].astype(f32)).astype(jnp.bfloat16), FIRST
+    )
+    def plane(k):
+        at = (z + k) % 4
+        pick = lambda v: lax.dynamic_index_in_dim(v, at, 0, keepdims=False).astype(f32)
+        return pick(keep[:, 0]) + pick(got[:, 0]) + pick(got_first)
+
+    total = plane(0)
+    for k in (1, 2, 3):
+        total = total + move(plane(k).astype(jnp.bfloat16), ZSHIFT[k]).astype(f32)
+    mine = lax.dynamic_slice_in_dim(total, core * rows, rows, axis=0)
+    other = move(lax.dynamic_slice_in_dim(total, (1 - core) * rows, rows, axis=0), CORE)
+    left = jnp.where(core == 0, mine, other)
+    right = jnp.where(core == 0, other, mine)
     results = []
     offset = 0
-    for t in terms:
-        owned_shape = (t.shape[0] // owners,) + t.shape[1:]
-        length = 1
-        for extent in owned_shape:
-            length = length * extent
-        results.append(packed_row[offset : offset + length].reshape(owned_shape))
-        offset = offset + length
+    for keep_part, _ in pairs:
+        width = keep_part.shape[1]
+        results.append(
+            jnp.concatenate(
+                [left[:, offset : offset + width], right[:, offset : offset + width]], axis=1
+            )
+        )
+        offset += width
     return results
 
 
+def contract_low(value, upstream_gradient):
+    return lax.dot_general(
+        value,
+        upstream_gradient,
+        (((0,), (0,)), ((), ())),
+        preferred_element_type=jnp.float32,
+    ).astype(jnp.bfloat16)
+
+
+def gather_plain(shards):
+    widths = [s.shape[1] for s in shards]
+    whole = lax.all_gather(jnp.concatenate(shards, axis=1), AXES, axis=0, tiled=True)
+    results = []
+    offset = 0
+    for width in widths:
+        results.append(whole[:, offset : offset + width])
+        offset += width
+    return results
+
+
+def reduce_plain(factors):
+    packed = jnp.concatenate([contract_low(v, u) for v, u in factors], axis=1)
+    summed = lax.psum_scatter(packed, AXES, scatter_dimension=0, tiled=True).astype(jnp.float32)
+    results = []
+    offset = 0
+    for _, u in factors:
+        results.append(summed[:, offset : offset + u.shape[1]])
+        offset += u.shape[1]
+    return results
+
+
 def local(
+    gather,
+    reduce,
     tokens,
     memory,
     suffix_len,
@@ -117,19 +328,21 @@
     shifts,
     mlp_bias,
 ):
-    whole = (
-        lax.all_gather(attn_in, ("fsdp", "dp"), axis=0, tiled=True),
-        lax.all_gather(attn_out, ("fsdp", "dp"), axis=0, tiled=True),
-        lax.all_gather(cross_query, ("fsdp", "dp"), axis=0, tiled=True),
-        lax.all_gather(cross_kv, ("fsdp", "dp"), axis=0, tiled=True),
-        lax.all_gather(cross_out, ("fsdp", "dp"), axis=0, tiled=True),
-        lax.all_gather(mlp_in, ("fsdp", "dp"), axis=0, tiled=True),
-        lax.all_gather(mlp_out, ("fsdp", "dp"), axis=0, tiled=True),
-        lax.all_gather(ln_gain, ("fsdp", "dp"), axis=0, tiled=True),
-        lax.all_gather(shifts, ("fsdp", "dp"), axis=0, tiled=True),
-        lax.all_gather(mlp_bias, ("fsdp", "dp"), axis=0, tiled=True),
-    )
-    w_qkv, w_out, w_cquery, w_ckv, w_cout, w_in, w_down, gains, biases, hidden_bias = whole
+    owned = attn_in.shape[0]
+    small = jnp.concatenate(
+        [
+            ln_gain,
+            shifts,
+            mlp_bias.reshape(owned, 4),
+            jnp.zeros((owned, 256 - 11), jnp.bfloat16),
+        ],
+        axis=1,
+    )
+    w_qkv, smalls = gather([attn_in, small])
+    w_out, w_cquery, w_ckv, w_cout = gather([attn_out, cross_query, cross_kv, cross_out])
+    (w_in,) = gather([mlp_in])
+    (w_down,) = gather([mlp_out])
+    gains, biases, hidden_bias = smalls[:, :3], smalls[:, 3:7], smalls[:, 7:11].reshape(-1)
     seqs, rows, width = tokens.shape
     position = jnp.arange(rows)
     live = position[None, :] < (PREFIX + suffix_len)[:, None]
@@ -161,33 +374,22 @@
     pre = project(third_normalized, w_in) + hidden_bias.astype(jnp.float32)
     activated = jax.nn.gelu(pre, approximate=True).astype(jnp.bfloat16)
     layer_out = (stream2 + project(activated, w_down) + bias_vals[:, 3]).astype(jnp.bfloat16)
-    w_qkv, w_out, w_cquery, w_ckv, w_cout, w_in, w_down, gains, biases, hidden_bias = (
-        lax.all_gather(attn_in, ("fsdp", "dp"), axis=0, tiled=True),
-        lax.all_gather(attn_out, ("fsdp", "dp"), axis=0, tiled=True),
-        lax.all_gather(cross_query, ("fsdp", "dp"), axis=0, tiled=True),
-        lax.all_gather(cross_kv, ("fsdp", "dp"), axis=0, tiled=True),
-        lax.all_gather(cross_out, ("fsdp", "dp"), axis=0, tiled=True),
-        lax.all_gather(mlp_in, ("fsdp", "dp"), axis=0, tiled=True),
-        lax.all_gather(mlp_out, ("fsdp", "dp"), axis=0, tiled=True),
-        lax.all_gather(ln_gain, ("fsdp", "dp"), axis=0, tiled=True),
-        lax.all_gather(shifts, ("fsdp", "dp"), axis=0, tiled=True),
-        lax.all_gather(mlp_bias, ("fsdp", "dp"), axis=0, tiled=True),
-    )
     upstream_gradient = cotangent.astype(jnp.float32) * live[..., None].astype(jnp.float32)
     grad_low = upstream_gradient.astype(jnp.bfloat16)
-    down_weight_grad = contract(activated, grad_low)
+    flat = lambda v: v.reshape(-1, v.shape[-1])
+    (mlp_out_grad,) = reduce([(flat(activated), flat(grad_low))])
     g_out_bias = jnp.sum(grad_low, axis=(0, 1), dtype=jnp.float32)
     grad_act = back_project(grad_low, w_down)
     _, gelu_back = jax.vjp(lambda v: jax.nn.gelu(v, approximate=True), pre)
     grad_pre = gelu_back(grad_act)[0].astype(jnp.bfloat16)
     g_hidden_bias = jnp.sum(grad_pre, axis=(0, 1), dtype=jnp.float32)
-    g_in = contract(third_normalized, grad_pre)
+    (mlp_in_grad,) = reduce([(flat(third_normalized), flat(grad_pre))])
     grad_back, g_gain3, g_shift3 = norm_backward(
         back_project(grad_pre, w_in), standard3, inverse3, gain_vals[:, 2]
     )
     upstream_gradient = upstream_gradient + grad_back
     grad_low = upstream_gradient.astype(jnp.bfloat16)
-    g_cout = contract(cjoined, grad_low)
+    cout_factors = (flat(cjoined), flat(grad_low))
     grad_cctx = (
         back_project(grad_low, w_cout).astype(jnp.bfloat16).reshape(seqs, rows, HEADS, HEAD_DIM)
     )
@@ -196,15 +398,16 @@
     grad_ckv = jnp.concatenate(
         (grad_ck.reshape(seqs, mem_rows, D), grad_cv.reshape(seqs, mem_rows, D)), axis=-1
     ).astype(jnp.bfloat16)
-    g_cquery = contract(normed2, grad_cq)
-    g_ckv = contract(memory, grad_ckv)
+    cross_query_grad, cross_kv_grad, cross_out_grad = reduce(
+        [(flat(normed2), flat(grad_cq)), (flat(memory), flat(grad_ckv)), cout_factors]
+    )
     memory_grad = back_project(grad_ckv, w_ckv)
     grad_back, g_gain2, g_shift2 = norm_backward(
         back_project(grad_cq, w_cquery), standard2, inverse2, gain_vals[:, 1]
     )
     upstream_gradient = upstream_gradient + grad_back
     grad_low = upstream_gradient.astype(jnp.bfloat16)
-    g_out = contract(joined, grad_low)
+    out_factors = (flat(joined), flat(grad_low))
     grad_ctx = (
         back_project(grad_low, w_out).astype(jnp.bfloat16).reshape(seqs, rows, HEADS, HEAD_DIM)
     )
@@ -217,46 +420,33 @@
         ),
         axis=-1,
     ).astype(jnp.bfloat16)
-    g_qkv = contract(normed1, grad_qkv)
     grad_back, g_gain1, g_shift1 = norm_backward(
         back_project(grad_qkv, w_qkv), standard1, inverse1, gain_vals[:, 0]
     )
     input_grad = upstream_gradient + grad_back
-    g_gains = jnp.stack((g_gain1, g_gain2, g_gain3), axis=1)
-    g_shifts = jnp.stack((g_shift1, g_shift2, g_shift3, g_out_bias), axis=1)
-    terms = [
-        g_qkv,
-        g_out,
-        g_cquery,
-        g_ckv,
-        g_cout,
-        g_in,
-        down_weight_grad,
-        g_gains,
-        g_shifts,
-        g_hidden_bias,
-    ]
-    outer = lax.axis_size("fsdp")
-    inner = lax.axis_size("dp")
-    owners = outer * inner
-    packed = pack_terms(terms, owners)
-    summed = lax.psum_scatter(packed, ("fsdp", "dp"), scatter_dimension=0, tiled=True)
-    packed_row = summed[0]
-    owned = unpack_terms(packed_row, terms, owners)
+    small_sums = jnp.stack(
+        (g_gain1, g_gain2, g_gain3, g_shift1, g_shift2, g_shift3, g_out_bias), axis=0
+    )
+    bias_sums = g_hidden_bias.reshape(D, 4).T
+    sums = jnp.concatenate([small_sums, bias_sums], axis=0)
+    picks = jnp.eye(11, 256, dtype=jnp.bfloat16)
+    attn_in_grad, attn_out_grad, small_grad = reduce(
+        [(flat(normed1), flat(grad_qkv)), out_factors, (sums.astype(jnp.bfloat16), picks)]
+    )
     return (
         layer_out,
         input_grad,
         memory_grad,
-        owned[0],
-        owned[1],
-        owned[2],
-        owned[3],
-        owned[4],
-        owned[5],
-        owned[6],
-        owned[7],
-        owned[8],
-        owned[9],
+        attn_in_grad,
+        attn_out_grad,
+        cross_query_grad,
+        cross_kv_grad,
+        cross_out_grad,
+        mlp_in_grad,
+        mlp_out_grad,
+        small_grad[:, :3],
+        small_grad[:, 3:7],
+        small_grad[:, 7:11].reshape(-1),
     )
 
 
@@ -292,4 +482,8 @@
         P(("fsdp", "dp"), None),
         P(("fsdp", "dp")),
     )
-    return jax.shard_map(local, mesh=mesh, in_specs=in_specs, out_specs=out_specs, check_vma=False)
+    if dict(mesh.shape) == {"fsdp": 8, "dp": 4}:
+        program = functools.partial(local, gather_grid, reduce_grid)
+    else:
+        program = functools.partial(local, gather_plain, reduce_plain)
+    return jax.shard_map(program, mesh=mesh, in_specs=in_specs, out_specs=out_specs, check_vma=False)

time: 1260 us -> 1110 us (0.88)
  waiting for transfers between devices: 787 us -> 111 us
  Pallas kernels: 0 us -> 606 us
  blocking collectives: 118 us -> 0 us
  starting transfers between devices: 0.3 us -> 62.7 us
  local copies, waits for them, and re-layouts: 131 us -> 102 us
  other arithmetic: 12.2 us -> 36.5 us
  between operations: 15.5 us -> 2.68 us
    pallas_call x0 -> x8, Pallas kernels: none -> 606 us  [the longest x4 588 us: assemble(): pl.pallas_call(functools.partial(assemble_body, rows, widths), out_shape=...]
    unnamed x9 -> x0, waiting for transfers between devices: 542 us -> none
    all_gather x7 -> x0, waiting for transfers between devices: 245 us -> none  [the longest x1 59.8 us: local(): lax.all_gather(mlp_in, ('fsdp', 'dp'), axis=0, tiled=True)]
    ppermute x0 -> x76, waiting for transfers between devices: none -> 111 us  [move(): return lax.ppermute(value, AXES, perm)]
    all_gather x2 -> x0, blocking collectives: 80.6 us -> none  [the longest x1 43.6 us: local(): lax.all_gather(shifts, ('fsdp', 'dp'), axis=0, tiled=True)]
    ppermute x0 -> x76, starting transfers between devices: none -> 62.7 us  [move(): return lax.ppermute(value, AXES, perm)]
    reshape x19 -> x4, local copies, waits for them, and re-layouts: 41.9 us -> 2.96 us  [the longest x1 1.18 us: local(): flat = lambda v: v.reshape(-1, v.shape[-1])]
    unnamed x1 -> x0, blocking collectives: 37.7 us -> none
  transfers between devices with their start and end apart: 8 -> 76, of which waited for: 6 -> 21; matrix products, arithmetic and copies ran while one was open for 5% -> 15% of each run, Pallas kernels for 0% -> 39%
where the time goes in v1:
time: 1110 us
  Pallas kernels  606 us (55%)
  matrix products  185 us (17%)
  waiting for transfers between devices  111 us (10%)
  local copies, waits for them, and re-layouts  102 us (9%)
  starting transfers between devices  62.7 us (6%)
  other arithmetic  36.5 us (3%)
    pallas_call x4, Pallas kernels, assemble(): pl.pallas_call(functools.partial(assemble_body, rows, widths), out_shape=...  588 us
    ppermute x76, waiting for transfers between devices, move(): return lax.ppermute(value, AXES, perm)  111 us
    ppermute x76, starting transfers between devices, move(): return lax.ppermute(value, AXES, perm)  62.7 us
    dot_general x16, matrix products, contract_low(): lax.dot_general(value, upstream_gradient, (((0,), (0,)), ((), ())), prefe...  38.8 us
    dot_general x2, matrix products, attend_backward(): jnp.einsum('shqk,skhe->sqhe', grad_scores, key, preferred_element_type=jn...  38.3 us
    dot_general x2, matrix products, attend_backward(): jnp.einsum('shqk,sqhe->skhe', grad_scores, query, preferred_element_type=...  37.8 us
    dot_general x7, matrix products, back_project(): jnp.einsum('rmj,aj->rma', upstream_gradient, weight_matrix, preferred_ele...  25.2 us
  transfers between devices with their start and end apart: 76, of which 21 were waited for; matrix products, arithmetic and copies ran while one was open for 15% of the time, Pallas kernels for 39%

profile of v1, /device:TPU:0, one launch (start us, length us, event | category | flops | bytes accessed | tf_op | source)
XLA Modules:
  0.0 1106.4 jit_solution(1605237484263978426)
XLA Ops:
  16.8 4.8 collective-permute-start.3
  25.4 7.5 collective-permute-done.2
  41.3 4.5 collective-permute-start.24
  45.8 10.1 collective-permute-done.35
  55.9 3.8 collective-permute-start.14
  64.4 2.9 collective-permute-start.13
  67.9 12.1 %collective-permute-done.13 = bf16[48,1920]{1,0:T(8,128)(2,1)S(1)} collective-permute-done((bf16[48,1920]{1,0:T(8,128)(2,1)S(1)}, bf16[48,1920]{1,0:T(8,128)(2,1)S(1)}, u32[]{:S(2)}, u32[]{:S(2)}) %collective-permute-start.13) | collective-permute-done | bytes 184352 | tf_op jit(solution)/shard_map/ppermute | solution.py:117
  87.5 120.2 %assemble.4 = (bf16[4,2,2,48,2304]{4,3,2,1,0:T(8,128)(2,1)}, bf16[4,2,2,48,256]{4,3,2,1,0:T(8,128)(2,1)}) custom-call(bf16[4,48,1280]{2,1,0:T(8,128)(2,1)} %copy-done.32, bf16[4,48,1280]{2,1,0:T(8,128)(2,1)} %copy-done.57, bf16[4,48,1280]{2,1,0:T(8,128)(2,1)} %copy-done.58, bf16[4,48,1280]{2,1,0:T(8,128)(2,1)} %copy-done.59, ...), custom_call_target="tpu_custom_call" | custom-call | tf_op jit(solution)/shard_map/assemble/pallas_call | solution.py:162
  216.4 4.3 collective-permute-done.37.refs_1_
  221.0 15.5 %collective-permute-done.15.refs_1_ = bf16[4,48,1920]{2,1,0:T(8,128)(2,1)} collective-permute-done((bf16[4,48,1920]{2,1,0:T(8,128)(2,1)}, bf16[4,48,1920]{2,1,0:T(8,128)(2,1)}, u32[]{:S(2)}, u32[]{:S(2)}) %collective-permute-start.15) | collective-permute-done | bytes 737312 | tf_op jit(solution)/shard_map/ppermute | solution.py:117
  236.8 3.6 convolution_convert_fusion.2
  248.8 5.8 collective-permute-done.39.refs_3_
  265.4 144.0 %assemble.6 = bf16[4,2,2,48,3072]{4,3,2,1,0:T(8,128)(2,1)} custom-call(bf16[4,48,1536]{2,1,0:T(8,128)(2,1)} %copy-done.25, bf16[4,48,1536]{2,1,0:T(8,128)(2,1)} %collective-permute-done.26.refs_1_, bf16[4,48,1536]{2,1,0:T(8,128)(2,1)} %collective-permute-done.27.refs_2_, bf16[4,48,1536]{2,1,0:T(8,128)(2,1)} %collective-permute-done.28.refs_3_, ...), custom_call_target="tpu_custom_call" | custom-call | tf_op jit(solution)/shard_map/assemble/pallas_call | solution.py:162
  409.5 144.1 %assemble.7 = bf16[4,2,2,192,768]{4,3,2,1,0:T(8,128)(2,1)} custom-call(bf16[4,192,384]{2,1,0:T(8,128)(2,1)} %copy-done.26, bf16[4,192,384]{2,1,0:T(8,128)(2,1)} %collective-permute-done.37.refs_1_, bf16[4,192,384]{2,1,0:T(8,128)(2,1)} %collective-permute-done.38.refs_2_, bf16[4,192,384]{2,1,0:T(8,128)(2,1)} %collective-permute-done.39.refs_3_, ...), custom_call_target="tpu_custom_call" | custom-call | tf_op jit(solution)/shard_map/assemble/pallas_call | solution.py:162
  553.6 179.8 %assemble.5 = (bf16[4,2,2,48,768]{4,3,2,1,0:T(8,128)(2,1)}, bf16[4,2,2,48,768]{4,3,2,1,0:T(8,128)(2,1)}, bf16[4,2,2,48,1536]{4,3,2,1,0:T(8,128)(2,1)}, bf16[4,2,2,48,768]{4,3,2,1,0:T(8,128)(2,1)}) custom-call(bf16[4,48,1920]{2,1,0:T(8,128)(2,1)} %pad_maximum_fusion.refs_0_, bf16[4,48,1920]{2,1,0:T(8,128)(2,1)} %collective-permute-done.15.refs_1_, ...), custom_call_target="tpu_custom_call" | custom-call | tf_op jit(solution)/shard_map/assemble/pallas_call | solution.py:162
  738.0 4.6 fusion.20
  758.5 4.5 multiply_convert_fusion.1
  763.0 5.7 fusion.187
  768.7 2.9 multiply_reduce_fusion.3
  776.5 4.5 fusion.188
  780.9 4.7 fusion.58
  785.6 33.7 %fusion.75 = bf16[4,12,64,96]{3,2,1,0:T(8,128)(2,1)} fusion(bf16[4,196,12,64]{1,3,2,0:T(8,128)(2,1)} %bitcast.287, f32[4,12,96,196]{3,2,1,0:T(8,128)} %fusion.188, f32[4,12,96,196]{3,2,1,0:T(8,128)} %copy-done, f32[4,12,96]{2,1,0:T(8,128)S(1)} %copy-done.71), kind=kOutput, calls=%fused_computation.82 | convolution fusion | flops 124033728 | bytes 9037824 | tf_op jit(solution)/shard_map/shqk,skhe->sqhe/dot_general | solution.py:80
  819.3 33.2 %fusion.55 = bf16[4,12,64,196]{3,2,1,0:T(8,128)(2,1)} fusion(bf16[4,96,12,64]{1,3,2,0:T(8,128)(2,1)S(1)} %bitcast.311, f32[4,12,96,196]{3,2,1,0:T(8,128)} %fusion.188, f32[4,12,96,196]{3,2,1,0:T(8,128)} %copy-done, f32[4,12,96]{2,1,0:T(8,128)S(1)} %copy-done.71), kind=kOutput, calls=%fused_computation.65 | convolution fusion | flops 124340928 | bytes 9037824 | tf_op jit(solution)/shard_map/shqk,sqhe->skhe/dot_general | solution.py:81
  852.6 3.4 multiply_reduce_fusion.4
  860.9 3.5 fusion.189
  866.2 4.6 fusion.68
  870.9 4.6 fusion.71
  886.5 4.4 concatenate.235
  900.1 5.3 fusion.88
  932.5 4.4 concatenate.234
  950.8 3.1 convolution_convert_fusion.1
  953.9 2.9 convolution_convert_fusion.6
  960.0 4.9 convolution_convert_fusion
  964.8 5.2 fusion.81
  972.9 4.5 split_add.5
  983.9 5.7 fusion.21
  989.6 4.4 collective-permute-done.56
  996.8 4.9 split_add.4
  1007.6 3.8 collective-permute-start.60
  1016.7 4.5 split_add.7
  1022.4 4.3 split_add.6
  1036.0 14.0 %collective-permute-done.48 = bf16[4,48,1664]{2,1,0:T(8,128)(2,1)S(1)} collective-permute-done((bf16[4,48,1664]{2,1,0:T(8,128)(2,1)S(1)}, bf16[4,48,1664]{2,1,0:T(8,128)(2,1)S(1)}, u32[]{:S(2)}, u32[]{:S(2)}) %collective-permute-start.48) | collective-permute-done | bytes 639008 | tf_op jit(solution)/shard_map/ppermute | solution.py:117
  1050.9 3.2 collective-permute-start.51
  1060.8 7.2 collective-permute-done.50
  1074.1 3.8 collective-permute-start.74
  1080.7 3.8 collective-permute-start.67
  1085.0 9.1 collective-permute-done.73
  1094.3 8.7 collective-permute-done.66
  (546 shorter events, 218.8 us)
Async XLA Ops:
  3.8 35.2 %collective-permute-start.11 = (bf16[24,1920]{1,0:T(8,128)(2,1)}, bf16[24,1920]{1,0:T(8,128)(2,1)S(1)}, u32[]{:S(2)}, u32[]{:S(2)}) collective-permute-start(bf16[24,1920]{1,0:T(8,128)(2,1)} %get-tuple-element.144), channel_id=1, source_target_pairs={{0,1},{1,0},{2,3},{3,2},{4,5},{5,4},{6,7},{7,6},{8,9},{9,8},{10,11... | collective-permute-start | bytes 276488 | tf_op jit(solution)/shard_map/ppermute | solution.py:117
  8.7 28.4 %collective-permute-start.22 = (bf16[24,1536]{1,0:T(8,128)(2,1)S(1)}, bf16[24,1536]{1,0:T(8,128)(2,1)S(1)}, u32[]{:S(2)}, u32[]{:S(2)}) collective-permute-start(bf16[24,1536]{1,0:T(8,128)(2,1)S(1)} %get-tuple-element.154), channel_id=1, source_target_pairs={{0,1},{1,0},{2,3},{3,2},{4,5},{5,4},{6,7},{7,6},{8,9},{9,8},{10,11... | collective-permute-start | bytes 221192 | tf_op jit(solution)/shard_map/ppermute | solution.py:117
  33.0 28.3 %collective-permute-start.4 = (bf16[4,48,1280]{2,1,0:T(8,128)(2,1)S(1)}, bf16[4,48,1280]{2,1,0:T(8,128)(2,1)S(1)}, u32[]{:S(2)}, u32[]{:S(2)}) collective-permute-start(bf16[4,48,1280]{2,1,0:T(8,128)(2,1)S(1)} %pad_maximum_fusion.3.refs_0_), channel_id=1, source_target_pairs={{0,4},{1,3},{2,6},{3,1},{4,0},{5,7},{6,2},{7,5},{8,12},{9,11},{10,... | collective-permute-start | bytes 1474568 | tf_op jit(solution)/shard_map/ppermute | solution.py:117
  36.1 19.8 %collective-permute-start.35 = (bf16[192,384]{1,0:T(8,128)(2,1)S(1)}, bf16[192,384]{1,0:T(8,128)(2,1)S(1)}, u32[]{:S(2)}, u32[]{:S(2)}) collective-permute-start(bf16[192,384]{1,0:T(8,128)(2,1)S(1)} %maximum_select_fusion.5), channel_id=1, source_target_pairs={{0,16},{1,17},{2,18},{3,19},{4,20},{5,21},{6,22},{7,23},{8,24},{9,... | collective-permute-start | bytes 442376 | tf_op jit(solution)/shard_map/ppermute | solution.py:117
  37.0 18.8 %collective-permute-start.34 = (bf16[192,384]{1,0:T(8,128)(2,1)S(1)}, bf16[192,384]{1,0:T(8,128)(2,1)S(1)}, u32[]{:S(2)}, u32[]{:S(2)}) collective-permute-start(bf16[192,384]{1,0:T(8,128)(2,1)S(1)} %maximum_select_fusion.5), channel_id=1, source_target_pairs={{0,8},{1,9},{2,10},{3,11},{4,12},{5,13},{6,14},{7,15},{8,16},{9,17... | collective-permute-start | bytes 442376 | tf_op jit(solution)/shard_map/ppermute | solution.py:117
  39.0 20.7 %collective-permute-start.25 = (bf16[48,1536]{1,0:T(8,128)(2,1)S(1)}, bf16[48,1536]{1,0:T(8,128)(2,1)S(1)}, u32[]{:S(2)}, u32[]{:S(2)}) collective-permute-start(bf16[48,1536]{1,0:T(8,128)(2,1)S(1)} %maximum_select_fusion.3), channel_id=1, source_target_pairs={{0,24},{1,25},{2,26},{3,27},{4,28},{5,29},{6,30},{7,31},{8,0},{9,1... | collective-permute-start | bytes 442376 | tf_op jit(solution)/shard_map/ppermute | solution.py:117
  41.3 21.4 %collective-permute-start.24 = (bf16[48,1536]{1,0:T(8,128)(2,1)S(1)}, bf16[48,1536]{1,0:T(8,128)(2,1)S(1)}, u32[]{:S(2)}, u32[]{:S(2)}) collective-permute-start(bf16[48,1536]{1,0:T(8,128)(2,1)S(1)} %maximum_select_fusion.3), channel_id=1, source_target_pairs={{0,16},{1,17},{2,18},{3,19},{4,20},{5,21},{6,22},{7,23},{8,24},{9,... | collective-permute-start | bytes 442376 | tf_op jit(solution)/shard_map/ppermute | solution.py:117
  59.7 20.8 %collective-permute-start.5 = (bf16[4,48,1280]{2,1,0:T(8,128)(2,1)S(1)}, bf16[4,48,1280]{2,1,0:T(8,128)(2,1)S(1)}, u32[]{:S(2)}, u32[]{:S(2)}) collective-permute-start(bf16[4,48,1280]{2,1,0:T(8,128)(2,1)S(1)} %pad_maximum_fusion.3.refs_0_), channel_id=1, source_target_pairs={{0,2},{1,5},{2,0},{3,7},{4,6},{5,1},{6,4},{7,3},{8,10},{9,13},{10,... | collective-permute-start | bytes 1474568 | tf_op jit(solution)/shard_map/ppermute | solution.py:117
  61.2 19.3 %collective-permute-start.6 = (bf16[4,48,1280]{2,1,0:T(8,128)(2,1)S(1)}, bf16[4,48,1280]{2,1,0:T(8,128)(2,1)S(1)}, u32[]{:S(2)}, u32[]{:S(2)}) collective-permute-start(bf16[4,48,1280]{2,1,0:T(8,128)(2,1)S(1)} %collective-permute-done.4.refs_1_), channel_id=1, source_target_pairs={{0,2},{1,5},{2,0},{3,7},{4,6},{5,1},{6,4},{7,3},{8,10},{9,13},{10,... | collective-permute-start | bytes 1474568 | tf_op jit(solution)/shard_map/ppermute | solution.py:117
  62.8 18.3 %collective-permute-start.7 = (bf16[4,48,1280]{2,1,0:T(8,128)(2,1)S(1)}, bf16[4,48,1280]{2,1,0:T(8,128)(2,1)S(1)}, u32[]{:S(2)}, u32[]{:S(2)}) collective-permute-start(bf16[4,48,1280]{2,1,0:T(8,128)(2,1)S(1)} %pad_maximum_fusion.3.refs_0_), channel_id=1, source_target_pairs={{0,1},{1,0},{2,3},{3,2},{4,5},{5,4},{6,7},{7,6},{8,9},{9,8},{10,11... | collective-permute-start | bytes 1474568 | tf_op jit(solution)/shard_map/ppermute | solution.py:117
  64.4 15.5 %collective-permute-start.13 = (bf16[48,1920]{1,0:T(8,128)(2,1)S(1)}, bf16[48,1920]{1,0:T(8,128)(2,1)S(1)}, u32[]{:S(2)}, u32[]{:S(2)}) collective-permute-start(bf16[48,1920]{1,0:T(8,128)(2,1)S(1)} %maximum_select_fusion.1), channel_id=1, source_target_pairs={{0,16},{1,17},{2,18},{3,19},{4,20},{5,21},{6,22},{7,23},{8,24},{9,... | collective-permute-start | bytes 552968 | tf_op jit(solution)/shard_map/ppermute | solution.py:117
  79.9 127.8 %collective-permute-start.29 = (bf16[4,48,1536]{2,1,0:T(8,128)(2,1)S(1)}, bf16[4,48,1536]{2,1,0:T(8,128)(2,1)}, u32[]{:S(2)}, u32[]{:S(2)}) collective-permute-start(bf16[4,48,1536]{2,1,0:T(8,128)(2,1)S(1)} %pad_maximum_fusion.1.refs_0_), channel_id=1, source_target_pairs={{0,1},{1,0},{2,3},{3,2},{4,5},{5,4},{6,7},{7,6},{8,9},{9,8},{10,11... | collective-permute-start | bytes 1769480 | tf_op jit(solution)/shard_map/ppermute | solution.py:117
  81.0 129.4 %collective-permute-start.27 = (bf16[4,48,1536]{2,1,0:T(8,128)(2,1)S(1)}, bf16[4,48,1536]{2,1,0:T(8,128)(2,1)}, u32[]{:S(2)}, u32[]{:S(2)}) collective-permute-start(bf16[4,48,1536]{2,1,0:T(8,128)(2,1)S(1)} %pad_maximum_fusion.1.refs_0_), channel_id=1, source_target_pairs={{0,2},{1,5},{2,0},{3,7},{4,6},{5,1},{6,4},{7,3},{8,10},{9,13},{10,... | collective-permute-start | bytes 1769480 | tf_op jit(solution)/shard_map/ppermute | solution.py:117
  83.4 130.2 %collective-permute-start.26 = (bf16[4,48,1536]{2,1,0:T(8,128)(2,1)S(1)}, bf16[4,48,1536]{2,1,0:T(8,128)(2,1)}, u32[]{:S(2)}, u32[]{:S(2)}) collective-permute-start(bf16[4,48,1536]{2,1,0:T(8,128)(2,1)S(1)} %pad_maximum_fusion.1.refs_0_), channel_id=1, source_target_pairs={{0,4},{1,3},{2,6},{3,1},{4,0},{5,7},{6,2},{7,5},{8,12},{9,11},{10,... | collective-permute-start | bytes 1769480 | tf_op jit(solution)/shard_map/ppermute | solution.py:117
  84.8 130.4 %collective-permute-start.40 = (bf16[4,192,384]{2,1,0:T(8,128)(2,1)S(1)}, bf16[4,192,384]{2,1,0:T(8,128)(2,1)S(1)}, u32[]{:S(2)}, u32[]{:S(2)}) collective-permute-start(bf16[4,192,384]{2,1,0:T(8,128)(2,1)S(1)} %pad_maximum_fusion.2.refs_0_), channel_id=1, source_target_pairs={{0,1},{1,0},{2,3},{3,2},{4,5},{5,4},{6,7},{7,6},{8,9},{9,8},{10,11... | collective-permute-start | bytes 1769480 | tf_op jit(solution)/shard_map/ppermute | solution.py:117
  86.4 128.8 %collective-permute-start.38 = (bf16[4,192,384]{2,1,0:T(8,128)(2,1)S(1)}, bf16[4,192,384]{2,1,0:T(8,128)(2,1)}, u32[]{:S(2)}, u32[]{:S(2)}) collective-permute-start(bf16[4,192,384]{2,1,0:T(8,128)(2,1)S(1)} %pad_maximum_fusion.2.refs_0_), channel_id=1, source_target_pairs={{0,2},{1,5},{2,0},{3,7},{4,6},{5,1},{6,4},{7,3},{8,10},{9,13},{10,... | collective-permute-start | bytes 1769480 | tf_op jit(solution)/shard_map/ppermute | solution.py:117
  210.5 26.0 %collective-permute-start.15 = (bf16[4,48,1920]{2,1,0:T(8,128)(2,1)}, bf16[4,48,1920]{2,1,0:T(8,128)(2,1)}, u32[]{:S(2)}, u32[]{:S(2)}) collective-permute-start(bf16[4,48,1920]{2,1,0:T(8,128)(2,1)} %pad_maximum_fusion.refs_0_), channel_id=1, source_target_pairs={{0,4},{1,3},{2,6},{3,1},{4,0},{5,7},{6,2},{7,5},{8,12},{9,11},{10,... | collective-permute-start | bytes 2211848 | tf_op jit(solution)/shard_map/ppermute | solution.py:117
  213.6 26.8 %collective-permute-start.16 = (bf16[4,48,1920]{2,1,0:T(8,128)(2,1)}, bf16[4,48,1920]{2,1,0:T(8,128)(2,1)}, u32[]{:S(2)}, u32[]{:S(2)}) collective-permute-start(bf16[4,48,1920]{2,1,0:T(8,128)(2,1)} %pad_maximum_fusion.refs_0_), channel_id=1, source_target_pairs={{0,2},{1,5},{2,0},{3,7},{4,6},{5,1},{6,4},{7,3},{8,10},{9,13},{10,... | collective-permute-start | bytes 2211848 | tf_op jit(solution)/shard_map/ppermute | solution.py:117
  215.2 27.0 %collective-permute-start.30 = (bf16[4,48,1536]{2,1,0:T(8,128)(2,1)}, bf16[4,48,1536]{2,1,0:T(8,128)(2,1)S(1)}, u32[]{:S(2)}, u32[]{:S(2)}) collective-permute-start(bf16[4,48,1536]{2,1,0:T(8,128)(2,1)} %collective-permute-done.26.refs_1_), channel_id=1, source_target_pairs={{0,1},{1,0},{2,3},{3,2},{4,5},{5,4},{6,7},{7,6},{8,9},{9,8},{10,11... | collective-permute-start | bytes 1769480 | tf_op jit(solution)/shard_map/ppermute | solution.py:117
  215.2 27.0 %collective-permute-start.28 = (bf16[4,48,1536]{2,1,0:T(8,128)(2,1)}, bf16[4,48,1536]{2,1,0:T(8,128)(2,1)}, u32[]{:S(2)}, u32[]{:S(2)}) collective-permute-start(bf16[4,48,1536]{2,1,0:T(8,128)(2,1)} %collective-permute-done.26.refs_1_), channel_id=1, source_target_pairs={{0,2},{1,5},{2,0},{3,7},{4,6},{5,1},{6,4},{7,3},{8,10},{9,13},{10,... | collective-permute-start | bytes 1769480 | tf_op jit(solution)/shard_map/ppermute | solution.py:117
  220.6 19.9 %collective-permute-start.31 = (bf16[4,48,1536]{2,1,0:T(8,128)(2,1)}, bf16[4,48,1536]{2,1,0:T(8,128)(2,1)S(1)}, u32[]{:S(2)}, u32[]{:S(2)}) collective-permute-start(bf16[4,48,1536]{2,1,0:T(8,128)(2,1)} %collective-permute-done.27.refs_2_), channel_id=1, source_target_pairs={{0,1},{1,0},{2,3},{3,2},{4,5},{5,4},{6,7},{7,6},{8,9},{9,8},{10,11... | collective-permute-start | bytes 1769480 | tf_op jit(solution)/shard_map/ppermute | solution.py:117
  236.4 18.1 %collective-permute-start.17 = (bf16[4,48,1920]{2,1,0:T(8,128)(2,1)}, bf16[4,48,1920]{2,1,0:T(8,128)(2,1)}, u32[]{:S(2)}, u32[]{:S(2)}) collective-permute-start(bf16[4,48,1920]{2,1,0:T(8,128)(2,1)} %collective-permute-done.15.refs_1_), channel_id=1, source_target_pairs={{0,2},{1,5},{2,0},{3,7},{4,6},{5,1},{6,4},{7,3},{8,10},{9,13},{10,... | collective-permute-start | bytes 2211848 | tf_op jit(solution)/shard_map/ppermute | solution.py:117
  240.5 14.0 %collective-permute-start.39 = (bf16[4,192,384]{2,1,0:T(8,128)(2,1)}, bf16[4,192,384]{2,1,0:T(8,128)(2,1)}, u32[]{:S(2)}, u32[]{:S(2)}) collective-permute-start(bf16[4,192,384]{2,1,0:T(8,128)(2,1)} %collective-permute-done.37.refs_1_), channel_id=1, source_target_pairs={{0,2},{1,5},{2,0},{3,7},{4,6},{5,1},{6,4},{7,3},{8,10},{9,13},{10,... | collective-permute-start | bytes 1769480 | tf_op jit(solution)/shard_map/ppermute | solution.py:117
  242.2 18.0 %collective-permute-start.32 = (bf16[4,48,1536]{2,1,0:T(8,128)(2,1)}, bf16[4,48,1536]{2,1,0:T(8,128)(2,1)}, u32[]{:S(2)}, u32[]{:S(2)}) collective-permute-start(bf16[4,48,1536]{2,1,0:T(8,128)(2,1)} %collective-permute-done.28.refs_3_), channel_id=1, source_target_pairs={{0,1},{1,0},{2,3},{3,2},{4,5},{5,4},{6,7},{7,6},{8,9},{9,8},{10,11... | collective-permute-start | bytes 1769480 | tf_op jit(solution)/shard_map/ppermute | solution.py:117
  248.2 305.4 %collective-permute-start.18 = (bf16[4,48,1920]{2,1,0:T(8,128)(2,1)}, bf16[4,48,1920]{2,1,0:T(8,128)(2,1)}, u32[]{:S(2)}, u32[]{:S(2)}) collective-permute-start(bf16[4,48,1920]{2,1,0:T(8,128)(2,1)} %pad_maximum_fusion.refs_0_), channel_id=1, source_target_pairs={{0,1},{1,0},{2,3},{3,2},{4,5},{5,4},{6,7},{7,6},{8,9},{9,8},{10,11... | collective-permute-start | bytes 2211848 | tf_op jit(solution)/shard_map/ppermute | solution.py:117
  248.3 305.2 %collective-permute-start.19 = (bf16[4,48,1920]{2,1,0:T(8,128)(2,1)}, bf16[4,48,1920]{2,1,0:T(8,128)(2,1)}, u32[]{:S(2)}, u32[]{:S(2)}) collective-permute-start(bf16[4,48,1920]{2,1,0:T(8,128)(2,1)} %collective-permute-done.15.refs_1_), channel_id=1, source_target_pairs={{0,1},{1,0},{2,3},{3,2},{4,5},{5,4},{6,7},{7,6},{8,9},{9,8},{10,11... | collective-permute-start | bytes 2211848 | tf_op jit(solution)/shard_map/ppermute | solution.py:117
  254.5 299.0 %collective-permute-start.20 = (bf16[4,48,1920]{2,1,0:T(8,128)(2,1)}, bf16[4,48,1920]{2,1,0:T(8,128)(2,1)}, u32[]{:S(2)}, u32[]{:S(2)}) collective-permute-start(bf16[4,48,1920]{2,1,0:T(8,128)(2,1)} %collective-permute-done.16.refs_2_), channel_id=1, source_target_pairs={{0,1},{1,0},{2,3},{3,2},{4,5},{5,4},{6,7},{7,6},{8,9},{9,8},{10,11... | collective-permute-start | bytes 2211848 | tf_op jit(solution)/shard_map/ppermute | solution.py:117
  254.5 299.0 %collective-permute-start.21 = (bf16[4,48,1920]{2,1,0:T(8,128)(2,1)}, bf16[4,48,1920]{2,1,0:T(8,128)(2,1)}, u32[]{:S(2)}, u32[]{:S(2)}) collective-permute-start(bf16[4,48,1920]{2,1,0:T(8,128)(2,1)} %collective-permute-done.17.refs_3_), channel_id=1, source_target_pairs={{0,1},{1,0},{2,3},{3,2},{4,5},{5,4},{6,7},{7,6},{8,9},{9,8},{10,11... | collective-permute-start | bytes 2211848 | tf_op jit(solution)/shard_map/ppermute | solution.py:117
  260.2 149.2 %collective-permute-start.43 = (bf16[4,192,384]{2,1,0:T(8,128)(2,1)}, bf16[4,192,384]{2,1,0:T(8,128)(2,1)}, u32[]{:S(2)}, u32[]{:S(2)}) collective-permute-start(bf16[4,192,384]{2,1,0:T(8,128)(2,1)} %collective-permute-done.39.refs_3_), channel_id=1, source_target_pairs={{0,1},{1,0},{2,3},{3,2},{4,5},{5,4},{6,7},{7,6},{8,9},{9,8},{10,11... | collective-permute-start | bytes 1769480 | tf_op jit(solution)/shard_map/ppermute | solution.py:117
  883.6 89.3 %collective-permute-start.55 = (bf16[768,384]{1,0:T(8,128)(2,1)}, bf16[768,384]{1,0:T(8,128)(2,1)}, u32[]{:S(2)}, u32[]{:S(2)}) collective-permute-start(bf16[768,384]{1,0:T(8,128)(2,1)} %convolution_convert_fusion.12), channel_id=1, source_target_pairs={{0,1},{1,0},{2,3},{3,2},{4,5},{5,4},{6,7},{7,6},{8,9},{9,8},{10,11... | collective-permute-start | bytes 1769480 | tf_op jit(solution)/shard_map/ppermute | solution.py:117
  893.3 103.4 %collective-permute-start.45 = (bf16[768,384]{1,0:T(8,128)(2,1)}, bf16[768,384]{1,0:T(8,128)(2,1)}, u32[]{:S(2)}, u32[]{:S(2)}) collective-permute-start(bf16[768,384]{1,0:T(8,128)(2,1)} %convolution_convert_fusion.16), channel_id=1, source_target_pairs={{0,1},{1,0},{2,3},{3,2},{4,5},{5,4},{6,7},{7,6},{8,9},{9,8},{10,11... | collective-permute-start | bytes 1769480 | tf_op jit(solution)/shard_map/ppermute | solution.py:117
  927.6 45.3 %collective-permute-start.53 = (bf16[768,384]{1,0:T(8,128)(2,1)}, bf16[768,384]{1,0:T(8,128)(2,1)}, u32[]{:S(2)}, u32[]{:S(2)}) collective-permute-start(bf16[768,384]{1,0:T(8,128)(2,1)} %convolution_convert_fusion.14), channel_id=1, source_target_pairs={{0,1},{1,0},{2,3},{3,2},{4,5},{5,4},{6,7},{7,6},{8,9},{9,8},{10,11... | collective-permute-start | bytes 1769480 | tf_op jit(solution)/shard_map/ppermute | solution.py:117
  944.8 25.2 %collective-permute-start.54 = (bf16[768,768]{0,1:T(8,128)(2,1)}, bf16[768,768]{0,1:T(8,128)(2,1)}, u32[]{:S(2)}, u32[]{:S(2)}) collective-permute-start(bf16[768,768]{0,1:T(8,128)(2,1)} %fusion.67), channel_id=1, source_target_pairs={{0,1},{1,0},{2,3},{3,2},{4,5},{5,4},{6,7},{7,6},{8,9},{9,8},{10,11... | collective-permute-start | bytes 3538952 | tf_op jit(solution)/shard_map/ppermute | solution.py:117
  950.8 46.0 %collective-permute-start.44 = (bf16[768,1152]{1,0:T(8,128)(2,1)}, bf16[768,1152]{1,0:T(8,128)(2,1)}, u32[]{:S(2)}, u32[]{:S(2)}) collective-permute-start(bf16[768,1152]{1,0:T(8,128)(2,1)} %convolution_convert_fusion.4), channel_id=1, source_target_pairs={{0,1},{1,0},{2,3},{3,2},{4,5},{5,4},{6,7},{7,6},{8,9},{9,8},{10,11... | collective-permute-start | bytes 5308424 | tf_op jit(solution)/shard_map/ppermute | solution.py:117
  970.0 41.4 %collective-permute-start.69 = (bf16[3072,384]{1,0:T(8,128)(2,1)}, bf16[3072,384]{1,0:T(8,128)(2,1)}, u32[]{:S(2)}, u32[]{:S(2)}) collective-permute-start(bf16[3072,384]{1,0:T(8,128)(2,1)} %convolution_convert_fusion), channel_id=1, source_target_pairs={{0,1},{1,0},{2,3},{3,2},{4,5},{5,4},{6,7},{7,6},{8,9},{9,8},{10,11... | collective-permute-start | bytes 7077896 | tf_op jit(solution)/shard_map/ppermute | solution.py:117
  977.5 16.5 %collective-permute-start.56 = (bf16[4,2,48,1536]{3,2,1,0:T(8,128)(2,1)}, bf16[4,2,48,1536]{3,2,1,0:T(8,128)(2,1)S(1)}, u32[]{:S(2)}, u32[]{:S(2)}) collective-permute-start(bf16[4,2,48,1536]{3,2,1,0:T(8,128)(2,1)} %get-tuple-element.36), channel_id=1, source_target_pairs={{0,2},{1,5},{2,0},{3,7},{4,6},{5,1},{6,4},{7,3},{8,10},{9,13},{10,... | collective-permute-start | bytes 3538952 | tf_op jit(solution)/shard_map/ppermute | solution.py:117
  979.8 42.6 %collective-permute-start.62 = (bf16[768,1536]{1,0:T(8,128)(2,1)}, bf16[768,1536]{1,0:T(8,128)(2,1)}, u32[]{:S(2)}, u32[]{:S(2)}) collective-permute-start(bf16[768,1536]{1,0:T(8,128)(2,1)} %convolution_convert_fusion.6), channel_id=1, source_target_pairs={{0,1},{1,0},{2,3},{3,2},{4,5},{5,4},{6,7},{7,6},{8,9},{9,8},{10,11... | collective-permute-start | bytes 7077896 | tf_op jit(solution)/shard_map/ppermute | solution.py:117
  1001.7 29.8 %collective-permute-start.47 = (bf16[4,2,48,1664]{3,2,1,0:T(8,128)(2,1)}, bf16[4,2,48,1664]{3,2,1,0:T(8,128)(2,1)}, u32[]{:S(2)}, u32[]{:S(2)}) collective-permute-start(bf16[4,2,48,1664]{3,2,1,0:T(8,128)(2,1)} %get-tuple-element.34), channel_id=1, source_target_pairs={{0,2},{1,5},{2,0},{3,7},{4,6},{5,1},{6,4},{7,3},{8,10},{9,13},{10,... | collective-permute-start | bytes 3833864 | tf_op jit(solution)/shard_map/ppermute | solution.py:117
  1007.5 20.4 %collective-permute-start.58 = (bf16[48,1536]{1,0:T(8,128)(2,1)S(1)}, bf16[48,1536]{1,0:T(8,128)(2,1)}, u32[]{:S(2)}, u32[]{:S(2)}) collective-permute-start(bf16[48,1536]{1,0:T(8,128)(2,1)S(1)} %get-tuple-element.127), channel_id=1, source_target_pairs={{0,8},{1,9},{2,10},{3,11},{4,12},{5,13},{6,14},{7,15},{8,16},{9,17... | collective-permute-start | bytes 442376 | tf_op jit(solution)/shard_map/ppermute | solution.py:117
  1007.6 22.5 %collective-permute-start.60 = (bf16[48,1536]{1,0:T(8,128)(2,1)S(1)}, bf16[48,1536]{1,0:T(8,128)(2,1)}, u32[]{:S(2)}, u32[]{:S(2)}) collective-permute-start(bf16[48,1536]{1,0:T(8,128)(2,1)S(1)} %get-tuple-element.128), channel_id=1, source_target_pairs={{0,24},{1,25},{2,26},{3,27},{4,28},{5,29},{6,30},{7,31},{8,0},{9,1... | collective-permute-start | bytes 442376 | tf_op jit(solution)/shard_map/ppermute | solution.py:117
  1011.4 18.7 %collective-permute-start.59 = (bf16[48,1536]{1,0:T(8,128)(2,1)S(1)}, bf16[48,1536]{1,0:T(8,128)(2,1)}, u32[]{:S(2)}, u32[]{:S(2)}) collective-permute-start(bf16[48,1536]{1,0:T(8,128)(2,1)S(1)} %get-tuple-element.129), channel_id=1, source_target_pairs={{0,16},{1,17},{2,18},{3,19},{4,20},{5,21},{6,22},{7,23},{8,24},{9,... | collective-permute-start | bytes 442376 | tf_op jit(solution)/shard_map/ppermute | solution.py:117
  1022.4 32.9 %collective-permute-start.70 = (bf16[4,2,192,384]{3,2,1,0:T(8,128)(2,1)}, bf16[4,2,192,384]{3,2,1,0:T(8,128)(2,1)}, u32[]{:S(2)}, u32[]{:S(2)}) collective-permute-start(bf16[4,2,192,384]{3,2,1,0:T(8,128)(2,1)} %get-tuple-element.40), channel_id=1, source_target_pairs={{0,2},{1,5},{2,0},{3,7},{4,6},{5,1},{6,4},{7,3},{8,10},{9,13},{10,... | collective-permute-start | bytes 3538952 | tf_op jit(solution)/shard_map/ppermute | solution.py:117
  1028.0 40.2 %collective-permute-start.63 = (bf16[4,2,48,1536]{3,2,1,0:T(8,128)(2,1)}, bf16[4,2,48,1536]{3,2,1,0:T(8,128)(2,1)S(1)}, u32[]{:S(2)}, u32[]{:S(2)}) collective-permute-start(bf16[4,2,48,1536]{3,2,1,0:T(8,128)(2,1)} %get-tuple-element.38), channel_id=1, source_target_pairs={{0,2},{1,5},{2,0},{3,7},{4,6},{5,1},{6,4},{7,3},{8,10},{9,13},{10,... | collective-permute-start | bytes 3538952 | tf_op jit(solution)/shard_map/ppermute | solution.py:117
  1032.7 17.3 %collective-permute-start.48 = (bf16[4,48,1664]{2,1,0:T(8,128)(2,1)S(1)}, bf16[4,48,1664]{2,1,0:T(8,128)(2,1)S(1)}, u32[]{:S(2)}, u32[]{:S(2)}) collective-permute-start(bf16[4,48,1664]{2,1,0:T(8,128)(2,1)S(1)} %fusion.103), channel_id=1, source_target_pairs={{0,4},{1,3},{2,6},{3,1},{4,0},{5,7},{6,2},{7,5},{8,12},{9,11},{10,... | collective-permute-start | bytes 1916936 | tf_op jit(solution)/shard_map/ppermute | solution.py:117
  1054.1 13.9 %collective-permute-start.50 = (bf16[48,1664]{1,0:T(8,128)(2,1)S(1)}, bf16[48,1664]{1,0:T(8,128)(2,1)S(1)}, u32[]{:S(2)}, u32[]{:S(2)}) collective-permute-start(bf16[48,1664]{1,0:T(8,128)(2,1)S(1)} %get-tuple-element.120), channel_id=1, source_target_pairs={{0,16},{1,17},{2,18},{3,19},{4,20},{5,21},{6,22},{7,23},{8,24},{9,... | collective-permute-start | bytes 479240 | tf_op jit(solution)/shard_map/ppermute | solution.py:117
  1057.3 16.7 %collective-permute-start.71 = (bf16[4,192,384]{2,1,0:T(8,128)(2,1)}, bf16[4,192,384]{2,1,0:T(8,128)(2,1)S(1)}, u32[]{:S(2)}, u32[]{:S(2)}) collective-permute-start(bf16[4,192,384]{2,1,0:T(8,128)(2,1)} %fusion.106), channel_id=1, source_target_pairs={{0,4},{1,3},{2,6},{3,1},{4,0},{5,7},{6,2},{7,5},{8,12},{9,11},{10,... | collective-permute-start | bytes 1769480 | tf_op jit(solution)/shard_map/ppermute | solution.py:117
  1078.0 16.1 %collective-permute-start.73 = (bf16[192,384]{1,0:T(8,128)(2,1)S(1)}, bf16[192,384]{1,0:T(8,128)(2,1)S(1)}, u32[]{:S(2)}, u32[]{:S(2)}) collective-permute-start(bf16[192,384]{1,0:T(8,128)(2,1)S(1)} %get-tuple-element.123), channel_id=1, source_target_pairs={{0,16},{1,17},{2,18},{3,19},{4,20},{5,21},{6,22},{7,23},{8,24},{9,... | collective-permute-start | bytes 442376 | tf_op jit(solution)/shard_map/ppermute | solution.py:117
  1084.5 18.5 %collective-permute-start.66 = (bf16[48,1536]{1,0:T(8,128)(2,1)S(1)}, bf16[48,1536]{1,0:T(8,128)(2,1)S(1)}, u32[]{:S(2)}, u32[]{:S(2)}) collective-permute-start(bf16[48,1536]{1,0:T(8,128)(2,1)S(1)} %get-tuple-element.126), channel_id=1, source_target_pairs={{0,16},{1,17},{2,18},{3,19},{4,20},{5,21},{6,22},{7,23},{8,24},{9,... | collective-permute-start | bytes 442376 | tf_op jit(solution)/shard_map/ppermute | solution.py:117
  (141 other events, 1762.1 us)

commit v2 on v1

--- a/solution.py
+++ b/solution.py
@@ -127,46 +127,52 @@
     return lax.dynamic_slice_in_dim(value, side * width, width, axis=1)
 
 
-def assemble_body(rows, widths, *refs):
-    parts, outs, sem = refs[:8], refs[8:-1], refs[-1]
-    z, x, y, core = place()
-    copies = []
-    for theirs in range(2):
-        side = 1 - core if theirs else core
-        for j in range(4):
-            flip_x = (0, 1 - side, side, 1)[j]
-            flip_y = (0, side, 1 - side, 1)[j]
-            at_x = lax.rem(x + flip_x, 2)
-            at_y = lax.rem(y + flip_y, 2)
-            for k in range(4):
-                at_z = lax.rem(z + 4 - k, 4)
+def assemble_body(widths, spot, *refs):
+    parts, outs = refs[:8], refs[8:]
+    x, y, core = spot[1], spot[2], spot[3]
+
+    def place_all(mine):
+        for theirs in range(2):
+            side = 1 - mine if theirs else mine
+            for j in range(4):
+                flip_x = (0, 1 - side, side, 1)[j]
+                flip_y = (0, side, 1 - side, 1)[j]
                 offset = 0
                 for width, out in zip(widths, outs):
                     part = width // 2
-                    target = pl.ds(pl.multiple_of(side * part, 128), part)
-                    copies.append(
-                        pltpu.make_async_copy(
-                            parts[theirs * 4 + j].at[k, :, pl.ds(offset, part)],
-                            out.at[at_z, at_x, at_y, :, target],
-                            sem,
-                        )
-                    )
+                    out[0, x ^ flip_x, y ^ flip_y, :, side * part : (side + 1) * part] = parts[
+                        theirs * 4 + j
+                    ][0, :, offset : offset + part]
                     offset += part
-    for copy in copies:
-        copy.start()
-    for copy in copies:
-        copy.wait()
-
-
-def assemble(parts, rows, widths):
+
+    @pl.when(core == 0)
+    def _():
+        place_all(0)
+
+    @pl.when(core == 1)
+    def _():
+        place_all(1)
+
+
+def assemble(parts, rows, widths, spot):
+    half = sum(widths) // 2
     outs = pl.pallas_call(
-        functools.partial(assemble_body, rows, widths),
+        functools.partial(assemble_body, widths),
         out_shape=[jax.ShapeDtypeStruct((4, 2, 2, 2 * rows, w), jnp.bfloat16) for w in widths],
-        in_specs=[pl.BlockSpec(memory_space=pl.ANY)] * 8,
-        out_specs=[pl.BlockSpec(memory_space=pl.ANY)] * len(widths),
-        scratch_shapes=[pltpu.SemaphoreType.DMA],
+        grid_spec=pltpu.PrefetchScalarGridSpec(
+            num_scalar_prefetch=1,
+            grid=(4,),
+            in_specs=[pl.BlockSpec((1, 2 * rows, half), lambda k, spot: (k, 0, 0))] * 8,
+            out_specs=[
+                pl.BlockSpec(
+                    (1, 2, 2, 2 * rows, w),
+                    lambda k, spot: (lax.rem(spot[0] + 4 - k, 4), 0, 0, 0, 0),
+                )
+                for w in widths
+            ],
+        ),
         name="assemble",
-    )(*parts)
+    )(spot, *parts)
     return [o.reshape(32 * rows, w) for o, w in zip(outs, widths)]
 
 
@@ -185,7 +191,7 @@
     both = move(one, SECOND)
     parts = [line, one, two, both]
     parts = parts + [move(p, CORE) for p in parts]
-    return assemble(parts, rows, widths)
+    return assemble(parts, rows, widths, jnp.stack(place()).astype(jnp.int32))
 
 
 def split_body(count, which, *refs):

time: 1110 us -> 556 us (0.50)
  Pallas kernels: 606 us -> 42.5 us
    pallas_call x4, Pallas kernels: 588 us -> 24.2 us  [assemble(): pl.pallas_call(functools.partial(assemble_body, widths), out_shape=[jax.S...]
  transfers between devices with their start and end apart: 76 -> 76, of which waited for: 21 -> 23; matrix products, arithmetic and copies ran while one was open for 15% -> 30% of each run, Pallas kernels for 39% -> 6%
where the time goes in v2:
time: 556 us; the launch traced here: 550 us
  matrix products  184 us (33%)
  waiting for transfers between devices  113 us (20%)
  local copies, waits for them, and re-layouts  102 us (18%)
  starting transfers between devices  68.7 us (12%)
  Pallas kernels  42.5 us (8%)
  other arithmetic  36.8 us (7%)
    ppermute x76, waiting for transfers between devices, move(): return lax.ppermute(value, AXES, perm)  113 us
    ppermute x76, starting transfers between devices, move(): return lax.ppermute(value, AXES, perm)  68.7 us
    dot_general x16, matrix products, contract_low(): lax.dot_general(value, upstream_gradient, (((0,), (0,)), ((), ())), prefe...  38.8 us
    dot_general x2, matrix products, attend_backward(): jnp.einsum('shqk,skhe->sqhe', grad_scores, key, preferred_element_type=jn...  38.3 us
    dot_general x2, matrix products, attend_backward(): jnp.einsum('shqk,sqhe->skhe', grad_scores, query, preferred_element_type=...  38 us
    dot_general x7, matrix products, back_project(): jnp.einsum('rmj,aj->rma', upstream_gradient, weight_matrix, preferred_ele...  25.2 us
    pallas_call x4, Pallas kernels, assemble(): pl.pallas_call(functools.partial(assemble_body, widths), out_shape=[jax.S...  24.2 us
    dot_general x7, matrix products, project(): jnp.einsum('owh,ht->owt', value_tensor, weight_matrix, preferred_element_...  21 us
  transfers between devices with their start and end apart: 76, of which 23 were waited for; matrix products, arithmetic and copies ran while one was open for 30% of the time, Pallas kernels for 6%

profile of v2, /device:TPU:0, one launch (start us, length us, event | category | flops | bytes accessed | tf_op | source)
XLA Modules:
  0.0 550.2 jit_solution(6532951950585523294)
XLA Ops:
  17.3 4.9 collective-permute-start.3
  26.0 7.5 %collective-permute-done.2 = bf16[48,1280]{1,0:T(8,128)(2,1)S(1)} collective-permute-done((bf16[48,1280]{1,0:T(8,128)(2,1)S(1)}, bf16[48,1280]{1,0:T(8,128)(2,1)S(1)}, u32[]{:S(2)}, u32[]{:S(2)}) %collective-permute-start.2) | collective-permute-done | bytes 122912 | tf_op jit(solution)/shard_map/ppermute | solution.py:117
  41.9 4.5 collective-permute-start.24
  46.3 10.1 %collective-permute-done.35 = bf16[192,384]{1,0:T(8,128)(2,1)S(1)} collective-permute-done((bf16[192,384]{1,0:T(8,128)(2,1)S(1)}, bf16[192,384]{1,0:T(8,128)(2,1)S(1)}, u32[]{:S(2)}, u32[]{:S(2)}) %collective-permute-start.35) | collective-permute-done | bytes 147488 | tf_op jit(solution)/shard_map/ppermute | solution.py:117
  56.5 3.8 collective-permute-start.14
  68.2 12.3 %collective-permute-done.13 = bf16[48,1920]{1,0:T(8,128)(2,1)S(1)} collective-permute-done((bf16[48,1920]{1,0:T(8,128)(2,1)S(1)}, bf16[48,1920]{1,0:T(8,128)(2,1)S(1)}, u32[]{:S(2)}, u32[]{:S(2)}) %collective-permute-start.13) | collective-permute-done | bytes 184352 | tf_op jit(solution)/shard_map/ppermute | solution.py:117
  88.0 5.4 assemble.4
  101.9 7.1 %collective-permute-done.38.refs_2_ = bf16[4,192,384]{2,1,0:T(8,128)(2,1)} collective-permute-done((bf16[4,192,384]{2,1,0:T(8,128)(2,1)S(1)}, bf16[4,192,384]{2,1,0:T(8,128)(2,1)}, u32[]{:S(2)}, u32[]{:S(2)}) %collective-permute-start.38) | collective-permute-done | bytes 589856 | tf_op jit(solution)/shard_map/ppermute | solution.py:117
  109.0 3.8 collective-permute-done.37.refs_1_
  113.2 15.5 %collective-permute-done.15.refs_1_ = bf16[4,48,1920]{2,1,0:T(8,128)(2,1)} collective-permute-done((bf16[4,48,1920]{2,1,0:T(8,128)(2,1)}, bf16[4,48,1920]{2,1,0:T(8,128)(2,1)}, u32[]{:S(2)}, u32[]{:S(2)}) %collective-permute-start.15) | collective-permute-done | bytes 737312 | tf_op jit(solution)/shard_map/ppermute | solution.py:117
  129.7 3.6 convolution_convert_fusion.2
  141.2 5.7 %collective-permute-done.39.refs_3_ = bf16[4,192,384]{2,1,0:T(8,128)(2,1)} collective-permute-done((bf16[4,192,384]{2,1,0:T(8,128)(2,1)}, bf16[4,192,384]{2,1,0:T(8,128)(2,1)}, u32[]{:S(2)}, u32[]{:S(2)}) %collective-permute-start.39) | collective-permute-done | bytes 589856 | tf_op jit(solution)/shard_map/ppermute | solution.py:117
  157.8 5.9 %assemble.6 = bf16[4,2,2,48,3072]{4,3,2,1,0:T(8,128)(2,1)} custom-call(s32[4]{0:T(128)} %pad_add_fusion.spot, bf16[4,48,1536]{2,1,0:T(8,128)(2,1)} %copy-done.25, bf16[4,48,1536]{2,1,0:T(8,128)(2,1)} %collective-permute-done.26.refs_1_, bf16[4,48,1536]{2,1,0:T(8,128)(2,1)} %collective-permute-done.27.refs_2_, ...), custom_call_target="tpu_custom_call" | custom-call | tf_op jit(solution)/shard_map/assemble/pallas_call | solution.py:159
  163.7 5.9 %assemble.7 = bf16[4,2,2,192,768]{4,3,2,1,0:T(8,128)(2,1)} custom-call(s32[4]{0:T(128)} %pad_add_fusion.spot, bf16[4,192,384]{2,1,0:T(8,128)(2,1)} %copy-done.26, bf16[4,192,384]{2,1,0:T(8,128)(2,1)} %collective-permute-done.37.refs_1_, bf16[4,192,384]{2,1,0:T(8,128)(2,1)} %collective-permute-done.38.refs_2_, ...), custom_call_target="tpu_custom_call" | custom-call | tf_op jit(solution)/shard_map/assemble/pallas_call | solution.py:159
  169.6 7.1 %assemble.5 = (bf16[4,2,2,48,768]{4,3,2,1,0:T(8,128)(2,1)}, bf16[4,2,2,48,768]{4,3,2,1,0:T(8,128)(2,1)}, bf16[4,2,2,48,1536]{4,3,2,1,0:T(8,128)(2,1)}, bf16[4,2,2,48,768]{4,3,2,1,0:T(8,128)(2,1)}) custom-call(s32[4]{0:T(128)} %pad_add_fusion.spot, bf16[4,48,1920]{2,1,0:T(8,128)(2,1)} %pad_maximum_fusion.refs_0_, ...), custom_call_target="tpu_custom_call" | custom-call | tf_op jit(solution)/shard_map/assemble/pallas_call | solution.py:159
  181.2 4.3 fusion.20
  201.5 4.5 multiply_convert_fusion.1
  206.1 5.6 %fusion.187 = (bf16[3072]{0:T(1024)(128)(2,1)}, bf16[4,96,3072]{2,1,0:T(8,128)(2,1)S(1)}) fusion(f32[4,96,3072]{2,1,0:T(8,128)S(1)} %get-tuple-element.178, bf16[4,96,768]{2,1,0:T(8,128)(2,1)S(1)} %copy-done.53, bf16[3072,768,1]{1,0,2:T(8,128)(2,1)S(1)} %bitcast.309), kind=kOutput, calls=%fused_computation.316 | convolution fusion | flops 1836708864 | bytes 12392448 | tf_op jit(solution)/shard_map/rmj,aj->rma/dot_general | solution.py:44
  211.7 2.9 multiply_reduce_fusion.3
  219.5 4.5 fusion.188
  223.9 4.7 fusion.58
  228.6 33.7 %fusion.75 = bf16[4,12,64,96]{3,2,1,0:T(8,128)(2,1)} fusion(bf16[4,196,12,64]{1,3,2,0:T(8,128)(2,1)} %bitcast.291, f32[4,12,96,196]{3,2,1,0:T(8,128)} %fusion.188, f32[4,12,96,196]{3,2,1,0:T(8,128)} %copy-done, f32[4,12,96]{2,1,0:T(8,128)S(1)} %copy-done.71), kind=kOutput, calls=%fused_computation.82 | convolution fusion | flops 124033728 | bytes 9037824 | tf_op jit(solution)/shard_map/shqk,skhe->sqhe/dot_general | solution.py:80
  262.3 33.4 %fusion.55 = bf16[4,12,64,196]{3,2,1,0:T(8,128)(2,1)} fusion(bf16[4,96,12,64]{1,3,2,0:T(8,128)(2,1)S(1)} %bitcast.315, f32[4,12,96,196]{3,2,1,0:T(8,128)} %fusion.188, f32[4,12,96,196]{3,2,1,0:T(8,128)} %copy-done, f32[4,12,96]{2,1,0:T(8,128)S(1)} %copy-done.71), kind=kOutput, calls=%fused_computation.65 | convolution fusion | flops 124340928 | bytes 9037824 | tf_op jit(solution)/shard_map/shqk,sqhe->skhe/dot_general | solution.py:81
  295.8 3.4 multiply_reduce_fusion.4
  303.7 3.5 fusion.189
  309.1 4.6 fusion.68
  313.7 4.6 fusion.71
  329.3 4.6 concatenate.235
  343.2 5.3 fusion.88
  375.5 4.3 concatenate.234
  393.9 3.1 convolution_convert_fusion.1
  397.0 2.9 convolution_convert_fusion.6
  402.8 4.9 convolution_convert_fusion
  407.7 5.2 fusion.81
  415.7 4.5 split_add.5
  427.5 5.7 %fusion.21 = f32[4,196,768]{2,1,0:T(8,128)} fusion(bf16[768,1536,1]{1,0,2:T(8,128)(2,1)} %bitcast.376, bf16[4,196,768]{2,1,0:T(8,128)(2,1)S(1)} %copy-done.35, bf16[4,196,768]{2,1,0:T(8,128)(2,1)} %copy.172), kind=kOutput, calls=%fused_computation.33 | convolution fusion | flops 1854504960 | bytes 7176192 | tf_op jit(solution)/shard_map/rmj,aj->rma/dot_general | solution.py:44
  433.2 3.5 collective-permute-done.56
  441.0 4.9 split_add.4
  450.4 3.8 collective-permute-start.60
  459.5 4.6 split_add.7
  466.5 4.3 split_add.6
  480.1 12.8 %collective-permute-done.48 = bf16[4,48,1664]{2,1,0:T(8,128)(2,1)S(1)} collective-permute-done((bf16[4,48,1664]{2,1,0:T(8,128)(2,1)S(1)}, bf16[4,48,1664]{2,1,0:T(8,128)(2,1)S(1)}, u32[]{:S(2)}, u32[]{:S(2)}) %collective-permute-start.48) | collective-permute-done | bytes 639008 | tf_op jit(solution)/shard_map/ppermute | solution.py:117
  493.8 3.2 collective-permute-start.51
  503.7 7.2 %collective-permute-done.50 = bf16[48,1664]{1,0:T(8,128)(2,1)S(1)} collective-permute-done((bf16[48,1664]{1,0:T(8,128)(2,1)S(1)}, bf16[48,1664]{1,0:T(8,128)(2,1)S(1)}, u32[]{:S(2)}, u32[]{:S(2)}) %collective-permute-start.50) | collective-permute-done | bytes 159776 | tf_op jit(solution)/shard_map/ppermute | solution.py:117
  518.2 3.8 collective-permute-start.74
  524.0 3.4 collective-permute-start.67
  528.7 9.7 %collective-permute-done.73 = bf16[192,384]{1,0:T(8,128)(2,1)S(1)} collective-permute-done((bf16[192,384]{1,0:T(8,128)(2,1)S(1)}, bf16[192,384]{1,0:T(8,128)(2,1)S(1)}, u32[]{:S(2)}, u32[]{:S(2)}) %collective-permute-start.73) | collective-permute-done | bytes 147488 | tf_op jit(solution)/shard_map/ppermute | solution.py:117
  538.7 8.1 %collective-permute-done.66 = bf16[48,1536]{1,0:T(8,128)(2,1)S(1)} collective-permute-done((bf16[48,1536]{1,0:T(8,128)(2,1)S(1)}, bf16[48,1536]{1,0:T(8,128)(2,1)S(1)}, u32[]{:S(2)}, u32[]{:S(2)}) %collective-permute-start.66) | collective-permute-done | bytes 147488 | tf_op jit(solution)/shard_map/ppermute | solution.py:117
  (547 shorter events, 224.9 us)
Async XLA Ops:
  3.8 35.8 %collective-permute-start.11 = (bf16[24,1920]{1,0:T(8,128)(2,1)}, bf16[24,1920]{1,0:T(8,128)(2,1)S(1)}, u32[]{:S(2)}, u32[]{:S(2)}) collective-permute-start(bf16[24,1920]{1,0:T(8,128)(2,1)} %get-tuple-element.144), channel_id=1, source_target_pairs={{0,1},{1,0},{2,3},{3,2},{4,5},{5,4},{6,7},{7,6},{8,9},{9,8},{10,11... | collective-permute-start | bytes 276488 | tf_op jit(solution)/shard_map/ppermute | solution.py:117
  8.7 28.9 %collective-permute-start.22 = (bf16[24,1536]{1,0:T(8,128)(2,1)S(1)}, bf16[24,1536]{1,0:T(8,128)(2,1)S(1)}, u32[]{:S(2)}, u32[]{:S(2)}) collective-permute-start(bf16[24,1536]{1,0:T(8,128)(2,1)S(1)} %get-tuple-element.154), channel_id=1, source_target_pairs={{0,1},{1,0},{2,3},{3,2},{4,5},{5,4},{6,7},{7,6},{8,9},{9,8},{10,11... | collective-permute-start | bytes 221192 | tf_op jit(solution)/shard_map/ppermute | solution.py:117
  33.5 28.3 %collective-permute-start.4 = (bf16[4,48,1280]{2,1,0:T(8,128)(2,1)S(1)}, bf16[4,48,1280]{2,1,0:T(8,128)(2,1)S(1)}, u32[]{:S(2)}, u32[]{:S(2)}) collective-permute-start(bf16[4,48,1280]{2,1,0:T(8,128)(2,1)S(1)} %pad_maximum_fusion.3.refs_0_), channel_id=1, source_target_pairs={{0,4},{1,3},{2,6},{3,1},{4,0},{5,7},{6,2},{7,5},{8,12},{9,11},{10,... | collective-permute-start | bytes 1474568 | tf_op jit(solution)/shard_map/ppermute | solution.py:117
  36.6 19.8 %collective-permute-start.35 = (bf16[192,384]{1,0:T(8,128)(2,1)S(1)}, bf16[192,384]{1,0:T(8,128)(2,1)S(1)}, u32[]{:S(2)}, u32[]{:S(2)}) collective-permute-start(bf16[192,384]{1,0:T(8,128)(2,1)S(1)} %maximum_select_fusion.5), channel_id=1, source_target_pairs={{0,16},{1,17},{2,18},{3,19},{4,20},{5,21},{6,22},{7,23},{8,24},{9,... | collective-permute-start | bytes 442376 | tf_op jit(solution)/shard_map/ppermute | solution.py:117
  37.6 18.8 %collective-permute-start.34 = (bf16[192,384]{1,0:T(8,128)(2,1)S(1)}, bf16[192,384]{1,0:T(8,128)(2,1)S(1)}, u32[]{:S(2)}, u32[]{:S(2)}) collective-permute-start(bf16[192,384]{1,0:T(8,128)(2,1)S(1)} %maximum_select_fusion.5), channel_id=1, source_target_pairs={{0,8},{1,9},{2,10},{3,11},{4,12},{5,13},{6,14},{7,15},{8,16},{9,17... | collective-permute-start | bytes 442376 | tf_op jit(solution)/shard_map/ppermute | solution.py:117
  39.6 20.7 %collective-permute-start.25 = (bf16[48,1536]{1,0:T(8,128)(2,1)S(1)}, bf16[48,1536]{1,0:T(8,128)(2,1)S(1)}, u32[]{:S(2)}, u32[]{:S(2)}) collective-permute-start(bf16[48,1536]{1,0:T(8,128)(2,1)S(1)} %maximum_select_fusion.3), channel_id=1, source_target_pairs={{0,24},{1,25},{2,26},{3,27},{4,28},{5,29},{6,30},{7,31},{8,0},{9,1... | collective-permute-start | bytes 442376 | tf_op jit(solution)/shard_map/ppermute | solution.py:117
  41.9 21.4 %collective-permute-start.24 = (bf16[48,1536]{1,0:T(8,128)(2,1)S(1)}, bf16[48,1536]{1,0:T(8,128)(2,1)S(1)}, u32[]{:S(2)}, u32[]{:S(2)}) collective-permute-start(bf16[48,1536]{1,0:T(8,128)(2,1)S(1)} %maximum_select_fusion.3), channel_id=1, source_target_pairs={{0,16},{1,17},{2,18},{3,19},{4,20},{5,21},{6,22},{7,23},{8,24},{9,... | collective-permute-start | bytes 442376 | tf_op jit(solution)/shard_map/ppermute | solution.py:117
  60.3 20.8 %collective-permute-start.5 = (bf16[4,48,1280]{2,1,0:T(8,128)(2,1)S(1)}, bf16[4,48,1280]{2,1,0:T(8,128)(2,1)S(1)}, u32[]{:S(2)}, u32[]{:S(2)}) collective-permute-start(bf16[4,48,1280]{2,1,0:T(8,128)(2,1)S(1)} %pad_maximum_fusion.3.refs_0_), channel_id=1, source_target_pairs={{0,2},{1,5},{2,0},{3,7},{4,6},{5,1},{6,4},{7,3},{8,10},{9,13},{10,... | collective-permute-start | bytes 1474568 | tf_op jit(solution)/shard_map/ppermute | solution.py:117
  61.8 19.3 %collective-permute-start.6 = (bf16[4,48,1280]{2,1,0:T(8,128)(2,1)S(1)}, bf16[4,48,1280]{2,1,0:T(8,128)(2,1)S(1)}, u32[]{:S(2)}, u32[]{:S(2)}) collective-permute-start(bf16[4,48,1280]{2,1,0:T(8,128)(2,1)S(1)} %collective-permute-done.4.refs_1_), channel_id=1, source_target_pairs={{0,2},{1,5},{2,0},{3,7},{4,6},{5,1},{6,4},{7,3},{8,10},{9,13},{10,... | collective-permute-start | bytes 1474568 | tf_op jit(solution)/shard_map/ppermute | solution.py:117
  63.3 18.3 %collective-permute-start.7 = (bf16[4,48,1280]{2,1,0:T(8,128)(2,1)S(1)}, bf16[4,48,1280]{2,1,0:T(8,128)(2,1)S(1)}, u32[]{:S(2)}, u32[]{:S(2)}) collective-permute-start(bf16[4,48,1280]{2,1,0:T(8,128)(2,1)S(1)} %pad_maximum_fusion.3.refs_0_), channel_id=1, source_target_pairs={{0,1},{1,0},{2,3},{3,2},{4,5},{5,4},{6,7},{7,6},{8,9},{9,8},{10,11... | collective-permute-start | bytes 1474568 | tf_op jit(solution)/shard_map/ppermute | solution.py:117
  65.0 15.5 %collective-permute-start.13 = (bf16[48,1920]{1,0:T(8,128)(2,1)S(1)}, bf16[48,1920]{1,0:T(8,128)(2,1)S(1)}, u32[]{:S(2)}, u32[]{:S(2)}) collective-permute-start(bf16[48,1920]{1,0:T(8,128)(2,1)S(1)} %maximum_select_fusion.1), channel_id=1, source_target_pairs={{0,16},{1,17},{2,18},{3,19},{4,20},{5,21},{6,22},{7,23},{8,24},{9,... | collective-permute-start | bytes 552968 | tf_op jit(solution)/shard_map/ppermute | solution.py:117
  81.6 14.8 %collective-permute-start.27 = (bf16[4,48,1536]{2,1,0:T(8,128)(2,1)S(1)}, bf16[4,48,1536]{2,1,0:T(8,128)(2,1)}, u32[]{:S(2)}, u32[]{:S(2)}) collective-permute-start(bf16[4,48,1536]{2,1,0:T(8,128)(2,1)S(1)} %pad_maximum_fusion.1.refs_0_), channel_id=1, source_target_pairs={{0,2},{1,5},{2,0},{3,7},{4,6},{5,1},{6,4},{7,3},{8,10},{9,13},{10,... | collective-permute-start | bytes 1769480 | tf_op jit(solution)/shard_map/ppermute | solution.py:117
  83.9 16.3 %collective-permute-start.26 = (bf16[4,48,1536]{2,1,0:T(8,128)(2,1)S(1)}, bf16[4,48,1536]{2,1,0:T(8,128)(2,1)}, u32[]{:S(2)}, u32[]{:S(2)}) collective-permute-start(bf16[4,48,1536]{2,1,0:T(8,128)(2,1)S(1)} %pad_maximum_fusion.1.refs_0_), channel_id=1, source_target_pairs={{0,4},{1,3},{2,6},{3,1},{4,0},{5,7},{6,2},{7,5},{8,12},{9,11},{10,... | collective-permute-start | bytes 1769480 | tf_op jit(solution)/shard_map/ppermute | solution.py:117
  85.4 16.5 %collective-permute-start.40 = (bf16[4,192,384]{2,1,0:T(8,128)(2,1)S(1)}, bf16[4,192,384]{2,1,0:T(8,128)(2,1)S(1)}, u32[]{:S(2)}, u32[]{:S(2)}) collective-permute-start(bf16[4,192,384]{2,1,0:T(8,128)(2,1)S(1)} %pad_maximum_fusion.2.refs_0_), channel_id=1, source_target_pairs={{0,1},{1,0},{2,3},{3,2},{4,5},{5,4},{6,7},{7,6},{8,9},{9,8},{10,11... | collective-permute-start | bytes 1769480 | tf_op jit(solution)/shard_map/ppermute | solution.py:117
  87.0 22.1 %collective-permute-start.38 = (bf16[4,192,384]{2,1,0:T(8,128)(2,1)S(1)}, bf16[4,192,384]{2,1,0:T(8,128)(2,1)}, u32[]{:S(2)}, u32[]{:S(2)}) collective-permute-start(bf16[4,192,384]{2,1,0:T(8,128)(2,1)S(1)} %pad_maximum_fusion.2.refs_0_), channel_id=1, source_target_pairs={{0,2},{1,5},{2,0},{3,7},{4,6},{5,1},{6,4},{7,3},{8,10},{9,13},{10,... | collective-permute-start | bytes 1769480 | tf_op jit(solution)/shard_map/ppermute | solution.py:117
  93.4 19.5 %collective-permute-start.37 = (bf16[4,192,384]{2,1,0:T(8,128)(2,1)S(1)}, bf16[4,192,384]{2,1,0:T(8,128)(2,1)}, u32[]{:S(2)}, u32[]{:S(2)}) collective-permute-start(bf16[4,192,384]{2,1,0:T(8,128)(2,1)S(1)} %pad_maximum_fusion.2.refs_0_), channel_id=1, source_target_pairs={{0,4},{1,3},{2,6},{3,1},{4,0},{5,7},{6,2},{7,5},{8,12},{9,11},{10,... | collective-permute-start | bytes 1769480 | tf_op jit(solution)/shard_map/ppermute | solution.py:117
  96.4 32.3 %collective-permute-start.15 = (bf16[4,48,1920]{2,1,0:T(8,128)(2,1)}, bf16[4,48,1920]{2,1,0:T(8,128)(2,1)}, u32[]{:S(2)}, u32[]{:S(2)}) collective-permute-start(bf16[4,48,1920]{2,1,0:T(8,128)(2,1)} %pad_maximum_fusion.refs_0_), channel_id=1, source_target_pairs={{0,4},{1,3},{2,6},{3,1},{4,0},{5,7},{6,2},{7,5},{8,12},{9,11},{10,... | collective-permute-start | bytes 2211848 | tf_op jit(solution)/shard_map/ppermute | solution.py:117
  100.2 33.1 %collective-permute-start.16 = (bf16[4,48,1920]{2,1,0:T(8,128)(2,1)}, bf16[4,48,1920]{2,1,0:T(8,128)(2,1)}, u32[]{:S(2)}, u32[]{:S(2)}) collective-permute-start(bf16[4,48,1920]{2,1,0:T(8,128)(2,1)} %pad_maximum_fusion.refs_0_), channel_id=1, source_target_pairs={{0,2},{1,5},{2,0},{3,7},{4,6},{5,1},{6,4},{7,3},{8,10},{9,13},{10,... | collective-permute-start | bytes 2211848 | tf_op jit(solution)/shard_map/ppermute | solution.py:117
  101.9 32.5 %collective-permute-start.30 = (bf16[4,48,1536]{2,1,0:T(8,128)(2,1)}, bf16[4,48,1536]{2,1,0:T(8,128)(2,1)S(1)}, u32[]{:S(2)}, u32[]{:S(2)}) collective-permute-start(bf16[4,48,1536]{2,1,0:T(8,128)(2,1)} %collective-permute-done.26.refs_1_), channel_id=1, source_target_pairs={{0,1},{1,0},{2,3},{3,2},{4,5},{5,4},{6,7},{7,6},{8,9},{9,8},{10,11... | collective-permute-start | bytes 1769480 | tf_op jit(solution)/shard_map/ppermute | solution.py:117
  109.0 26.1 %collective-permute-start.28 = (bf16[4,48,1536]{2,1,0:T(8,128)(2,1)}, bf16[4,48,1536]{2,1,0:T(8,128)(2,1)}, u32[]{:S(2)}, u32[]{:S(2)}) collective-permute-start(bf16[4,48,1536]{2,1,0:T(8,128)(2,1)} %collective-permute-done.26.refs_1_), channel_id=1, source_target_pairs={{0,2},{1,5},{2,0},{3,7},{4,6},{5,1},{6,4},{7,3},{8,10},{9,13},{10,... | collective-permute-start | bytes 1769480 | tf_op jit(solution)/shard_map/ppermute | solution.py:117
  112.9 20.5 %collective-permute-start.31 = (bf16[4,48,1536]{2,1,0:T(8,128)(2,1)}, bf16[4,48,1536]{2,1,0:T(8,128)(2,1)S(1)}, u32[]{:S(2)}, u32[]{:S(2)}) collective-permute-start(bf16[4,48,1536]{2,1,0:T(8,128)(2,1)} %collective-permute-done.27.refs_2_), channel_id=1, source_target_pairs={{0,1},{1,0},{2,3},{3,2},{4,5},{5,4},{6,7},{7,6},{8,9},{9,8},{10,11... | collective-permute-start | bytes 1769480 | tf_op jit(solution)/shard_map/ppermute | solution.py:117
  128.7 18.3 %collective-permute-start.17 = (bf16[4,48,1920]{2,1,0:T(8,128)(2,1)}, bf16[4,48,1920]{2,1,0:T(8,128)(2,1)}, u32[]{:S(2)}, u32[]{:S(2)}) collective-permute-start(bf16[4,48,1920]{2,1,0:T(8,128)(2,1)} %collective-permute-done.15.refs_1_), channel_id=1, source_target_pairs={{0,2},{1,5},{2,0},{3,7},{4,6},{5,1},{6,4},{7,3},{8,10},{9,13},{10,... | collective-permute-start | bytes 2211848 | tf_op jit(solution)/shard_map/ppermute | solution.py:117
  135.1 17.5 %collective-permute-start.32 = (bf16[4,48,1536]{2,1,0:T(8,128)(2,1)}, bf16[4,48,1536]{2,1,0:T(8,128)(2,1)}, u32[]{:S(2)}, u32[]{:S(2)}) collective-permute-start(bf16[4,48,1536]{2,1,0:T(8,128)(2,1)} %collective-permute-done.28.refs_3_), channel_id=1, source_target_pairs={{0,1},{1,0},{2,3},{3,2},{4,5},{5,4},{6,7},{7,6},{8,9},{9,8},{10,11... | collective-permute-start | bytes 1769480 | tf_op jit(solution)/shard_map/ppermute | solution.py:117
  140.6 28.9 %collective-permute-start.18 = (bf16[4,48,1920]{2,1,0:T(8,128)(2,1)}, bf16[4,48,1920]{2,1,0:T(8,128)(2,1)}, u32[]{:S(2)}, u32[]{:S(2)}) collective-permute-start(bf16[4,48,1920]{2,1,0:T(8,128)(2,1)} %pad_maximum_fusion.refs_0_), channel_id=1, source_target_pairs={{0,1},{1,0},{2,3},{3,2},{4,5},{5,4},{6,7},{7,6},{8,9},{9,8},{10,11... | collective-permute-start | bytes 2211848 | tf_op jit(solution)/shard_map/ppermute | solution.py:117
  141.1 28.5 %collective-permute-start.19 = (bf16[4,48,1920]{2,1,0:T(8,128)(2,1)}, bf16[4,48,1920]{2,1,0:T(8,128)(2,1)}, u32[]{:S(2)}, u32[]{:S(2)}) collective-permute-start(bf16[4,48,1920]{2,1,0:T(8,128)(2,1)} %collective-permute-done.15.refs_1_), channel_id=1, source_target_pairs={{0,1},{1,0},{2,3},{3,2},{4,5},{5,4},{6,7},{7,6},{8,9},{9,8},{10,11... | collective-permute-start | bytes 2211848 | tf_op jit(solution)/shard_map/ppermute | solution.py:117
  147.0 22.6 %collective-permute-start.20 = (bf16[4,48,1920]{2,1,0:T(8,128)(2,1)}, bf16[4,48,1920]{2,1,0:T(8,128)(2,1)}, u32[]{:S(2)}, u32[]{:S(2)}) collective-permute-start(bf16[4,48,1920]{2,1,0:T(8,128)(2,1)} %collective-permute-done.16.refs_2_), channel_id=1, source_target_pairs={{0,1},{1,0},{2,3},{3,2},{4,5},{5,4},{6,7},{7,6},{8,9},{9,8},{10,11... | collective-permute-start | bytes 2211848 | tf_op jit(solution)/shard_map/ppermute | solution.py:117
  147.0 22.6 %collective-permute-start.21 = (bf16[4,48,1920]{2,1,0:T(8,128)(2,1)}, bf16[4,48,1920]{2,1,0:T(8,128)(2,1)}, u32[]{:S(2)}, u32[]{:S(2)}) collective-permute-start(bf16[4,48,1920]{2,1,0:T(8,128)(2,1)} %collective-permute-done.17.refs_3_), channel_id=1, source_target_pairs={{0,1},{1,0},{2,3},{3,2},{4,5},{5,4},{6,7},{7,6},{8,9},{9,8},{10,11... | collective-permute-start | bytes 2211848 | tf_op jit(solution)/shard_map/ppermute | solution.py:117
  326.4 89.3 %collective-permute-start.55 = (bf16[768,384]{1,0:T(8,128)(2,1)}, bf16[768,384]{1,0:T(8,128)(2,1)}, u32[]{:S(2)}, u32[]{:S(2)}) collective-permute-start(bf16[768,384]{1,0:T(8,128)(2,1)} %convolution_convert_fusion.12), channel_id=1, source_target_pairs={{0,1},{1,0},{2,3},{3,2},{4,5},{5,4},{6,7},{7,6},{8,9},{9,8},{10,11... | collective-permute-start | bytes 1769480 | tf_op jit(solution)/shard_map/ppermute | solution.py:117
  336.3 104.7 %collective-permute-start.45 = (bf16[768,384]{1,0:T(8,128)(2,1)}, bf16[768,384]{1,0:T(8,128)(2,1)}, u32[]{:S(2)}, u32[]{:S(2)}) collective-permute-start(bf16[768,384]{1,0:T(8,128)(2,1)} %convolution_convert_fusion.16), channel_id=1, source_target_pairs={{0,1},{1,0},{2,3},{3,2},{4,5},{5,4},{6,7},{7,6},{8,9},{9,8},{10,11... | collective-permute-start | bytes 1769480 | tf_op jit(solution)/shard_map/ppermute | solution.py:117
  370.6 45.1 %collective-permute-start.53 = (bf16[768,384]{1,0:T(8,128)(2,1)}, bf16[768,384]{1,0:T(8,128)(2,1)}, u32[]{:S(2)}, u32[]{:S(2)}) collective-permute-start(bf16[768,384]{1,0:T(8,128)(2,1)} %convolution_convert_fusion.14), channel_id=1, source_target_pairs={{0,1},{1,0},{2,3},{3,2},{4,5},{5,4},{6,7},{7,6},{8,9},{9,8},{10,11... | collective-permute-start | bytes 1769480 | tf_op jit(solution)/shard_map/ppermute | solution.py:117
  387.8 25.0 %collective-permute-start.54 = (bf16[768,768]{0,1:T(8,128)(2,1)}, bf16[768,768]{0,1:T(8,128)(2,1)}, u32[]{:S(2)}, u32[]{:S(2)}) collective-permute-start(bf16[768,768]{0,1:T(8,128)(2,1)} %fusion.67), channel_id=1, source_target_pairs={{0,1},{1,0},{2,3},{3,2},{4,5},{5,4},{6,7},{7,6},{8,9},{9,8},{10,11... | collective-permute-start | bytes 3538952 | tf_op jit(solution)/shard_map/ppermute | solution.py:117
  393.8 47.2 %collective-permute-start.44 = (bf16[768,1152]{1,0:T(8,128)(2,1)}, bf16[768,1152]{1,0:T(8,128)(2,1)}, u32[]{:S(2)}, u32[]{:S(2)}) collective-permute-start(bf16[768,1152]{1,0:T(8,128)(2,1)} %convolution_convert_fusion.4), channel_id=1, source_target_pairs={{0,1},{1,0},{2,3},{3,2},{4,5},{5,4},{6,7},{7,6},{8,9},{9,8},{10,11... | collective-permute-start | bytes 5308424 | tf_op jit(solution)/shard_map/ppermute | solution.py:117
  412.8 41.4 %collective-permute-start.69 = (bf16[3072,384]{1,0:T(8,128)(2,1)}, bf16[3072,384]{1,0:T(8,128)(2,1)}, u32[]{:S(2)}, u32[]{:S(2)}) collective-permute-start(bf16[3072,384]{1,0:T(8,128)(2,1)} %convolution_convert_fusion), channel_id=1, source_target_pairs={{0,1},{1,0},{2,3},{3,2},{4,5},{5,4},{6,7},{7,6},{8,9},{9,8},{10,11... | collective-permute-start | bytes 7077896 | tf_op jit(solution)/shard_map/ppermute | solution.py:117
  420.3 16.5 %collective-permute-start.56 = (bf16[4,2,48,1536]{3,2,1,0:T(8,128)(2,1)}, bf16[4,2,48,1536]{3,2,1,0:T(8,128)(2,1)S(1)}, u32[]{:S(2)}, u32[]{:S(2)}) collective-permute-start(bf16[4,2,48,1536]{3,2,1,0:T(8,128)(2,1)} %get-tuple-element.36), channel_id=1, source_target_pairs={{0,2},{1,5},{2,0},{3,7},{4,6},{5,1},{6,4},{7,3},{8,10},{9,13},{10,... | collective-permute-start | bytes 3538952 | tf_op jit(solution)/shard_map/ppermute | solution.py:117
  423.1 42.2 %collective-permute-start.62 = (bf16[768,1536]{1,0:T(8,128)(2,1)}, bf16[768,1536]{1,0:T(8,128)(2,1)}, u32[]{:S(2)}, u32[]{:S(2)}) collective-permute-start(bf16[768,1536]{1,0:T(8,128)(2,1)} %convolution_convert_fusion.6), channel_id=1, source_target_pairs={{0,1},{1,0},{2,3},{3,2},{4,5},{5,4},{6,7},{7,6},{8,9},{9,8},{10,11... | collective-permute-start | bytes 7077896 | tf_op jit(solution)/shard_map/ppermute | solution.py:117
  445.9 28.4 %collective-permute-start.47 = (bf16[4,2,48,1664]{3,2,1,0:T(8,128)(2,1)}, bf16[4,2,48,1664]{3,2,1,0:T(8,128)(2,1)}, u32[]{:S(2)}, u32[]{:S(2)}) collective-permute-start(bf16[4,2,48,1664]{3,2,1,0:T(8,128)(2,1)} %get-tuple-element.34), channel_id=1, source_target_pairs={{0,2},{1,5},{2,0},{3,7},{4,6},{5,1},{6,4},{7,3},{8,10},{9,13},{10,... | collective-permute-start | bytes 3833864 | tf_op jit(solution)/shard_map/ppermute | solution.py:117
  450.3 21.7 %collective-permute-start.58 = (bf16[48,1536]{1,0:T(8,128)(2,1)S(1)}, bf16[48,1536]{1,0:T(8,128)(2,1)}, u32[]{:S(2)}, u32[]{:S(2)}) collective-permute-start(bf16[48,1536]{1,0:T(8,128)(2,1)S(1)} %get-tuple-element.127), channel_id=1, source_target_pairs={{0,8},{1,9},{2,10},{3,11},{4,12},{5,13},{6,14},{7,15},{8,16},{9,17... | collective-permute-start | bytes 442376 | tf_op jit(solution)/shard_map/ppermute | solution.py:117
  450.4 22.5 %collective-permute-start.60 = (bf16[48,1536]{1,0:T(8,128)(2,1)S(1)}, bf16[48,1536]{1,0:T(8,128)(2,1)}, u32[]{:S(2)}, u32[]{:S(2)}) collective-permute-start(bf16[48,1536]{1,0:T(8,128)(2,1)S(1)} %get-tuple-element.128), channel_id=1, source_target_pairs={{0,24},{1,25},{2,26},{3,27},{4,28},{5,29},{6,30},{7,31},{8,0},{9,1... | collective-permute-start | bytes 442376 | tf_op jit(solution)/shard_map/ppermute | solution.py:117
  454.2 18.7 %collective-permute-start.59 = (bf16[48,1536]{1,0:T(8,128)(2,1)S(1)}, bf16[48,1536]{1,0:T(8,128)(2,1)}, u32[]{:S(2)}, u32[]{:S(2)}) collective-permute-start(bf16[48,1536]{1,0:T(8,128)(2,1)S(1)} %get-tuple-element.129), channel_id=1, source_target_pairs={{0,16},{1,17},{2,18},{3,19},{4,20},{5,21},{6,22},{7,23},{8,24},{9,... | collective-permute-start | bytes 442376 | tf_op jit(solution)/shard_map/ppermute | solution.py:117
  465.2 32.9 %collective-permute-start.70 = (bf16[4,2,192,384]{3,2,1,0:T(8,128)(2,1)}, bf16[4,2,192,384]{3,2,1,0:T(8,128)(2,1)}, u32[]{:S(2)}, u32[]{:S(2)}) collective-permute-start(bf16[4,2,192,384]{3,2,1,0:T(8,128)(2,1)} %get-tuple-element.40), channel_id=1, source_target_pairs={{0,2},{1,5},{2,0},{3,7},{4,6},{5,1},{6,4},{7,3},{8,10},{9,13},{10,... | collective-permute-start | bytes 3538952 | tf_op jit(solution)/shard_map/ppermute | solution.py:117
  472.0 39.1 %collective-permute-start.63 = (bf16[4,2,48,1536]{3,2,1,0:T(8,128)(2,1)}, bf16[4,2,48,1536]{3,2,1,0:T(8,128)(2,1)S(1)}, u32[]{:S(2)}, u32[]{:S(2)}) collective-permute-start(bf16[4,2,48,1536]{3,2,1,0:T(8,128)(2,1)} %get-tuple-element.38), channel_id=1, source_target_pairs={{0,2},{1,5},{2,0},{3,7},{4,6},{5,1},{6,4},{7,3},{8,10},{9,13},{10,... | collective-permute-start | bytes 3538952 | tf_op jit(solution)/shard_map/ppermute | solution.py:117
  475.6 17.3 %collective-permute-start.48 = (bf16[4,48,1664]{2,1,0:T(8,128)(2,1)S(1)}, bf16[4,48,1664]{2,1,0:T(8,128)(2,1)S(1)}, u32[]{:S(2)}, u32[]{:S(2)}) collective-permute-start(bf16[4,48,1664]{2,1,0:T(8,128)(2,1)S(1)} %fusion.103), channel_id=1, source_target_pairs={{0,4},{1,3},{2,6},{3,1},{4,0},{5,7},{6,2},{7,5},{8,12},{9,11},{10,... | collective-permute-start | bytes 1916936 | tf_op jit(solution)/shard_map/ppermute | solution.py:117
  497.0 13.9 %collective-permute-start.50 = (bf16[48,1664]{1,0:T(8,128)(2,1)S(1)}, bf16[48,1664]{1,0:T(8,128)(2,1)S(1)}, u32[]{:S(2)}, u32[]{:S(2)}) collective-permute-start(bf16[48,1664]{1,0:T(8,128)(2,1)S(1)} %get-tuple-element.120), channel_id=1, source_target_pairs={{0,16},{1,17},{2,18},{3,19},{4,20},{5,21},{6,22},{7,23},{8,24},{9,... | collective-permute-start | bytes 479240 | tf_op jit(solution)/shard_map/ppermute | solution.py:117
  500.1 17.8 %collective-permute-start.71 = (bf16[4,192,384]{2,1,0:T(8,128)(2,1)}, bf16[4,192,384]{2,1,0:T(8,128)(2,1)S(1)}, u32[]{:S(2)}, u32[]{:S(2)}) collective-permute-start(bf16[4,192,384]{2,1,0:T(8,128)(2,1)} %fusion.106), channel_id=1, source_target_pairs={{0,4},{1,3},{2,6},{3,1},{4,0},{5,7},{6,2},{7,5},{8,12},{9,11},{10,... | collective-permute-start | bytes 1769480 | tf_op jit(solution)/shard_map/ppermute | solution.py:117
  522.0 16.4 %collective-permute-start.73 = (bf16[192,384]{1,0:T(8,128)(2,1)S(1)}, bf16[192,384]{1,0:T(8,128)(2,1)S(1)}, u32[]{:S(2)}, u32[]{:S(2)}) collective-permute-start(bf16[192,384]{1,0:T(8,128)(2,1)S(1)} %get-tuple-element.123), channel_id=1, source_target_pairs={{0,16},{1,17},{2,18},{3,19},{4,20},{5,21},{6,22},{7,23},{8,24},{9,... | collective-permute-start | bytes 442376 | tf_op jit(solution)/shard_map/ppermute | solution.py:117
  523.5 15.1 %collective-permute-start.65 = (bf16[48,1536]{1,0:T(8,128)(2,1)S(1)}, bf16[48,1536]{1,0:T(8,128)(2,1)S(1)}, u32[]{:S(2)}, u32[]{:S(2)}) collective-permute-start(bf16[48,1536]{1,0:T(8,128)(2,1)S(1)} %get-tuple-element.124), channel_id=1, source_target_pairs={{0,8},{1,9},{2,10},{3,11},{4,12},{5,13},{6,14},{7,15},{8,16},{9,17... | collective-permute-start | bytes 442376 | tf_op jit(solution)/shard_map/ppermute | solution.py:117
  524.0 14.6 %collective-permute-start.67 = (bf16[48,1536]{1,0:T(8,128)(2,1)S(1)}, bf16[48,1536]{1,0:T(8,128)(2,1)S(1)}, u32[]{:S(2)}, u32[]{:S(2)}) collective-permute-start(bf16[48,1536]{1,0:T(8,128)(2,1)S(1)} %get-tuple-element.125), channel_id=1, source_target_pairs={{0,24},{1,25},{2,26},{3,27},{4,28},{5,29},{6,30},{7,31},{8,0},{9,1... | collective-permute-start | bytes 442376 | tf_op jit(solution)/shard_map/ppermute | solution.py:117
  527.4 19.3 %collective-permute-start.66 = (bf16[48,1536]{1,0:T(8,128)(2,1)S(1)}, bf16[48,1536]{1,0:T(8,128)(2,1)S(1)}, u32[]{:S(2)}, u32[]{:S(2)}) collective-permute-start(bf16[48,1536]{1,0:T(8,128)(2,1)S(1)} %get-tuple-element.126), channel_id=1, source_target_pairs={{0,16},{1,17},{2,18},{3,19},{4,20},{5,21},{6,22},{7,23},{8,24},{9,... | collective-permute-start | bytes 442376 | tf_op jit(solution)/shard_map/ppermute | solution.py:117
  (141 other events, 1147.3 us)

commit v3 on v2

v3 whole, which is shorter than its diff:
```python
import functools

import jax
import jax.numpy as jnp
from jax import lax
from jax.experimental import pallas as pl
from jax.experimental.pallas import tpu as pltpu
from jax.sharding import PartitionSpec as P

D = 768
HEADS = 12
HEAD_DIM = 64
PREFIX = 32


EPS = 1e-05


def norm_forward(value_tensor, gain, shift):
    mean = jnp.mean(value_tensor, axis=-1, keepdims=True)
    centred = value_tensor - mean
    spread = jnp.mean(centred * centred, axis=-1, keepdims=True)
    scale_inv = lax.rsqrt(spread + EPS)
    standard = centred * scale_inv
    return (standard * gain + shift, standard, scale_inv)


def norm_backward(upstream_gradient, standard, scale_inv, gain):
    grad_gain = jnp.sum(upstream_gradient * standard, axis=0)
    grad_shift = jnp.sum(upstream_gradient, axis=0)
    inner = upstream_gradient * gain
    first = jnp.mean(inner, axis=-1, keepdims=True)
    second = jnp.mean(inner * standard, axis=-1, keepdims=True)
    return (scale_inv * (inner - first - standard * second), grad_gain, grad_shift)


def project(value_tensor, weight_matrix):
    return jnp.einsum("...h,ht->...t", value_tensor, weight_matrix, preferred_element_type=jnp.float32)


def back_project(upstream_gradient, weight_matrix):
    return jnp.einsum(
        "...j,aj->...a", upstream_gradient, weight_matrix, preferred_element_type=jnp.float32
    )


PAIRS = HEADS // 2
LANES = 2 * HEAD_DIM


def dot(a, b, over):
    return lax.dot_general(a, b, (over, ((), ())), preferred_element_type=jnp.float32)


NATURAL = ((1,), (0,))
BOTH_LAST = ((1,), (1,))
BOTH_FIRST = ((0,), (0,))


def low_lanes(rows):
    return lax.broadcasted_iota(jnp.int32, (rows, LANES), 1) < HEAD_DIM


def stacked(pair, level):
    low = low_lanes(pair.shape[0])
    first = jnp.where(low, level, 0.0).astype(jnp.bfloat16)
    second = jnp.where(low, 0.0, level).astype(jnp.bfloat16)
    return jnp.concatenate([pair * first, pair * second], axis=0)


def unstacked(value):
    rows = value.shape[0] // 2
    return jnp.where(low_lanes(rows), value[:rows], value[rows:])


def lanes_of(ref, start):
    return ref[0, :, start : start + LANES]


def forward_pair(query, key, value, allowed):
    scores = dot(key, stacked(query, HEAD_DIM**-0.5), BOTH_LAST)
    if allowed is not None:
        scores = jnp.where(allowed, scores, -1e30)
    weights = jnp.exp(scores - jnp.max(scores, axis=0, keepdims=True))
    probs = (weights * (1.0 / jnp.sum(weights, axis=0, keepdims=True))).astype(jnp.bfloat16)
    context = unstacked(dot(probs, value, BOTH_FIRST)).astype(jnp.bfloat16)
    return context, probs


def backward_pair(query, key, value, probs, grad):
    scale = HEAD_DIM**-0.5
    grads = stacked(grad, 1.0)
    grad_probs = dot(value, grads, BOTH_LAST)
    wide = probs.astype(jnp.float32)
    delta = jnp.sum(grad_probs * wide, axis=0, keepdims=True)
    grad_scores = (wide * (grad_probs - delta)).astype(jnp.bfloat16)
    grad_key = dot(grad_scores, stacked(query, scale), NATURAL).astype(jnp.bfloat16)
    grad_value = dot(probs, grads, NATURAL).astype(jnp.bfloat16)
    grad_query = (unstacked(dot(grad_scores, key, BOTH_FIRST)) * scale).astype(jnp.bfloat16)
    return grad_query, grad_key, grad_value


def self_forward_body(lens, qkv, context, probs):
    rows = qkv.shape[1]
    at_key = lax.broadcasted_iota(jnp.int32, (rows, 2 * rows), 0)
    at_query = lax.broadcasted_iota(jnp.int32, (rows, 2 * rows), 1)
    at_query = jnp.where(at_query < rows, at_query, at_query - rows)
    allowed = (at_key <= at_query) & (at_key < PREFIX + lens[pl.program_id(0)])
    for p in range(PAIRS):
        at = p * LANES
        out, kept = forward_pair(
            lanes_of(qkv, at), lanes_of(qkv, D + at), lanes_of(qkv, 2 * D + at), allowed
        )
        context[0, :, at : at + LANES] = out
        probs[0, p] = kept


def self_backward_body(qkv, probs, grad, grad_qkv):
    for p in range(PAIRS):
        at = p * LANES
        gq, gk, gv = backward_pair(
            lanes_of(qkv, at),
            lanes_of(qkv, D + at),
            lanes_of(qkv, 2 * D + at),
            probs[0, p],
            lanes_of(grad, at),
        )
        grad_qkv[0, :, at : at + LANES] = gq
        grad_qkv[0, :, D + at : D + at + LANES] = gk
        grad_qkv[0, :, 2 * D + at : 2 * D + at + LANES] = gv


def cross_forward_body(query, kv, context, probs):
    for p in range(PAIRS):
        at = p * LANES
        out, kept = forward_pair(lanes_of(query, at), lanes_of(kv, at), lanes_of(kv, D + at), None)
        context[0, :, at : at + LANES] = out
        probs[0, p] = kept


def cross_backward_body(query, kv, probs, grad, grad_query, grad_kv):
    for p in range(PAIRS):
        at = p * LANES
        gq, gk, gv = backward_pair(
            lanes_of(query, at),
            lanes_of(kv, at),
            lanes_of(kv, D + at),
            probs[0, p],
            lanes_of(grad, at),
        )
        grad_query[0, :, at : at + LANES] = gq
        grad_kv[0, :, at : at + LANES] = gk
        grad_kv[0, :, D + at : D + at + LANES] = gv


def whole_block(shape):
    rest = len(shape) - 1
    return pl.BlockSpec((1,) + tuple(shape[1:]), lambda s, *_: (s,) + (0,) * rest)


def per_sequence(body, name, inputs, shapes, lens=None):
    outs = [jax.ShapeDtypeStruct(shape, jnp.bfloat16) for shape in shapes]
    return pl.pallas_call(
        body,
        out_shape=outs,
        grid_spec=pltpu.PrefetchScalarGridSpec(
            num_scalar_prefetch=0 if lens is None else 1,
            grid=(inputs[0].shape[0],),
            in_specs=[whole_block(v.shape) for v in inputs],
            out_specs=[whole_block(shape) for shape in shapes],
        ),
        name=name,
    )(*(() if lens is None else (lens,)), *inputs)


def self_forward(qkv, lens):
    seqs, rows, _ = qkv.shape
    return per_sequence(
        self_forward_body,
        "self_forward",
        [qkv],
        [(seqs, rows, D), (seqs, PAIRS, rows, 2 * rows)],
        lens,
    )


def self_backward(qkv, probs, grad):
    return per_sequence(self_backward_body, "self_backward", [qkv, probs, grad], [qkv.shape])[0]


def cross_forward(query, kv):
    seqs, rows, _ = query.shape
    return per_sequence(
        cross_forward_body,
        "cross_forward",
        [query, kv],
        [query.shape, (seqs, PAIRS, kv.shape[1], 2 * rows)],
    )


def cross_backward(query, kv, probs, grad):
    return per_sequence(
        cross_backward_body,
        "cross_backward",
        [query, kv, probs, grad],
        [query.shape, kv.shape],
    )


AXES = ("fsdp", "dp")


def grid_rank(z, x, y, core):
    return ((z * 2 + x) * 2 + y) * 2 + core


def grid_perm(move):
    return [
        (grid_rank(z, x, y, core), grid_rank(*move(z, x, y, core)))
        for z in range(4)
        for x in range(2)
        for y in range(2)
        for core in range(2)
    ]


CORE = grid_perm(lambda z, x, y, core: (z, x, y, core ^ 1))
ZSHIFT = [
    grid_perm(lambda z, x, y, core, k=k: ((z + k) % 4, x, y, core)) for k in range(4)
]
FIRST = grid_perm(lambda z, x, y, core: (z, x ^ (1 - core), y ^ core, core))
SECOND = grid_perm(lambda z, x, y, core: (z, x ^ core, y ^ (1 - core), core))


def move(value, perm):
    return lax.ppermute(value, AXES, perm)


def place():
    outer, inner = lax.axis_index("fsdp"), lax.axis_index("dp")
    return outer // 2, outer % 2, inner // 2, inner % 2


def half_of(value, side):
    width = value.shape[-1] // 2
    return lax.dynamic_slice_in_dim(value, side * width, width, axis=-1)


def after(value, *earlier):
    return lax.optimization_barrier((value,) + earlier)[0]


def assemble_body(widths, spot, *refs):
    parts, outs = refs[:8], refs[8:]
    x, y, core = spot[1], spot[2], spot[3]
    for theirs in range(2):
        side = 1 - core if theirs else core
        for j in range(4):
            at_x = x ^ (0, 1 - side, side, 1)[j]
            at_y = y ^ (0, side, 1 - side, 1)[j]
            offset = 0
            for width, out in zip(widths, outs):
                out[0, at_x, at_y, side] = parts[theirs * 4 + j][0, :, offset : offset + width]
                offset += width


def assemble(parts, rows, widths, spot):
    outs = pl.pallas_call(
        functools.partial(assemble_body, widths),
        out_shape=[jax.ShapeDtypeStruct((4, 2, 2, 2, rows, w), jnp.bfloat16) for w in widths],
        grid_spec=pltpu.PrefetchScalarGridSpec(
            num_scalar_prefetch=1,
            grid=(4,),
            in_specs=[pl.BlockSpec((1, rows, sum(widths)), lambda k, spot: (k, 0, 0))] * 8,
            out_specs=[
                pl.BlockSpec(
                    (1, 2, 2, 2, rows, w),
                    lambda k, spot: (lax.rem(spot[0] + 4 - k, 4), 0, 0, 0, 0, 0),
                )
                for w in widths
            ],
        ),
        name="assemble",
    )(spot, *parts)
    return [o.reshape(32 * rows, w) for o, w in zip(outs, widths)]


class GridGather:
    def __init__(self):
        self.lines = ()
        self.crossed = ()

    def spread(self, shards):
        own = jnp.concatenate(shards, axis=1) if len(shards) > 1 else shards[0]
        own = after(own, *self.lines)
        self.lines = tuple(move(own, ZSHIFT[k]) for k in (1, 2, 3))
        return jnp.stack((own,) + self.lines)

    def cross(self, line, *earlier):
        ready = after(line, *self.crossed, *earlier)
        one = move(ready, FIRST)
        two = move(ready, SECOND)
        both = move(one, SECOND)
        self.crossed = (one, two) if earlier else (both,)
        parts = [line, one, two, both]
        return parts + [move(p, CORE) for p in parts]

    def join(self, parts, shards, *earlier):
        rows = shards[0].shape[0]
        widths = [s.shape[1] for s in shards]
        if earlier:
            parts = lax.optimization_barrier(tuple(parts) + earlier)[: len(parts)]
        return assemble(parts, rows, widths, jnp.stack(place()).astype(jnp.int32))


class PlainGather:
    def spread(self, shards):
        return None

    def cross(self, line, *earlier):
        return None

    def join(self, parts, shards, *earlier):
        widths = [s.shape[1] for s in shards]
        whole = lax.all_gather(jnp.concatenate(shards, axis=1), AXES, axis=0, tiled=True)
        results = []
        offset = 0
        for width in widths:
            results.append(whole[:, offset : offset + width])
            offset += width
        return results


def split_body(count, which, *refs):
    del which
    keeps, sends, outs = refs[: 2 * count], refs[2 * count : 4 * count], refs[4 * count :]
    for source, out in ((keeps, outs[0]), (sends, outs[1])):
        offset = 0
        for i in range(count):
            width = source[2 * i].shape[-1]
            total = source[2 * i][...].astype(jnp.float32) + source[2 * i + 1][...].astype(
                jnp.float32
            )
            out[:, :, :, offset : offset + width] = total.astype(jnp.bfloat16)
            offset += width


def split_add(pairs, rows):
    z, x, y, core = place()
    first = jnp.where(core == 0, x, y)
    second = jnp.where(core == 0, y, x)
    first_weight = jnp.where(core == 0, 2, 1)
    second_weight = 3 - first_weight
    which = jnp.stack(
        [
            (first ^ f) * first_weight + (second ^ s) * second_weight
            for s in range(2)
            for f in range(2)
        ]
    ).astype(jnp.int32)
    views, keep_specs, send_specs = [], [], []
    for keep, got in pairs:
        width = keep.shape[1]
        block = (4, 1, 2 * rows, width)
        for value in (keep, got):
            views.append(value.reshape(4, 4, 2 * rows, width))
            keep_specs.append(pl.BlockSpec(block, lambda f, which: (0, which[f], 0, 0)))
            send_specs.append(pl.BlockSpec(block, lambda f, which: (0, which[2 + f], 0, 0)))
    total = sum(keep.shape[1] for keep, _ in pairs)
    shape = jax.ShapeDtypeStruct((4, 2, 2 * rows, total), jnp.bfloat16)
    out_spec = pl.BlockSpec((4, 1, 2 * rows, total), lambda f, which: (0, f, 0, 0))
    return pl.pallas_call(
        functools.partial(split_body, len(pairs)),
        out_shape=[shape, shape],
        grid_spec=pltpu.PrefetchScalarGridSpec(
            num_scalar_prefetch=1,
            grid=(2,),
            in_specs=keep_specs + send_specs,
            out_specs=[out_spec, out_spec],
        ),
        name="split_add",
    )(which, *views, *views)


class GridReduction:
    def __init__(self, factors):
        core = place()[3]
        self.rows = factors[0][0].shape[-1] // 32
        self.sends = [contract_low(v, half_of(u, 1 - core)) for v, u in factors]
        self.factors = factors
        self.stage = 0

    def step(self):
        self.stage += 1
        return getattr(self, "hop%d" % self.stage)()

    def hop1(self):
        core = place()[3]
        self.got = [move(send, CORE) for send in self.sends]
        self.keeps = [contract_low(v, half_of(u, core)) for v, u in self.factors]
        return self.got

    def hop2(self):
        self.keep, send = split_add(list(zip(self.keeps, self.got)), self.rows)
        self.got = move(send, SECOND)
        return [self.got]

    def hop3(self):
        f32 = jnp.float32
        total = self.keep[:, 1].astype(f32) + self.got[:, 1].astype(f32)
        self.got_first = move(total.astype(jnp.bfloat16), FIRST)
        return [self.got_first]

    def hop4(self):
        z = place()[0]
        f32 = jnp.float32

        def plane(k):
            at = (z + k) % 4
            pick = lambda v: lax.dynamic_index_in_dim(v, at, 0, keepdims=False).astype(f32)
            return pick(self.keep[:, 0]) + pick(self.got[:, 0]) + pick(self.got_first)

        self.own = plane(0)
        self.planes = [move(plane(k).astype(jnp.bfloat16), ZSHIFT[k]) for k in (1, 2, 3)]
        return self.planes

    def results(self):
        while self.stage < 4:
            self.step()
        core, rows = place()[3], self.rows
        total = self.own + sum(p.astype(jnp.float32) for p in self.planes)
        mine = lax.dynamic_slice_in_dim(total, core * rows, rows, axis=0)
        other = move(lax.dynamic_slice_in_dim(total, (1 - core) * rows, rows, axis=0), CORE)
        left = jnp.where(core == 0, mine, other)
        right = jnp.where(core == 0, other, mine)
        results = []
        offset = 0
        for keep in self.keeps:
            width = keep.shape[1]
            results.append(
                jnp.concatenate(
                    [left[:, offset : offset + width], right[:, offset : offset + width]], axis=1
                )
            )
            offset += width
        return results


class PlainReduction:
    def __init__(self, factors):
        self.factors = factors
        self.sends = []

    def step(self):
        return []

    def results(self):
        packed = jnp.concatenate([contract_low(v, u) for v, u in self.factors], axis=1)
        summed = lax.psum_scatter(packed, AXES, scatter_dimension=0, tiled=True)
        summed = summed.astype(jnp.float32)
        results = []
        offset = 0
        for _, u in self.factors:
            results.append(summed[:, offset : offset + u.shape[-1]])
            offset += u.shape[-1]
        return results


def contract_low(value, upstream_gradient):
    over = tuple(range(value.ndim - 1))
    return lax.dot_general(
        value,
        upstream_gradient,
        ((over, over), ((), ())),
        preferred_element_type=jnp.float32,
    ).astype(jnp.bfloat16)


def local(
    gathering,
    reduction,
    tokens,
    memory,
    suffix_len,
    cotangent,
    attn_in,
    attn_out,
    cross_query,
    cross_kv,
    cross_out,
    mlp_in,
    mlp_out,
    ln_gain,
    shifts,
    mlp_bias,
):
    owned = attn_in.shape[0]
    small = jnp.concatenate(
        [
            ln_gain,
            shifts,
            mlp_bias.reshape(owned, 4),
            jnp.zeros((owned, 256 - 11), jnp.bfloat16),
        ],
        axis=1,
    )
    gather = gathering()
    first, second, third, fourth = (
        [attn_in, small],
        [attn_out, cross_query, cross_kv, cross_out],
        [mlp_in],
        [mlp_out],
    )
    lines = [gather.spread(shards) for shards in (first, second, third, fourth)]
    first_parts = gather.cross(lines[0])
    second_parts = gather.cross(lines[1])
    w_qkv, smalls = gather.join(first_parts, first)
    gains, biases, hidden_bias = smalls[:, :3], smalls[:, 3:7], smalls[:, 7:11].reshape(-1)
    seqs, rows, width = tokens.shape
    low = lambda v: v.astype(jnp.bfloat16)
    flat = lambda v: v.reshape(seqs * rows, v.shape[-1])
    by_seq = lambda v: v.reshape(seqs, rows, v.shape[-1])
    live = jnp.arange(rows)[None, :] < (PREFIX + suffix_len)[:, None]
    gain_vals = gains.astype(jnp.float32)
    bias_vals = biases.astype(jnp.float32)
    stream0 = flat(tokens).astype(jnp.float32)
    normed1, standard1, inverse1 = norm_forward(stream0, gain_vals[:, 0], bias_vals[:, 0])
    normed1 = low(normed1)
    qkv = by_seq(low(project(normed1, w_qkv)))
    context, probs = self_forward(qkv, suffix_len)
    third_parts = gather.cross(lines[2], context)
    w_out, w_cquery, w_ckv, w_cout = gather.join(second_parts, second, context)
    context = flat(context)
    stream1 = stream0 + project(context, w_out)
    normed2, standard2, inverse2 = norm_forward(stream1, gain_vals[:, 1], bias_vals[:, 1])
    normed2 = low(normed2)
    cquery = by_seq(low(project(normed2, w_cquery)))
    ckv = low(project(memory, w_ckv))
    fourth_parts = gather.cross(lines[3], cquery)
    ccontext, cprobs = cross_forward(cquery, ckv)
    (w_in,) = gather.join(third_parts, third, ccontext)
    ccontext = flat(ccontext)
    stream2 = stream1 + project(ccontext, w_cout)
    normed3, standard3, inverse3 = norm_forward(stream2, gain_vals[:, 2], bias_vals[:, 2])
    normed3 = low(normed3)
    pre = project(normed3, w_in) + hidden_bias.astype(jnp.float32)
    activated, gelu_back = jax.vjp(lambda v: jax.nn.gelu(v, approximate=True), pre)
    activated = low(activated)
    (w_down,) = gather.join(fourth_parts, fourth, activated)
    layer_out = by_seq(low(stream2 + project(activated, w_down) + bias_vals[:, 3]))

    upstream = flat(cotangent.astype(jnp.float32) * live[..., None].astype(jnp.float32))
    dout3 = low(upstream)
    down_sum = reduction([(activated, dout3)])
    g_out_bias = jnp.sum(dout3, axis=0, dtype=jnp.float32)
    grad_act = back_project(after(dout3, *down_sum.sends), w_down)
    dpre = low(gelu_back(grad_act)[0])
    g_hidden_bias = jnp.sum(dpre, axis=0, dtype=jnp.float32)
    in_sum = reduction([(normed3, dpre)])
    dpre = after(dpre, *down_sum.step(), *in_sum.sends)
    grad_back, g_gain3, g_shift3 = norm_backward(
        back_project(dpre, w_in), standard3, inverse3, gain_vals[:, 2]
    )
    upstream = upstream + grad_back
    dout2 = low(upstream)
    dccontext = by_seq(low(back_project(dout2, w_cout)))
    dccontext = after(dccontext, *down_sum.step(), *in_sum.step())
    dcquery, dckv = cross_backward(cquery, ckv, cprobs, dccontext)
    dcq = flat(dcquery)
    cross_sum = reduction([(normed2, dcq), (memory, dckv), (ccontext, dout2)])
    dcq = after(dcq, *down_sum.step(), *in_sum.step(), *cross_sum.sends)
    grad_back, g_gain2, g_shift2 = norm_backward(
        back_project(dcq, w_cquery), standard2, inverse2, gain_vals[:, 1]
    )
    upstream = upstream + grad_back
    dout1 = low(upstream)
    dcontext = by_seq(low(back_project(dout1, w_out)))
    dcontext = after(dcontext, *down_sum.step(), *in_sum.step(), *cross_sum.step())
    dqkv = flat(self_backward(qkv, probs, dcontext))
    grad_back, g_gain1, g_shift1 = norm_backward(
        back_project(dqkv, w_qkv), standard1, inverse1, gain_vals[:, 0]
    )
    input_grad = by_seq(upstream + grad_back)
    small_sums = jnp.stack(
        (g_gain1, g_gain2, g_gain3, g_shift1, g_shift2, g_shift3, g_out_bias), axis=0
    )
    bias_sums = g_hidden_bias.reshape(D, 4).T
    sums = jnp.concatenate([small_sums, bias_sums], axis=0)
    picks = jnp.eye(11, 256, dtype=jnp.bfloat16)
    attn_sum = reduction([(normed1, dqkv), (context, dout1), (low(sums), picks)])
    memory_grad = back_project(after(dckv, *attn_sum.sends), w_ckv)
    (mlp_out_grad,) = down_sum.results()
    (mlp_in_grad,) = in_sum.results()
    cross_query_grad, cross_kv_grad, cross_out_grad = cross_sum.results()
    attn_in_grad, attn_out_grad, small_grad = attn_sum.results()
    return (
        layer_out,
        input_grad,
        memory_grad,
        attn_in_grad,
        attn_out_grad,
        cross_query_grad,
        cross_kv_grad,
        cross_out_grad,
        mlp_in_grad,
        mlp_out_grad,
        small_grad[:, :3],
        small_grad[:, 3:7],
        small_grad[:, 7:11].reshape(-1),
    )


def solution(mesh):
    in_specs = (
        P(("fsdp", "dp"), None, None),
        P(("fsdp", "dp"), None, None),
        P(("fsdp", "dp")),
        P(("fsdp", "dp"), None, None),
        P(("fsdp", "dp"), None),
        P(("fsdp", "dp"), None),
        P(("fsdp", "dp"), None),
        P(("fsdp", "dp"), None),
        P(("fsdp", "dp"), None),
        P(("fsdp", "dp"), None),
        P(("fsdp", "dp"), None),
        P(("fsdp", "dp"), None),
        P(("fsdp", "dp"), None),
        P(("fsdp", "dp")),
    )
    out_specs = (
        P(("fsdp", "dp"), None, None),
        P(("fsdp", "dp"), None, None),
        P(("fsdp", "dp"), None, None),
        P(("fsdp", "dp"), None),
        P(("fsdp", "dp"), None),
        P(("fsdp", "dp"), None),
        P(("fsdp", "dp"), None),
        P(("fsdp", "dp"), None),
        P(("fsdp", "dp"), None),
        P(("fsdp", "dp"), None),
        P(("fsdp", "dp"), None),
        P(("fsdp", "dp"), None),
        P(("fsdp", "dp")),
    )
    if dict(mesh.shape) == {"fsdp": 8, "dp": 4}:
        program = functools.partial(local, GridGather, GridReduction)
    else:
        program = functools.partial(local, PlainGather, PlainReduction)
    return jax.shard_map(program, mesh=mesh, in_specs=in_specs, out_specs=out_specs, check_vma=False)
```

time: 556 us -> 395 us (0.71)
  matrix products: 184 us -> 85.6 us
  local copies, waits for them, and re-layouts: 102 us -> 30 us
  Pallas kernels: 42.5 us -> 73.2 us
  waiting for transfers between devices: 113 us -> 97.4 us
    dot_general x42 -> x30, matrix products: 184 us -> 85.6 us  [the longest x16 33.6 us: contract_low(): lax.dot_general(value, upstream_gradient, ((over, over), ((), ())), prefe...]
    pallas_call x0 -> x4, Pallas kernels: none -> 31.5 us  [per_sequence(): pl.pallas_call(body, out_shape=outs, grid_spec=pltpu.PrefetchScalarGridSp...]
    another operation x8 -> x0, local copies, waits for them, and re-layouts: 16.1 us -> none
    concatenate x7 -> x1, local copies, waits for them, and re-layouts: 16.7 us -> 1.03 us  [spread(): own = jnp.concatenate(shards, axis=1) if len(shards) > 1 else shards[0]]
    ppermute x76 -> x72, waiting for transfers between devices: 113 us -> 97.4 us  [move(): return lax.ppermute(value, AXES, perm)]
    slice x28 -> x16, local copies, waits for them, and re-layouts: 20.4 us -> 8.35 us  [the longest x8 8.3 us: plane(): return pick(self.keep[:, 0]) + pick(self.got[:, 0]) + pick(self.got_first)]
    reshape x6 -> x0, local copies, waits for them, and re-layouts: 12.1 us -> none  [the longest x1 2.61 us: local(): grad_ck.reshape(seqs, mem_rows, D)]
    convert_element_type x7 -> x1, local copies, waits for them, and re-layouts: 9.87 us -> 0.22 us  [local(): pre = project(normed3, w_in) + hidden_bias.astype(jnp.float32)]
  transfers between devices with their start and end apart: 76 -> 72, of which waited for: 23 -> 21; matrix products, arithmetic and copies ran while one was open for 30% -> 35% of each run, Pallas kernels for 6% -> 19%
where the time goes in v3:
time: 395 us; the launch traced here: 389 us
  waiting for transfers between devices  97.4 us (25%)
  matrix products  85.6 us (22%)
  Pallas kernels  73.2 us (19%)
  starting transfers between devices  63.8 us (16%)
  other arithmetic  37 us (9%)
  local copies, waits for them, and re-layouts  30 us (8%)
    ppermute x72, waiting for transfers between devices, move(): return lax.ppermute(value, AXES, perm)  97.4 us
    ppermute x72, starting transfers between devices, move(): return lax.ppermute(value, AXES, perm)  63.8 us
    dot_general x16, matrix products, contract_low(): lax.dot_general(value, upstream_gradient, ((over, over), ((), ())), prefe...  33.6 us
    pallas_call x4, Pallas kernels, per_sequence(): pl.pallas_call(body, out_shape=outs, grid_spec=pltpu.PrefetchScalarGridSp...  31.5 us
    dot_general x7, matrix products, back_project(): jnp.einsum('...j,aj->...a', upstream_gradient, weight_matrix, preferred_e...  27 us
    dot_general x7, matrix products, project(): jnp.einsum('...h,ht->...t', value_tensor, weight_matrix, preferred_elemen...  25.1 us
    pallas_call x4, Pallas kernels, assemble(): pl.pallas_call(functools.partial(assemble_body, widths), out_shape=[jax.S...  23.8 us
    pallas_call x4, Pallas kernels, split_add(): pl.pallas_call(functools.partial(split_body, len(pairs)), out_shape=[shap...  17.9 us
  transfers between devices with their start and end apart: 72, of which 21 were waited for; matrix products, arithmetic and copies ran while one was open for 35% of the time, Pallas kernels for 19%

profile of v3, /device:TPU:0, one launch (start us, length us, event | category | flops | bytes accessed | tf_op | source)
XLA Modules:
  0.0 389.2 jit_solution(5755838575422630282)
XLA Ops:
  4.2 5.1 %collective-permute-start.2 = (bf16[24,2560]{1,0:T(8,128)(2,1)S(1)}, bf16[24,2560]{1,0:T(8,128)(2,1)S(1)}, u32[]{:S(2)}, u32[]{:S(2)}) collective-permute-start(bf16[24,2560]{1,0:T(8,128)(2,1)S(1)} %concatenate.31), channel_id=1, source_target_pairs={{0,24},{1,25},{2,26},{3,27},{4,28},{5,29},{6,30},{7,31},{8,0},{9,1... | collective-permute-start | bytes 368648 | tf_op jit(solution)/shard_map/ppermute | solution.py:236
  13.0 6.9 %collective-permute-done.1 = bf16[24,2560]{1,0:T(8,128)(2,1)S(1)} collective-permute-done((bf16[24,2560]{1,0:T(8,128)(2,1)S(1)}, bf16[24,2560]{1,0:T(8,128)(2,1)S(1)}, u32[]{:S(2)}, u32[]{:S(2)}) %collective-permute-start.1) | collective-permute-done | bytes 122912 | tf_op jit(solution)/shard_map/ppermute | solution.py:236
  28.7 2.8 collective-permute-done.3.refs_1_
  31.5 2.5 collective-permute-start.5
  34.7 5.9 %collective-permute-done.11 = bf16[24,3840]{1,0:T(8,128)(2,1)S(1)} collective-permute-done((bf16[24,3840]{1,0:T(8,128)(2,1)S(1)}, bf16[24,3840]{1,0:T(8,128)(2,1)S(1)}, u32[]{:S(2)}, u32[]{:S(2)}) %collective-permute-start.11) | collective-permute-done | bytes 184352 | tf_op jit(solution)/shard_map/ppermute | solution.py:236
  47.2 8.0 %collective-permute-done.21 = bf16[24,3072]{1,0:T(8,128)(2,1)S(1)} collective-permute-done((bf16[24,3072]{1,0:T(8,128)(2,1)}, bf16[24,3072]{1,0:T(8,128)(2,1)S(1)}, u32[]{:S(2)}, u32[]{:S(2)}) %collective-permute-start.21) | collective-permute-done | bytes 147488 | tf_op jit(solution)/shard_map/ppermute | solution.py:236
  62.4 5.3 %assemble.4 = (bf16[4,2,2,2,24,2304]{5,4,3,2,1,0:T(8,128)(2,1)}, bf16[4,2,2,2,24,256]{5,4,3,2,1,0:T(8,128)(2,1)}) custom-call(s32[4]{0:T(128)} %pad_add_fusion.spot, bf16[4,24,2560]{2,1,0:T(8,128)(2,1)} %pad_maximum_fusion.3.refs_0_, bf16[4,24,2560]{2,1,0:T(8,128)(2,1)} %collective-permute-done.3.refs_1_, ...), custom_call_target="tpu_custom_call" | custom-call | tf_op jit(solution)/shard_map/assemble/pallas_call | solution.py:268
  77.6 4.9 %collective-permute-done.15.refs_3_ = bf16[4,24,3840]{2,1,0:T(8,128)(2,1)} collective-permute-done((bf16[4,24,3840]{2,1,0:T(8,128)(2,1)}, bf16[4,24,3840]{2,1,0:T(8,128)(2,1)}, u32[]{:S(2)}, u32[]{:S(2)}) %collective-permute-start.15) | collective-permute-done | bytes 737312 | tf_op jit(solution)/shard_map/ppermute | solution.py:236
  83.1 4.7 %convolution_convert_fusion.2 = bf16[384,2304]{1,0:T(8,128)(2,1)} fusion(bf16[384,768]{1,0:T(8,128)(2,1)S(1)} %bitcast.268, bf16[768,2304]{1,0:T(8,128)(2,1)} %bitcast.282), kind=kOutput, calls=%fused_computation.13 | convolution fusion | flops 1359839232 | bytes 5898240 | tf_op jit(solution)/shard_map/...h,ht->...t/dot_general | solution.py:38
  87.8 9.0 %self_forward.1 = (bf16[4,96,768]{2,1,0:T(8,128)(2,1)}, bf16[4,6,96,192]{3,2,1,0:T(8,128)(2,1)}) custom-call(s32[4]{0:T(128)} %lens.1, bf16[4,96,2304]{2,1,0:T(8,128)(2,1)} %bitcast.230), custom_call_target="tpu_custom_call" | custom-call | tf_op jit(solution)/shard_map/self_forward/pallas_call | solution.py:163
  102.2 10.9 %collective-permute-done.23.refs_1_ = bf16[4,24,3072]{2,1,0:T(8,128)(2,1)} collective-permute-done((bf16[4,24,3072]{2,1,0:T(8,128)(2,1)}, bf16[4,24,3072]{2,1,0:T(8,128)(2,1)}, u32[]{:S(2)}, u32[]{:S(2)}) %collective-permute-start.23) | collective-permute-done | bytes 589856 | tf_op jit(solution)/shard_map/ppermute | solution.py:236
  114.8 6.4 %assemble.5 = (bf16[4,2,2,2,24,768]{5,4,3,2,1,0:T(8,128)(2,1)}, bf16[4,2,2,2,24,768]{5,4,3,2,1,0:T(8,128)(2,1)}, bf16[4,2,2,2,24,1536]{5,4,3,2,1,0:T(8,128)(2,1)}, bf16[4,2,2,2,24,768]{5,4,3,2,1,0:T(8,128)(2,1)}) custom-call(s32[4]{0:T(128)} %pad_add_fusion.spot, bf16[4,24,3840]{2,1,0:T(8,128)(2,1)} %copy-done.10, ...), custom_call_target="tpu_custom_call" | custom-call | tf_op jit(solution)/shard_map/assemble/pallas_call | solution.py:268
  121.2 2.3 fusion.71
  123.8 3.5 fusion.7.kv
  130.3 6.5 %cross_forward.1 = (bf16[4,96,768]{2,1,0:T(8,128)(2,1)}, bf16[4,6,196,192]{3,2,1,0:T(8,128)(2,1)}) custom-call(bf16[4,96,768]{2,1,0:T(8,128)(2,1)} %bitcast.246, bf16[4,196,1536]{2,1,0:T(8,128)(2,1)} %fusion.7.kv), custom_call_target="tpu_custom_call" | custom-call | tf_op jit(solution)/shard_map/cross_forward/pallas_call | solution.py:163
  142.1 9.3 %collective-permute-done.33.refs_1_ = bf16[4,96,768]{2,1,0:T(8,128)(2,1)} collective-permute-done((bf16[4,96,768]{2,1,0:T(8,128)(2,1)}, bf16[4,96,768]{2,1,0:T(8,128)(2,1)}, u32[]{:S(2)}, u32[]{:S(2)}) %collective-permute-start.33) | collective-permute-done | bytes 589856 | tf_op jit(solution)/shard_map/ppermute | solution.py:236
  153.1 6.3 %assemble.6 = bf16[4,2,2,2,24,3072]{5,4,3,2,1,0:T(8,128)(2,1)} custom-call(s32[4]{0:T(128)} %pad_add_fusion.spot, bf16[4,24,3072]{2,1,0:T(8,128)(2,1)} %pad_maximum_fusion.1.refs_0_, bf16[4,24,3072]{2,1,0:T(8,128)(2,1)} %collective-permute-done.23.refs_1_, bf16[4,24,3072]{2,1,0:T(8,128)(2,1)} %collective-permute-done.24.refs_2_, ...), custom_call_target="tpu_custom_call" | custom-call | tf_op jit(solution)/shard_map/assemble/pallas_call | solution.py:268
  159.4 8.0 %multiply_convert_fusion = (bf16[384,3072]{1,0:T(8,128)(2,1)S(1)}, f32[384,3072]{1,0:T(8,128)}) fusion(f32[3072]{0:T(1024)S(1)} %reshape.482, bf16[768,3072]{1,0:T(8,128)(2,1)} %bitcast.234, f32[384,768]{1,0:T(8,128)} %copy-done.2, f32[768]{0:T(1024)S(1)} %copy-done.42, f32[768]{0:T(1024)S(1)} %get-tuple-element.189, f32[384]{0:T(512)S(1)} %add_rsqrt_fusion, ...), kind=kOutput, calls=%fused_computation.9 | convolution fusion | flops 1825210368 | bytes 12997632 | tf_op jit(solution)/shard_map/...h,ht->...t/dot_general | solution.py:38
  167.4 3.1 convolution_convert_fusion.1
  171.0 3.1 convolution_convert_fusion
  174.1 5.8 %assemble.7 = bf16[4,2,2,2,96,768]{5,4,3,2,1,0:T(8,128)(2,1)} custom-call(s32[4]{0:T(128)} %pad_add_fusion.spot, bf16[4,96,768]{2,1,0:T(8,128)(2,1)} %pad_maximum_fusion.2.refs_0_, bf16[4,96,768]{2,1,0:T(8,128)(2,1)} %collective-permute-done.33.refs_1_, bf16[4,96,768]{2,1,0:T(8,128)(2,1)} %collective-permute-done.34.refs_2_, ...), custom_call_target="tpu_custom_call" | custom-call | tf_op jit(solution)/shard_map/assemble/pallas_call | solution.py:268
  179.9 7.4 %fusion.64 = (bf16[3072]{0:T(1024)(128)(2,1)S(1)}, bf16[384,3072]{1,0:T(8,128)(2,1)S(1)}) fusion(f32[384,3072]{1,0:T(8,128)} %get-tuple-element.236, bf16[384,768]{1,0:T(8,128)(2,1)} %bitcast_convert_fusion.2, bf16[3072,768]{1,0:T(8,128)(2,1)} %bitcast.236), kind=kOutput, calls=%fused_computation.191 | convolution fusion | flops 1836708864 | bytes 12392448 | tf_op jit(solution)/shard_map/...j,aj->...a/dot_general | solution.py:42
  187.4 3.1 convolution_convert_fusion.7
  192.1 2.8 fusion.10
  195.5 4.7 %convolution_convert_fusion.6 = bf16[768,1536]{1,0:T(8,128)(2,1)} fusion(bf16[384,3072]{1,0:T(8,128)(2,1)} %copy-done.55, s32[]{:T(128)S(6)} %select_n.308, f32[384,768]{1,0:T(8,128)} %copy-done.2, f32[768]{0:T(1024)S(1)} %copy-done.42, f32[768]{0:T(1024)S(1)} %get-tuple-element.189, f32[384]{0:T(512)S(1)} %add_rsqrt_fusion, ...), kind=kOutput, calls=%fused_computation.17 | convolution fusion | flops 908623872 | bytes 4727812 | tf_op jit(solution)/shard_map/dot_general | solution.py:471
  200.2 4.4 %split_add.4 = (bf16[4,2,192,384]{3,2,1,0:T(8,128)(2,1)}, bf16[4,2,192,384]{3,2,1,0:T(8,128)(2,1)}) custom-call(s32[4]{0:T(128)} %pad_add_fusion.1.which, bf16[4,4,192,384]{3,2,1,0:T(8,128)(2,1)} %bitcast.226, bf16[4,4,192,384]{3,2,1,0:T(8,128)(2,1)} %bitcast.44.refs_1_.refs_3_, bf16[4,4,192,384]{3,2,1,0:T(8,128)(2,1)} %bitcast.227, ...), custom_call_target="tpu_custom_call" | custom-call | tf_op jit(solution)/shard_map/split_add/pallas_call | solution.py:372
  205.4 5.8 %multiply_reduce_fusion = (bf16[768]{0:T(1024)(128)(2,1)S(1)}, f32[384]{0:T(512)S(1)}, f32[384]{0:T(512)S(1)}, bf16[768]{0:T(1024)(128)(2,1)S(1)}, f32[384,768]{1,0:T(8,128)S(1)}) fusion(f32[384,768]{1,0:T(8,128)} %copy-done.2, f32[384]{0:T(512)S(1)} %add_rsqrt_fusion, f32[384]{0:T(512)S(1)} %broadcast_multiply_fusion.6, f32[768]{0:T(1024)S(1)} %get-tuple-element.189, ...), kind=kOutput, calls=%fused_computation.45 | convolution fusion | flops 1814591232 | bytes 9449472 | tf_op jit(solution)/shard_map/...j,aj->...a/dot_general | solution.py:42
  218.9 4.4 %split_add.5 = (bf16[4,2,48,1536]{3,2,1,0:T(8,128)(2,1)}, bf16[4,2,48,1536]{3,2,1,0:T(8,128)(2,1)}) custom-call(s32[4]{0:T(128)} %pad_add_fusion.1.which, bf16[4,4,48,1536]{3,2,1,0:T(8,128)(2,1)} %bitcast.224, bf16[4,4,48,1536]{3,2,1,0:T(8,128)(2,1)} %bitcast.48.refs_1_.refs_3_, bf16[4,4,48,1536]{3,2,1,0:T(8,128)(2,1)} %bitcast.225, ...), custom_call_target="tpu_custom_call" | custom-call | tf_op jit(solution)/shard_map/split_add/pallas_call | solution.py:372
  229.5 7.8 %cross_backward.1 = (bf16[4,96,768]{2,1,0:T(8,128)(2,1)}, bf16[4,196,1536]{2,1,0:T(8,128)(2,1)}) custom-call(bf16[4,96,768]{2,1,0:T(8,128)(2,1)} %bitcast.247, bf16[4,196,1536]{2,1,0:T(8,128)(2,1)} %fusion.7.kv, bf16[4,6,196,192]{3,2,1,0:T(8,128)(2,1)} %get-tuple-element.109.probs, bf16[4,96,768]{2,1,0:T(8,128)(2,1)} %bitcast.267), custom_call_target="tpu_custom_call" | custom-call | tf_op jit(solution)/shard_map/cross_backward/pallas_call | solution.py:163
  237.2 2.7 convolution_convert_fusion.14
  241.1 2.5 bitcast_convert_fusion
  249.1 2.9 collective-permute-start.46
  256.5 5.9 %collective-permute-done.46 = bf16[192,384]{1,0:T(8,128)(2,1)S(1)} collective-permute-done((bf16[192,384]{1,0:T(8,128)(2,1)S(1)}, bf16[192,384]{1,0:T(8,128)(2,1)S(1)}, u32[]{:S(2)}, u32[]{:S(2)}) %collective-permute-start.46) | collective-permute-done | bytes 147488 | tf_op jit(solution)/shard_map/ppermute | solution.py:236
  273.5 2.6 copy.85
  276.1 4.5 %split_add.7 = (bf16[4,2,48,1536]{3,2,1,0:T(8,128)(2,1)}, bf16[4,2,48,1536]{3,2,1,0:T(8,128)(2,1)}) custom-call(s32[4]{0:T(128)} %pad_add_fusion.1.which, bf16[4,4,48,384]{3,2,1,0:T(8,128)(2,1)} %bitcast.244, bf16[4,4,48,384]{3,2,1,0:T(8,128)(2,1)} %bitcast.79.refs_1_.refs_7_, bf16[4,4,48,768]{3,2,1,0:T(8,128)(2,1)} %bitcast.232, ...), custom_call_target="tpu_custom_call" | custom-call | tf_op jit(solution)/shard_map/split_add/pallas_call | solution.py:372
  283.2 8.3 %self_backward.1 = bf16[4,96,2304]{2,1,0:T(8,128)(2,1)} custom-call(bf16[4,96,2304]{2,1,0:T(8,128)(2,1)} %bitcast.231, bf16[4,6,96,192]{3,2,1,0:T(8,128)(2,1)} %get-tuple-element.117.probs, bf16[4,96,768]{2,1,0:T(8,128)(2,1)} %bitcast.272), custom_call_target="tpu_custom_call" | custom-call | tf_op jit(solution)/shard_map/self_backward/pallas_call | solution.py:163
  291.5 5.4 %multiply_reduce_fusion.2 = (bf16[768]{0:T(1024)(128)(2,1)S(1)}, f32[384]{0:T(512)S(1)}, f32[384]{0:T(512)S(1)}, bf16[768]{0:T(1024)(128)(2,1)S(1)}, bf16[384,768]{1,0:T(8,128)(2,1)S(1)}, /*index=5*/f32[384,768]{1,0:T(8,128)}) fusion(bf16[4,96,768]{2,1,0:T(8,128)(2,1)S(1)} %copy-done.1, f32[384]{0:T(512)S(1)} %copy-done.40, f32[384]{0:T(512)S(1)} %copy-done.41, ...), kind=kOutput, calls=%fused_computation.47 | convolution fusion | flops 1362786048 | bytes 7683072 | tf_op jit(solution)/shard_map/...j,aj->...a/dot_general | solution.py:42
  297.7 2.5 convolution_convert_fusion.5
  300.6 4.5 %fusion.73 = f32[4,196,768]{2,1,0:T(8,128)S(1)} fusion(bf16[4,196,1536]{2,1,0:T(8,128)(2,1)} %get-tuple-element.120, bf16[768,1536,1]{1,0,2:T(8,128)(2,1)} %bitcast.284), kind=kOutput, calls=%fused_computation.199 | convolution fusion | flops 1849688064 | bytes 7176192 | tf_op jit(solution)/shard_map/...j,aj->...a/dot_general | solution.py:42
  305.1 2.4 copy.86
  308.8 4.5 %collective-permute-start.69 = (bf16[48,1536]{1,0:T(8,128)(2,1)S(1)}, bf16[48,1536]{1,0:T(8,128)(2,1)S(1)}, u32[]{:S(2)}, u32[]{:S(2)}) collective-permute-start(bf16[48,1536]{1,0:T(8,128)(2,1)S(1)} %get-tuple-element.206), channel_id=1, source_target_pairs={{0,24},{1,25},{2,26},{3,27},{4,28},{5,29},{6,30},{7,31},{8,0},{9,1... | collective-permute-start | bytes 442376 | tf_op jit(solution)/shard_map/ppermute | solution.py:236
  316.0 2.4 convolution_convert_fusion.4
  318.5 7.2 %collective-permute-done.68 = bf16[48,1536]{1,0:T(8,128)(2,1)S(1)} collective-permute-done((bf16[48,1536]{1,0:T(8,128)(2,1)S(1)}, bf16[48,1536]{1,0:T(8,128)(2,1)S(1)}, u32[]{:S(2)}, u32[]{:S(2)}) %collective-permute-start.68) | collective-permute-done | bytes 147488 | tf_op jit(solution)/shard_map/ppermute | solution.py:236
  333.5 4.7 %split_add.6 = (bf16[4,2,48,1664]{3,2,1,0:T(8,128)(2,1)}, bf16[4,2,48,1664]{3,2,1,0:T(8,128)(2,1)}) custom-call(s32[4]{0:T(128)} %pad_add_fusion.1.which, bf16[4,4,48,1152]{3,2,1,0:T(8,128)(2,1)} %bitcast.228, bf16[4,4,48,1152]{3,2,1,0:T(8,128)(2,1)} %bitcast.64.refs_1_.refs_7_, bf16[4,4,48,384]{3,2,1,0:T(8,128)(2,1)} %bitcast.238, ...), custom_call_target="tpu_custom_call" | custom-call | tf_op jit(solution)/shard_map/split_add/pallas_call | solution.py:372
  346.4 9.7 %collective-permute-done.64 = bf16[48,1536]{1,0:T(8,128)(2,1)S(1)} collective-permute-done((bf16[48,1536]{1,0:T(8,128)(2,1)S(1)}, bf16[48,1536]{1,0:T(8,128)(2,1)S(1)}, u32[]{:S(2)}, u32[]{:S(2)}) %collective-permute-start.64) | collective-permute-done | bytes 147488 | tf_op jit(solution)/shard_map/ppermute | solution.py:236
  359.4 8.6 %collective-permute-done.56 = bf16[4,48,1664]{2,1,0:T(8,128)(2,1)S(1)} collective-permute-done((bf16[4,48,1664]{2,1,0:T(8,128)(2,1)S(1)}, bf16[4,48,1664]{2,1,0:T(8,128)(2,1)S(1)}, u32[]{:S(2)}, u32[]{:S(2)}) %collective-permute-start.56) | collective-permute-done | bytes 639008 | tf_op jit(solution)/shard_map/ppermute | solution.py:236
  371.6 3.1 collective-permute-done.59
  374.7 9.1 %collective-permute-done.58 = bf16[48,1664]{1,0:T(8,128)(2,1)S(1)} collective-permute-done((bf16[48,1664]{1,0:T(8,128)(2,1)S(1)}, bf16[48,1664]{1,0:T(8,128)(2,1)S(1)}, u32[]{:S(2)}, u32[]{:S(2)}) %collective-permute-start.58) | collective-permute-done | bytes 159776 | tf_op jit(solution)/shard_map/ppermute | solution.py:236
  (357 shorter events, 133.3 us)
Async XLA Ops:
  24.0 16.6 %collective-permute-start.11 = (bf16[24,3840]{1,0:T(8,128)(2,1)S(1)}, bf16[24,3840]{1,0:T(8,128)(2,1)S(1)}, u32[]{:S(2)}, u32[]{:S(2)}) collective-permute-start(bf16[24,3840]{1,0:T(8,128)(2,1)S(1)} %pad_maximum_fusion.7), channel_id=1, source_target_pairs={{0,16},{1,17},{2,18},{3,19},{4,20},{5,21},{6,22},{7,23},{8,24},{9,... | collective-permute-start | bytes 552968 | tf_op jit(solution)/shard_map/ppermute | solution.py:236
  25.0 15.6 %collective-permute-start.10 = (bf16[24,3840]{1,0:T(8,128)(2,1)S(1)}, bf16[24,3840]{1,0:T(8,128)(2,1)S(1)}, u32[]{:S(2)}, u32[]{:S(2)}) collective-permute-start(bf16[24,3840]{1,0:T(8,128)(2,1)S(1)} %pad_maximum_fusion.7), channel_id=1, source_target_pairs={{0,8},{1,9},{2,10},{3,11},{4,12},{5,13},{6,14},{7,15},{8,16},{9,17... | collective-permute-start | bytes 552968 | tf_op jit(solution)/shard_map/ppermute | solution.py:236
  27.1 19.4 %collective-permute-start.4 = (bf16[4,24,2560]{2,1,0:T(8,128)(2,1)}, bf16[4,24,2560]{2,1,0:T(8,128)(2,1)}, u32[]{:S(2)}, u32[]{:S(2)}) collective-permute-start(bf16[4,24,2560]{2,1,0:T(8,128)(2,1)} %pad_maximum_fusion.3.refs_0_), channel_id=1, source_target_pairs={{0,2},{1,5},{2,0},{3,7},{4,6},{5,1},{6,4},{7,3},{8,10},{9,13},{10,... | collective-permute-start | bytes 1474568 | tf_op jit(solution)/shard_map/ppermute | solution.py:236
  31.5 13.1 %collective-permute-start.5 = (bf16[4,24,2560]{2,1,0:T(8,128)(2,1)}, bf16[4,24,2560]{2,1,0:T(8,128)(2,1)}, u32[]{:S(2)}, u32[]{:S(2)}) collective-permute-start(bf16[4,24,2560]{2,1,0:T(8,128)(2,1)} %collective-permute-done.3.refs_1_), channel_id=1, source_target_pairs={{0,2},{1,5},{2,0},{3,7},{4,6},{5,1},{6,4},{7,3},{8,10},{9,13},{10,... | collective-permute-start | bytes 1474568 | tf_op jit(solution)/shard_map/ppermute | solution.py:236
  40.6 14.6 %collective-permute-start.21 = (bf16[24,3072]{1,0:T(8,128)(2,1)}, bf16[24,3072]{1,0:T(8,128)(2,1)S(1)}, u32[]{:S(2)}, u32[]{:S(2)}) collective-permute-start(bf16[24,3072]{1,0:T(8,128)(2,1)} %param.23), channel_id=1, source_target_pairs={{0,16},{1,17},{2,18},{3,19},{4,20},{5,21},{6,22},{7,23},{8,24},{9,... | collective-permute-start | bytes 442376 | tf_op jit(solution)/shard_map/ppermute | solution.py:236
  41.4 16.0 %collective-permute-start.20 = (bf16[24,3072]{1,0:T(8,128)(2,1)}, bf16[24,3072]{1,0:T(8,128)(2,1)}, u32[]{:S(2)}, u32[]{:S(2)}) collective-permute-start(bf16[24,3072]{1,0:T(8,128)(2,1)} %param.23), channel_id=1, source_target_pairs={{0,8},{1,9},{2,10},{3,11},{4,12},{5,13},{6,14},{7,15},{8,16},{9,17... | collective-permute-start | bytes 442376 | tf_op jit(solution)/shard_map/ppermute | solution.py:236
  44.6 16.7 %collective-permute-start.6 = (bf16[4,24,2560]{2,1,0:T(8,128)(2,1)}, bf16[4,24,2560]{2,1,0:T(8,128)(2,1)}, u32[]{:S(2)}, u32[]{:S(2)}) collective-permute-start(bf16[4,24,2560]{2,1,0:T(8,128)(2,1)} %pad_maximum_fusion.3.refs_0_), channel_id=1, source_target_pairs={{0,1},{1,0},{2,3},{3,2},{4,5},{5,4},{6,7},{7,6},{8,9},{9,8},{10,11... | collective-permute-start | bytes 1474568 | tf_op jit(solution)/shard_map/ppermute | solution.py:236
  46.5 15.3 %collective-permute-start.7 = (bf16[4,24,2560]{2,1,0:T(8,128)(2,1)}, bf16[4,24,2560]{2,1,0:T(8,128)(2,1)}, u32[]{:S(2)}, u32[]{:S(2)}) collective-permute-start(bf16[4,24,2560]{2,1,0:T(8,128)(2,1)} %collective-permute-done.3.refs_1_), channel_id=1, source_target_pairs={{0,1},{1,0},{2,3},{3,2},{4,5},{5,4},{6,7},{7,6},{8,9},{9,8},{10,11... | collective-permute-start | bytes 1474568 | tf_op jit(solution)/shard_map/ppermute | solution.py:236
  46.6 15.3 %collective-permute-start.8 = (bf16[4,24,2560]{2,1,0:T(8,128)(2,1)}, bf16[4,24,2560]{2,1,0:T(8,128)(2,1)}, u32[]{:S(2)}, u32[]{:S(2)}) collective-permute-start(bf16[4,24,2560]{2,1,0:T(8,128)(2,1)} %collective-permute-done.4.refs_2_), channel_id=1, source_target_pairs={{0,1},{1,0},{2,3},{3,2},{4,5},{5,4},{6,7},{7,6},{8,9},{9,8},{10,11... | collective-permute-start | bytes 1474568 | tf_op jit(solution)/shard_map/ppermute | solution.py:236
  55.9 14.7 %collective-permute-start.13 = (bf16[4,24,3840]{2,1,0:T(8,128)(2,1)S(1)}, bf16[4,24,3840]{2,1,0:T(8,128)(2,1)}, u32[]{:S(2)}, u32[]{:S(2)}) collective-permute-start(bf16[4,24,3840]{2,1,0:T(8,128)(2,1)S(1)} %pad_maximum_fusion.refs_0_), channel_id=1, source_target_pairs={{0,4},{1,3},{2,6},{3,1},{4,0},{5,7},{6,2},{7,5},{8,12},{9,11},{10,... | collective-permute-start | bytes 2211848 | tf_op jit(solution)/shard_map/ppermute | solution.py:236
  61.3 37.0 %collective-permute-start.16 = (bf16[4,24,3840]{2,1,0:T(8,128)(2,1)S(1)}, bf16[4,24,3840]{2,1,0:T(8,128)(2,1)}, u32[]{:S(2)}, u32[]{:S(2)}) collective-permute-start(bf16[4,24,3840]{2,1,0:T(8,128)(2,1)S(1)} %pad_maximum_fusion.refs_0_), channel_id=1, source_target_pairs={{0,1},{1,0},{2,3},{3,2},{4,5},{5,4},{6,7},{7,6},{8,9},{9,8},{10,11... | collective-permute-start | bytes 2211848 | tf_op jit(solution)/shard_map/ppermute | solution.py:236
  61.8 13.0 %collective-permute-start.32 = (bf16[96,768]{1,0:T(8,128)(2,1)}, bf16[96,768]{1,0:T(8,128)(2,1)}, u32[]{:S(2)}, u32[]{:S(2)}) collective-permute-start(bf16[96,768]{1,0:T(8,128)(2,1)} %param.24), channel_id=1, source_target_pairs={{0,24},{1,25},{2,26},{3,27},{4,28},{5,29},{6,30},{7,31},{8,0},{9,1... | collective-permute-start | bytes 442376 | tf_op jit(solution)/shard_map/ppermute | solution.py:236
  61.8 15.2 %collective-permute-start.31 = (bf16[96,768]{1,0:T(8,128)(2,1)}, bf16[96,768]{1,0:T(8,128)(2,1)}, u32[]{:S(2)}, u32[]{:S(2)}) collective-permute-start(bf16[96,768]{1,0:T(8,128)(2,1)} %param.24), channel_id=1, source_target_pairs={{0,16},{1,17},{2,18},{3,19},{4,20},{5,21},{6,22},{7,23},{8,24},{9,... | collective-permute-start | bytes 442376 | tf_op jit(solution)/shard_map/ppermute | solution.py:236
  61.9 15.2 %collective-permute-start.14 = (bf16[4,24,3840]{2,1,0:T(8,128)(2,1)S(1)}, bf16[4,24,3840]{2,1,0:T(8,128)(2,1)}, u32[]{:S(2)}, u32[]{:S(2)}) collective-permute-start(bf16[4,24,3840]{2,1,0:T(8,128)(2,1)S(1)} %pad_maximum_fusion.refs_0_), channel_id=1, source_target_pairs={{0,2},{1,5},{2,0},{3,7},{4,6},{5,1},{6,4},{7,3},{8,10},{9,13},{10,... | collective-permute-start | bytes 2211848 | tf_op jit(solution)/shard_map/ppermute | solution.py:236
  74.8 22.0 %collective-permute-start.30 = (bf16[96,768]{1,0:T(8,128)(2,1)}, bf16[96,768]{1,0:T(8,128)(2,1)}, u32[]{:S(2)}, u32[]{:S(2)}) collective-permute-start(bf16[96,768]{1,0:T(8,128)(2,1)} %param.24), channel_id=1, source_target_pairs={{0,8},{1,9},{2,10},{3,11},{4,12},{5,13},{6,14},{7,15},{8,16},{9,17... | collective-permute-start | bytes 442376 | tf_op jit(solution)/shard_map/ppermute | solution.py:236
  77.1 25.1 %collective-permute-start.17 = (bf16[4,24,3840]{2,1,0:T(8,128)(2,1)}, bf16[4,24,3840]{2,1,0:T(8,128)(2,1)}, u32[]{:S(2)}, u32[]{:S(2)}) collective-permute-start(bf16[4,24,3840]{2,1,0:T(8,128)(2,1)} %collective-permute-done.13.refs_1_), channel_id=1, source_target_pairs={{0,1},{1,0},{2,3},{3,2},{4,5},{5,4},{6,7},{7,6},{8,9},{9,8},{10,11... | collective-permute-start | bytes 2211848 | tf_op jit(solution)/shard_map/ppermute | solution.py:236
  77.1 37.2 %collective-permute-start.18 = (bf16[4,24,3840]{2,1,0:T(8,128)(2,1)}, bf16[4,24,3840]{2,1,0:T(8,128)(2,1)}, u32[]{:S(2)}, u32[]{:S(2)}) collective-permute-start(bf16[4,24,3840]{2,1,0:T(8,128)(2,1)} %collective-permute-done.14.refs_2_), channel_id=1, source_target_pairs={{0,1},{1,0},{2,3},{3,2},{4,5},{5,4},{6,7},{7,6},{8,9},{9,8},{10,11... | collective-permute-start | bytes 2211848 | tf_op jit(solution)/shard_map/ppermute | solution.py:236
  82.5 32.3 %collective-permute-start.19 = (bf16[4,24,3840]{2,1,0:T(8,128)(2,1)}, bf16[4,24,3840]{2,1,0:T(8,128)(2,1)}, u32[]{:S(2)}, u32[]{:S(2)}) collective-permute-start(bf16[4,24,3840]{2,1,0:T(8,128)(2,1)} %collective-permute-done.15.refs_3_), channel_id=1, source_target_pairs={{0,1},{1,0},{2,3},{3,2},{4,5},{5,4},{6,7},{7,6},{8,9},{9,8},{10,11... | collective-permute-start | bytes 2211848 | tf_op jit(solution)/shard_map/ppermute | solution.py:236
  96.9 16.2 %collective-permute-start.23 = (bf16[4,24,3072]{2,1,0:T(8,128)(2,1)}, bf16[4,24,3072]{2,1,0:T(8,128)(2,1)}, u32[]{:S(2)}, u32[]{:S(2)}) collective-permute-start(bf16[4,24,3072]{2,1,0:T(8,128)(2,1)} %pad_maximum_fusion.1.refs_0_), channel_id=1, source_target_pairs={{0,4},{1,3},{2,6},{3,1},{4,0},{5,7},{6,2},{7,5},{8,12},{9,11},{10,... | collective-permute-start | bytes 1769480 | tf_op jit(solution)/shard_map/ppermute | solution.py:236
  98.3 15.9 %collective-permute-start.24 = (bf16[4,24,3072]{2,1,0:T(8,128)(2,1)}, bf16[4,24,3072]{2,1,0:T(8,128)(2,1)}, u32[]{:S(2)}, u32[]{:S(2)}) collective-permute-start(bf16[4,24,3072]{2,1,0:T(8,128)(2,1)} %pad_maximum_fusion.1.refs_0_), channel_id=1, source_target_pairs={{0,2},{1,5},{2,0},{3,7},{4,6},{5,1},{6,4},{7,3},{8,10},{9,13},{10,... | collective-permute-start | bytes 1769480 | tf_op jit(solution)/shard_map/ppermute | solution.py:236
  102.2 37.1 %collective-permute-start.26 = (bf16[4,24,3072]{2,1,0:T(8,128)(2,1)}, bf16[4,24,3072]{2,1,0:T(8,128)(2,1)}, u32[]{:S(2)}, u32[]{:S(2)}) collective-permute-start(bf16[4,24,3072]{2,1,0:T(8,128)(2,1)} %pad_maximum_fusion.1.refs_0_), channel_id=1, source_target_pairs={{0,1},{1,0},{2,3},{3,2},{4,5},{5,4},{6,7},{7,6},{8,9},{9,8},{10,11... | collective-permute-start | bytes 1769480 | tf_op jit(solution)/shard_map/ppermute | solution.py:236
  113.1 28.1 %collective-permute-start.25 = (bf16[4,24,3072]{2,1,0:T(8,128)(2,1)}, bf16[4,24,3072]{2,1,0:T(8,128)(2,1)}, u32[]{:S(2)}, u32[]{:S(2)}) collective-permute-start(bf16[4,24,3072]{2,1,0:T(8,128)(2,1)} %collective-permute-done.23.refs_1_), channel_id=1, source_target_pairs={{0,2},{1,5},{2,0},{3,7},{4,6},{5,1},{6,4},{7,3},{8,10},{9,13},{10,... | collective-permute-start | bytes 1769480 | tf_op jit(solution)/shard_map/ppermute | solution.py:236
  114.3 27.2 %collective-permute-start.27 = (bf16[4,24,3072]{2,1,0:T(8,128)(2,1)}, bf16[4,24,3072]{2,1,0:T(8,128)(2,1)}, u32[]{:S(2)}, u32[]{:S(2)}) collective-permute-start(bf16[4,24,3072]{2,1,0:T(8,128)(2,1)} %collective-permute-done.23.refs_1_), channel_id=1, source_target_pairs={{0,1},{1,0},{2,3},{3,2},{4,5},{5,4},{6,7},{7,6},{8,9},{9,8},{10,11... | collective-permute-start | bytes 1769480 | tf_op jit(solution)/shard_map/ppermute | solution.py:236
  114.3 37.6 %collective-permute-start.28 = (bf16[4,24,3072]{2,1,0:T(8,128)(2,1)}, bf16[4,24,3072]{2,1,0:T(8,128)(2,1)}, u32[]{:S(2)}, u32[]{:S(2)}) collective-permute-start(bf16[4,24,3072]{2,1,0:T(8,128)(2,1)} %collective-permute-done.24.refs_2_), channel_id=1, source_target_pairs={{0,1},{1,0},{2,3},{3,2},{4,5},{5,4},{6,7},{7,6},{8,9},{9,8},{10,11... | collective-permute-start | bytes 1769480 | tf_op jit(solution)/shard_map/ppermute | solution.py:236
  136.7 14.6 %collective-permute-start.33 = (bf16[4,96,768]{2,1,0:T(8,128)(2,1)}, bf16[4,96,768]{2,1,0:T(8,128)(2,1)}, u32[]{:S(2)}, u32[]{:S(2)}) collective-permute-start(bf16[4,96,768]{2,1,0:T(8,128)(2,1)} %pad_maximum_fusion.2.refs_0_), channel_id=1, source_target_pairs={{0,4},{1,3},{2,6},{3,1},{4,0},{5,7},{6,2},{7,5},{8,12},{9,11},{10,... | collective-permute-start | bytes 1769480 | tf_op jit(solution)/shard_map/ppermute | solution.py:236
  139.2 13.1 %collective-permute-start.34 = (bf16[4,96,768]{2,1,0:T(8,128)(2,1)}, bf16[4,96,768]{2,1,0:T(8,128)(2,1)}, u32[]{:S(2)}, u32[]{:S(2)}) collective-permute-start(bf16[4,96,768]{2,1,0:T(8,128)(2,1)} %pad_maximum_fusion.2.refs_0_), channel_id=1, source_target_pairs={{0,2},{1,5},{2,0},{3,7},{4,6},{5,1},{6,4},{7,3},{8,10},{9,13},{10,... | collective-permute-start | bytes 1769480 | tf_op jit(solution)/shard_map/ppermute | solution.py:236
  141.5 32.6 %collective-permute-start.36 = (bf16[4,96,768]{2,1,0:T(8,128)(2,1)}, bf16[4,96,768]{2,1,0:T(8,128)(2,1)}, u32[]{:S(2)}, u32[]{:S(2)}) collective-permute-start(bf16[4,96,768]{2,1,0:T(8,128)(2,1)} %pad_maximum_fusion.2.refs_0_), channel_id=1, source_target_pairs={{0,1},{1,0},{2,3},{3,2},{4,5},{5,4},{6,7},{7,6},{8,9},{9,8},{10,11... | collective-permute-start | bytes 1769480 | tf_op jit(solution)/shard_map/ppermute | solution.py:236
  151.3 16.1 %collective-permute-start.35 = (bf16[4,96,768]{2,1,0:T(8,128)(2,1)}, bf16[4,96,768]{2,1,0:T(8,128)(2,1)}, u32[]{:S(2)}, u32[]{:S(2)}) collective-permute-start(bf16[4,96,768]{2,1,0:T(8,128)(2,1)} %collective-permute-done.33.refs_1_), channel_id=1, source_target_pairs={{0,2},{1,5},{2,0},{3,7},{4,6},{5,1},{6,4},{7,3},{8,10},{9,13},{10,... | collective-permute-start | bytes 1769480 | tf_op jit(solution)/shard_map/ppermute | solution.py:236
  151.9 22.2 %collective-permute-start.37 = (bf16[4,96,768]{2,1,0:T(8,128)(2,1)}, bf16[4,96,768]{2,1,0:T(8,128)(2,1)}, u32[]{:S(2)}, u32[]{:S(2)}) collective-permute-start(bf16[4,96,768]{2,1,0:T(8,128)(2,1)} %collective-permute-done.33.refs_1_), channel_id=1, source_target_pairs={{0,1},{1,0},{2,3},{3,2},{4,5},{5,4},{6,7},{7,6},{8,9},{9,8},{10,11... | collective-permute-start | bytes 1769480 | tf_op jit(solution)/shard_map/ppermute | solution.py:236
  152.4 21.7 %collective-permute-start.38 = (bf16[4,96,768]{2,1,0:T(8,128)(2,1)}, bf16[4,96,768]{2,1,0:T(8,128)(2,1)}, u32[]{:S(2)}, u32[]{:S(2)}) collective-permute-start(bf16[4,96,768]{2,1,0:T(8,128)(2,1)} %collective-permute-done.34.refs_2_), channel_id=1, source_target_pairs={{0,1},{1,0},{2,3},{3,2},{4,5},{5,4},{6,7},{7,6},{8,9},{9,8},{10,11... | collective-permute-start | bytes 1769480 | tf_op jit(solution)/shard_map/ppermute | solution.py:236
  170.5 29.7 %collective-permute-start.40 = (bf16[3072,384]{1,0:T(8,128)(2,1)}, bf16[3072,384]{1,0:T(8,128)(2,1)}, u32[]{:S(2)}, u32[]{:S(2)}) collective-permute-start(bf16[3072,384]{1,0:T(8,128)(2,1)} %convolution_convert_fusion.1), channel_id=1, source_target_pairs={{0,1},{1,0},{2,3},{3,2},{4,5},{5,4},{6,7},{7,6},{8,9},{9,8},{10,11... | collective-permute-start | bytes 7077896 | tf_op jit(solution)/shard_map/ppermute | solution.py:236
  190.5 28.4 %collective-permute-start.42 = (bf16[768,1536]{1,0:T(8,128)(2,1)}, bf16[768,1536]{1,0:T(8,128)(2,1)}, u32[]{:S(2)}, u32[]{:S(2)}) collective-permute-start(bf16[768,1536]{1,0:T(8,128)(2,1)} %convolution_convert_fusion.7), channel_id=1, source_target_pairs={{0,1},{1,0},{2,3},{3,2},{4,5},{5,4},{6,7},{7,6},{8,9},{9,8},{10,11... | collective-permute-start | bytes 7077896 | tf_op jit(solution)/shard_map/ppermute | solution.py:236
  204.5 21.4 %collective-permute-start.41 = (bf16[4,2,192,384]{3,2,1,0:T(8,128)(2,1)}, bf16[4,2,192,384]{3,2,1,0:T(8,128)(2,1)}, u32[]{:S(2)}, u32[]{:S(2)}) collective-permute-start(bf16[4,2,192,384]{3,2,1,0:T(8,128)(2,1)} %get-tuple-element.110), channel_id=1, source_target_pairs={{0,2},{1,5},{2,0},{3,7},{4,6},{5,1},{6,4},{7,3},{8,10},{9,13},{10,... | collective-permute-start | bytes 3538952 | tf_op jit(solution)/shard_map/ppermute | solution.py:236
  215.5 60.6 %collective-permute-start.51 = (bf16[768,384]{1,0:T(8,128)(2,1)}, bf16[768,384]{1,0:T(8,128)(2,1)}, u32[]{:S(2)}, u32[]{:S(2)}) collective-permute-start(bf16[768,384]{1,0:T(8,128)(2,1)} %convolution_convert_fusion.13), channel_id=1, source_target_pairs={{0,1},{1,0},{2,3},{3,2},{4,5},{5,4},{6,7},{7,6},{8,9},{9,8},{10,11... | collective-permute-start | bytes 1769480 | tf_op jit(solution)/shard_map/ppermute | solution.py:236
  223.2 28.8 %collective-permute-start.44 = (bf16[4,2,48,1536]{3,2,1,0:T(8,128)(2,1)}, bf16[4,2,48,1536]{3,2,1,0:T(8,128)(2,1)}, u32[]{:S(2)}, u32[]{:S(2)}) collective-permute-start(bf16[4,2,48,1536]{3,2,1,0:T(8,128)(2,1)} %get-tuple-element.114), channel_id=1, source_target_pairs={{0,2},{1,5},{2,0},{3,7},{4,6},{5,1},{6,4},{7,3},{8,10},{9,13},{10,... | collective-permute-start | bytes 3538952 | tf_op jit(solution)/shard_map/ppermute | solution.py:236
  228.0 18.5 %collective-permute-start.43 = (bf16[4,192,384]{2,1,0:T(8,128)(2,1)}, bf16[4,192,384]{2,1,0:T(8,128)(2,1)}, u32[]{:S(2)}, u32[]{:S(2)}) collective-permute-start(bf16[4,192,384]{2,1,0:T(8,128)(2,1)} %fusion.22), channel_id=1, source_target_pairs={{0,4},{1,3},{2,6},{3,1},{4,0},{5,7},{6,2},{7,5},{8,12},{9,11},{10,... | collective-permute-start | bytes 1769480 | tf_op jit(solution)/shard_map/ppermute | solution.py:236
  239.9 36.2 %collective-permute-start.49 = (bf16[768,384]{1,0:T(8,128)(2,1)}, bf16[768,384]{1,0:T(8,128)(2,1)}, u32[]{:S(2)}, u32[]{:S(2)}) collective-permute-start(bf16[768,384]{1,0:T(8,128)(2,1)} %convolution_convert_fusion.14), channel_id=1, source_target_pairs={{0,1},{1,0},{2,3},{3,2},{4,5},{5,4},{6,7},{7,6},{8,9},{9,8},{10,11... | collective-permute-start | bytes 1769480 | tf_op jit(solution)/shard_map/ppermute | solution.py:236
  249.1 13.2 %collective-permute-start.46 = (bf16[192,384]{1,0:T(8,128)(2,1)S(1)}, bf16[192,384]{1,0:T(8,128)(2,1)S(1)}, u32[]{:S(2)}, u32[]{:S(2)}) collective-permute-start(bf16[192,384]{1,0:T(8,128)(2,1)S(1)} %get-tuple-element.212), channel_id=1, source_target_pairs={{0,16},{1,17},{2,18},{3,19},{4,20},{5,21},{6,22},{7,23},{8,24},{9,... | collective-permute-start | bytes 442376 | tf_op jit(solution)/shard_map/ppermute | solution.py:236
  256.5 17.0 %collective-permute-start.50 = (bf16[768,768]{0,1:T(8,128)(2,1)S(1)}, bf16[768,768]{0,1:T(8,128)(2,1)}, u32[]{:S(2)}, u32[]{:S(2)}) collective-permute-start(bf16[768,768]{0,1:T(8,128)(2,1)S(1)} %fusion.8), channel_id=1, source_target_pairs={{0,1},{1,0},{2,3},{3,2},{4,5},{5,4},{6,7},{7,6},{8,9},{9,8},{10,11... | collective-permute-start | bytes 3538952 | tf_op jit(solution)/shard_map/ppermute | solution.py:236
  262.3 20.8 %collective-permute-start.48 = (bf16[4,48,1536]{2,1,0:T(8,128)(2,1)}, bf16[4,48,1536]{2,1,0:T(8,128)(2,1)}, u32[]{:S(2)}, u32[]{:S(2)}) collective-permute-start(bf16[4,48,1536]{2,1,0:T(8,128)(2,1)} %fusion.23), channel_id=1, source_target_pairs={{0,4},{1,3},{2,6},{3,1},{4,0},{5,7},{6,2},{7,5},{8,12},{9,11},{10,... | collective-permute-start | bytes 1769480 | tf_op jit(solution)/shard_map/ppermute | solution.py:236
  272.2 60.3 %collective-permute-start.53 = (bf16[768,384]{1,0:T(8,128)(2,1)}, bf16[768,384]{1,0:T(8,128)(2,1)S(1)}, u32[]{:S(2)}, u32[]{:S(2)}) collective-permute-start(bf16[768,384]{1,0:T(8,128)(2,1)} %convolution_convert_fusion.11), channel_id=1, source_target_pairs={{0,1},{1,0},{2,3},{3,2},{4,5},{5,4},{6,7},{7,6},{8,9},{9,8},{10,11... | collective-permute-start | bytes 1769480 | tf_op jit(solution)/shard_map/ppermute | solution.py:236
  280.6 46.7 %collective-permute-start.61 = (bf16[4,2,48,1536]{3,2,1,0:T(8,128)(2,1)}, bf16[4,2,48,1536]{3,2,1,0:T(8,128)(2,1)}, u32[]{:S(2)}, u32[]{:S(2)}) collective-permute-start(bf16[4,2,48,1536]{3,2,1,0:T(8,128)(2,1)} %get-tuple-element.124), channel_id=1, source_target_pairs={{0,2},{1,5},{2,0},{3,7},{4,6},{5,1},{6,4},{7,3},{8,10},{9,13},{10,... | collective-permute-start | bytes 3538952 | tf_op jit(solution)/shard_map/ppermute | solution.py:236
  318.4 14.2 %collective-permute-start.52 = (bf16[768,1152]{1,0:T(8,128)(2,1)S(1)}, bf16[768,1152]{1,0:T(8,128)(2,1)}, u32[]{:S(2)}, u32[]{:S(2)}) collective-permute-start(bf16[768,1152]{1,0:T(8,128)(2,1)S(1)} %copy-done.47), channel_id=1, source_target_pairs={{0,1},{1,0},{2,3},{3,2},{4,5},{5,4},{6,7},{7,6},{8,9},{9,8},{10,11... | collective-permute-start | bytes 5308424 | tf_op jit(solution)/shard_map/ppermute | solution.py:236
  338.1 19.2 %collective-permute-start.55 = (bf16[4,2,48,1664]{3,2,1,0:T(8,128)(2,1)}, bf16[4,2,48,1664]{3,2,1,0:T(8,128)(2,1)S(1)}, u32[]{:S(2)}, u32[]{:S(2)}) collective-permute-start(bf16[4,2,48,1664]{3,2,1,0:T(8,128)(2,1)} %get-tuple-element.122), channel_id=1, source_target_pairs={{0,2},{1,5},{2,0},{3,7},{4,6},{5,1},{6,4},{7,3},{8,10},{9,13},{10,... | collective-permute-start | bytes 3833864 | tf_op jit(solution)/shard_map/ppermute | solution.py:236
  342.0 14.1 %collective-permute-start.64 = (bf16[48,1536]{1,0:T(8,128)(2,1)S(1)}, bf16[48,1536]{1,0:T(8,128)(2,1)S(1)}, u32[]{:S(2)}, u32[]{:S(2)}) collective-permute-start(bf16[48,1536]{1,0:T(8,128)(2,1)S(1)} %get-tuple-element.210), channel_id=1, source_target_pairs={{0,16},{1,17},{2,18},{3,19},{4,20},{5,21},{6,22},{7,23},{8,24},{9,... | collective-permute-start | bytes 442376 | tf_op jit(solution)/shard_map/ppermute | solution.py:236
  343.0 13.1 %collective-permute-start.63 = (bf16[48,1536]{1,0:T(8,128)(2,1)S(1)}, bf16[48,1536]{1,0:T(8,128)(2,1)S(1)}, u32[]{:S(2)}, u32[]{:S(2)}) collective-permute-start(bf16[48,1536]{1,0:T(8,128)(2,1)S(1)} %get-tuple-element.208), channel_id=1, source_target_pairs={{0,8},{1,9},{2,10},{3,11},{4,12},{5,13},{6,14},{7,15},{8,16},{9,17... | collective-permute-start | bytes 442376 | tf_op jit(solution)/shard_map/ppermute | solution.py:236
  368.2 15.5 %collective-permute-start.58 = (bf16[48,1664]{1,0:T(8,128)(2,1)S(1)}, bf16[48,1664]{1,0:T(8,128)(2,1)S(1)}, u32[]{:S(2)}, u32[]{:S(2)}) collective-permute-start(bf16[48,1664]{1,0:T(8,128)(2,1)S(1)} %get-tuple-element.204), channel_id=1, source_target_pairs={{0,16},{1,17},{2,18},{3,19},{4,20},{5,21},{6,22},{7,23},{8,24},{9,... | collective-permute-start | bytes 479240 | tf_op jit(solution)/shard_map/ppermute | solution.py:236
  369.6 14.1 %collective-permute-start.57 = (bf16[48,1664]{1,0:T(8,128)(2,1)S(1)}, bf16[48,1664]{1,0:T(8,128)(2,1)S(1)}, u32[]{:S(2)}, u32[]{:S(2)}) collective-permute-start(bf16[48,1664]{1,0:T(8,128)(2,1)S(1)} %get-tuple-element.202), channel_id=1, source_target_pairs={{0,8},{1,9},{2,10},{3,11},{4,12},{5,13},{6,14},{7,15},{8,16},{9,17... | collective-permute-start | bytes 479240 | tf_op jit(solution)/shard_map/ppermute | solution.py:236
  (80 other events, 674.8 us)

commit v4 on v3

--- a/solution.py
+++ b/solution.py
@@ -225,9 +225,8 @@
 
 
 CORE = grid_perm(lambda z, x, y, core: (z, x, y, core ^ 1))
-ZSHIFT = [
-    grid_perm(lambda z, x, y, core, k=k: ((z + k) % 4, x, y, core)) for k in range(4)
-]
+ZNEAR = grid_perm(lambda z, x, y, core: (z ^ 1, x, y, core))
+ZFAR = grid_perm(lambda z, x, y, core: (z ^ 2, x, y, core))
 FIRST = grid_perm(lambda z, x, y, core: (z, x ^ (1 - core), y ^ core, core))
 SECOND = grid_perm(lambda z, x, y, core: (z, x ^ core, y ^ (1 - core), core))
 
@@ -275,7 +274,7 @@
             out_specs=[
                 pl.BlockSpec(
                     (1, 2, 2, 2, rows, w),
-                    lambda k, spot: (lax.rem(spot[0] + 4 - k, 4), 0, 0, 0, 0, 0),
+                    lambda k, spot: (spot[0] ^ (2 * lax.rem(k, 2) + k // 2), 0, 0, 0, 0, 0),
                 )
                 for w in widths
             ],
@@ -286,43 +285,57 @@
 
 
 class GridGather:
-    def __init__(self):
-        self.lines = ()
-        self.crossed = ()
-
-    def spread(self, shards):
-        own = jnp.concatenate(shards, axis=1) if len(shards) > 1 else shards[0]
-        own = after(own, *self.lines)
-        self.lines = tuple(move(own, ZSHIFT[k]) for k in (1, 2, 3))
-        return jnp.stack((own,) + self.lines)
-
-    def cross(self, line, *earlier):
-        ready = after(line, *self.crossed, *earlier)
-        one = move(ready, FIRST)
-        two = move(ready, SECOND)
-        both = move(one, SECOND)
-        self.crossed = (one, two) if earlier else (both,)
-        parts = [line, one, two, both]
-        return parts + [move(p, CORE) for p in parts]
-
-    def join(self, parts, shards, *earlier):
-        rows = shards[0].shape[0]
-        widths = [s.shape[1] for s in shards]
+    def __init__(self, shards):
+        self.shards = shards
+        self.own = jnp.concatenate(shards, axis=1) if len(shards) > 1 else shards[0]
+
+    def spread(self, *earlier):
+        own = after(self.own, *earlier)
+        self.two = jnp.stack((self.own, move(own, ZFAR)))
+        self.along = (move(self.two, ZNEAR),)
+        return self.along
+
+    def cross(self, *earlier):
+        self.line = jnp.concatenate((self.two,) + self.along)
+        ready = after(self.line, *earlier)
+        self.sides = (move(ready, FIRST), move(ready, SECOND))
+        return self.sides
+
+    def corner(self, *earlier):
+        self.both = (move(after(self.sides[0], *earlier), SECOND),)
+        return self.both
+
+    def swap(self):
+        parts = (self.line,) + self.sides + self.both
+        self.parts = parts + tuple(move(p, CORE) for p in parts)
+        return self.parts
+
+    def join(self, *earlier):
+        parts = self.parts
         if earlier:
-            parts = lax.optimization_barrier(tuple(parts) + earlier)[: len(parts)]
+            parts = lax.optimization_barrier(parts + earlier)[: len(parts)]
+        rows = self.shards[0].shape[0]
+        widths = [s.shape[1] for s in self.shards]
         return assemble(parts, rows, widths, jnp.stack(place()).astype(jnp.int32))
 
 
 class PlainGather:
-    def spread(self, shards):
-        return None
-
-    def cross(self, line, *earlier):
-        return None
-
-    def join(self, parts, shards, *earlier):
-        widths = [s.shape[1] for s in shards]
-        whole = lax.all_gather(jnp.concatenate(shards, axis=1), AXES, axis=0, tiled=True)
+    def __init__(self, shards):
+        self.shards = shards
+
+    along = ()
+
+    def spread(self, *earlier):
+        return ()
+
+    cross = corner = spread
+
+    def swap(self):
+        return ()
+
+    def join(self, *earlier):
+        widths = [s.shape[1] for s in self.shards]
+        whole = lax.all_gather(jnp.concatenate(self.shards, axis=1), AXES, axis=0, tiled=True)
         results = []
         offset = 0
         for width in widths:
@@ -382,6 +395,10 @@
     )(which, *views, *views)
 
 
+def summed(partial):
+    return lax.psum_scatter(partial, AXES, scatter_dimension=0, tiled=True)
+
+
 class GridReduction:
     def __init__(self, factors):
         core = place()[3]
@@ -390,9 +407,14 @@
         self.factors = factors
         self.stage = 0
 
-    def step(self):
+    def add(self, value, upstream_gradient):
+        side = 1 - place()[3]
+        self.sends.append(contract_low(value, half_of(upstream_gradient, side)))
+        self.factors.append((value, upstream_gradient))
+
+    def step(self, *earlier):
         self.stage += 1
-        return getattr(self, "hop%d" % self.stage)()
+        return getattr(self, "hop%d" % self.stage)(*earlier)
 
     def hop1(self):
         core = place()[3]
@@ -400,35 +422,45 @@
         self.keeps = [contract_low(v, half_of(u, core)) for v, u in self.factors]
         return self.got
 
-    def hop2(self):
-        self.keep, send = split_add(list(zip(self.keeps, self.got)), self.rows)
+    def hop2(self, *earlier):
+        keeps = [after(self.keeps[0], *earlier)] + self.keeps[1:]
+        self.keep, send = split_add(list(zip(keeps, self.got)), self.rows)
         self.got = move(send, SECOND)
         return [self.got]
 
-    def hop3(self):
+    def hop3(self, *earlier):
         f32 = jnp.float32
+        self.got = after(self.got, *earlier)
         total = self.keep[:, 1].astype(f32) + self.got[:, 1].astype(f32)
-        self.got_first = move(total.astype(jnp.bfloat16), FIRST)
+        self.half = total.astype(jnp.bfloat16)
+        self.got_first = move(self.half, FIRST)
         return [self.got_first]
 
-    def hop4(self):
+    def hop4(self, *earlier):
         z = place()[0]
+        self.got_first = after(self.got_first, *earlier)
         f32 = jnp.float32
 
         def plane(k):
-            at = (z + k) % 4
+            at = z ^ k
             pick = lambda v: lax.dynamic_index_in_dim(v, at, 0, keepdims=False).astype(f32)
             return pick(self.keep[:, 0]) + pick(self.got[:, 0]) + pick(self.got_first)
 
-        self.own = plane(0)
-        self.planes = [move(plane(k).astype(jnp.bfloat16), ZSHIFT[k]) for k in (1, 2, 3)]
-        return self.planes
+        self.own, self.far = plane(0), plane(2)
+        self.near = move(jnp.stack([plane(1), plane(3)]).astype(jnp.bfloat16), ZNEAR)
+        return [self.near]
+
+    def hop5(self, *earlier):
+        near = after(self.near, *earlier).astype(jnp.float32)
+        self.own = self.own + near[0]
+        self.last = move((self.far + near[1]).astype(jnp.bfloat16), ZFAR)
+        return [self.last]
 
     def results(self):
-        while self.stage < 4:
+        while self.stage < 5:
             self.step()
         core, rows = place()[3], self.rows
-        total = self.own + sum(p.astype(jnp.float32) for p in self.planes)
+        total = self.own + self.last.astype(jnp.float32)
         mine = lax.dynamic_slice_in_dim(total, core * rows, rows, axis=0)
         other = move(lax.dynamic_slice_in_dim(total, (1 - core) * rows, rows, axis=0), CORE)
         left = jnp.where(core == 0, mine, other)
@@ -450,18 +482,21 @@
     def __init__(self, factors):
         self.factors = factors
         self.sends = []
-
-    def step(self):
+        self.keep = self.half = self.got_first = self.own = jnp.zeros((), jnp.bfloat16)
+
+    def add(self, value, upstream_gradient):
+        self.factors.append((value, upstream_gradient))
+
+    def step(self, *earlier):
         return []
 
     def results(self):
         packed = jnp.concatenate([contract_low(v, u) for v, u in self.factors], axis=1)
-        summed = lax.psum_scatter(packed, AXES, scatter_dimension=0, tiled=True)
-        summed = summed.astype(jnp.float32)
+        total = summed(packed).astype(jnp.float32)
         results = []
         offset = 0
         for _, u in self.factors:
-            results.append(summed[:, offset : offset + u.shape[-1]])
+            results.append(total[:, offset : offset + u.shape[-1]])
             offset += u.shape[-1]
         return results
 
@@ -504,17 +539,16 @@
         ],
         axis=1,
     )
-    gather = gathering()
-    first, second, third, fourth = (
-        [attn_in, small],
-        [attn_out, cross_query, cross_kv, cross_out],
-        [mlp_in],
-        [mlp_out],
-    )
-    lines = [gather.spread(shards) for shards in (first, second, third, fourth)]
-    first_parts = gather.cross(lines[0])
-    second_parts = gather.cross(lines[1])
-    w_qkv, smalls = gather.join(first_parts, first)
+    first = gathering([attn_in, small])
+    third = gathering([mlp_in])
+    whole = lambda v: lax.all_gather(v, AXES, axis=0, tiled=True)
+    w_second = whole(jnp.concatenate([attn_out, cross_query, cross_kv, cross_out], axis=1))
+    fourth = gathering([mlp_out])
+    third.spread(*first.spread())
+    first.cross()
+    third.cross(*first.corner())
+    fourth.spread(*first.swap(), *third.along)
+    w_qkv, smalls = first.join()
     gains, biases, hidden_bias = smalls[:, :3], smalls[:, 3:7], smalls[:, 7:11].reshape(-1)
     seqs, rows, width = tokens.shape
     low = lambda v: v.astype(jnp.bfloat16)
@@ -528,57 +562,72 @@
     normed1 = low(normed1)
     qkv = by_seq(low(project(normed1, w_qkv)))
     context, probs = self_forward(qkv, suffix_len)
-    third_parts = gather.cross(lines[2], context)
-    w_out, w_cquery, w_ckv, w_cout = gather.join(second_parts, second, context)
+    third.corner(context)
+    third.swap()
+    w_out, w_cquery = w_second[:, :D], w_second[:, D : 2 * D]
+    w_ckv, w_cout = w_second[:, 2 * D : 4 * D], w_second[:, 4 * D :]
     context = flat(context)
     stream1 = stream0 + project(context, w_out)
     normed2, standard2, inverse2 = norm_forward(stream1, gain_vals[:, 1], bias_vals[:, 1])
     normed2 = low(normed2)
     cquery = by_seq(low(project(normed2, w_cquery)))
     ckv = low(project(memory, w_ckv))
-    fourth_parts = gather.cross(lines[3], cquery)
+    fourth.cross(cquery)
     ccontext, cprobs = cross_forward(cquery, ckv)
-    (w_in,) = gather.join(third_parts, third, ccontext)
     ccontext = flat(ccontext)
     stream2 = stream1 + project(ccontext, w_cout)
     normed3, standard3, inverse3 = norm_forward(stream2, gain_vals[:, 2], bias_vals[:, 2])
     normed3 = low(normed3)
+    (w_in,) = third.join(ccontext)
+    fourth.corner(ccontext)
+    fourth.swap()
     pre = project(normed3, w_in) + hidden_bias.astype(jnp.float32)
     activated, gelu_back = jax.vjp(lambda v: jax.nn.gelu(v, approximate=True), pre)
     activated = low(activated)
-    (w_down,) = gather.join(fourth_parts, fourth, activated)
-    layer_out = by_seq(low(stream2 + project(activated, w_down) + bias_vals[:, 3]))
 
     upstream = flat(cotangent.astype(jnp.float32) * live[..., None].astype(jnp.float32))
     dout3 = low(upstream)
-    down_sum = reduction([(activated, dout3)])
+    down_partial = contract_low(activated, dout3)
+    mlp_out_sum = summed(down_partial)
     g_out_bias = jnp.sum(dout3, axis=0, dtype=jnp.float32)
-    grad_act = back_project(after(dout3, *down_sum.sends), w_down)
+    (w_down,) = fourth.join(down_partial)
+    grad_act = back_project(dout3, w_down)
     dpre = low(gelu_back(grad_act)[0])
     g_hidden_bias = jnp.sum(dpre, axis=0, dtype=jnp.float32)
     in_sum = reduction([(normed3, dpre)])
-    dpre = after(dpre, *down_sum.step(), *in_sum.sends)
+    dpre = after(dpre, *in_sum.sends)
     grad_back, g_gain3, g_shift3 = norm_backward(
         back_project(dpre, w_in), standard3, inverse3, gain_vals[:, 2]
     )
     upstream = upstream + grad_back
     dout2 = low(upstream)
     dccontext = by_seq(low(back_project(dout2, w_cout)))
-    dccontext = after(dccontext, *down_sum.step(), *in_sum.step())
+    in_sum.step()
+    arriving = in_sum.step()
+    dccontext = after(dccontext, in_sum.keep)
     dcquery, dckv = cross_backward(cquery, ckv, cprobs, dccontext)
     dcq = flat(dcquery)
-    cross_sum = reduction([(normed2, dcq), (memory, dckv), (ccontext, dout2)])
-    dcq = after(dcq, *down_sum.step(), *in_sum.step(), *cross_sum.sends)
     grad_back, g_gain2, g_shift2 = norm_backward(
         back_project(dcq, w_cquery), standard2, inverse2, gain_vals[:, 1]
     )
     upstream = upstream + grad_back
     dout1 = low(upstream)
+    cross_sum = reduction(
+        [(normed2, dcq), (memory, dckv), (ccontext, dout2), (context, dout1)]
+    )
     dcontext = by_seq(low(back_project(dout1, w_out)))
-    dcontext = after(dcontext, *down_sum.step(), *in_sum.step(), *cross_sum.step())
+    dcontext = after(dcontext, *cross_sum.sends)
     dqkv = flat(self_backward(qkv, probs, dcontext))
+    dqkv = after(dqkv, *arriving, *cross_sum.step())
+    in_sum.step(dqkv)
+    in_sum.step()
+    in_sum.step()
+    attn_sum = reduction([(normed1, dqkv)])
     grad_back, g_gain1, g_shift1 = norm_backward(
-        back_project(dqkv, w_qkv), standard1, inverse1, gain_vals[:, 0]
+        back_project(after(dqkv, *attn_sum.sends), w_qkv),
+        standard1,
+        inverse1,
+        gain_vals[:, 0],
     )
     input_grad = by_seq(upstream + grad_back)
     small_sums = jnp.stack(
@@ -587,12 +636,22 @@
     bias_sums = g_hidden_bias.reshape(D, 4).T
     sums = jnp.concatenate([small_sums, bias_sums], axis=0)
     picks = jnp.eye(11, 256, dtype=jnp.bfloat16)
-    attn_sum = reduction([(normed1, dqkv), (context, dout1), (low(sums), picks)])
-    memory_grad = back_project(after(dckv, *attn_sum.sends), w_ckv)
-    (mlp_out_grad,) = down_sum.results()
+    attn_sum.add(low(sums), picks)
+    attn_sum.step()
+    cross_sum.step()
+    cross_sum.step()
+    arrived = attn_sum.step(cross_sum.half)
+    attn_sum.step()
+    memory_grad = back_project(after(dckv, *arrived), w_ckv)
+    attn_sum.step(memory_grad)
+    attn_sum.step()
+    late = after(activated, attn_sum.got_first)
+    layer_out = by_seq(low(stream2 + project(late, w_down) + bias_vals[:, 3]))
+    mlp_out_grad = after(mlp_out_sum, attn_sum.got_first).astype(jnp.float32)
+    attn_sum.own = after(attn_sum.own, layer_out, mlp_out_grad)
     (mlp_in_grad,) = in_sum.results()
-    cross_query_grad, cross_kv_grad, cross_out_grad = cross_sum.results()
-    attn_in_grad, attn_out_grad, small_grad = attn_sum.results()
+    cross_query_grad, cross_kv_grad, cross_out_grad, attn_out_grad = cross_sum.results()
+    attn_in_grad, small_grad = attn_sum.results()
     return (
         layer_out,
         input_grad,

time: 395 us -> 355 us (0.90)
  waiting for transfers between devices: 97.4 us -> 79.1 us
  starting transfers between devices: 63.8 us -> 45.7 us
  between operations: 2.21 us -> 15.6 us
  Pallas kernels: 73.2 us -> 62.8 us
  local copies, waits for them, and re-layouts: 30 us -> 20.8 us
    ppermute x72 -> x49, waiting for transfers between devices: 97.4 us -> 79 us  [move(): return lax.ppermute(value, AXES, perm)]
    ppermute x72 -> x49, starting transfers between devices: 63.8 us -> 45.6 us  [move(): return lax.ppermute(value, AXES, perm)]
    pallas_call x4 -> x3, Pallas kernels: 23.8 us -> 17.3 us  [assemble(): pl.pallas_call(functools.partial(assemble_body, widths), out_shape=[jax.S...]
    concatenate x1 -> x4, other arithmetic: 0.02 us -> 5.64 us  [the longest x3 3.9 us: cross(): self.line = jnp.concatenate((self.two,) + self.along)]
    slice x8 -> x6, local copies, waits for them, and re-layouts: 8.3 us -> 3.33 us  [plane(): return pick(self.keep[:, 0]) + pick(self.got[:, 0]) + pick(self.got_first)]
    unnamed x118 -> x104, local copies, waits for them, and re-layouts: 13 us -> 8.86 us
    pallas_call x4 -> x3, Pallas kernels: 17.9 us -> 13.8 us  [split_add(): pl.pallas_call(functools.partial(split_body, len(pairs)), out_shape=[shap...]
    dot_general x16 -> x15, matrix products: 33.6 us -> 36.7 us  [contract_low(): lax.dot_general(value, upstream_gradient, ((over, over), ((), ())), prefe...]
  transfers between devices with their start and end apart: 72 -> 51, of which waited for: 21 -> 17; matrix products, arithmetic and copies ran while one was open for 35% -> 37% of each run, Pallas kernels for 19% -> 16%
where the time goes in v4:
time: 355 us; the launch traced here: 351 us
  matrix products  87.4 us (25%)
  waiting for transfers between devices  79.1 us (22%)
  Pallas kernels  62.8 us (18%)
  starting transfers between devices  45.7 us (13%)
  other arithmetic  39.3 us (11%)
  local copies, waits for them, and re-layouts  20.8 us (6%)
  between operations  15.6 us (4%)
    ppermute x49, waiting for transfers between devices, move(): return lax.ppermute(value, AXES, perm)  79 us
    ppermute x49, starting transfers between devices, move(): return lax.ppermute(value, AXES, perm)  45.6 us
    dot_general x15, matrix products, contract_low(): lax.dot_general(value, upstream_gradient, ((over, over), ((), ())), prefe...  36.7 us
    pallas_call x4, Pallas kernels, per_sequence(): pl.pallas_call(body, out_shape=outs, grid_spec=pltpu.PrefetchScalarGridSp...  31.7 us
    dot_general x7, matrix products, back_project(): jnp.einsum('...j,aj->...a', upstream_gradient, weight_matrix, preferred_e...  28.3 us
    dot_general x7, matrix products, project(): jnp.einsum('...h,ht->...t', value_tensor, weight_matrix, preferred_elemen...  22.4 us
    pallas_call x3, Pallas kernels, assemble(): pl.pallas_call(functools.partial(assemble_body, widths), out_shape=[jax.S...  17.3 us
    pallas_call x3, Pallas kernels, split_add(): pl.pallas_call(functools.partial(split_body, len(pairs)), out_shape=[shap...  13.8 us
  transfers between devices with their start and end apart: 51, of which 17 were waited for; matrix products, arithmetic and copies ran while one was open for 37% of the time, Pallas kernels for 16%

profile of v4, /device:TPU:0, one launch (start us, length us, event | category | flops | bytes accessed | tf_op | source)
XLA Modules:
  0.0 350.7 jit_solution(14576713266773706085)
XLA Ops:
  12.4 4.1 %collective-permute-start = (bf16[24,2560]{1,0:T(8,128)(2,1)S(1)}, bf16[24,2560]{1,0:T(8,128)(2,1)S(1)}, u32[]{:S(2)}, u32[]{:S(2)}) collective-permute-start(bf16[24,2560]{1,0:T(8,128)(2,1)S(1)} %concatenate.40), channel_id=1, source_target_pairs={{0,16},{1,17},{2,18},{3,19},{4,20},{5,21},{6,22},{7,23},{8,24},{9,... | collective-permute-start | bytes 368648 | tf_op jit(solution)/shard_map/ppermute | solution.py:235
  17.4 5.1 %collective-permute-done = bf16[24,2560]{1,0:T(8,128)(2,1)S(1)} collective-permute-done((bf16[24,2560]{1,0:T(8,128)(2,1)S(1)}, bf16[24,2560]{1,0:T(8,128)(2,1)S(1)}, u32[]{:S(2)}, u32[]{:S(2)}) %collective-permute-start) | collective-permute-done | bytes 122912 | tf_op jit(solution)/shard_map/ppermute | solution.py:235
  24.3 7.9 %collective-permute-done.1 = bf16[2,24,2560]{2,1,0:T(8,128)(2,1)S(1)} collective-permute-done((bf16[2,24,2560]{2,1,0:T(8,128)(2,1)S(1)}, bf16[2,24,2560]{2,1,0:T(8,128)(2,1)S(1)}, u32[]{:S(2)}, u32[]{:S(2)}) %collective-permute-start.1) | collective-permute-done | bytes 245792 | tf_op jit(solution)/shard_map/ppermute | solution.py:235
  33.7 4.7 %collective-permute-start.9 = (bf16[24,3072]{1,0:T(8,128)(2,1)S(1)}, bf16[24,3072]{1,0:T(8,128)(2,1)S(1)}, u32[]{:S(2)}, u32[]{:S(2)}) collective-permute-start(bf16[24,3072]{1,0:T(8,128)(2,1)S(1)} %copy-done.32), channel_id=1, source_target_pairs={{0,16},{1,17},{2,18},{3,19},{4,20},{5,21},{6,22},{7,23},{8,24},{9,... | collective-permute-start | bytes 442376 | tf_op jit(solution)/shard_map/ppermute | solution.py:235
  43.9 2.4 collective-permute-done.9
  51.9 3.7 %collective-permute-done.4.refs_3_ = bf16[4,24,2560]{2,1,0:T(8,128)(2,1)} collective-permute-done((bf16[4,24,2560]{2,1,0:T(8,128)(2,1)}, bf16[4,24,2560]{2,1,0:T(8,128)(2,1)}, u32[]{:S(2)}, u32[]{:S(2)}) %collective-permute-start.4) | collective-permute-done | bytes 491552 | tf_op jit(solution)/shard_map/ppermute | solution.py:235
  57.8 2.4 collective-permute-done.10
  63.8 7.2 %collective-permute-start.18 = (bf16[96,768]{1,0:T(8,128)(2,1)}, bf16[96,768]{1,0:T(8,128)(2,1)S(1)}, u32[]{:S(2)}, u32[]{:S(2)}) collective-permute-start(bf16[96,768]{1,0:T(8,128)(2,1)} %param.24), channel_id=1, source_target_pairs={{0,16},{1,17},{2,18},{3,19},{4,20},{5,21},{6,22},{7,23},{8,24},{9,... | collective-permute-start | bytes 442376 | tf_op jit(solution)/shard_map/ppermute | solution.py:235
  71.0 5.8 %assemble.3 = (bf16[4,2,2,2,24,2304]{5,4,3,2,1,0:T(8,128)(2,1)}, bf16[4,2,2,2,24,256]{5,4,3,2,1,0:T(8,128)(2,1)}) custom-call(s32[4]{0:T(128)} %pad_add_fusion.spot, bf16[4,24,2560]{2,1,0:T(8,128)(2,1)} %copy-done.17, bf16[4,24,2560]{2,1,0:T(8,128)(2,1)} %collective-permute-done.2.refs_1_, bf16[4,24,2560]{2,1,0:T(8,128)(2,1)} %collective-permute-done.3.refs_2_, ...), custom_call_target="tpu_custom_call" | custom-call | tf_op jit(solution)/shard_map/assemble/pallas_call | solution.py:267
  82.2 4.8 %convolution_convert_fusion.1 = bf16[384,2304]{1,0:T(8,128)(2,1)} fusion(bf16[384,768]{1,0:T(8,128)(2,1)S(1)} %bitcast.263, bf16[768,2304]{1,0:T(8,128)(2,1)} %bitcast.267), kind=kOutput, calls=%fused_computation.12 | convolution fusion | flops 1359839232 | bytes 5898240 | tf_op jit(solution)/shard_map/...h,ht->...t/dot_general | solution.py:38
  87.0 9.0 %self_forward.1 = (bf16[4,96,768]{2,1,0:T(8,128)(2,1)}, bf16[4,6,96,192]{3,2,1,0:T(8,128)(2,1)}) custom-call(s32[4]{0:T(128)} %lens.1, bf16[4,96,2304]{2,1,0:T(8,128)(2,1)} %bitcast.215), custom_call_target="tpu_custom_call" | custom-call | tf_op jit(solution)/shard_map/self_forward/pallas_call | solution.py:163
  102.0 4.6 %collective-permute-done.19 = bf16[2,96,768]{2,1,0:T(8,128)(2,1)} collective-permute-done((bf16[2,96,768]{2,1,0:T(8,128)(2,1)}, bf16[2,96,768]{2,1,0:T(8,128)(2,1)}, u32[]{:S(2)}, u32[]{:S(2)}) %collective-permute-start.19) | collective-permute-done | bytes 294944 | tf_op jit(solution)/shard_map/ppermute | solution.py:235
  114.4 3.5 %fusion.7.kv = bf16[4,196,1536]{2,1,0:T(8,128)(2,1)} fusion(bf16[768,3840]{1,0:T(8,128)(2,1)S(1)} %copy-done.35, bf16[4,196,768]{2,0,1:T(4,128)(2,1)S(1)} %copy-done), kind=kOutput, calls=%fused_computation.18 | convolution fusion | flops 1850892288 | bytes 5971968 | tf_op jit(solution)/shard_map/...h,ht->...t/dot_general | solution.py:38
  117.9 6.5 %cross_forward.1 = (bf16[4,96,768]{2,1,0:T(8,128)(2,1)}, bf16[4,6,196,192]{3,2,1,0:T(8,128)(2,1)}) custom-call(bf16[4,96,768]{2,1,0:T(8,128)(2,1)} %bitcast.237, bf16[4,196,1536]{2,1,0:T(8,128)(2,1)} %fusion.7.kv), custom_call_target="tpu_custom_call" | custom-call | tf_op jit(solution)/shard_map/cross_forward/pallas_call | solution.py:163
  125.5 5.7 %assemble.4 = bf16[4,2,2,2,24,3072]{5,4,3,2,1,0:T(8,128)(2,1)} custom-call(s32[4]{0:T(128)} %pad_add_fusion.spot, bf16[4,24,3072]{2,1,0:T(8,128)(2,1)} %pad_maximum_fusion.refs_0_, bf16[4,24,3072]{2,1,0:T(8,128)(2,1)} %collective-permute-done.11.refs_1_, bf16[4,24,3072]{2,1,0:T(8,128)(2,1)} %collective-permute-done.12.refs_2_, ...), custom_call_target="tpu_custom_call" | custom-call | tf_op jit(solution)/shard_map/assemble/pallas_call | solution.py:267
  135.6 8.3 %collective-permute-done.22.refs_3_ = bf16[4,96,768]{2,1,0:T(8,128)(2,1)} collective-permute-done((bf16[4,96,768]{2,1,0:T(8,128)(2,1)}, bf16[4,96,768]{2,1,0:T(8,128)(2,1)}, u32[]{:S(2)}, u32[]{:S(2)}) %collective-permute-start.22) | collective-permute-done | bytes 589856 | tf_op jit(solution)/shard_map/ppermute | solution.py:235
  143.9 5.1 %multiply_convert_fusion = (bf16[384,3072]{1,0:T(8,128)(2,1)S(1)}, f32[384,3072]{1,0:T(8,128)}) fusion(f32[3072]{0:T(1024)S(1)} %copy-done.36, bf16[768,3072]{1,0:T(8,128)(2,1)S(1)} %bitcast.226, f32[384,768]{1,0:T(8,128)S(1)} %get-tuple-element.213, f32[768]{0:T(1024)S(1)} %copy-done.38, f32[768]{0:T(1024)S(1)} %get-tuple-element.173, ...), kind=kOutput, calls=%fused_computation.10 | convolution fusion | flops 1825210368 | bytes 12997632 | tf_op jit(solution)/shard_map/...h,ht->...t/dot_general | solution.py:38
  150.4 4.5 %convolution_convert_fusion = bf16[3072,768]{1,0:T(8,128)(2,1)} fusion(bf16[384,3072]{1,0:T(8,128)(2,1)S(1)} %get-tuple-element.105, bf16[384,768]{1,0:T(8,128)(2,1)S(1)} %copy-done.31), kind=kOutput, calls=%fused_computation.2 | convolution fusion | flops 1814298624 | bytes 7667712 | tf_op jit(solution)/shard_map/dot_general | solution.py:506
  154.9 5.8 %assemble.5 = bf16[4,2,2,2,96,768]{5,4,3,2,1,0:T(8,128)(2,1)} custom-call(s32[4]{0:T(128)} %pad_add_fusion.spot, bf16[4,96,768]{2,1,0:T(8,128)(2,1)} %pad_maximum_fusion.1.refs_0_, bf16[4,96,768]{2,1,0:T(8,128)(2,1)} %collective-permute-done.20.refs_1_, bf16[4,96,768]{2,1,0:T(8,128)(2,1)} %collective-permute-done.21.refs_2_, ...), custom_call_target="tpu_custom_call" | custom-call | tf_op jit(solution)/shard_map/assemble/pallas_call | solution.py:267
  160.7 7.2 %fusion.69 = (bf16[3072]{0:T(1024)(128)(2,1)S(1)}, bf16[384,3072]{1,0:T(8,128)(2,1)S(1)}) fusion(f32[384,3072]{1,0:T(8,128)} %get-tuple-element.215, bf16[384,768]{1,0:T(8,128)(2,1)} %bitcast.262, bf16[3072,768]{1,0:T(8,128)(2,1)} %bitcast.221), kind=kOutput, calls=%fused_computation.199 | convolution fusion | flops 1836708864 | bytes 12392448 | tf_op jit(solution)/shard_map/...j,aj->...a/dot_general | solution.py:42
  167.9 3.1 convolution_convert_fusion.6
  173.2 4.8 %convolution_convert_fusion.5 = bf16[768,1536]{1,0:T(8,128)(2,1)} fusion(bf16[384,3072]{1,0:T(8,128)(2,1)} %copy-done.45, s32[]{:T(128)S(6)} %select_n.219, f32[384,768]{1,0:T(8,128)} %copy-done.2, f32[768]{0:T(1024)S(1)} %copy-done.38, f32[768]{0:T(1024)S(1)} %get-tuple-element.173, f32[384]{0:T(512)S(1)} %add_rsqrt_fusion, ...), kind=kOutput, calls=%fused_computation.16 | convolution fusion | flops 908623872 | bytes 4727812 | tf_op jit(solution)/shard_map/dot_general | solution.py:506
  178.0 5.0 %multiply_reduce_fusion.1 = (bf16[768]{0:T(1024)(128)(2,1)S(1)}, f32[384]{0:T(512)S(1)}, f32[384]{0:T(512)S(1)}, bf16[768]{0:T(1024)(128)(2,1)S(1)}, f32[384,768]{1,0:T(8,128)S(1)}) fusion(f32[384,768]{1,0:T(8,128)S(1)} %copy-done.4, f32[384]{0:T(512)S(1)} %add_rsqrt_fusion, f32[384]{0:T(512)S(1)} %broadcast_multiply_fusion.6, ...), kind=kOutput, calls=%fused_computation.48 | convolution fusion | flops 1814591232 | bytes 9449472 | tf_op jit(solution)/shard_map/...j,aj->...a/dot_general | solution.py:42
  187.4 2.8 convolution_convert_fusion.14
  190.2 4.4 %split_add.3 = (bf16[4,2,48,1536]{3,2,1,0:T(8,128)(2,1)}, bf16[4,2,48,1536]{3,2,1,0:T(8,128)(2,1)}) custom-call(s32[4]{0:T(128)} %pad_add_fusion.1.which, bf16[4,4,48,1536]{3,2,1,0:T(8,128)(2,1)} %bitcast.213, bf16[4,4,48,1536]{3,2,1,0:T(8,128)(2,1)} %bitcast.30.refs_1_.refs_3_, bf16[4,4,48,1536]{3,2,1,0:T(8,128)(2,1)} %bitcast.214, ...), custom_call_target="tpu_custom_call" | custom-call | tf_op jit(solution)/shard_map/split_add/pallas_call | solution.py:385
  194.6 7.9 %cross_backward.1 = (bf16[4,96,768]{2,1,0:T(8,128)(2,1)}, bf16[4,196,1536]{2,1,0:T(8,128)(2,1)}) custom-call(bf16[4,96,768]{2,1,0:T(8,128)(2,1)} %bitcast.238, bf16[4,196,1536]{2,1,0:T(8,128)(2,1)} %fusion.7.kv, bf16[4,6,196,192]{3,2,1,0:T(8,128)(2,1)} %get-tuple-element.89.probs, bf16[4,96,768]{2,1,0:T(8,128)(2,1)} %bitcast.255), custom_call_target="tpu_custom_call" | custom-call | tf_op jit(solution)/shard_map/cross_backward/pallas_call | solution.py:163
  202.5 2.6 convolution_convert_fusion.12
  205.1 2.4 multiply_reduce_fusion.2
  207.6 2.5 fusion.9
  215.1 2.7 convolution_convert_fusion.13
  220.1 8.3 %self_backward.1 = bf16[4,96,2304]{2,1,0:T(8,128)(2,1)} custom-call(bf16[4,96,2304]{2,1,0:T(8,128)(2,1)} %bitcast.216, bf16[4,6,96,192]{3,2,1,0:T(8,128)(2,1)} %get-tuple-element.76.probs, bf16[4,96,768]{2,1,0:T(8,128)(2,1)} %bitcast.264), custom_call_target="tpu_custom_call" | custom-call | tf_op jit(solution)/shard_map/self_backward/pallas_call | solution.py:163
  228.4 2.5 convolution_convert_fusion.7
  231.0 3.9 %bitcast_convert_fusion = bf16[768,768]{0,1:T(8,128)(2,1)} fusion(bf16[4,196,1536]{2,1,0:T(8,128)(2,1)} %get-tuple-element.103, s32[]{:T(128)S(6)} %select_n.224, bf16[4,196,768]{2,0,1:T(4,128)(2,1)S(1)} %copy-done), kind=kOutput, calls=%fused_computation.20 | convolution fusion | flops 925433856 | bytes 3612676 | tf_op jit(solution)/shard_map/dot_general | solution.py:506
  235.6 2.4 convolution_convert_fusion.3
  240.4 2.4 copy.88
  242.8 5.4 %split_add.4 = (bf16[4,2,48,1920]{3,2,1,0:T(8,128)(2,1)}, bf16[4,2,48,1920]{3,2,1,0:T(8,128)(2,1)}) custom-call(s32[4]{0:T(128)} %pad_add_fusion.1.which, bf16[4,4,48,384]{3,2,1,0:T(8,128)(2,1)} %bitcast.233, bf16[4,4,48,384]{3,2,1,0:T(8,128)(2,1)} %bitcast.231, bf16[4,4,48,768]{3,2,1,0:T(8,128)(2,1)} %bitcast.219, bf16[4,4,48,768]{3,2,1,0:T(8,128)(2,1)} %bitcast.211, ...), custom_call_target="tpu_custom_call" | custom-call | tf_op jit(solution)/shard_map/split_add/pallas_call | solution.py:385
  249.2 4.4 %multiply_reduce_fusion = (f32[384]{0:T(512)S(1)}, bf16[768]{0:T(1024)(128)(2,1)S(1)}, f32[384]{0:T(512)S(1)}, bf16[768]{0:T(1024)(128)(2,1)S(1)}, f32[384,768]{1,0:T(8,128)S(1)}) fusion(bf16[4,96,768]{2,1,0:T(8,128)(2,1)S(1)} %copy-done.1, f32[768]{0:T(1024)S(1)} %get-tuple-element.175, f32[384]{0:T(512)S(1)} %rsqrt.31, f32[384]{0:T(512)S(1)} %div.75, ...), kind=kOutput, calls=%fused_computation.47 | convolution fusion | flops 1361901312 | bytes 7090176 | tf_op jit(solution)/shard_map/...j,aj->...a/dot_general | solution.py:42
  259.3 3.5 convolution_convert_fusion.4
  262.8 6.2 %collective-permute-done.46 = bf16[2,48,1536]{2,1,0:T(8,128)(2,1)S(1)} collective-permute-done((bf16[2,48,1536]{2,1,0:T(8,128)(2,1)S(1)}, bf16[2,48,1536]{2,1,0:T(8,128)(2,1)S(1)}, u32[]{:S(2)}, u32[]{:S(2)}) %collective-permute-start.46) | collective-permute-done | bytes 294944 | tf_op jit(solution)/shard_map/ppermute | solution.py:235
  275.5 5.5 %collective-permute-done.47 = bf16[48,1536]{1,0:T(8,128)(2,1)S(1)} collective-permute-done((bf16[48,1536]{1,0:T(8,128)(2,1)S(1)}, bf16[48,1536]{1,0:T(8,128)(2,1)S(1)}, u32[]{:S(2)}, u32[]{:S(2)}) %collective-permute-start.47) | collective-permute-done | bytes 147488 | tf_op jit(solution)/shard_map/ppermute | solution.py:235
  284.8 4.1 %split_add.5 = (bf16[4,2,48,1280]{3,2,1,0:T(8,128)(2,1)}, bf16[4,2,48,1280]{3,2,1,0:T(8,128)(2,1)}) custom-call(s32[4]{0:T(128)} %pad_add_fusion.1.which, bf16[4,4,48,1152]{3,2,1,0:T(8,128)(2,1)} %bitcast.217, bf16[4,4,48,1152]{3,2,1,0:T(8,128)(2,1)} %bitcast.48.refs_1_.refs_5_, bf16[4,4,48,128]{3,2,1,0:T(8,128)(2,1)} %bitcast.242, ...), custom_call_target="tpu_custom_call" | custom-call | tf_op jit(solution)/shard_map/split_add/pallas_call | solution.py:385
  293.2 9.2 %collective-permute-done.42 = bf16[2,48,1920]{2,1,0:T(8,128)(2,1)S(1)} collective-permute-done((bf16[2,48,1920]{2,1,0:T(8,128)(2,1)S(1)}, bf16[2,48,1920]{2,1,0:T(8,128)(2,1)S(1)}, u32[]{:S(2)}, u32[]{:S(2)}) %collective-permute-start.42) | collective-permute-done | bytes 368672 | tf_op jit(solution)/shard_map/ppermute | solution.py:235
  305.0 9.7 %collective-permute-done.43 = bf16[48,1920]{1,0:T(8,128)(2,1)S(1)} collective-permute-done((bf16[48,1920]{1,0:T(8,128)(2,1)S(1)}, bf16[48,1920]{1,0:T(8,128)(2,1)S(1)}, u32[]{:S(2)}, u32[]{:S(2)}) %collective-permute-start.43) | collective-permute-done | bytes 184352 | tf_op jit(solution)/shard_map/ppermute | solution.py:235
  315.9 3.8 %fusion.8 = f32[4,196,768]{2,1,0:T(8,128)S(1)} fusion(bf16[4,196,1536]{2,1,0:T(8,128)(2,1)S(1)} %copy-done.40, bf16[768,3840]{1,0:T(8,128)(2,1)} %all-gather.2.cloned.1.call-done), kind=kOutput, calls=%fused_computation.22 | convolution fusion | flops 1849688064 | bytes 7176192 | tf_op jit(solution)/shard_map/...j,aj->...a/dot_general | solution.py:42
  319.7 2.4 copy.94
  323.7 7.0 %collective-permute-done.38 = bf16[2,48,1280]{2,1,0:T(8,128)(2,1)S(1)} collective-permute-done((bf16[2,48,1280]{2,1,0:T(8,128)(2,1)S(1)}, bf16[2,48,1280]{2,1,0:T(8,128)(2,1)S(1)}, u32[]{:S(2)}, u32[]{:S(2)}) %collective-permute-start.38) | collective-permute-done | bytes 245792 | tf_op jit(solution)/shard_map/ppermute | solution.py:235
  331.0 2.9 fusion.11
  335.5 3.7 %collective-permute-done.39 = bf16[48,1280]{1,0:T(8,128)(2,1)S(1)} collective-permute-done((bf16[48,1280]{1,0:T(8,128)(2,1)S(1)}, bf16[48,1280]{1,0:T(8,128)(2,1)S(1)}, u32[]{:S(2)}, u32[]{:S(2)}) %collective-permute-start.39) | collective-permute-done | bytes 122912 | tf_op jit(solution)/shard_map/ppermute | solution.py:235
  (304 shorter events, 101.5 us)
Async XLA Ops:
  7.2 101.3 %all-gather.2.cloned.1.call-start = ((), (), s32[]{:S(2)}) async-start(), calls=%async_computation.1 | async-start | bytes 6082560 | tf_op jit(solution)/shard_map/all_gather | solution.py:544
  9.0 324.8 %reduce-scatter.2.cloned.1.call-start = ((), (), s32[]{:S(2)}) async-start(), calls=%async_computation.2 | async-start | bytes 4866048 | tf_op jit(solution)/shard_map/reduce_scatter | solution.py:399
  12.4 10.1 %collective-permute-start = (bf16[24,2560]{1,0:T(8,128)(2,1)S(1)}, bf16[24,2560]{1,0:T(8,128)(2,1)S(1)}, u32[]{:S(2)}, u32[]{:S(2)}) collective-permute-start(bf16[24,2560]{1,0:T(8,128)(2,1)S(1)} %concatenate.40), channel_id=1, source_target_pairs={{0,16},{1,17},{2,18},{3,19},{4,20},{5,21},{6,22},{7,23},{8,24},{9,... | collective-permute-start | bytes 368648 | tf_op jit(solution)/shard_map/ppermute | solution.py:235
  22.5 9.7 %collective-permute-start.1 = (bf16[2,24,2560]{2,1,0:T(8,128)(2,1)S(1)}, bf16[2,24,2560]{2,1,0:T(8,128)(2,1)S(1)}, u32[]{:S(2)}, u32[]{:S(2)}) collective-permute-start(bf16[2,24,2560]{2,1,0:T(8,128)(2,1)S(1)} %pad_maximum_fusion.8), channel_id=1, source_target_pairs={{0,8},{1,9},{2,10},{3,11},{4,12},{5,13},{6,14},{7,15},{8,0},{9,1},... | collective-permute-start | bytes 737288 | tf_op jit(solution)/shard_map/ppermute | solution.py:235
  32.3 9.7 %collective-permute-start.2 = (bf16[4,24,2560]{2,1,0:T(8,128)(2,1)S(1)}, bf16[4,24,2560]{2,1,0:T(8,128)(2,1)}, u32[]{:S(2)}, u32[]{:S(2)}) collective-permute-start(bf16[4,24,2560]{2,1,0:T(8,128)(2,1)S(1)} %pad_maximum_fusion.2.refs_0_), channel_id=1, source_target_pairs={{0,4},{1,3},{2,6},{3,1},{4,0},{5,7},{6,2},{7,5},{8,12},{9,11},{10,... | collective-permute-start | bytes 1474568 | tf_op jit(solution)/shard_map/ppermute | solution.py:235
  33.7 12.6 %collective-permute-start.9 = (bf16[24,3072]{1,0:T(8,128)(2,1)S(1)}, bf16[24,3072]{1,0:T(8,128)(2,1)S(1)}, u32[]{:S(2)}, u32[]{:S(2)}) collective-permute-start(bf16[24,3072]{1,0:T(8,128)(2,1)S(1)} %copy-done.32), channel_id=1, source_target_pairs={{0,16},{1,17},{2,18},{3,19},{4,20},{5,21},{6,22},{7,23},{8,24},{9,... | collective-permute-start | bytes 442376 | tf_op jit(solution)/shard_map/ppermute | solution.py:235
  38.8 11.6 %collective-permute-start.3 = (bf16[4,24,2560]{2,1,0:T(8,128)(2,1)S(1)}, bf16[4,24,2560]{2,1,0:T(8,128)(2,1)}, u32[]{:S(2)}, u32[]{:S(2)}) collective-permute-start(bf16[4,24,2560]{2,1,0:T(8,128)(2,1)S(1)} %pad_maximum_fusion.2.refs_0_), channel_id=1, source_target_pairs={{0,2},{1,5},{2,0},{3,7},{4,6},{5,1},{6,4},{7,3},{8,10},{9,13},{10,... | collective-permute-start | bytes 1474568 | tf_op jit(solution)/shard_map/ppermute | solution.py:235
  42.0 13.7 %collective-permute-start.4 = (bf16[4,24,2560]{2,1,0:T(8,128)(2,1)}, bf16[4,24,2560]{2,1,0:T(8,128)(2,1)}, u32[]{:S(2)}, u32[]{:S(2)}) collective-permute-start(bf16[4,24,2560]{2,1,0:T(8,128)(2,1)} %collective-permute-done.2.refs_1_), channel_id=1, source_target_pairs={{0,2},{1,5},{2,0},{3,7},{4,6},{5,1},{6,4},{7,3},{8,10},{9,13},{10,... | collective-permute-start | bytes 1474568 | tf_op jit(solution)/shard_map/ppermute | solution.py:235
  47.0 13.2 %collective-permute-start.10 = (bf16[2,24,3072]{2,1,0:T(8,128)(2,1)}, bf16[2,24,3072]{2,1,0:T(8,128)(2,1)}, u32[]{:S(2)}, u32[]{:S(2)}) collective-permute-start(bf16[2,24,3072]{2,1,0:T(8,128)(2,1)} %pad_maximum_fusion.4), channel_id=1, source_target_pairs={{0,8},{1,9},{2,10},{3,11},{4,12},{5,13},{6,14},{7,15},{8,0},{9,1},... | collective-permute-start | bytes 884744 | tf_op jit(solution)/shard_map/ppermute | solution.py:235
  49.1 13.1 %collective-permute-start.5 = (bf16[4,24,2560]{2,1,0:T(8,128)(2,1)S(1)}, bf16[4,24,2560]{2,1,0:T(8,128)(2,1)}, u32[]{:S(2)}, u32[]{:S(2)}) collective-permute-start(bf16[4,24,2560]{2,1,0:T(8,128)(2,1)S(1)} %pad_maximum_fusion.2.refs_0_), channel_id=1, source_target_pairs={{0,1},{1,0},{2,3},{3,2},{4,5},{5,4},{6,7},{7,6},{8,9},{9,8},{10,11... | collective-permute-start | bytes 1474568 | tf_op jit(solution)/shard_map/ppermute | solution.py:235
  49.1 14.7 %collective-permute-start.6 = (bf16[4,24,2560]{2,1,0:T(8,128)(2,1)}, bf16[4,24,2560]{2,1,0:T(8,128)(2,1)}, u32[]{:S(2)}, u32[]{:S(2)}) collective-permute-start(bf16[4,24,2560]{2,1,0:T(8,128)(2,1)} %collective-permute-done.2.refs_1_), channel_id=1, source_target_pairs={{0,1},{1,0},{2,3},{3,2},{4,5},{5,4},{6,7},{7,6},{8,9},{9,8},{10,11... | collective-permute-start | bytes 1474568 | tf_op jit(solution)/shard_map/ppermute | solution.py:235
  50.4 13.4 %collective-permute-start.7 = (bf16[4,24,2560]{2,1,0:T(8,128)(2,1)}, bf16[4,24,2560]{2,1,0:T(8,128)(2,1)}, u32[]{:S(2)}, u32[]{:S(2)}) collective-permute-start(bf16[4,24,2560]{2,1,0:T(8,128)(2,1)} %collective-permute-done.3.refs_2_), channel_id=1, source_target_pairs={{0,1},{1,0},{2,3},{3,2},{4,5},{5,4},{6,7},{7,6},{8,9},{9,8},{10,11... | collective-permute-start | bytes 1474568 | tf_op jit(solution)/shard_map/ppermute | solution.py:235
  62.2 39.8 %collective-permute-start.12 = (bf16[4,24,3072]{2,1,0:T(8,128)(2,1)}, bf16[4,24,3072]{2,1,0:T(8,128)(2,1)}, u32[]{:S(2)}, u32[]{:S(2)}) collective-permute-start(bf16[4,24,3072]{2,1,0:T(8,128)(2,1)} %pad_maximum_fusion.refs_0_), channel_id=1, source_target_pairs={{0,2},{1,5},{2,0},{3,7},{4,6},{5,1},{6,4},{7,3},{8,10},{9,13},{10,... | collective-permute-start | bytes 1769480 | tf_op jit(solution)/shard_map/ppermute | solution.py:235
  62.2 33.8 %collective-permute-start.11 = (bf16[4,24,3072]{2,1,0:T(8,128)(2,1)}, bf16[4,24,3072]{2,1,0:T(8,128)(2,1)}, u32[]{:S(2)}, u32[]{:S(2)}) collective-permute-start(bf16[4,24,3072]{2,1,0:T(8,128)(2,1)} %pad_maximum_fusion.refs_0_), channel_id=1, source_target_pairs={{0,4},{1,3},{2,6},{3,1},{4,0},{5,7},{6,2},{7,5},{8,12},{9,11},{10,... | collective-permute-start | bytes 1769480 | tf_op jit(solution)/shard_map/ppermute | solution.py:235
  63.8 32.3 %collective-permute-start.18 = (bf16[96,768]{1,0:T(8,128)(2,1)}, bf16[96,768]{1,0:T(8,128)(2,1)S(1)}, u32[]{:S(2)}, u32[]{:S(2)}) collective-permute-start(bf16[96,768]{1,0:T(8,128)(2,1)} %param.24), channel_id=1, source_target_pairs={{0,16},{1,17},{2,18},{3,19},{4,20},{5,21},{6,22},{7,23},{8,24},{9,... | collective-permute-start | bytes 442376 | tf_op jit(solution)/shard_map/ppermute | solution.py:235
  96.0 12.5 %collective-permute-start.13 = (bf16[4,24,3072]{2,1,0:T(8,128)(2,1)}, bf16[4,24,3072]{2,1,0:T(8,128)(2,1)}, u32[]{:S(2)}, u32[]{:S(2)}) collective-permute-start(bf16[4,24,3072]{2,1,0:T(8,128)(2,1)} %collective-permute-done.11.refs_1_), channel_id=1, source_target_pairs={{0,2},{1,5},{2,0},{3,7},{4,6},{5,1},{6,4},{7,3},{8,10},{9,13},{10,... | collective-permute-start | bytes 1769480 | tf_op jit(solution)/shard_map/ppermute | solution.py:235
  97.7 8.8 %collective-permute-start.19 = (bf16[2,96,768]{2,1,0:T(8,128)(2,1)}, bf16[2,96,768]{2,1,0:T(8,128)(2,1)}, u32[]{:S(2)}, u32[]{:S(2)}) collective-permute-start(bf16[2,96,768]{2,1,0:T(8,128)(2,1)} %pad_maximum_fusion.5), channel_id=1, source_target_pairs={{0,8},{1,9},{2,10},{3,11},{4,12},{5,13},{6,14},{7,15},{8,0},{9,1},... | collective-permute-start | bytes 884744 | tf_op jit(solution)/shard_map/ppermute | solution.py:235
  100.6 23.8 %collective-permute-start.14 = (bf16[4,24,3072]{2,1,0:T(8,128)(2,1)}, bf16[4,24,3072]{2,1,0:T(8,128)(2,1)}, u32[]{:S(2)}, u32[]{:S(2)}) collective-permute-start(bf16[4,24,3072]{2,1,0:T(8,128)(2,1)} %pad_maximum_fusion.refs_0_), channel_id=1, source_target_pairs={{0,1},{1,0},{2,3},{3,2},{4,5},{5,4},{6,7},{7,6},{8,9},{9,8},{10,11... | collective-permute-start | bytes 1769480 | tf_op jit(solution)/shard_map/ppermute | solution.py:235
  101.4 24.1 %collective-permute-start.15 = (bf16[4,24,3072]{2,1,0:T(8,128)(2,1)}, bf16[4,24,3072]{2,1,0:T(8,128)(2,1)}, u32[]{:S(2)}, u32[]{:S(2)}) collective-permute-start(bf16[4,24,3072]{2,1,0:T(8,128)(2,1)} %collective-permute-done.11.refs_1_), channel_id=1, source_target_pairs={{0,1},{1,0},{2,3},{3,2},{4,5},{5,4},{6,7},{7,6},{8,9},{9,8},{10,11... | collective-permute-start | bytes 1769480 | tf_op jit(solution)/shard_map/ppermute | solution.py:235
  101.9 22.5 %collective-permute-start.16 = (bf16[4,24,3072]{2,1,0:T(8,128)(2,1)}, bf16[4,24,3072]{2,1,0:T(8,128)(2,1)}, u32[]{:S(2)}, u32[]{:S(2)}) collective-permute-start(bf16[4,24,3072]{2,1,0:T(8,128)(2,1)} %collective-permute-done.12.refs_2_), channel_id=1, source_target_pairs={{0,1},{1,0},{2,3},{3,2},{4,5},{5,4},{6,7},{7,6},{8,9},{9,8},{10,11... | collective-permute-start | bytes 1769480 | tf_op jit(solution)/shard_map/ppermute | solution.py:235
  108.5 17.1 %collective-permute-start.17 = (bf16[4,24,3072]{2,1,0:T(8,128)(2,1)}, bf16[4,24,3072]{2,1,0:T(8,128)(2,1)}, u32[]{:S(2)}, u32[]{:S(2)}) collective-permute-start(bf16[4,24,3072]{2,1,0:T(8,128)(2,1)} %collective-permute-done.13.refs_3_), channel_id=1, source_target_pairs={{0,1},{1,0},{2,3},{3,2},{4,5},{5,4},{6,7},{7,6},{8,9},{9,8},{10,11... | collective-permute-start | bytes 1769480 | tf_op jit(solution)/shard_map/ppermute | solution.py:235
  113.2 20.4 %collective-permute-start.20 = (bf16[4,96,768]{2,1,0:T(8,128)(2,1)}, bf16[4,96,768]{2,1,0:T(8,128)(2,1)}, u32[]{:S(2)}, u32[]{:S(2)}) collective-permute-start(bf16[4,96,768]{2,1,0:T(8,128)(2,1)} %pad_maximum_fusion.1.refs_0_), channel_id=1, source_target_pairs={{0,4},{1,3},{2,6},{3,1},{4,0},{5,7},{6,2},{7,5},{8,12},{9,11},{10,... | collective-permute-start | bytes 1769480 | tf_op jit(solution)/shard_map/ppermute | solution.py:235
  124.4 30.5 %collective-permute-start.23 = (bf16[4,96,768]{2,1,0:T(8,128)(2,1)}, bf16[4,96,768]{2,1,0:T(8,128)(2,1)}, u32[]{:S(2)}, u32[]{:S(2)}) collective-permute-start(bf16[4,96,768]{2,1,0:T(8,128)(2,1)} %pad_maximum_fusion.1.refs_0_), channel_id=1, source_target_pairs={{0,1},{1,0},{2,3},{3,2},{4,5},{5,4},{6,7},{7,6},{8,9},{9,8},{10,11... | collective-permute-start | bytes 1769480 | tf_op jit(solution)/shard_map/ppermute | solution.py:235
  124.5 10.6 %collective-permute-start.21 = (bf16[4,96,768]{2,1,0:T(8,128)(2,1)}, bf16[4,96,768]{2,1,0:T(8,128)(2,1)}, u32[]{:S(2)}, u32[]{:S(2)}) collective-permute-start(bf16[4,96,768]{2,1,0:T(8,128)(2,1)} %pad_maximum_fusion.1.refs_0_), channel_id=1, source_target_pairs={{0,2},{1,5},{2,0},{3,7},{4,6},{5,1},{6,4},{7,3},{8,10},{9,13},{10,... | collective-permute-start | bytes 1769480 | tf_op jit(solution)/shard_map/ppermute | solution.py:235
  133.6 10.3 %collective-permute-start.22 = (bf16[4,96,768]{2,1,0:T(8,128)(2,1)}, bf16[4,96,768]{2,1,0:T(8,128)(2,1)}, u32[]{:S(2)}, u32[]{:S(2)}) collective-permute-start(bf16[4,96,768]{2,1,0:T(8,128)(2,1)} %collective-permute-done.20.refs_1_), channel_id=1, source_target_pairs={{0,2},{1,5},{2,0},{3,7},{4,6},{5,1},{6,4},{7,3},{8,10},{9,13},{10,... | collective-permute-start | bytes 1769480 | tf_op jit(solution)/shard_map/ppermute | solution.py:235
  135.0 19.8 %collective-permute-start.24 = (bf16[4,96,768]{2,1,0:T(8,128)(2,1)}, bf16[4,96,768]{2,1,0:T(8,128)(2,1)}, u32[]{:S(2)}, u32[]{:S(2)}) collective-permute-start(bf16[4,96,768]{2,1,0:T(8,128)(2,1)} %collective-permute-done.20.refs_1_), channel_id=1, source_target_pairs={{0,1},{1,0},{2,3},{3,2},{4,5},{5,4},{6,7},{7,6},{8,9},{9,8},{10,11... | collective-permute-start | bytes 1769480 | tf_op jit(solution)/shard_map/ppermute | solution.py:235
  135.1 19.8 %collective-permute-start.25 = (bf16[4,96,768]{2,1,0:T(8,128)(2,1)}, bf16[4,96,768]{2,1,0:T(8,128)(2,1)}, u32[]{:S(2)}, u32[]{:S(2)}) collective-permute-start(bf16[4,96,768]{2,1,0:T(8,128)(2,1)} %collective-permute-done.21.refs_2_), channel_id=1, source_target_pairs={{0,1},{1,0},{2,3},{3,2},{4,5},{5,4},{6,7},{7,6},{8,9},{9,8},{10,11... | collective-permute-start | bytes 1769480 | tf_op jit(solution)/shard_map/ppermute | solution.py:235
  143.9 11.0 %collective-permute-start.26 = (bf16[4,96,768]{2,1,0:T(8,128)(2,1)}, bf16[4,96,768]{2,1,0:T(8,128)(2,1)}, u32[]{:S(2)}, u32[]{:S(2)}) collective-permute-start(bf16[4,96,768]{2,1,0:T(8,128)(2,1)} %collective-permute-done.22.refs_3_), channel_id=1, source_target_pairs={{0,1},{1,0},{2,3},{3,2},{4,5},{5,4},{6,7},{7,6},{8,9},{9,8},{10,11... | collective-permute-start | bytes 1769480 | tf_op jit(solution)/shard_map/ppermute | solution.py:235
  171.0 19.1 %collective-permute-start.27 = (bf16[768,1536]{1,0:T(8,128)(2,1)}, bf16[768,1536]{1,0:T(8,128)(2,1)}, u32[]{:S(2)}, u32[]{:S(2)}) collective-permute-start(bf16[768,1536]{1,0:T(8,128)(2,1)} %convolution_convert_fusion.6), channel_id=1, source_target_pairs={{0,1},{1,0},{2,3},{3,2},{4,5},{5,4},{6,7},{7,6},{8,9},{9,8},{10,11... | collective-permute-start | bytes 7077896 | tf_op jit(solution)/shard_map/ppermute | solution.py:235
  185.9 48.9 %collective-permute-start.31 = (bf16[768,384]{1,0:T(8,128)(2,1)}, bf16[768,384]{1,0:T(8,128)(2,1)}, u32[]{:S(2)}, u32[]{:S(2)}) collective-permute-start(bf16[768,384]{1,0:T(8,128)(2,1)} %convolution_convert_fusion.11), channel_id=1, source_target_pairs={{0,1},{1,0},{2,3},{3,2},{4,5},{5,4},{6,7},{7,6},{8,9},{9,8},{10,11... | collective-permute-start | bytes 1769480 | tf_op jit(solution)/shard_map/ppermute | solution.py:235
  210.1 24.8 %collective-permute-start.30 = (bf16[768,768]{0,1:T(8,128)(2,1)}, bf16[768,768]{0,1:T(8,128)(2,1)}, u32[]{:S(2)}, u32[]{:S(2)}) collective-permute-start(bf16[768,768]{0,1:T(8,128)(2,1)} %fusion.9), channel_id=1, source_target_pairs={{0,1},{1,0},{2,3},{3,2},{4,5},{5,4},{6,7},{7,6},{8,9},{9,8},{10,11... | collective-permute-start | bytes 3538952 | tf_op jit(solution)/shard_map/ppermute | solution.py:235
  210.6 24.9 %collective-permute-start.28 = (bf16[4,2,48,1536]{3,2,1,0:T(8,128)(2,1)}, bf16[4,2,48,1536]{3,2,1,0:T(8,128)(2,1)}, u32[]{:S(2)}, u32[]{:S(2)}) collective-permute-start(bf16[4,2,48,1536]{3,2,1,0:T(8,128)(2,1)} %get-tuple-element.95), channel_id=1, source_target_pairs={{0,2},{1,5},{2,0},{3,7},{4,6},{5,1},{6,4},{7,3},{8,10},{9,13},{10,... | collective-permute-start | bytes 3538952 | tf_op jit(solution)/shard_map/ppermute | solution.py:235
  214.6 20.3 %collective-permute-start.32 = (bf16[768,384]{1,0:T(8,128)(2,1)}, bf16[768,384]{1,0:T(8,128)(2,1)S(1)}, u32[]{:S(2)}, u32[]{:S(2)}) collective-permute-start(bf16[768,384]{1,0:T(8,128)(2,1)} %convolution_convert_fusion.10), channel_id=1, source_target_pairs={{0,1},{1,0},{2,3},{3,2},{4,5},{5,4},{6,7},{7,6},{8,9},{9,8},{10,11... | collective-permute-start | bytes 1769480 | tf_op jit(solution)/shard_map/ppermute | solution.py:235
  214.6 20.3 %collective-permute-start.29 = (bf16[768,384]{1,0:T(8,128)(2,1)}, bf16[768,384]{1,0:T(8,128)(2,1)S(1)}, u32[]{:S(2)}, u32[]{:S(2)}) collective-permute-start(bf16[768,384]{1,0:T(8,128)(2,1)} %convolution_convert_fusion.12), channel_id=1, source_target_pairs={{0,1},{1,0},{2,3},{3,2},{4,5},{5,4},{6,7},{7,6},{8,9},{9,8},{10,11... | collective-permute-start | bytes 1769480 | tf_op jit(solution)/shard_map/ppermute | solution.py:235
  238.0 46.1 %collective-permute-start.34 = (bf16[768,1152]{1,0:T(8,128)(2,1)}, bf16[768,1152]{1,0:T(8,128)(2,1)}, u32[]{:S(2)}, u32[]{:S(2)}) collective-permute-start(bf16[768,1152]{1,0:T(8,128)(2,1)} %convolution_convert_fusion.3), channel_id=1, source_target_pairs={{0,1},{1,0},{2,3},{3,2},{4,5},{5,4},{6,7},{7,6},{8,9},{9,8},{10,11... | collective-permute-start | bytes 5308424 | tf_op jit(solution)/shard_map/ppermute | solution.py:235
  239.3 17.3 %collective-permute-start.45 = (bf16[4,48,1536]{2,1,0:T(8,128)(2,1)S(1)}, bf16[4,48,1536]{2,1,0:T(8,128)(2,1)}, u32[]{:S(2)}, u32[]{:S(2)}) collective-permute-start(bf16[4,48,1536]{2,1,0:T(8,128)(2,1)S(1)} %fusion.30), channel_id=1, source_target_pairs={{0,4},{1,3},{2,6},{3,1},{4,0},{5,7},{6,2},{7,5},{8,12},{9,11},{10,... | collective-permute-start | bytes 1769480 | tf_op jit(solution)/shard_map/ppermute | solution.py:235
  248.2 22.6 %collective-permute-start.33 = (bf16[4,2,48,1920]{3,2,1,0:T(8,128)(2,1)}, bf16[4,2,48,1920]{3,2,1,0:T(8,128)(2,1)}, u32[]{:S(2)}, u32[]{:S(2)}) collective-permute-start(bf16[4,2,48,1920]{3,2,1,0:T(8,128)(2,1)} %get-tuple-element.98), channel_id=1, source_target_pairs={{0,2},{1,5},{2,0},{3,7},{4,6},{5,1},{6,4},{7,3},{8,10},{9,13},{10,... | collective-permute-start | bytes 4423688 | tf_op jit(solution)/shard_map/ppermute | solution.py:235
  257.8 11.2 %collective-permute-start.46 = (bf16[2,48,1536]{2,1,0:T(8,128)(2,1)S(1)}, bf16[2,48,1536]{2,1,0:T(8,128)(2,1)S(1)}, u32[]{:S(2)}, u32[]{:S(2)}) collective-permute-start(bf16[2,48,1536]{2,1,0:T(8,128)(2,1)S(1)} %pad_maximum_fusion.6), channel_id=1, source_target_pairs={{0,8},{1,9},{2,10},{3,11},{4,12},{5,13},{6,14},{7,15},{8,0},{9,1},... | collective-permute-start | bytes 884744 | tf_op jit(solution)/shard_map/ppermute | solution.py:235
  270.1 10.9 %collective-permute-start.47 = (bf16[48,1536]{1,0:T(8,128)(2,1)S(1)}, bf16[48,1536]{1,0:T(8,128)(2,1)S(1)}, u32[]{:S(2)}, u32[]{:S(2)}) collective-permute-start(bf16[48,1536]{1,0:T(8,128)(2,1)S(1)} %fusion.39), channel_id=1, source_target_pairs={{0,16},{1,17},{2,18},{3,19},{4,20},{5,21},{6,22},{7,23},{8,24},{9,... | collective-permute-start | bytes 442376 | tf_op jit(solution)/shard_map/ppermute | solution.py:235
  273.0 17.1 %collective-permute-start.41 = (bf16[4,48,1920]{2,1,0:T(8,128)(2,1)}, bf16[4,48,1920]{2,1,0:T(8,128)(2,1)}, u32[]{:S(2)}, u32[]{:S(2)}) collective-permute-start(bf16[4,48,1920]{2,1,0:T(8,128)(2,1)} %fusion.29), channel_id=1, source_target_pairs={{0,4},{1,3},{2,6},{3,1},{4,0},{5,7},{6,2},{7,5},{8,12},{9,11},{10,... | collective-permute-start | bytes 2211848 | tf_op jit(solution)/shard_map/ppermute | solution.py:235
  275.5 8.6 %collective-permute-start.35 = (bf16[768,128]{1,0:T(8,128)(2,1)S(1)}, bf16[768,128]{1,0:T(8,128)(2,1)S(1)}, u32[]{:S(2)}, u32[]{:S(2)}) collective-permute-start(bf16[768,128]{1,0:T(8,128)(2,1)S(1)} %convolution_convert_fusion.16), channel_id=1, source_target_pairs={{0,1},{1,0},{2,3},{3,2},{4,5},{5,4},{6,7},{7,6},{8,9},{9,8},{10,11... | collective-permute-start | bytes 589832 | tf_op jit(solution)/shard_map/ppermute | solution.py:235
  282.9 8.5 %collective-permute-start.48 = (f32[24,1536]{1,0:T(8,128)}, f32[24,1536]{1,0:T(8,128)}, u32[]{:S(2)}, u32[]{:S(2)}) collective-permute-start(f32[24,1536]{1,0:T(8,128)} %constant_dynamic-slice_fusion.2), channel_id=1, source_target_pairs={{0,1},{1,0},{2,3},{3,2},{4,5},{5,4},{6,7},{7,6},{8,9},{9,8},{10,11... | collective-permute-start | bytes 442376 | tf_op jit(solution)/shard_map/ppermute | solution.py:235
  288.8 14.8 %collective-permute-start.36 = (bf16[4,2,48,1280]{3,2,1,0:T(8,128)(2,1)}, bf16[4,2,48,1280]{3,2,1,0:T(8,128)(2,1)S(1)}, u32[]{:S(2)}, u32[]{:S(2)}) collective-permute-start(bf16[4,2,48,1280]{3,2,1,0:T(8,128)(2,1)} %get-tuple-element.102), channel_id=1, source_target_pairs={{0,2},{1,5},{2,0},{3,7},{4,6},{5,1},{6,4},{7,3},{8,10},{9,13},{10,... | collective-permute-start | bytes 2949128 | tf_op jit(solution)/shard_map/ppermute | solution.py:235
  291.3 11.1 %collective-permute-start.42 = (bf16[2,48,1920]{2,1,0:T(8,128)(2,1)S(1)}, bf16[2,48,1920]{2,1,0:T(8,128)(2,1)S(1)}, u32[]{:S(2)}, u32[]{:S(2)}) collective-permute-start(bf16[2,48,1920]{2,1,0:T(8,128)(2,1)S(1)} %pad_maximum_fusion.3), channel_id=1, source_target_pairs={{0,8},{1,9},{2,10},{3,11},{4,12},{5,13},{6,14},{7,15},{8,0},{9,1},... | collective-permute-start | bytes 1105928 | tf_op jit(solution)/shard_map/ppermute | solution.py:235
  303.5 11.2 %collective-permute-start.43 = (bf16[48,1920]{1,0:T(8,128)(2,1)S(1)}, bf16[48,1920]{1,0:T(8,128)(2,1)S(1)}, u32[]{:S(2)}, u32[]{:S(2)}) collective-permute-start(bf16[48,1920]{1,0:T(8,128)(2,1)S(1)} %fusion.33), channel_id=1, source_target_pairs={{0,16},{1,17},{2,18},{3,19},{4,20},{5,21},{6,22},{7,23},{8,24},{9,... | collective-permute-start | bytes 552968 | tf_op jit(solution)/shard_map/ppermute | solution.py:235
  303.8 18.3 %collective-permute-start.37 = (bf16[4,48,1280]{2,1,0:T(8,128)(2,1)S(1)}, bf16[4,48,1280]{2,1,0:T(8,128)(2,1)S(1)}, u32[]{:S(2)}, u32[]{:S(2)}) collective-permute-start(bf16[4,48,1280]{2,1,0:T(8,128)(2,1)S(1)} %fusion.31), channel_id=1, source_target_pairs={{0,4},{1,3},{2,6},{3,1},{4,0},{5,7},{6,2},{7,5},{8,12},{9,11},{10,... | collective-permute-start | bytes 1474568 | tf_op jit(solution)/shard_map/ppermute | solution.py:235
  322.3 8.4 %collective-permute-start.38 = (bf16[2,48,1280]{2,1,0:T(8,128)(2,1)S(1)}, bf16[2,48,1280]{2,1,0:T(8,128)(2,1)S(1)}, u32[]{:S(2)}, u32[]{:S(2)}) collective-permute-start(bf16[2,48,1280]{2,1,0:T(8,128)(2,1)S(1)} %pad_maximum_fusion.9), channel_id=1, source_target_pairs={{0,8},{1,9},{2,10},{3,11},{4,12},{5,13},{6,14},{7,15},{8,0},{9,1},... | collective-permute-start | bytes 737288 | tf_op jit(solution)/shard_map/ppermute | solution.py:235
  330.8 8.4 %collective-permute-start.39 = (bf16[48,1280]{1,0:T(8,128)(2,1)S(1)}, bf16[48,1280]{1,0:T(8,128)(2,1)S(1)}, u32[]{:S(2)}, u32[]{:S(2)}) collective-permute-start(bf16[48,1280]{1,0:T(8,128)(2,1)S(1)} %get-tuple-element.190), channel_id=1, source_target_pairs={{0,16},{1,17},{2,18},{3,19},{4,20},{5,21},{6,22},{7,23},{8,24},{9,... | collective-permute-start | bytes 368648 | tf_op jit(solution)/shard_map/ppermute | solution.py:235
  (52 other events, 493.1 us)
Sparse Core Ops, SparseCore 0:
  11.5 85.0 all-gather.1
  172.8 113.3 reduce-scatter.1

commit v5 on v4

--- a/solution.py
+++ b/solution.py
@@ -453,7 +453,8 @@
     def hop5(self, *earlier):
         near = after(self.near, *earlier).astype(jnp.float32)
         self.own = self.own + near[0]
-        self.last = move((self.far + near[1]).astype(jnp.bfloat16), ZFAR)
+        self.turn = (self.far + near[1]).astype(jnp.bfloat16)
+        self.last = move(self.turn, ZFAR)
         return [self.last]
 
     def results(self):
@@ -482,7 +483,7 @@
     def __init__(self, factors):
         self.factors = factors
         self.sends = []
-        self.keep = self.half = self.got_first = self.own = jnp.zeros((), jnp.bfloat16)
+        self.keep = self.half = self.got_first = self.turn = self.own = self.last = jnp.zeros((), jnp.bfloat16)
 
     def add(self, value, upstream_gradient):
         self.factors.append((value, upstream_gradient))
@@ -547,19 +548,19 @@
     third.spread(*first.spread())
     first.cross()
     third.cross(*first.corner())
-    fourth.spread(*first.swap(), *third.along)
+    first.swap()
     w_qkv, smalls = first.join()
-    gains, biases, hidden_bias = smalls[:, :3], smalls[:, 3:7], smalls[:, 7:11].reshape(-1)
+    columns = dot(jnp.eye(16, smalls.shape[1], dtype=jnp.bfloat16), smalls, BOTH_LAST)
+    gains, biases, hidden_bias = columns[:3], columns[3:7], columns[7:11].T.reshape(-1)
     seqs, rows, width = tokens.shape
     low = lambda v: v.astype(jnp.bfloat16)
     flat = lambda v: v.reshape(seqs * rows, v.shape[-1])
     by_seq = lambda v: v.reshape(seqs, rows, v.shape[-1])
     live = jnp.arange(rows)[None, :] < (PREFIX + suffix_len)[:, None]
-    gain_vals = gains.astype(jnp.float32)
-    bias_vals = biases.astype(jnp.float32)
     stream0 = flat(tokens).astype(jnp.float32)
-    normed1, standard1, inverse1 = norm_forward(stream0, gain_vals[:, 0], bias_vals[:, 0])
+    normed1, standard1, inverse1 = norm_forward(stream0, gains[0], biases[0])
     normed1 = low(normed1)
+    fourth.spread(w_qkv)
     qkv = by_seq(low(project(normed1, w_qkv)))
     context, probs = self_forward(qkv, suffix_len)
     third.corner(context)
@@ -568,7 +569,7 @@
     w_ckv, w_cout = w_second[:, 2 * D : 4 * D], w_second[:, 4 * D :]
     context = flat(context)
     stream1 = stream0 + project(context, w_out)
-    normed2, standard2, inverse2 = norm_forward(stream1, gain_vals[:, 1], bias_vals[:, 1])
+    normed2, standard2, inverse2 = norm_forward(stream1, gains[1], biases[1])
     normed2 = low(normed2)
     cquery = by_seq(low(project(normed2, w_cquery)))
     ckv = low(project(memory, w_ckv))
@@ -576,12 +577,12 @@
     ccontext, cprobs = cross_forward(cquery, ckv)
     ccontext = flat(ccontext)
     stream2 = stream1 + project(ccontext, w_cout)
-    normed3, standard3, inverse3 = norm_forward(stream2, gain_vals[:, 2], bias_vals[:, 2])
+    normed3, standard3, inverse3 = norm_forward(stream2, gains[2], biases[2])
     normed3 = low(normed3)
     (w_in,) = third.join(ccontext)
     fourth.corner(ccontext)
     fourth.swap()
-    pre = project(normed3, w_in) + hidden_bias.astype(jnp.float32)
+    pre = project(normed3, w_in) + hidden_bias
     activated, gelu_back = jax.vjp(lambda v: jax.nn.gelu(v, approximate=True), pre)
     activated = low(activated)
 
@@ -597,7 +598,7 @@
     in_sum = reduction([(normed3, dpre)])
     dpre = after(dpre, *in_sum.sends)
     grad_back, g_gain3, g_shift3 = norm_backward(
-        back_project(dpre, w_in), standard3, inverse3, gain_vals[:, 2]
+        back_project(dpre, w_in), standard3, inverse3, gains[2]
     )
     upstream = upstream + grad_back
     dout2 = low(upstream)
@@ -607,27 +608,26 @@
     dccontext = after(dccontext, in_sum.keep)
     dcquery, dckv = cross_backward(cquery, ckv, cprobs, dccontext)
     dcq = flat(dcquery)
+    cross_sum = reduction([(normed2, dcq), (memory, dckv), (ccontext, dout2)])
+    dcq = after(dcq, *arriving, *cross_sum.sends)
     grad_back, g_gain2, g_shift2 = norm_backward(
-        back_project(dcq, w_cquery), standard2, inverse2, gain_vals[:, 1]
+        back_project(dcq, w_cquery), standard2, inverse2, gains[1]
     )
     upstream = upstream + grad_back
     dout1 = low(upstream)
-    cross_sum = reduction(
-        [(normed2, dcq), (memory, dckv), (ccontext, dout2), (context, dout1)]
-    )
+    attn_sum = reduction([(context, dout1)])
     dcontext = by_seq(low(back_project(dout1, w_out)))
-    dcontext = after(dcontext, *cross_sum.sends)
+    cross_sum.step()
+    crossing = cross_sum.step()
+    dcontext = after(dcontext, cross_sum.keep, *attn_sum.sends)
     dqkv = flat(self_backward(qkv, probs, dcontext))
-    dqkv = after(dqkv, *arriving, *cross_sum.step())
     in_sum.step(dqkv)
-    in_sum.step()
-    in_sum.step()
-    attn_sum = reduction([(normed1, dqkv)])
+    attn_sum.add(normed1, dqkv)
     grad_back, g_gain1, g_shift1 = norm_backward(
-        back_project(after(dqkv, *attn_sum.sends), w_qkv),
+        back_project(after(dqkv, *attn_sum.sends, *crossing), w_qkv),
         standard1,
         inverse1,
-        gain_vals[:, 0],
+        gains[0],
     )
     input_grad = by_seq(upstream + grad_back)
     small_sums = jnp.stack(
@@ -639,19 +639,23 @@
     attn_sum.add(low(sums), picks)
     attn_sum.step()
     cross_sum.step()
-    cross_sum.step()
-    arrived = attn_sum.step(cross_sum.half)
     attn_sum.step()
-    memory_grad = back_project(after(dckv, *arrived), w_ckv)
+    attn_sum.step()
+    in_sum.step()
+    in_sum.step(attn_sum.keep)
+    cross_sum.step(attn_sum.keep)
+    cross_sum.step(attn_sum.half)
+    mlp_out_grad = after(mlp_out_sum, attn_sum.half).astype(jnp.float32)
+    attn_sum.step(mlp_out_grad)
+    cross_sum.last = after(cross_sum.last, attn_sum.got_first)
+    memory_grad = back_project(after(dckv, attn_sum.got_first), w_ckv)
     attn_sum.step(memory_grad)
-    attn_sum.step()
-    late = after(activated, attn_sum.got_first)
-    layer_out = by_seq(low(stream2 + project(late, w_down) + bias_vals[:, 3]))
-    mlp_out_grad = after(mlp_out_sum, attn_sum.got_first).astype(jnp.float32)
-    attn_sum.own = after(attn_sum.own, layer_out, mlp_out_grad)
+    late = after(activated, attn_sum.turn)
+    layer_out = by_seq(low(stream2 + project(late, w_down) + biases[3]))
+    attn_sum.own = after(attn_sum.own, layer_out)
     (mlp_in_grad,) = in_sum.results()
-    cross_query_grad, cross_kv_grad, cross_out_grad, attn_out_grad = cross_sum.results()
-    attn_in_grad, small_grad = attn_sum.results()
+    cross_query_grad, cross_kv_grad, cross_out_grad = cross_sum.results()
+    attn_out_grad, attn_in_grad, small_grad = attn_sum.results()
     return (
         layer_out,
         input_grad,

time: 355 us -> 343 us (0.966)
  other arithmetic: 39.3 us -> 33.6 us
  waiting for transfers between devices: 79.1 us -> 74.3 us
    ppermute x49, waiting for transfers between devices: 79 us -> 74.3 us  [move(): return lax.ppermute(value, AXES, perm)]
    convert_element_type x7 -> x3, other arithmetic: 6.62 us -> 2.71 us  [the longest x1 1.64 us: local(): mlp_out_grad = after(mlp_out_sum, attn_sum.half).astype(jnp.float32)]
    slice x6, local copies, waits for them, and re-layouts: 3.33 us -> 7.22 us  [plane(): return pick(self.keep[:, 0]) + pick(self.got[:, 0]) + pick(self.got_first)]
    unnamed x104 -> x107, local copies, waits for them, and re-layouts: 8.86 us -> 8.53 us
  transfers between devices with their start and end apart: 51 -> 51, of which waited for: 17 -> 19; matrix products, arithmetic and copies ran while one was open for 37% -> 35% of each run, Pallas kernels for 16% -> 17%
where the time goes in v5:
time: 343 us; the launch traced here: 339 us
  matrix products  85.3 us (25%)
  waiting for transfers between devices  74.3 us (22%)
  Pallas kernels  63.1 us (18%)
  starting transfers between devices  45.2 us (13%)
  other arithmetic  33.6 us (10%)
  local copies, waits for them, and re-layouts  22.1 us (6%)
  between operations  15.3 us (4%)
    ppermute x49, waiting for transfers between devices, move(): return lax.ppermute(value, AXES, perm)  74.3 us
    ppermute x49, starting transfers between devices, move(): return lax.ppermute(value, AXES, perm)  45.1 us
    dot_general x15, matrix products, contract_low(): lax.dot_general(value, upstream_gradient, ((over, over), ((), ())), prefe...  35.6 us
    pallas_call x4, Pallas kernels, per_sequence(): pl.pallas_call(body, out_shape=outs, grid_spec=pltpu.PrefetchScalarGridSp...  32.1 us
    dot_general x7, matrix products, back_project(): jnp.einsum('...j,aj->...a', upstream_gradient, weight_matrix, preferred_e...  26.1 us
    dot_general x7, matrix products, project(): jnp.einsum('...h,ht->...t', value_tensor, weight_matrix, preferred_elemen...  22.4 us
    pallas_call x3, Pallas kernels, assemble(): pl.pallas_call(functools.partial(assemble_body, widths), out_shape=[jax.S...  17.1 us
    pallas_call x3, Pallas kernels, split_add(): pl.pallas_call(functools.partial(split_body, len(pairs)), out_shape=[shap...  13.9 us
  transfers between devices with their start and end apart: 51, of which 19 were waited for; matrix products, arithmetic and copies ran while one was open for 35% of the time, Pallas kernels for 17%

profile of v5, /device:TPU:0, one launch (start us, length us, event | category | flops | bytes accessed | tf_op | source)
XLA Modules:
  0.0 339.0 jit_solution(17967145265818350129)
XLA Ops:
  12.4 4.1 %collective-permute-start = (bf16[24,2560]{1,0:T(8,128)(2,1)S(1)}, bf16[24,2560]{1,0:T(8,128)(2,1)S(1)}, u32[]{:S(2)}, u32[]{:S(2)}) collective-permute-start(bf16[24,2560]{1,0:T(8,128)(2,1)S(1)} %concatenate.40), channel_id=1, source_target_pairs={{0,16},{1,17},{2,18},{3,19},{4,20},{5,21},{6,22},{7,23},{8,24},{9,... | collective-permute-start | bytes 368648 | tf_op jit(solution)/shard_map/ppermute | solution.py:235
  17.4 5.1 %collective-permute-done = bf16[24,2560]{1,0:T(8,128)(2,1)S(1)} collective-permute-done((bf16[24,2560]{1,0:T(8,128)(2,1)S(1)}, bf16[24,2560]{1,0:T(8,128)(2,1)S(1)}, u32[]{:S(2)}, u32[]{:S(2)}) %collective-permute-start) | collective-permute-done | bytes 122912 | tf_op jit(solution)/shard_map/ppermute | solution.py:235
  23.5 8.7 %collective-permute-done.1 = bf16[2,24,2560]{2,1,0:T(8,128)(2,1)S(1)} collective-permute-done((bf16[2,24,2560]{2,1,0:T(8,128)(2,1)S(1)}, bf16[2,24,2560]{2,1,0:T(8,128)(2,1)S(1)}, u32[]{:S(2)}, u32[]{:S(2)}) %collective-permute-start.1) | collective-permute-done | bytes 245792 | tf_op jit(solution)/shard_map/ppermute | solution.py:235
  36.0 4.6 %collective-permute-start.9 = (bf16[24,3072]{1,0:T(8,128)(2,1)S(1)}, bf16[24,3072]{1,0:T(8,128)(2,1)S(1)}, u32[]{:S(2)}, u32[]{:S(2)}) collective-permute-start(bf16[24,3072]{1,0:T(8,128)(2,1)S(1)} %copy-done.33), channel_id=1, source_target_pairs={{0,16},{1,17},{2,18},{3,19},{4,20},{5,21},{6,22},{7,23},{8,24},{9,... | collective-permute-start | bytes 442376 | tf_op jit(solution)/shard_map/ppermute | solution.py:235
  40.6 8.2 %collective-permute-done.2.refs_1_ = bf16[4,24,2560]{2,1,0:T(8,128)(2,1)} collective-permute-done((bf16[4,24,2560]{2,1,0:T(8,128)(2,1)S(1)}, bf16[4,24,2560]{2,1,0:T(8,128)(2,1)}, u32[]{:S(2)}, u32[]{:S(2)}) %collective-permute-start.2) | collective-permute-done | bytes 491552 | tf_op jit(solution)/shard_map/ppermute | solution.py:235
  51.5 3.0 collective-permute-start.10
  55.0 2.9 collective-permute-done.4.refs_3_
  58.5 6.2 %collective-permute-done.10 = bf16[2,24,3072]{2,1,0:T(8,128)(2,1)} collective-permute-done((bf16[2,24,3072]{2,1,0:T(8,128)(2,1)}, bf16[2,24,3072]{2,1,0:T(8,128)(2,1)}, u32[]{:S(2)}, u32[]{:S(2)}) %collective-permute-start.10) | collective-permute-done | bytes 294944 | tf_op jit(solution)/shard_map/ppermute | solution.py:235
  69.3 5.6 %assemble.3 = (bf16[4,2,2,2,24,2304]{5,4,3,2,1,0:T(8,128)(2,1)}, bf16[4,2,2,2,24,256]{5,4,3,2,1,0:T(8,128)(2,1)}) custom-call(s32[4]{0:T(128)} %pad_add_fusion.spot, bf16[4,24,2560]{2,1,0:T(8,128)(2,1)} %copy-done.18, bf16[4,24,2560]{2,1,0:T(8,128)(2,1)} %collective-permute-done.2.refs_1_, bf16[4,24,2560]{2,1,0:T(8,128)(2,1)} %collective-permute-done.3.refs_2_, ...), custom_call_target="tpu_custom_call" | custom-call | tf_op jit(solution)/shard_map/assemble/pallas_call | solution.py:267
  74.8 2.9 collective-permute-start.18
  79.4 4.8 %convolution_convert_fusion.1 = bf16[384,2304]{1,0:T(8,128)(2,1)} fusion(bf16[384,768]{1,0:T(8,128)(2,1)S(1)} %bitcast.256, bf16[768,2304]{1,0:T(8,128)(2,1)} %bitcast.261), kind=kOutput, calls=%fused_computation.12 | convolution fusion | flops 1359839232 | bytes 5898240 | tf_op jit(solution)/shard_map/...h,ht->...t/dot_general | solution.py:38
  84.2 9.0 %self_forward.1 = (bf16[4,96,768]{2,1,0:T(8,128)(2,1)}, bf16[4,6,96,192]{3,2,1,0:T(8,128)(2,1)}) custom-call(s32[4]{0:T(128)} %lens.1, bf16[4,96,2304]{2,1,0:T(8,128)(2,1)} %bitcast.212), custom_call_target="tpu_custom_call" | custom-call | tf_op jit(solution)/shard_map/self_forward/pallas_call | solution.py:163
  98.4 3.6 %collective-permute-done.19 = bf16[2,96,768]{2,1,0:T(8,128)(2,1)S(1)} collective-permute-done((bf16[2,96,768]{2,1,0:T(8,128)(2,1)S(1)}, bf16[2,96,768]{2,1,0:T(8,128)(2,1)S(1)}, u32[]{:S(2)}, u32[]{:S(2)}) %collective-permute-start.19) | collective-permute-done | bytes 294944 | tf_op jit(solution)/shard_map/ppermute | solution.py:235
  103.4 2.3 fusion.79
  109.1 3.6 %fusion.7.kv = bf16[4,196,1536]{2,1,0:T(8,128)(2,1)} fusion(bf16[768,3840]{1,0:T(8,128)(2,1)S(1)} %copy-done.38, bf16[4,196,768]{2,0,1:T(4,128)(2,1)S(1)} %copy-done), kind=kOutput, calls=%fused_computation.18 | convolution fusion | flops 1850892288 | bytes 5971968 | tf_op jit(solution)/shard_map/...h,ht->...t/dot_general | solution.py:38
  112.7 6.5 %cross_forward.1 = (bf16[4,96,768]{2,1,0:T(8,128)(2,1)}, bf16[4,6,196,192]{3,2,1,0:T(8,128)(2,1)}) custom-call(bf16[4,96,768]{2,1,0:T(8,128)(2,1)} %bitcast.230, bf16[4,196,1536]{2,1,0:T(8,128)(2,1)} %fusion.7.kv), custom_call_target="tpu_custom_call" | custom-call | tf_op jit(solution)/shard_map/cross_forward/pallas_call | solution.py:163
  120.4 5.7 %assemble.4 = bf16[4,2,2,2,24,3072]{5,4,3,2,1,0:T(8,128)(2,1)} custom-call(s32[4]{0:T(128)} %pad_add_fusion.spot, bf16[4,24,3072]{2,1,0:T(8,128)(2,1)} %pad_maximum_fusion.refs_0_, bf16[4,24,3072]{2,1,0:T(8,128)(2,1)} %collective-permute-done.11.refs_1_, bf16[4,24,3072]{2,1,0:T(8,128)(2,1)} %collective-permute-done.12.refs_2_, ...), custom_call_target="tpu_custom_call" | custom-call | tf_op jit(solution)/shard_map/assemble/pallas_call | solution.py:267
  126.2 2.3 fusion.80
  131.2 7.6 %collective-permute-done.22.refs_3_ = bf16[4,96,768]{2,1,0:T(8,128)(2,1)} collective-permute-done((bf16[4,96,768]{2,1,0:T(8,128)(2,1)}, bf16[4,96,768]{2,1,0:T(8,128)(2,1)}, u32[]{:S(2)}, u32[]{:S(2)}) %collective-permute-start.22) | collective-permute-done | bytes 589856 | tf_op jit(solution)/shard_map/ppermute | solution.py:235
  138.8 5.2 %multiply_convert_fusion = (bf16[384,3072]{1,0:T(8,128)(2,1)S(1)}, f32[384,3072]{1,0:T(8,128)}) fusion(f32[3072]{0:T(1024)S(1)} %add.462, bf16[768,3072]{1,0:T(8,128)(2,1)S(1)} %bitcast.221, f32[384,768]{1,0:T(8,128)S(1)} %get-tuple-element.219, f32[768]{0:T(1024)S(1)} %get-tuple-element.182, f32[768]{0:T(1024)S(1)} %get-tuple-element.183, ...), kind=kOutput, calls=%fused_computation.10 | convolution fusion | flops 1825210368 | bytes 12997632 | tf_op jit(solution)/shard_map/...h,ht->...t/dot_general | solution.py:38
  145.4 4.5 %convolution_convert_fusion = bf16[3072,768]{1,0:T(8,128)(2,1)} fusion(bf16[384,3072]{1,0:T(8,128)(2,1)S(1)} %get-tuple-element.110, bf16[384,768]{1,0:T(8,128)(2,1)S(1)} %copy-done.32), kind=kOutput, calls=%fused_computation.2 | convolution fusion | flops 1814298624 | bytes 7667712 | tf_op jit(solution)/shard_map/dot_general | solution.py:507
  149.9 5.8 %assemble.5 = bf16[4,2,2,2,96,768]{5,4,3,2,1,0:T(8,128)(2,1)} custom-call(s32[4]{0:T(128)} %pad_add_fusion.spot, bf16[4,96,768]{2,1,0:T(8,128)(2,1)} %pad_maximum_fusion.1.refs_0_, bf16[4,96,768]{2,1,0:T(8,128)(2,1)} %collective-permute-done.20.refs_1_, bf16[4,96,768]{2,1,0:T(8,128)(2,1)} %collective-permute-done.21.refs_2_, ...), custom_call_target="tpu_custom_call" | custom-call | tf_op jit(solution)/shard_map/assemble/pallas_call | solution.py:267
  155.7 7.2 %fusion.70 = (bf16[3072]{0:T(1024)(128)(2,1)S(1)}, bf16[384,3072]{1,0:T(8,128)(2,1)S(1)}) fusion(f32[384,3072]{1,0:T(8,128)} %get-tuple-element.221, bf16[384,768]{1,0:T(8,128)(2,1)} %bitcast.255, bf16[3072,768]{1,0:T(8,128)(2,1)} %bitcast.216), kind=kOutput, calls=%fused_computation.198 | convolution fusion | flops 1836708864 | bytes 12392448 | tf_op jit(solution)/shard_map/...j,aj->...a/dot_general | solution.py:42
  162.9 3.1 convolution_convert_fusion.6
  168.5 4.8 %convolution_convert_fusion.5 = bf16[768,1536]{1,0:T(8,128)(2,1)} fusion(bf16[384,3072]{1,0:T(8,128)(2,1)} %copy-done.47, s32[]{:T(128)S(6)} %select_n.216, f32[384,768]{1,0:T(8,128)} %copy-done.2, f32[768]{0:T(1024)S(1)} %get-tuple-element.182, f32[768]{0:T(1024)S(1)} %get-tuple-element.183, f32[384]{0:T(512)S(1)} %add_rsqrt_fusion, ...), kind=kOutput, calls=%fused_computation.16 | convolution fusion | flops 908623872 | bytes 4727812 | tf_op jit(solution)/shard_map/dot_general | solution.py:507
  173.3 5.0 %multiply_reduce_fusion.1 = (bf16[768]{0:T(1024)(128)(2,1)S(1)}, f32[384]{0:T(512)S(1)}, f32[384]{0:T(512)S(1)}, bf16[768]{0:T(1024)(128)(2,1)S(1)}, f32[384,768]{1,0:T(8,128)S(1)}) fusion(f32[384,768]{1,0:T(8,128)S(1)} %copy-done.4, f32[384]{0:T(512)S(1)} %add_rsqrt_fusion, f32[384]{0:T(512)S(1)} %broadcast_multiply_fusion.6, ...), kind=kOutput, calls=%fused_computation.49 | convolution fusion | flops 1814591232 | bytes 9449472 | tf_op jit(solution)/shard_map/...j,aj->...a/dot_general | solution.py:42
  179.8 3.0 convolution_convert_fusion.14
  182.8 4.4 %split_add.3 = (bf16[4,2,48,1536]{3,2,1,0:T(8,128)(2,1)}, bf16[4,2,48,1536]{3,2,1,0:T(8,128)(2,1)}) custom-call(s32[4]{0:T(128)} %pad_add_fusion.1.which, bf16[4,4,48,1536]{3,2,1,0:T(8,128)(2,1)} %bitcast.208, bf16[4,4,48,1536]{3,2,1,0:T(8,128)(2,1)} %bitcast.31.refs_1_.refs_3_, bf16[4,4,48,1536]{3,2,1,0:T(8,128)(2,1)} %bitcast.209, ...), custom_call_target="tpu_custom_call" | custom-call | tf_op jit(solution)/shard_map/split_add/pallas_call | solution.py:385
  187.2 8.1 %cross_backward.1 = (bf16[4,96,768]{2,1,0:T(8,128)(2,1)}, bf16[4,196,1536]{2,1,0:T(8,128)(2,1)}) custom-call(bf16[4,96,768]{2,1,0:T(8,128)(2,1)} %bitcast.231, bf16[4,196,1536]{2,1,0:T(8,128)(2,1)} %fusion.7.kv, bf16[4,6,196,192]{3,2,1,0:T(8,128)(2,1)} %get-tuple-element.92.probs, bf16[4,96,768]{2,1,0:T(8,128)(2,1)} %bitcast.246), custom_call_target="tpu_custom_call" | custom-call | tf_op jit(solution)/shard_map/cross_backward/pallas_call | solution.py:163
  195.4 3.9 %fusion.9 = bf16[768,768]{0,1:T(8,128)(2,1)} fusion(bf16[4,196,1536]{2,1,0:T(8,128)(2,1)} %get-tuple-element.108, s32[]{:T(128)S(6)} %select_n.218, bf16[4,196,768]{2,0,1:T(4,128)(2,1)S(1)} %copy-done), kind=kOutput, calls=%fused_computation.25 | convolution fusion | flops 925433856 | bytes 3612676 | tf_op jit(solution)/shard_map/dot_general | solution.py:507
  206.4 2.0 slice.197
  209.9 3.7 %bitcast_convert_fusion = bf16[768,768]{0,1:T(8,128)(2,1)} fusion(bf16[4,196,1536]{2,1,0:T(8,128)(2,1)} %get-tuple-element.108, s32[]{:T(128)S(6)} %select_n.220, bf16[4,196,768]{2,0,1:T(4,128)(2,1)S(1)} %copy-done), kind=kOutput, calls=%fused_computation.20 | convolution fusion | flops 925433856 | bytes 3612676 | tf_op jit(solution)/shard_map/dot_general | solution.py:507
  213.6 2.4 copy.76
  216.0 4.5 %split_add.4 = (bf16[4,2,48,1536]{3,2,1,0:T(8,128)(2,1)}, bf16[4,2,48,1536]{3,2,1,0:T(8,128)(2,1)}) custom-call(s32[4]{0:T(128)} %pad_add_fusion.1.which, bf16[4,4,48,384]{3,2,1,0:T(8,128)(2,1)} %bitcast.228, bf16[4,4,48,384]{3,2,1,0:T(8,128)(2,1)} %bitcast.39.refs_1_.refs_7_, bf16[4,4,48,768]{3,2,1,0:T(8,128)(2,1)} %bitcast.214, ...), custom_call_target="tpu_custom_call" | custom-call | tf_op jit(solution)/shard_map/split_add/pallas_call | solution.py:385
  221.4 2.4 multiply_reduce_fusion.2
  226.8 2.8 convolution_convert_fusion.9
  229.6 8.5 %self_backward.1 = bf16[4,96,2304]{2,1,0:T(8,128)(2,1)} custom-call(bf16[4,96,2304]{2,1,0:T(8,128)(2,1)} %bitcast.213, bf16[4,6,96,192]{3,2,1,0:T(8,128)(2,1)} %get-tuple-element.99.probs, bf16[4,96,768]{2,1,0:T(8,128)(2,1)} %bitcast.257), custom_call_target="tpu_custom_call" | custom-call | tf_op jit(solution)/shard_map/self_backward/pallas_call | solution.py:163
  241.1 3.5 %convolution_convert_fusion.3 = bf16[768,1152]{1,0:T(8,128)(2,1)} fusion(bf16[384,768]{1,0:T(8,128)(2,1)} %add_convert_fusion.3, bf16[384,2304]{1,0:T(8,128)(2,1)S(1)} %bitcast.232, s32[]{:T(128)S(6)} %select_n.222), kind=kOutput, calls=%fused_computation.14 | convolution fusion | flops 680361984 | bytes 3244036 | tf_op jit(solution)/shard_map/dot_general | solution.py:507
  246.8 2.4 convolution_convert_fusion.4
  265.7 4.9 %split_add.5 = (bf16[4,2,48,1664]{3,2,1,0:T(8,128)(2,1)}, bf16[4,2,48,1664]{3,2,1,0:T(8,128)(2,1)}) custom-call(s32[4]{0:T(128)} %pad_add_fusion.1.which, bf16[4,4,48,384]{3,2,1,0:T(8,128)(2,1)} %bitcast.224, bf16[4,4,48,384]{3,2,1,0:T(8,128)(2,1)} %bitcast.222, bf16[4,4,48,1152]{3,2,1,0:T(8,128)(2,1)} %bitcast.210, ...), custom_call_target="tpu_custom_call" | custom-call | tf_op jit(solution)/shard_map/split_add/pallas_call | solution.py:385
  274.2 8.6 %collective-permute-done.47 = bf16[48,1536]{1,0:T(8,128)(2,1)S(1)} collective-permute-done((bf16[48,1536]{1,0:T(8,128)(2,1)S(1)}, bf16[48,1536]{1,0:T(8,128)(2,1)S(1)}, u32[]{:S(2)}, u32[]{:S(2)}) %collective-permute-start.47) | collective-permute-done | bytes 147488 | tf_op jit(solution)/shard_map/ppermute | solution.py:235
  284.4 5.3 %collective-permute-done.36 = bf16[4,2,48,1664]{3,2,1,0:T(8,128)(2,1)S(1)} collective-permute-done((bf16[4,2,48,1664]{3,2,1,0:T(8,128)(2,1)}, bf16[4,2,48,1664]{3,2,1,0:T(8,128)(2,1)S(1)}, u32[]{:S(2)}, u32[]{:S(2)}) %collective-permute-start.36) | collective-permute-done | bytes 1277984 | tf_op jit(solution)/shard_map/ppermute | solution.py:235
  297.5 3.9 %collective-permute-done.37 = bf16[4,48,1664]{2,1,0:T(8,128)(2,1)} collective-permute-done((bf16[4,48,1664]{2,1,0:T(8,128)(2,1)}, bf16[4,48,1664]{2,1,0:T(8,128)(2,1)}, u32[]{:S(2)}, u32[]{:S(2)}) %collective-permute-start.37) | collective-permute-done | bytes 639008 | tf_op jit(solution)/shard_map/ppermute | solution.py:235
  305.7 3.8 %fusion.8 = f32[4,196,768]{2,1,0:T(8,128)S(1)} fusion(bf16[4,196,1536]{2,1,0:T(8,128)(2,1)S(1)} %copy-done.40, bf16[768,3840]{1,0:T(8,128)(2,1)} %all-gather.2.cloned.1.call-done), kind=kOutput, calls=%fused_computation.22 | convolution fusion | flops 1849688064 | bytes 7176192 | tf_op jit(solution)/shard_map/...j,aj->...a/dot_general | solution.py:42
  309.6 2.4 copy.78
  312.7 2.9 collective-permute-done.38
  318.3 2.8 fusion.11
  321.1 5.9 %collective-permute-done.39 = bf16[48,1664]{1,0:T(8,128)(2,1)S(1)} collective-permute-done((bf16[48,1664]{1,0:T(8,128)(2,1)S(1)}, bf16[48,1664]{1,0:T(8,128)(2,1)S(1)}, u32[]{:S(2)}, u32[]{:S(2)}) %collective-permute-start.39) | collective-permute-done | bytes 159776 | tf_op jit(solution)/shard_map/ppermute | solution.py:235
  (308 shorter events, 99.1 us)
Async XLA Ops:
  7.2 96.2 %all-gather.2.cloned.1.call-start = ((), (), s32[]{:S(2)}) async-start(), calls=%async_computation.1 | async-start | bytes 6082560 | tf_op jit(solution)/shard_map/all_gather | solution.py:545
  9.0 286.8 %reduce-scatter.2.cloned.1.call-start = ((), (), s32[]{:S(2)}) async-start(), calls=%async_computation.2 | async-start | bytes 4866048 | tf_op jit(solution)/shard_map/reduce_scatter | solution.py:399
  12.4 10.1 %collective-permute-start = (bf16[24,2560]{1,0:T(8,128)(2,1)S(1)}, bf16[24,2560]{1,0:T(8,128)(2,1)S(1)}, u32[]{:S(2)}, u32[]{:S(2)}) collective-permute-start(bf16[24,2560]{1,0:T(8,128)(2,1)S(1)} %concatenate.40), channel_id=1, source_target_pairs={{0,16},{1,17},{2,18},{3,19},{4,20},{5,21},{6,22},{7,23},{8,24},{9,... | collective-permute-start | bytes 368648 | tf_op jit(solution)/shard_map/ppermute | solution.py:235
  22.5 9.7 %collective-permute-start.1 = (bf16[2,24,2560]{2,1,0:T(8,128)(2,1)S(1)}, bf16[2,24,2560]{2,1,0:T(8,128)(2,1)S(1)}, u32[]{:S(2)}, u32[]{:S(2)}) collective-permute-start(bf16[2,24,2560]{2,1,0:T(8,128)(2,1)S(1)} %pad_maximum_fusion.9), channel_id=1, source_target_pairs={{0,8},{1,9},{2,10},{3,11},{4,12},{5,13},{6,14},{7,15},{8,0},{9,1},... | collective-permute-start | bytes 737288 | tf_op jit(solution)/shard_map/ppermute | solution.py:235
  32.3 16.5 %collective-permute-start.2 = (bf16[4,24,2560]{2,1,0:T(8,128)(2,1)S(1)}, bf16[4,24,2560]{2,1,0:T(8,128)(2,1)}, u32[]{:S(2)}, u32[]{:S(2)}) collective-permute-start(bf16[4,24,2560]{2,1,0:T(8,128)(2,1)S(1)} %pad_maximum_fusion.2.refs_0_), channel_id=1, source_target_pairs={{0,4},{1,3},{2,6},{3,1},{4,0},{5,7},{6,2},{7,5},{8,12},{9,11},{10,... | collective-permute-start | bytes 1474568 | tf_op jit(solution)/shard_map/ppermute | solution.py:235
  34.3 20.3 %collective-permute-start.3 = (bf16[4,24,2560]{2,1,0:T(8,128)(2,1)S(1)}, bf16[4,24,2560]{2,1,0:T(8,128)(2,1)}, u32[]{:S(2)}, u32[]{:S(2)}) collective-permute-start(bf16[4,24,2560]{2,1,0:T(8,128)(2,1)S(1)} %pad_maximum_fusion.2.refs_0_), channel_id=1, source_target_pairs={{0,2},{1,5},{2,0},{3,7},{4,6},{5,1},{6,4},{7,3},{8,10},{9,13},{10,... | collective-permute-start | bytes 1474568 | tf_op jit(solution)/shard_map/ppermute | solution.py:235
  36.0 14.7 %collective-permute-start.9 = (bf16[24,3072]{1,0:T(8,128)(2,1)S(1)}, bf16[24,3072]{1,0:T(8,128)(2,1)S(1)}, u32[]{:S(2)}, u32[]{:S(2)}) collective-permute-start(bf16[24,3072]{1,0:T(8,128)(2,1)S(1)} %copy-done.33), channel_id=1, source_target_pairs={{0,16},{1,17},{2,18},{3,19},{4,20},{5,21},{6,22},{7,23},{8,24},{9,... | collective-permute-start | bytes 442376 | tf_op jit(solution)/shard_map/ppermute | solution.py:235
  48.7 9.1 %collective-permute-start.4 = (bf16[4,24,2560]{2,1,0:T(8,128)(2,1)}, bf16[4,24,2560]{2,1,0:T(8,128)(2,1)}, u32[]{:S(2)}, u32[]{:S(2)}) collective-permute-start(bf16[4,24,2560]{2,1,0:T(8,128)(2,1)} %collective-permute-done.2.refs_1_), channel_id=1, source_target_pairs={{0,2},{1,5},{2,0},{3,7},{4,6},{5,1},{6,4},{7,3},{8,10},{9,13},{10,... | collective-permute-start | bytes 1474568 | tf_op jit(solution)/shard_map/ppermute | solution.py:235
  50.6 16.8 %collective-permute-start.5 = (bf16[4,24,2560]{2,1,0:T(8,128)(2,1)S(1)}, bf16[4,24,2560]{2,1,0:T(8,128)(2,1)}, u32[]{:S(2)}, u32[]{:S(2)}) collective-permute-start(bf16[4,24,2560]{2,1,0:T(8,128)(2,1)S(1)} %pad_maximum_fusion.2.refs_0_), channel_id=1, source_target_pairs={{0,1},{1,0},{2,3},{3,2},{4,5},{5,4},{6,7},{7,6},{8,9},{9,8},{10,11... | collective-permute-start | bytes 1474568 | tf_op jit(solution)/shard_map/ppermute | solution.py:235
  51.5 13.3 %collective-permute-start.10 = (bf16[2,24,3072]{2,1,0:T(8,128)(2,1)}, bf16[2,24,3072]{2,1,0:T(8,128)(2,1)}, u32[]{:S(2)}, u32[]{:S(2)}) collective-permute-start(bf16[2,24,3072]{2,1,0:T(8,128)(2,1)} %pad_maximum_fusion.4), channel_id=1, source_target_pairs={{0,8},{1,9},{2,10},{3,11},{4,12},{5,13},{6,14},{7,15},{8,0},{9,1},... | collective-permute-start | bytes 884744 | tf_op jit(solution)/shard_map/ppermute | solution.py:235
  54.5 14.8 %collective-permute-start.6 = (bf16[4,24,2560]{2,1,0:T(8,128)(2,1)}, bf16[4,24,2560]{2,1,0:T(8,128)(2,1)}, u32[]{:S(2)}, u32[]{:S(2)}) collective-permute-start(bf16[4,24,2560]{2,1,0:T(8,128)(2,1)} %collective-permute-done.2.refs_1_), channel_id=1, source_target_pairs={{0,1},{1,0},{2,3},{3,2},{4,5},{5,4},{6,7},{7,6},{8,9},{9,8},{10,11... | collective-permute-start | bytes 1474568 | tf_op jit(solution)/shard_map/ppermute | solution.py:235
  54.7 14.6 %collective-permute-start.7 = (bf16[4,24,2560]{2,1,0:T(8,128)(2,1)}, bf16[4,24,2560]{2,1,0:T(8,128)(2,1)}, u32[]{:S(2)}, u32[]{:S(2)}) collective-permute-start(bf16[4,24,2560]{2,1,0:T(8,128)(2,1)} %collective-permute-done.3.refs_2_), channel_id=1, source_target_pairs={{0,1},{1,0},{2,3},{3,2},{4,5},{5,4},{6,7},{7,6},{8,9},{9,8},{10,11... | collective-permute-start | bytes 1474568 | tf_op jit(solution)/shard_map/ppermute | solution.py:235
  57.9 11.4 %collective-permute-start.8 = (bf16[4,24,2560]{2,1,0:T(8,128)(2,1)}, bf16[4,24,2560]{2,1,0:T(8,128)(2,1)}, u32[]{:S(2)}, u32[]{:S(2)}) collective-permute-start(bf16[4,24,2560]{2,1,0:T(8,128)(2,1)} %collective-permute-done.4.refs_3_), channel_id=1, source_target_pairs={{0,1},{1,0},{2,3},{3,2},{4,5},{5,4},{6,7},{7,6},{8,9},{9,8},{10,11... | collective-permute-start | bytes 1474568 | tf_op jit(solution)/shard_map/ppermute | solution.py:235
  66.6 31.7 %collective-permute-start.12 = (bf16[4,24,3072]{2,1,0:T(8,128)(2,1)}, bf16[4,24,3072]{2,1,0:T(8,128)(2,1)}, u32[]{:S(2)}, u32[]{:S(2)}) collective-permute-start(bf16[4,24,3072]{2,1,0:T(8,128)(2,1)} %pad_maximum_fusion.refs_0_), channel_id=1, source_target_pairs={{0,2},{1,5},{2,0},{3,7},{4,6},{5,1},{6,4},{7,3},{8,10},{9,13},{10,... | collective-permute-start | bytes 1769480 | tf_op jit(solution)/shard_map/ppermute | solution.py:235
  67.4 25.8 %collective-permute-start.11 = (bf16[4,24,3072]{2,1,0:T(8,128)(2,1)}, bf16[4,24,3072]{2,1,0:T(8,128)(2,1)}, u32[]{:S(2)}, u32[]{:S(2)}) collective-permute-start(bf16[4,24,3072]{2,1,0:T(8,128)(2,1)} %pad_maximum_fusion.refs_0_), channel_id=1, source_target_pairs={{0,4},{1,3},{2,6},{3,1},{4,0},{5,7},{6,2},{7,5},{8,12},{9,11},{10,... | collective-permute-start | bytes 1769480 | tf_op jit(solution)/shard_map/ppermute | solution.py:235
  74.8 20.1 %collective-permute-start.18 = (bf16[96,768]{1,0:T(8,128)(2,1)S(1)}, bf16[96,768]{1,0:T(8,128)(2,1)S(1)}, u32[]{:S(2)}, u32[]{:S(2)}) collective-permute-start(bf16[96,768]{1,0:T(8,128)(2,1)S(1)} %copy-done.34), channel_id=1, source_target_pairs={{0,16},{1,17},{2,18},{3,19},{4,20},{5,21},{6,22},{7,23},{8,24},{9,... | collective-permute-start | bytes 442376 | tf_op jit(solution)/shard_map/ppermute | solution.py:235
  93.2 10.2 %collective-permute-start.13 = (bf16[4,24,3072]{2,1,0:T(8,128)(2,1)}, bf16[4,24,3072]{2,1,0:T(8,128)(2,1)}, u32[]{:S(2)}, u32[]{:S(2)}) collective-permute-start(bf16[4,24,3072]{2,1,0:T(8,128)(2,1)} %collective-permute-done.11.refs_1_), channel_id=1, source_target_pairs={{0,2},{1,5},{2,0},{3,7},{4,6},{5,1},{6,4},{7,3},{8,10},{9,13},{10,... | collective-permute-start | bytes 1769480 | tf_op jit(solution)/shard_map/ppermute | solution.py:235
  95.0 7.0 %collective-permute-start.19 = (bf16[2,96,768]{2,1,0:T(8,128)(2,1)S(1)}, bf16[2,96,768]{2,1,0:T(8,128)(2,1)S(1)}, u32[]{:S(2)}, u32[]{:S(2)}) collective-permute-start(bf16[2,96,768]{2,1,0:T(8,128)(2,1)S(1)} %pad_maximum_fusion.5), channel_id=1, source_target_pairs={{0,8},{1,9},{2,10},{3,11},{4,12},{5,13},{6,14},{7,15},{8,0},{9,1},... | collective-permute-start | bytes 884744 | tf_op jit(solution)/shard_map/ppermute | solution.py:235
  97.3 21.9 %collective-permute-start.14 = (bf16[4,24,3072]{2,1,0:T(8,128)(2,1)}, bf16[4,24,3072]{2,1,0:T(8,128)(2,1)}, u32[]{:S(2)}, u32[]{:S(2)}) collective-permute-start(bf16[4,24,3072]{2,1,0:T(8,128)(2,1)} %pad_maximum_fusion.refs_0_), channel_id=1, source_target_pairs={{0,1},{1,0},{2,3},{3,2},{4,5},{5,4},{6,7},{7,6},{8,9},{9,8},{10,11... | collective-permute-start | bytes 1769480 | tf_op jit(solution)/shard_map/ppermute | solution.py:235
  97.7 22.7 %collective-permute-start.15 = (bf16[4,24,3072]{2,1,0:T(8,128)(2,1)}, bf16[4,24,3072]{2,1,0:T(8,128)(2,1)}, u32[]{:S(2)}, u32[]{:S(2)}) collective-permute-start(bf16[4,24,3072]{2,1,0:T(8,128)(2,1)} %collective-permute-done.11.refs_1_), channel_id=1, source_target_pairs={{0,1},{1,0},{2,3},{3,2},{4,5},{5,4},{6,7},{7,6},{8,9},{9,8},{10,11... | collective-permute-start | bytes 1769480 | tf_op jit(solution)/shard_map/ppermute | solution.py:235
  98.3 21.8 %collective-permute-start.16 = (bf16[4,24,3072]{2,1,0:T(8,128)(2,1)}, bf16[4,24,3072]{2,1,0:T(8,128)(2,1)}, u32[]{:S(2)}, u32[]{:S(2)}) collective-permute-start(bf16[4,24,3072]{2,1,0:T(8,128)(2,1)} %collective-permute-done.12.refs_2_), channel_id=1, source_target_pairs={{0,1},{1,0},{2,3},{3,2},{4,5},{5,4},{6,7},{7,6},{8,9},{9,8},{10,11... | collective-permute-start | bytes 1769480 | tf_op jit(solution)/shard_map/ppermute | solution.py:235
  103.4 17.1 %collective-permute-start.17 = (bf16[4,24,3072]{2,1,0:T(8,128)(2,1)}, bf16[4,24,3072]{2,1,0:T(8,128)(2,1)}, u32[]{:S(2)}, u32[]{:S(2)}) collective-permute-start(bf16[4,24,3072]{2,1,0:T(8,128)(2,1)} %collective-permute-done.13.refs_3_), channel_id=1, source_target_pairs={{0,1},{1,0},{2,3},{3,2},{4,5},{5,4},{6,7},{7,6},{8,9},{9,8},{10,11... | collective-permute-start | bytes 1769480 | tf_op jit(solution)/shard_map/ppermute | solution.py:235
  108.0 20.5 %collective-permute-start.20 = (bf16[4,96,768]{2,1,0:T(8,128)(2,1)}, bf16[4,96,768]{2,1,0:T(8,128)(2,1)}, u32[]{:S(2)}, u32[]{:S(2)}) collective-permute-start(bf16[4,96,768]{2,1,0:T(8,128)(2,1)} %pad_maximum_fusion.1.refs_0_), channel_id=1, source_target_pairs={{0,4},{1,3},{2,6},{3,1},{4,0},{5,7},{6,2},{7,5},{8,12},{9,11},{10,... | collective-permute-start | bytes 1769480 | tf_op jit(solution)/shard_map/ppermute | solution.py:235
  119.2 30.7 %collective-permute-start.23 = (bf16[4,96,768]{2,1,0:T(8,128)(2,1)}, bf16[4,96,768]{2,1,0:T(8,128)(2,1)}, u32[]{:S(2)}, u32[]{:S(2)}) collective-permute-start(bf16[4,96,768]{2,1,0:T(8,128)(2,1)} %pad_maximum_fusion.1.refs_0_), channel_id=1, source_target_pairs={{0,1},{1,0},{2,3},{3,2},{4,5},{5,4},{6,7},{7,6},{8,9},{9,8},{10,11... | collective-permute-start | bytes 1769480 | tf_op jit(solution)/shard_map/ppermute | solution.py:235
  120.1 10.5 %collective-permute-start.21 = (bf16[4,96,768]{2,1,0:T(8,128)(2,1)}, bf16[4,96,768]{2,1,0:T(8,128)(2,1)}, u32[]{:S(2)}, u32[]{:S(2)}) collective-permute-start(bf16[4,96,768]{2,1,0:T(8,128)(2,1)} %pad_maximum_fusion.1.refs_0_), channel_id=1, source_target_pairs={{0,2},{1,5},{2,0},{3,7},{4,6},{5,1},{6,4},{7,3},{8,10},{9,13},{10,... | collective-permute-start | bytes 1769480 | tf_op jit(solution)/shard_map/ppermute | solution.py:235
  128.5 10.3 %collective-permute-start.22 = (bf16[4,96,768]{2,1,0:T(8,128)(2,1)}, bf16[4,96,768]{2,1,0:T(8,128)(2,1)}, u32[]{:S(2)}, u32[]{:S(2)}) collective-permute-start(bf16[4,96,768]{2,1,0:T(8,128)(2,1)} %collective-permute-done.20.refs_1_), channel_id=1, source_target_pairs={{0,2},{1,5},{2,0},{3,7},{4,6},{5,1},{6,4},{7,3},{8,10},{9,13},{10,... | collective-permute-start | bytes 1769480 | tf_op jit(solution)/shard_map/ppermute | solution.py:235
  130.6 19.3 %collective-permute-start.24 = (bf16[4,96,768]{2,1,0:T(8,128)(2,1)}, bf16[4,96,768]{2,1,0:T(8,128)(2,1)}, u32[]{:S(2)}, u32[]{:S(2)}) collective-permute-start(bf16[4,96,768]{2,1,0:T(8,128)(2,1)} %collective-permute-done.20.refs_1_), channel_id=1, source_target_pairs={{0,1},{1,0},{2,3},{3,2},{4,5},{5,4},{6,7},{7,6},{8,9},{9,8},{10,11... | collective-permute-start | bytes 1769480 | tf_op jit(solution)/shard_map/ppermute | solution.py:235
  130.7 19.2 %collective-permute-start.25 = (bf16[4,96,768]{2,1,0:T(8,128)(2,1)}, bf16[4,96,768]{2,1,0:T(8,128)(2,1)}, u32[]{:S(2)}, u32[]{:S(2)}) collective-permute-start(bf16[4,96,768]{2,1,0:T(8,128)(2,1)} %collective-permute-done.21.refs_2_), channel_id=1, source_target_pairs={{0,1},{1,0},{2,3},{3,2},{4,5},{5,4},{6,7},{7,6},{8,9},{9,8},{10,11... | collective-permute-start | bytes 1769480 | tf_op jit(solution)/shard_map/ppermute | solution.py:235
  138.8 11.2 %collective-permute-start.26 = (bf16[4,96,768]{2,1,0:T(8,128)(2,1)}, bf16[4,96,768]{2,1,0:T(8,128)(2,1)}, u32[]{:S(2)}, u32[]{:S(2)}) collective-permute-start(bf16[4,96,768]{2,1,0:T(8,128)(2,1)} %collective-permute-done.22.refs_3_), channel_id=1, source_target_pairs={{0,1},{1,0},{2,3},{3,2},{4,5},{5,4},{6,7},{7,6},{8,9},{9,8},{10,11... | collective-permute-start | bytes 1769480 | tf_op jit(solution)/shard_map/ppermute | solution.py:235
  166.0 16.8 %collective-permute-start.27 = (bf16[768,1536]{1,0:T(8,128)(2,1)}, bf16[768,1536]{1,0:T(8,128)(2,1)}, u32[]{:S(2)}, u32[]{:S(2)}) collective-permute-start(bf16[768,1536]{1,0:T(8,128)(2,1)} %convolution_convert_fusion.6), channel_id=1, source_target_pairs={{0,1},{1,0},{2,3},{3,2},{4,5},{5,4},{6,7},{7,6},{8,9},{9,8},{10,11... | collective-permute-start | bytes 7077896 | tf_op jit(solution)/shard_map/ppermute | solution.py:235
  199.3 14.3 %collective-permute-start.31 = (bf16[768,768]{0,1:T(8,128)(2,1)}, bf16[768,768]{0,1:T(8,128)(2,1)}, u32[]{:S(2)}, u32[]{:S(2)}) collective-permute-start(bf16[768,768]{0,1:T(8,128)(2,1)} %fusion.9), channel_id=1, source_target_pairs={{0,1},{1,0},{2,3},{3,2},{4,5},{5,4},{6,7},{7,6},{8,9},{9,8},{10,11... | collective-permute-start | bytes 3538952 | tf_op jit(solution)/shard_map/ppermute | solution.py:235
  199.3 22.2 %collective-permute-start.28 = (bf16[4,2,48,1536]{3,2,1,0:T(8,128)(2,1)}, bf16[4,2,48,1536]{3,2,1,0:T(8,128)(2,1)}, u32[]{:S(2)}, u32[]{:S(2)}) collective-permute-start(bf16[4,2,48,1536]{3,2,1,0:T(8,128)(2,1)} %get-tuple-element.96), channel_id=1, source_target_pairs={{0,2},{1,5},{2,0},{3,7},{4,6},{5,1},{6,4},{7,3},{8,10},{9,13},{10,... | collective-permute-start | bytes 3538952 | tf_op jit(solution)/shard_map/ppermute | solution.py:235
  202.5 13.5 %collective-permute-start.32 = (bf16[768,384]{1,0:T(8,128)(2,1)}, bf16[768,384]{1,0:T(8,128)(2,1)}, u32[]{:S(2)}, u32[]{:S(2)}) collective-permute-start(bf16[768,384]{1,0:T(8,128)(2,1)} %convolution_convert_fusion.12), channel_id=1, source_target_pairs={{0,1},{1,0},{2,3},{3,2},{4,5},{5,4},{6,7},{7,6},{8,9},{9,8},{10,11... | collective-permute-start | bytes 1769480 | tf_op jit(solution)/shard_map/ppermute | solution.py:235
  203.9 12.1 %collective-permute-start.30 = (bf16[768,384]{1,0:T(8,128)(2,1)}, bf16[768,384]{1,0:T(8,128)(2,1)}, u32[]{:S(2)}, u32[]{:S(2)}) collective-permute-start(bf16[768,384]{1,0:T(8,128)(2,1)} %convolution_convert_fusion.13), channel_id=1, source_target_pairs={{0,1},{1,0},{2,3},{3,2},{4,5},{5,4},{6,7},{7,6},{8,9},{9,8},{10,11... | collective-permute-start | bytes 1769480 | tf_op jit(solution)/shard_map/ppermute | solution.py:235
  220.5 33.3 %collective-permute-start.34 = (bf16[4,2,48,1536]{3,2,1,0:T(8,128)(2,1)}, bf16[4,2,48,1536]{3,2,1,0:T(8,128)(2,1)}, u32[]{:S(2)}, u32[]{:S(2)}) collective-permute-start(bf16[4,2,48,1536]{3,2,1,0:T(8,128)(2,1)} %get-tuple-element.102), channel_id=1, source_target_pairs={{0,2},{1,5},{2,0},{3,7},{4,6},{5,1},{6,4},{7,3},{8,10},{9,13},{10,... | collective-permute-start | bytes 3538952 | tf_op jit(solution)/shard_map/ppermute | solution.py:235
  239.6 12.1 %collective-permute-start.45 = (bf16[4,48,1536]{2,1,0:T(8,128)(2,1)S(1)}, bf16[4,48,1536]{2,1,0:T(8,128)(2,1)S(1)}, u32[]{:S(2)}, u32[]{:S(2)}) collective-permute-start(bf16[4,48,1536]{2,1,0:T(8,128)(2,1)S(1)} %fusion.31), channel_id=1, source_target_pairs={{0,4},{1,3},{2,6},{3,1},{4,0},{5,7},{6,2},{7,5},{8,12},{9,11},{10,... | collective-permute-start | bytes 1769480 | tf_op jit(solution)/shard_map/ppermute | solution.py:235
  246.7 18.1 %collective-permute-start.29 = (bf16[768,384]{1,0:T(8,128)(2,1)}, bf16[768,384]{1,0:T(8,128)(2,1)S(1)}, u32[]{:S(2)}, u32[]{:S(2)}) collective-permute-start(bf16[768,384]{1,0:T(8,128)(2,1)} %convolution_convert_fusion.10), channel_id=1, source_target_pairs={{0,1},{1,0},{2,3},{3,2},{4,5},{5,4},{6,7},{7,6},{8,9},{9,8},{10,11... | collective-permute-start | bytes 1769480 | tf_op jit(solution)/shard_map/ppermute | solution.py:235
  250.6 14.3 %collective-permute-start.33 = (bf16[768,1152]{1,0:T(8,128)(2,1)}, bf16[768,1152]{1,0:T(8,128)(2,1)}, u32[]{:S(2)}, u32[]{:S(2)}) collective-permute-start(bf16[768,1152]{1,0:T(8,128)(2,1)} %convolution_convert_fusion.3), channel_id=1, source_target_pairs={{0,1},{1,0},{2,3},{3,2},{4,5},{5,4},{6,7},{7,6},{8,9},{9,8},{10,11... | collective-permute-start | bytes 5308424 | tf_op jit(solution)/shard_map/ppermute | solution.py:235
  252.5 19.3 %collective-permute-start.46 = (bf16[2,48,1536]{2,1,0:T(8,128)(2,1)}, bf16[2,48,1536]{2,1,0:T(8,128)(2,1)S(1)}, u32[]{:S(2)}, u32[]{:S(2)}) collective-permute-start(bf16[2,48,1536]{2,1,0:T(8,128)(2,1)} %pad_maximum_fusion.7), channel_id=1, source_target_pairs={{0,8},{1,9},{2,10},{3,11},{4,12},{5,13},{6,14},{7,15},{8,0},{9,1},... | collective-permute-start | bytes 884744 | tf_op jit(solution)/shard_map/ppermute | solution.py:235
  255.8 16.0 %collective-permute-start.41 = (bf16[4,48,1536]{2,1,0:T(8,128)(2,1)}, bf16[4,48,1536]{2,1,0:T(8,128)(2,1)}, u32[]{:S(2)}, u32[]{:S(2)}) collective-permute-start(bf16[4,48,1536]{2,1,0:T(8,128)(2,1)} %fusion.30), channel_id=1, source_target_pairs={{0,4},{1,3},{2,6},{3,1},{4,0},{5,7},{6,2},{7,5},{8,12},{9,11},{10,... | collective-permute-start | bytes 1769480 | tf_op jit(solution)/shard_map/ppermute | solution.py:235
  272.1 10.7 %collective-permute-start.47 = (bf16[48,1536]{1,0:T(8,128)(2,1)S(1)}, bf16[48,1536]{1,0:T(8,128)(2,1)S(1)}, u32[]{:S(2)}, u32[]{:S(2)}) collective-permute-start(bf16[48,1536]{1,0:T(8,128)(2,1)S(1)} %fusion.38), channel_id=1, source_target_pairs={{0,16},{1,17},{2,18},{3,19},{4,20},{5,21},{6,22},{7,23},{8,24},{9,... | collective-permute-start | bytes 442376 | tf_op jit(solution)/shard_map/ppermute | solution.py:235
  272.2 17.5 %collective-permute-start.36 = (bf16[4,2,48,1664]{3,2,1,0:T(8,128)(2,1)}, bf16[4,2,48,1664]{3,2,1,0:T(8,128)(2,1)S(1)}, u32[]{:S(2)}, u32[]{:S(2)}) collective-permute-start(bf16[4,2,48,1664]{3,2,1,0:T(8,128)(2,1)} %get-tuple-element.105), channel_id=1, source_target_pairs={{0,2},{1,5},{2,0},{3,7},{4,6},{5,1},{6,4},{7,3},{8,10},{9,13},{10,... | collective-permute-start | bytes 3833864 | tf_op jit(solution)/shard_map/ppermute | solution.py:235
  283.0 9.5 %collective-permute-start.42 = (bf16[2,48,1536]{2,1,0:T(8,128)(2,1)S(1)}, bf16[2,48,1536]{2,1,0:T(8,128)(2,1)S(1)}, u32[]{:S(2)}, u32[]{:S(2)}) collective-permute-start(bf16[2,48,1536]{2,1,0:T(8,128)(2,1)S(1)} %pad_maximum_fusion.6), channel_id=1, source_target_pairs={{0,8},{1,9},{2,10},{3,11},{4,12},{5,13},{6,14},{7,15},{8,0},{9,1},... | collective-permute-start | bytes 884744 | tf_op jit(solution)/shard_map/ppermute | solution.py:235
  290.7 10.7 %collective-permute-start.37 = (bf16[4,48,1664]{2,1,0:T(8,128)(2,1)}, bf16[4,48,1664]{2,1,0:T(8,128)(2,1)}, u32[]{:S(2)}, u32[]{:S(2)}) collective-permute-start(bf16[4,48,1664]{2,1,0:T(8,128)(2,1)} %fusion.29), channel_id=1, source_target_pairs={{0,4},{1,3},{2,6},{3,1},{4,0},{5,7},{6,2},{7,5},{8,12},{9,11},{10,... | collective-permute-start | bytes 1916936 | tf_op jit(solution)/shard_map/ppermute | solution.py:235
  293.6 9.5 %collective-permute-start.43 = (bf16[48,1536]{1,0:T(8,128)(2,1)S(1)}, bf16[48,1536]{1,0:T(8,128)(2,1)S(1)}, u32[]{:S(2)}, u32[]{:S(2)}) collective-permute-start(bf16[48,1536]{1,0:T(8,128)(2,1)S(1)} %fusion.42), channel_id=1, source_target_pairs={{0,16},{1,17},{2,18},{3,19},{4,20},{5,21},{6,22},{7,23},{8,24},{9,... | collective-permute-start | bytes 442376 | tf_op jit(solution)/shard_map/ppermute | solution.py:235
  304.4 7.5 %collective-permute-start.44 = (f32[24,1536]{1,0:T(8,128)S(1)}, f32[24,1536]{1,0:T(8,128)S(1)}, u32[]{:S(2)}, u32[]{:S(2)}) collective-permute-start(f32[24,1536]{1,0:T(8,128)S(1)} %constant_dynamic-slice_fusion.1), channel_id=1, source_target_pairs={{0,1},{1,0},{2,3},{3,2},{4,5},{5,4},{6,7},{7,6},{8,9},{9,8},{10,11... | collective-permute-start | bytes 442376 | tf_op jit(solution)/shard_map/ppermute | solution.py:235
  305.7 10.0 %collective-permute-start.38 = (bf16[2,48,1664]{2,1,0:T(8,128)(2,1)S(1)}, bf16[2,48,1664]{2,1,0:T(8,128)(2,1)S(1)}, u32[]{:S(2)}, u32[]{:S(2)}) collective-permute-start(bf16[2,48,1664]{2,1,0:T(8,128)(2,1)S(1)} %pad_maximum_fusion.3), channel_id=1, source_target_pairs={{0,8},{1,9},{2,10},{3,11},{4,12},{5,13},{6,14},{7,15},{8,0},{9,1},... | collective-permute-start | bytes 958472 | tf_op jit(solution)/shard_map/ppermute | solution.py:235
  317.0 10.0 %collective-permute-start.39 = (bf16[48,1664]{1,0:T(8,128)(2,1)S(1)}, bf16[48,1664]{1,0:T(8,128)(2,1)S(1)}, u32[]{:S(2)}, u32[]{:S(2)}) collective-permute-start(bf16[48,1664]{1,0:T(8,128)(2,1)S(1)} %get-tuple-element.197), channel_id=1, source_target_pairs={{0,16},{1,17},{2,18},{3,19},{4,20},{5,21},{6,22},{7,23},{8,24},{9,... | collective-permute-start | bytes 479240 | tf_op jit(solution)/shard_map/ppermute | solution.py:235
  (54 other events, 390.2 us)
Sparse Core Ops, SparseCore 0:
  11.5 84.7 all-gather.1
  168.6 113.0 reduce-scatter.1

commit v6 on v5

--- a/solution.py
+++ b/solution.py
@@ -354,7 +354,7 @@
             total = source[2 * i][...].astype(jnp.float32) + source[2 * i + 1][...].astype(
                 jnp.float32
             )
-            out[:, :, :, offset : offset + width] = total.astype(jnp.bfloat16)
+            out[0, :, :, offset : offset + width] = total[:, 0].astype(jnp.bfloat16)
             offset += width
 
 
@@ -380,8 +380,8 @@
             keep_specs.append(pl.BlockSpec(block, lambda f, which: (0, which[f], 0, 0)))
             send_specs.append(pl.BlockSpec(block, lambda f, which: (0, which[2 + f], 0, 0)))
     total = sum(keep.shape[1] for keep, _ in pairs)
-    shape = jax.ShapeDtypeStruct((4, 2, 2 * rows, total), jnp.bfloat16)
-    out_spec = pl.BlockSpec((4, 1, 2 * rows, total), lambda f, which: (0, f, 0, 0))
+    shape = jax.ShapeDtypeStruct((2, 4, 2 * rows, total), jnp.bfloat16)
+    out_spec = pl.BlockSpec((1, 4, 2 * rows, total), lambda f, which: (f, 0, 0, 0))
     return pl.pallas_call(
         functools.partial(split_body, len(pairs)),
         out_shape=[shape, shape],
@@ -431,7 +431,7 @@
     def hop3(self, *earlier):
         f32 = jnp.float32
         self.got = after(self.got, *earlier)
-        total = self.keep[:, 1].astype(f32) + self.got[:, 1].astype(f32)
+        total = self.keep[1].astype(f32) + self.got[1].astype(f32)
         self.half = total.astype(jnp.bfloat16)
         self.got_first = move(self.half, FIRST)
         return [self.got_first]
@@ -443,8 +443,9 @@
 
         def plane(k):
             at = z ^ k
-            pick = lambda v: lax.dynamic_index_in_dim(v, at, 0, keepdims=False).astype(f32)
-            return pick(self.keep[:, 0]) + pick(self.got[:, 0]) + pick(self.got_first)
+            pick = lambda v: lax.dynamic_slice(v, (0, at, 0, 0), (1, 1) + v.shape[2:])[0, 0]
+            first = lax.dynamic_index_in_dim(self.got_first, at, 0, keepdims=False)
+            return pick(self.keep).astype(f32) + pick(self.got).astype(f32) + first.astype(f32)
 
         self.own, self.far = plane(0), plane(2)
         self.near = move(jnp.stack([plane(1), plane(3)]).astype(jnp.bfloat16), ZNEAR)
@@ -647,9 +648,10 @@
     cross_sum.step(attn_sum.half)
     mlp_out_grad = after(mlp_out_sum, attn_sum.half).astype(jnp.float32)
     attn_sum.step(mlp_out_grad)
-    cross_sum.last = after(cross_sum.last, attn_sum.got_first)
     memory_grad = back_project(after(dckv, attn_sum.got_first), w_ckv)
     attn_sum.step(memory_grad)
+    cross_sum.last = after(cross_sum.last, attn_sum.turn)
+    in_sum.last = after(in_sum.last, attn_sum.half)
     late = after(activated, attn_sum.turn)
     layer_out = by_seq(low(stream2 + project(late, w_down) + biases[3]))
     attn_sum.own = after(attn_sum.own, layer_out)

time: 343 us -> 337 us (0.983)
  local copies, waits for them, and re-layouts: 22.1 us -> 14.4 us
  other arithmetic: 33.6 us -> 40.8 us
  waiting for transfers between devices: 74.3 us -> 67.6 us
    slice x6 -> x0, local copies, waits for them, and re-layouts: 7.22 us -> none  [plane(): return pick(self.keep[:, 0]) + pick(self.got[:, 0]) + pick(self.got_first)]
    ppermute x49, waiting for transfers between devices: 74.3 us -> 67.6 us  [move(): return lax.ppermute(value, AXES, perm)]
    unnamed x107 -> x93, local copies, waits for them, and re-layouts: 8.53 us -> 7.98 us
  transfers between devices with their start and end apart: 51 -> 51, of which waited for: 19 -> 15; matrix products, arithmetic and copies ran while one was open for 35% -> 38% of each run, Pallas kernels for 17% -> 17%
where the time goes in v6:
time: 337 us; the launch traced here: 333 us
  matrix products  87.9 us (26%)
  waiting for transfers between devices  67.6 us (20%)
  Pallas kernels  63 us (19%)
  starting transfers between devices  43.7 us (13%)
  other arithmetic  40.8 us (12%)
  between operations  15.2 us (5%)
  local copies, waits for them, and re-layouts  14.4 us (4%)
    ppermute x49, waiting for transfers between devices, move(): return lax.ppermute(value, AXES, perm)  67.6 us
    ppermute x49, starting transfers between devices, move(): return lax.ppermute(value, AXES, perm)  43.6 us
    dot_general x15, matrix products, contract_low(): lax.dot_general(value, upstream_gradient, ((over, over), ((), ())), prefe...  36.8 us
    pallas_call x4, Pallas kernels, per_sequence(): pl.pallas_call(body, out_shape=outs, grid_spec=pltpu.PrefetchScalarGridSp...  32.1 us
    dot_general x7, matrix products, back_project(): jnp.einsum('...j,aj->...a', upstream_gradient, weight_matrix, preferred_e...  27.6 us
    dot_general x7, matrix products, project(): jnp.einsum('...h,ht->...t', value_tensor, weight_matrix, preferred_elemen...  22.4 us
    pallas_call x3, Pallas kernels, assemble(): pl.pallas_call(functools.partial(assemble_body, widths), out_shape=[jax.S...  17 us
    pallas_call x3, Pallas kernels, split_add(): pl.pallas_call(functools.partial(split_body, len(pairs)), out_shape=[shap...  13.8 us
  transfers between devices with their start and end apart: 51, of which 15 were waited for; matrix products, arithmetic and copies ran while one was open for 38% of the time, Pallas kernels for 17%

profile of v6, /device:TPU:0, one launch (start us, length us, event | category | flops | bytes accessed | tf_op | source)
XLA Modules:
  0.0 332.6 jit_solution(1399350364068762117)
XLA Ops:
  12.4 4.1 %collective-permute-start = (bf16[24,2560]{1,0:T(8,128)(2,1)S(1)}, bf16[24,2560]{1,0:T(8,128)(2,1)S(1)}, u32[]{:S(2)}, u32[]{:S(2)}) collective-permute-start(bf16[24,2560]{1,0:T(8,128)(2,1)S(1)} %concatenate.40), channel_id=1, source_target_pairs={{0,16},{1,17},{2,18},{3,19},{4,20},{5,21},{6,22},{7,23},{8,24},{9,... | collective-permute-start | bytes 368648 | tf_op jit(solution)/shard_map/ppermute | solution.py:235
  17.4 5.1 %collective-permute-done = bf16[24,2560]{1,0:T(8,128)(2,1)S(1)} collective-permute-done((bf16[24,2560]{1,0:T(8,128)(2,1)S(1)}, bf16[24,2560]{1,0:T(8,128)(2,1)S(1)}, u32[]{:S(2)}, u32[]{:S(2)}) %collective-permute-start) | collective-permute-done | bytes 122912 | tf_op jit(solution)/shard_map/ppermute | solution.py:235
  23.5 8.7 %collective-permute-done.1 = bf16[2,24,2560]{2,1,0:T(8,128)(2,1)S(1)} collective-permute-done((bf16[2,24,2560]{2,1,0:T(8,128)(2,1)S(1)}, bf16[2,24,2560]{2,1,0:T(8,128)(2,1)S(1)}, u32[]{:S(2)}, u32[]{:S(2)}) %collective-permute-start.1) | collective-permute-done | bytes 245792 | tf_op jit(solution)/shard_map/ppermute | solution.py:235
  36.1 4.6 %collective-permute-start.9 = (bf16[24,3072]{1,0:T(8,128)(2,1)S(1)}, bf16[24,3072]{1,0:T(8,128)(2,1)S(1)}, u32[]{:S(2)}, u32[]{:S(2)}) collective-permute-start(bf16[24,3072]{1,0:T(8,128)(2,1)S(1)} %copy-done.29), channel_id=1, source_target_pairs={{0,16},{1,17},{2,18},{3,19},{4,20},{5,21},{6,22},{7,23},{8,24},{9,... | collective-permute-start | bytes 442376 | tf_op jit(solution)/shard_map/ppermute | solution.py:235
  40.6 8.1 %collective-permute-done.2.refs_1_ = bf16[4,24,2560]{2,1,0:T(8,128)(2,1)} collective-permute-done((bf16[4,24,2560]{2,1,0:T(8,128)(2,1)S(1)}, bf16[4,24,2560]{2,1,0:T(8,128)(2,1)}, u32[]{:S(2)}, u32[]{:S(2)}) %collective-permute-start.2) | collective-permute-done | bytes 491552 | tf_op jit(solution)/shard_map/ppermute | solution.py:235
  51.5 3.0 collective-permute-start.10
  55.0 2.8 collective-permute-done.4.refs_3_
  58.5 6.3 %collective-permute-done.10 = bf16[2,24,3072]{2,1,0:T(8,128)(2,1)} collective-permute-done((bf16[2,24,3072]{2,1,0:T(8,128)(2,1)}, bf16[2,24,3072]{2,1,0:T(8,128)(2,1)}, u32[]{:S(2)}, u32[]{:S(2)}) %collective-permute-start.10) | collective-permute-done | bytes 294944 | tf_op jit(solution)/shard_map/ppermute | solution.py:235
  69.3 5.5 %assemble.3 = (bf16[4,2,2,2,24,2304]{5,4,3,2,1,0:T(8,128)(2,1)}, bf16[4,2,2,2,24,256]{5,4,3,2,1,0:T(8,128)(2,1)}) custom-call(s32[4]{0:T(128)} %pad_add_fusion.spot, bf16[4,24,2560]{2,1,0:T(8,128)(2,1)} %copy-done.13, bf16[4,24,2560]{2,1,0:T(8,128)(2,1)} %collective-permute-done.2.refs_1_, bf16[4,24,2560]{2,1,0:T(8,128)(2,1)} %collective-permute-done.3.refs_2_, ...), custom_call_target="tpu_custom_call" | custom-call | tf_op jit(solution)/shard_map/assemble/pallas_call | solution.py:267
  74.8 2.9 collective-permute-start.18
  79.4 4.7 %convolution_convert_fusion.1 = bf16[384,2304]{1,0:T(8,128)(2,1)} fusion(bf16[384,768]{1,0:T(8,128)(2,1)S(1)} %bitcast.256, bf16[768,2304]{1,0:T(8,128)(2,1)} %bitcast.261), kind=kOutput, calls=%fused_computation.12 | convolution fusion | flops 1359839232 | bytes 5898240 | tf_op jit(solution)/shard_map/...h,ht->...t/dot_general | solution.py:38
  84.1 9.0 %self_forward.1 = (bf16[4,96,768]{2,1,0:T(8,128)(2,1)}, bf16[4,6,96,192]{3,2,1,0:T(8,128)(2,1)}) custom-call(s32[4]{0:T(128)} %lens.1, bf16[4,96,2304]{2,1,0:T(8,128)(2,1)} %bitcast.212), custom_call_target="tpu_custom_call" | custom-call | tf_op jit(solution)/shard_map/self_forward/pallas_call | solution.py:163
  98.4 3.6 %collective-permute-done.19 = bf16[2,96,768]{2,1,0:T(8,128)(2,1)S(1)} collective-permute-done((bf16[2,96,768]{2,1,0:T(8,128)(2,1)S(1)}, bf16[2,96,768]{2,1,0:T(8,128)(2,1)S(1)}, u32[]{:S(2)}, u32[]{:S(2)}) %collective-permute-start.19) | collective-permute-done | bytes 294944 | tf_op jit(solution)/shard_map/ppermute | solution.py:235
  109.1 3.6 %fusion.7.kv = bf16[4,196,1536]{2,1,0:T(8,128)(2,1)} fusion(bf16[768,3840]{1,0:T(8,128)(2,1)S(1)} %copy-done.34, bf16[4,196,768]{2,0,1:T(4,128)(2,1)S(1)} %copy-done), kind=kOutput, calls=%fused_computation.18 | convolution fusion | flops 1850892288 | bytes 5971968 | tf_op jit(solution)/shard_map/...h,ht->...t/dot_general | solution.py:38
  112.7 6.5 %cross_forward.1 = (bf16[4,96,768]{2,1,0:T(8,128)(2,1)}, bf16[4,6,196,192]{3,2,1,0:T(8,128)(2,1)}) custom-call(bf16[4,96,768]{2,1,0:T(8,128)(2,1)} %bitcast.230, bf16[4,196,1536]{2,1,0:T(8,128)(2,1)} %fusion.7.kv), custom_call_target="tpu_custom_call" | custom-call | tf_op jit(solution)/shard_map/cross_forward/pallas_call | solution.py:163
  120.5 5.7 %assemble.4 = bf16[4,2,2,2,24,3072]{5,4,3,2,1,0:T(8,128)(2,1)} custom-call(s32[4]{0:T(128)} %pad_add_fusion.spot, bf16[4,24,3072]{2,1,0:T(8,128)(2,1)} %pad_maximum_fusion.refs_0_, bf16[4,24,3072]{2,1,0:T(8,128)(2,1)} %collective-permute-done.11.refs_1_, bf16[4,24,3072]{2,1,0:T(8,128)(2,1)} %collective-permute-done.12.refs_2_, ...), custom_call_target="tpu_custom_call" | custom-call | tf_op jit(solution)/shard_map/assemble/pallas_call | solution.py:267
  131.2 7.6 %collective-permute-done.22.refs_3_ = bf16[4,96,768]{2,1,0:T(8,128)(2,1)} collective-permute-done((bf16[4,96,768]{2,1,0:T(8,128)(2,1)}, bf16[4,96,768]{2,1,0:T(8,128)(2,1)}, u32[]{:S(2)}, u32[]{:S(2)}) %collective-permute-start.22) | collective-permute-done | bytes 589856 | tf_op jit(solution)/shard_map/ppermute | solution.py:235
  138.8 5.2 %multiply_convert_fusion = (bf16[384,3072]{1,0:T(8,128)(2,1)S(1)}, f32[384,3072]{1,0:T(8,128)}) fusion(f32[3072]{0:T(1024)S(1)} %add.462, bf16[768,3072]{1,0:T(8,128)(2,1)S(1)} %bitcast.221, f32[384,768]{1,0:T(8,128)S(1)} %get-tuple-element.221, f32[768]{0:T(1024)S(1)} %get-tuple-element.184, f32[768]{0:T(1024)S(1)} %get-tuple-element.185, ...), kind=kOutput, calls=%fused_computation.10 | convolution fusion | flops 1825210368 | bytes 12997632 | tf_op jit(solution)/shard_map/...h,ht->...t/dot_general | solution.py:38
  145.3 4.5 %convolution_convert_fusion = bf16[3072,768]{1,0:T(8,128)(2,1)} fusion(bf16[384,3072]{1,0:T(8,128)(2,1)S(1)} %get-tuple-element.111, bf16[384,768]{1,0:T(8,128)(2,1)S(1)} %copy-done.28), kind=kOutput, calls=%fused_computation.2 | convolution fusion | flops 1814298624 | bytes 7667712 | tf_op jit(solution)/shard_map/dot_general | solution.py:508
  149.9 5.8 %assemble.5 = bf16[4,2,2,2,96,768]{5,4,3,2,1,0:T(8,128)(2,1)} custom-call(s32[4]{0:T(128)} %pad_add_fusion.spot, bf16[4,96,768]{2,1,0:T(8,128)(2,1)} %pad_maximum_fusion.1.refs_0_, bf16[4,96,768]{2,1,0:T(8,128)(2,1)} %collective-permute-done.20.refs_1_, bf16[4,96,768]{2,1,0:T(8,128)(2,1)} %collective-permute-done.21.refs_2_, ...), custom_call_target="tpu_custom_call" | custom-call | tf_op jit(solution)/shard_map/assemble/pallas_call | solution.py:267
  155.7 7.2 %fusion.70 = (bf16[3072]{0:T(1024)(128)(2,1)S(1)}, bf16[384,3072]{1,0:T(8,128)(2,1)S(1)}) fusion(f32[384,3072]{1,0:T(8,128)} %get-tuple-element.223, bf16[384,768]{1,0:T(8,128)(2,1)} %bitcast.255, bf16[3072,768]{1,0:T(8,128)(2,1)} %bitcast.216), kind=kOutput, calls=%fused_computation.198 | convolution fusion | flops 1836708864 | bytes 12392448 | tf_op jit(solution)/shard_map/...j,aj->...a/dot_general | solution.py:42
  162.9 3.1 convolution_convert_fusion.6
  168.5 4.8 %convolution_convert_fusion.5 = bf16[768,1536]{1,0:T(8,128)(2,1)} fusion(bf16[384,3072]{1,0:T(8,128)(2,1)} %copy-done.40, s32[]{:T(128)S(6)} %select_n.216, f32[384,768]{1,0:T(8,128)} %copy-done.2, f32[768]{0:T(1024)S(1)} %get-tuple-element.184, f32[768]{0:T(1024)S(1)} %get-tuple-element.185, f32[384]{0:T(512)S(1)} %add_rsqrt_fusion, ...), kind=kOutput, calls=%fused_computation.16 | convolution fusion | flops 908623872 | bytes 4727812 | tf_op jit(solution)/shard_map/dot_general | solution.py:508
  173.3 5.0 %multiply_reduce_fusion.1 = (bf16[768]{0:T(1024)(128)(2,1)S(1)}, f32[384]{0:T(512)S(1)}, f32[384]{0:T(512)S(1)}, bf16[768]{0:T(1024)(128)(2,1)S(1)}, f32[384,768]{1,0:T(8,128)S(1)}) fusion(f32[384,768]{1,0:T(8,128)S(1)} %copy-done.4, f32[384]{0:T(512)S(1)} %add_rsqrt_fusion, f32[384]{0:T(512)S(1)} %broadcast_multiply_fusion.6, ...), kind=kOutput, calls=%fused_computation.49 | convolution fusion | flops 1814591232 | bytes 9449472 | tf_op jit(solution)/shard_map/...j,aj->...a/dot_general | solution.py:42
  179.8 3.0 convolution_convert_fusion.14
  182.7 4.4 %split_add.3 = (bf16[2,4,48,1536]{3,2,1,0:T(8,128)(2,1)}, bf16[2,4,48,1536]{3,2,1,0:T(8,128)(2,1)}) custom-call(s32[4]{0:T(128)} %pad_add_fusion.1.which, bf16[4,4,48,1536]{3,2,1,0:T(8,128)(2,1)} %bitcast.208, bf16[4,4,48,1536]{3,2,1,0:T(8,128)(2,1)} %bitcast.31.refs_1_.refs_3_, bf16[4,4,48,1536]{3,2,1,0:T(8,128)(2,1)} %bitcast.209, ...), custom_call_target="tpu_custom_call" | custom-call | tf_op jit(solution)/shard_map/split_add/pallas_call | solution.py:385
  187.1 8.1 %cross_backward.1 = (bf16[4,96,768]{2,1,0:T(8,128)(2,1)}, bf16[4,196,1536]{2,1,0:T(8,128)(2,1)}) custom-call(bf16[4,96,768]{2,1,0:T(8,128)(2,1)} %bitcast.231, bf16[4,196,1536]{2,1,0:T(8,128)(2,1)} %fusion.7.kv, bf16[4,6,196,192]{3,2,1,0:T(8,128)(2,1)} %get-tuple-element.93.probs, bf16[4,96,768]{2,1,0:T(8,128)(2,1)} %bitcast.246), custom_call_target="tpu_custom_call" | custom-call | tf_op jit(solution)/shard_map/cross_backward/pallas_call | solution.py:163
  195.3 4.0 %fusion.9 = bf16[768,768]{0,1:T(8,128)(2,1)} fusion(bf16[4,196,1536]{2,1,0:T(8,128)(2,1)} %get-tuple-element.109, s32[]{:T(128)S(6)} %select_n.218, bf16[4,196,768]{2,0,1:T(4,128)(2,1)S(1)} %copy-done), kind=kOutput, calls=%fused_computation.25 | convolution fusion | flops 925433856 | bytes 3612676 | tf_op jit(solution)/shard_map/dot_general | solution.py:508
  206.4 2.6 convolution_convert_fusion.8
  209.0 3.7 %bitcast_convert_fusion = bf16[768,768]{0,1:T(8,128)(2,1)} fusion(bf16[4,196,1536]{2,1,0:T(8,128)(2,1)} %get-tuple-element.109, s32[]{:T(128)S(6)} %select_n.220, bf16[4,196,768]{2,0,1:T(4,128)(2,1)S(1)} %copy-done), kind=kOutput, calls=%fused_computation.20 | convolution fusion | flops 925433856 | bytes 3612676 | tf_op jit(solution)/shard_map/dot_general | solution.py:508
  212.7 2.4 copy.76
  215.1 4.5 %split_add.4 = (bf16[2,4,48,1536]{3,2,1,0:T(8,128)(2,1)}, bf16[2,4,48,1536]{3,2,1,0:T(8,128)(2,1)}) custom-call(s32[4]{0:T(128)} %pad_add_fusion.1.which, bf16[4,4,48,384]{3,2,1,0:T(8,128)(2,1)} %bitcast.228, bf16[4,4,48,384]{3,2,1,0:T(8,128)(2,1)} %bitcast.39.refs_1_.refs_7_, bf16[4,4,48,768]{3,2,1,0:T(8,128)(2,1)} %bitcast.214, ...), custom_call_target="tpu_custom_call" | custom-call | tf_op jit(solution)/shard_map/split_add/pallas_call | solution.py:385
  220.9 2.4 multiply_reduce_fusion.2
  226.2 2.7 convolution_convert_fusion.9
  229.0 8.5 %self_backward.1 = bf16[4,96,2304]{2,1,0:T(8,128)(2,1)} custom-call(bf16[4,96,2304]{2,1,0:T(8,128)(2,1)} %bitcast.213, bf16[4,6,96,192]{3,2,1,0:T(8,128)(2,1)} %get-tuple-element.100.probs, bf16[4,96,768]{2,1,0:T(8,128)(2,1)} %bitcast.257), custom_call_target="tpu_custom_call" | custom-call | tf_op jit(solution)/shard_map/self_backward/pallas_call | solution.py:163
  240.8 2.4 convolution_convert_fusion.11
  243.3 2.4 convolution_convert_fusion.3
  246.2 2.4 convolution_convert_fusion.4
  248.6 2.4 collective-permute-done.45
  258.1 2.7 multiply_reduce_fusion
  264.1 4.9 %split_add.5 = (bf16[2,4,48,1664]{3,2,1,0:T(8,128)(2,1)}, bf16[2,4,48,1664]{3,2,1,0:T(8,128)(2,1)}) custom-call(s32[4]{0:T(128)} %pad_add_fusion.1.which, bf16[4,4,48,384]{3,2,1,0:T(8,128)(2,1)} %bitcast.222, bf16[4,4,48,384]{3,2,1,0:T(8,128)(2,1)} %bitcast.224, bf16[4,4,48,1152]{3,2,1,0:T(8,128)(2,1)} %bitcast.210, ...), custom_call_target="tpu_custom_call" | custom-call | tf_op jit(solution)/shard_map/split_add/pallas_call | solution.py:385
  269.5 2.8 multiply_add_fusion
  275.4 11.1 %collective-permute-done.36 = bf16[2,4,48,1664]{3,2,1,0:T(8,128)(2,1)S(1)} collective-permute-done((bf16[2,4,48,1664]{3,2,1,0:T(8,128)(2,1)}, bf16[2,4,48,1664]{3,2,1,0:T(8,128)(2,1)S(1)}, u32[]{:S(2)}, u32[]{:S(2)}) %collective-permute-start.36) | collective-permute-done | bytes 1277984 | tf_op jit(solution)/shard_map/ppermute | solution.py:235
  294.2 4.2 %collective-permute-done.37 = bf16[4,48,1664]{2,1,0:T(8,128)(2,1)} collective-permute-done((bf16[4,48,1664]{2,1,0:T(8,128)(2,1)}, bf16[4,48,1664]{2,1,0:T(8,128)(2,1)}, u32[]{:S(2)}, u32[]{:S(2)}) %collective-permute-start.37) | collective-permute-done | bytes 639008 | tf_op jit(solution)/shard_map/ppermute | solution.py:235
  300.3 4.5 %fusion.8 = f32[4,196,768]{2,1,0:T(8,128)S(1)} fusion(bf16[4,196,1536]{2,1,0:T(8,128)(2,1)} %get-tuple-element.109, bf16[768,3840]{1,0:T(8,128)(2,1)} %all-gather.2.cloned.1.call-done), kind=kOutput, calls=%fused_computation.22 | convolution fusion | flops 1849688064 | bytes 7225344 | tf_op jit(solution)/shard_map/...j,aj->...a/dot_general | solution.py:42
  307.1 2.8 collective-permute-done.38
  312.9 2.8 fusion.11
  316.5 4.1 %collective-permute-done.39 = bf16[48,1664]{1,0:T(8,128)(2,1)S(1)} collective-permute-done((bf16[48,1664]{1,0:T(8,128)(2,1)S(1)}, bf16[48,1664]{1,0:T(8,128)(2,1)S(1)}, u32[]{:S(2)}, u32[]{:S(2)}) %collective-permute-start.39) | collective-permute-done | bytes 159776 | tf_op jit(solution)/shard_map/ppermute | solution.py:235
  (288 shorter events, 94.0 us)
Async XLA Ops:
  7.2 96.1 %all-gather.2.cloned.1.call-start = ((), (), s32[]{:S(2)}) async-start(), calls=%async_computation.1 | async-start | bytes 6082560 | tf_op jit(solution)/shard_map/all_gather | solution.py:546
  9.0 281.8 %reduce-scatter.2.cloned.1.call-start = ((), (), s32[]{:S(2)}) async-start(), calls=%async_computation.2 | async-start | bytes 4866048 | tf_op jit(solution)/shard_map/reduce_scatter | solution.py:399
  12.4 10.1 %collective-permute-start = (bf16[24,2560]{1,0:T(8,128)(2,1)S(1)}, bf16[24,2560]{1,0:T(8,128)(2,1)S(1)}, u32[]{:S(2)}, u32[]{:S(2)}) collective-permute-start(bf16[24,2560]{1,0:T(8,128)(2,1)S(1)} %concatenate.40), channel_id=1, source_target_pairs={{0,16},{1,17},{2,18},{3,19},{4,20},{5,21},{6,22},{7,23},{8,24},{9,... | collective-permute-start | bytes 368648 | tf_op jit(solution)/shard_map/ppermute | solution.py:235
  22.5 9.7 %collective-permute-start.1 = (bf16[2,24,2560]{2,1,0:T(8,128)(2,1)S(1)}, bf16[2,24,2560]{2,1,0:T(8,128)(2,1)S(1)}, u32[]{:S(2)}, u32[]{:S(2)}) collective-permute-start(bf16[2,24,2560]{2,1,0:T(8,128)(2,1)S(1)} %pad_maximum_fusion.9), channel_id=1, source_target_pairs={{0,8},{1,9},{2,10},{3,11},{4,12},{5,13},{6,14},{7,15},{8,0},{9,1},... | collective-permute-start | bytes 737288 | tf_op jit(solution)/shard_map/ppermute | solution.py:235
  32.3 16.4 %collective-permute-start.2 = (bf16[4,24,2560]{2,1,0:T(8,128)(2,1)S(1)}, bf16[4,24,2560]{2,1,0:T(8,128)(2,1)}, u32[]{:S(2)}, u32[]{:S(2)}) collective-permute-start(bf16[4,24,2560]{2,1,0:T(8,128)(2,1)S(1)} %pad_maximum_fusion.2.refs_0_), channel_id=1, source_target_pairs={{0,4},{1,3},{2,6},{3,1},{4,0},{5,7},{6,2},{7,5},{8,12},{9,11},{10,... | collective-permute-start | bytes 1474568 | tf_op jit(solution)/shard_map/ppermute | solution.py:235
  34.4 20.3 %collective-permute-start.3 = (bf16[4,24,2560]{2,1,0:T(8,128)(2,1)S(1)}, bf16[4,24,2560]{2,1,0:T(8,128)(2,1)}, u32[]{:S(2)}, u32[]{:S(2)}) collective-permute-start(bf16[4,24,2560]{2,1,0:T(8,128)(2,1)S(1)} %pad_maximum_fusion.2.refs_0_), channel_id=1, source_target_pairs={{0,2},{1,5},{2,0},{3,7},{4,6},{5,1},{6,4},{7,3},{8,10},{9,13},{10,... | collective-permute-start | bytes 1474568 | tf_op jit(solution)/shard_map/ppermute | solution.py:235
  36.1 14.7 %collective-permute-start.9 = (bf16[24,3072]{1,0:T(8,128)(2,1)S(1)}, bf16[24,3072]{1,0:T(8,128)(2,1)S(1)}, u32[]{:S(2)}, u32[]{:S(2)}) collective-permute-start(bf16[24,3072]{1,0:T(8,128)(2,1)S(1)} %copy-done.29), channel_id=1, source_target_pairs={{0,16},{1,17},{2,18},{3,19},{4,20},{5,21},{6,22},{7,23},{8,24},{9,... | collective-permute-start | bytes 442376 | tf_op jit(solution)/shard_map/ppermute | solution.py:235
  48.7 9.1 %collective-permute-start.4 = (bf16[4,24,2560]{2,1,0:T(8,128)(2,1)}, bf16[4,24,2560]{2,1,0:T(8,128)(2,1)}, u32[]{:S(2)}, u32[]{:S(2)}) collective-permute-start(bf16[4,24,2560]{2,1,0:T(8,128)(2,1)} %collective-permute-done.2.refs_1_), channel_id=1, source_target_pairs={{0,2},{1,5},{2,0},{3,7},{4,6},{5,1},{6,4},{7,3},{8,10},{9,13},{10,... | collective-permute-start | bytes 1474568 | tf_op jit(solution)/shard_map/ppermute | solution.py:235
  50.6 16.8 %collective-permute-start.5 = (bf16[4,24,2560]{2,1,0:T(8,128)(2,1)S(1)}, bf16[4,24,2560]{2,1,0:T(8,128)(2,1)}, u32[]{:S(2)}, u32[]{:S(2)}) collective-permute-start(bf16[4,24,2560]{2,1,0:T(8,128)(2,1)S(1)} %pad_maximum_fusion.2.refs_0_), channel_id=1, source_target_pairs={{0,1},{1,0},{2,3},{3,2},{4,5},{5,4},{6,7},{7,6},{8,9},{9,8},{10,11... | collective-permute-start | bytes 1474568 | tf_op jit(solution)/shard_map/ppermute | solution.py:235
  51.5 13.2 %collective-permute-start.10 = (bf16[2,24,3072]{2,1,0:T(8,128)(2,1)}, bf16[2,24,3072]{2,1,0:T(8,128)(2,1)}, u32[]{:S(2)}, u32[]{:S(2)}) collective-permute-start(bf16[2,24,3072]{2,1,0:T(8,128)(2,1)} %pad_maximum_fusion.4), channel_id=1, source_target_pairs={{0,8},{1,9},{2,10},{3,11},{4,12},{5,13},{6,14},{7,15},{8,0},{9,1},... | collective-permute-start | bytes 884744 | tf_op jit(solution)/shard_map/ppermute | solution.py:235
  54.5 14.8 %collective-permute-start.6 = (bf16[4,24,2560]{2,1,0:T(8,128)(2,1)}, bf16[4,24,2560]{2,1,0:T(8,128)(2,1)}, u32[]{:S(2)}, u32[]{:S(2)}) collective-permute-start(bf16[4,24,2560]{2,1,0:T(8,128)(2,1)} %collective-permute-done.2.refs_1_), channel_id=1, source_target_pairs={{0,1},{1,0},{2,3},{3,2},{4,5},{5,4},{6,7},{7,6},{8,9},{9,8},{10,11... | collective-permute-start | bytes 1474568 | tf_op jit(solution)/shard_map/ppermute | solution.py:235
  54.7 14.6 %collective-permute-start.7 = (bf16[4,24,2560]{2,1,0:T(8,128)(2,1)}, bf16[4,24,2560]{2,1,0:T(8,128)(2,1)}, u32[]{:S(2)}, u32[]{:S(2)}) collective-permute-start(bf16[4,24,2560]{2,1,0:T(8,128)(2,1)} %collective-permute-done.3.refs_2_), channel_id=1, source_target_pairs={{0,1},{1,0},{2,3},{3,2},{4,5},{5,4},{6,7},{7,6},{8,9},{9,8},{10,11... | collective-permute-start | bytes 1474568 | tf_op jit(solution)/shard_map/ppermute | solution.py:235
  57.8 11.4 %collective-permute-start.8 = (bf16[4,24,2560]{2,1,0:T(8,128)(2,1)}, bf16[4,24,2560]{2,1,0:T(8,128)(2,1)}, u32[]{:S(2)}, u32[]{:S(2)}) collective-permute-start(bf16[4,24,2560]{2,1,0:T(8,128)(2,1)} %collective-permute-done.4.refs_3_), channel_id=1, source_target_pairs={{0,1},{1,0},{2,3},{3,2},{4,5},{5,4},{6,7},{7,6},{8,9},{9,8},{10,11... | collective-permute-start | bytes 1474568 | tf_op jit(solution)/shard_map/ppermute | solution.py:235
  66.6 31.7 %collective-permute-start.12 = (bf16[4,24,3072]{2,1,0:T(8,128)(2,1)}, bf16[4,24,3072]{2,1,0:T(8,128)(2,1)}, u32[]{:S(2)}, u32[]{:S(2)}) collective-permute-start(bf16[4,24,3072]{2,1,0:T(8,128)(2,1)} %pad_maximum_fusion.refs_0_), channel_id=1, source_target_pairs={{0,2},{1,5},{2,0},{3,7},{4,6},{5,1},{6,4},{7,3},{8,10},{9,13},{10,... | collective-permute-start | bytes 1769480 | tf_op jit(solution)/shard_map/ppermute | solution.py:235
  67.4 25.7 %collective-permute-start.11 = (bf16[4,24,3072]{2,1,0:T(8,128)(2,1)}, bf16[4,24,3072]{2,1,0:T(8,128)(2,1)}, u32[]{:S(2)}, u32[]{:S(2)}) collective-permute-start(bf16[4,24,3072]{2,1,0:T(8,128)(2,1)} %pad_maximum_fusion.refs_0_), channel_id=1, source_target_pairs={{0,4},{1,3},{2,6},{3,1},{4,0},{5,7},{6,2},{7,5},{8,12},{9,11},{10,... | collective-permute-start | bytes 1769480 | tf_op jit(solution)/shard_map/ppermute | solution.py:235
  74.8 20.1 %collective-permute-start.18 = (bf16[96,768]{1,0:T(8,128)(2,1)S(1)}, bf16[96,768]{1,0:T(8,128)(2,1)S(1)}, u32[]{:S(2)}, u32[]{:S(2)}) collective-permute-start(bf16[96,768]{1,0:T(8,128)(2,1)S(1)} %copy-done.30), channel_id=1, source_target_pairs={{0,16},{1,17},{2,18},{3,19},{4,20},{5,21},{6,22},{7,23},{8,24},{9,... | collective-permute-start | bytes 442376 | tf_op jit(solution)/shard_map/ppermute | solution.py:235
  93.1 10.2 %collective-permute-start.13 = (bf16[4,24,3072]{2,1,0:T(8,128)(2,1)}, bf16[4,24,3072]{2,1,0:T(8,128)(2,1)}, u32[]{:S(2)}, u32[]{:S(2)}) collective-permute-start(bf16[4,24,3072]{2,1,0:T(8,128)(2,1)} %collective-permute-done.11.refs_1_), channel_id=1, source_target_pairs={{0,2},{1,5},{2,0},{3,7},{4,6},{5,1},{6,4},{7,3},{8,10},{9,13},{10,... | collective-permute-start | bytes 1769480 | tf_op jit(solution)/shard_map/ppermute | solution.py:235
  94.9 7.0 %collective-permute-start.19 = (bf16[2,96,768]{2,1,0:T(8,128)(2,1)S(1)}, bf16[2,96,768]{2,1,0:T(8,128)(2,1)S(1)}, u32[]{:S(2)}, u32[]{:S(2)}) collective-permute-start(bf16[2,96,768]{2,1,0:T(8,128)(2,1)S(1)} %pad_maximum_fusion.5), channel_id=1, source_target_pairs={{0,8},{1,9},{2,10},{3,11},{4,12},{5,13},{6,14},{7,15},{8,0},{9,1},... | collective-permute-start | bytes 884744 | tf_op jit(solution)/shard_map/ppermute | solution.py:235
  97.3 21.9 %collective-permute-start.14 = (bf16[4,24,3072]{2,1,0:T(8,128)(2,1)}, bf16[4,24,3072]{2,1,0:T(8,128)(2,1)}, u32[]{:S(2)}, u32[]{:S(2)}) collective-permute-start(bf16[4,24,3072]{2,1,0:T(8,128)(2,1)} %pad_maximum_fusion.refs_0_), channel_id=1, source_target_pairs={{0,1},{1,0},{2,3},{3,2},{4,5},{5,4},{6,7},{7,6},{8,9},{9,8},{10,11... | collective-permute-start | bytes 1769480 | tf_op jit(solution)/shard_map/ppermute | solution.py:235
  97.7 22.8 %collective-permute-start.15 = (bf16[4,24,3072]{2,1,0:T(8,128)(2,1)}, bf16[4,24,3072]{2,1,0:T(8,128)(2,1)}, u32[]{:S(2)}, u32[]{:S(2)}) collective-permute-start(bf16[4,24,3072]{2,1,0:T(8,128)(2,1)} %collective-permute-done.11.refs_1_), channel_id=1, source_target_pairs={{0,1},{1,0},{2,3},{3,2},{4,5},{5,4},{6,7},{7,6},{8,9},{9,8},{10,11... | collective-permute-start | bytes 1769480 | tf_op jit(solution)/shard_map/ppermute | solution.py:235
  98.3 21.9 %collective-permute-start.16 = (bf16[4,24,3072]{2,1,0:T(8,128)(2,1)}, bf16[4,24,3072]{2,1,0:T(8,128)(2,1)}, u32[]{:S(2)}, u32[]{:S(2)}) collective-permute-start(bf16[4,24,3072]{2,1,0:T(8,128)(2,1)} %collective-permute-done.12.refs_2_), channel_id=1, source_target_pairs={{0,1},{1,0},{2,3},{3,2},{4,5},{5,4},{6,7},{7,6},{8,9},{9,8},{10,11... | collective-permute-start | bytes 1769480 | tf_op jit(solution)/shard_map/ppermute | solution.py:235
  103.3 17.1 %collective-permute-start.17 = (bf16[4,24,3072]{2,1,0:T(8,128)(2,1)}, bf16[4,24,3072]{2,1,0:T(8,128)(2,1)}, u32[]{:S(2)}, u32[]{:S(2)}) collective-permute-start(bf16[4,24,3072]{2,1,0:T(8,128)(2,1)} %collective-permute-done.13.refs_3_), channel_id=1, source_target_pairs={{0,1},{1,0},{2,3},{3,2},{4,5},{5,4},{6,7},{7,6},{8,9},{9,8},{10,11... | collective-permute-start | bytes 1769480 | tf_op jit(solution)/shard_map/ppermute | solution.py:235
  108.0 20.5 %collective-permute-start.20 = (bf16[4,96,768]{2,1,0:T(8,128)(2,1)}, bf16[4,96,768]{2,1,0:T(8,128)(2,1)}, u32[]{:S(2)}, u32[]{:S(2)}) collective-permute-start(bf16[4,96,768]{2,1,0:T(8,128)(2,1)} %pad_maximum_fusion.1.refs_0_), channel_id=1, source_target_pairs={{0,4},{1,3},{2,6},{3,1},{4,0},{5,7},{6,2},{7,5},{8,12},{9,11},{10,... | collective-permute-start | bytes 1769480 | tf_op jit(solution)/shard_map/ppermute | solution.py:235
  119.2 30.7 %collective-permute-start.23 = (bf16[4,96,768]{2,1,0:T(8,128)(2,1)}, bf16[4,96,768]{2,1,0:T(8,128)(2,1)}, u32[]{:S(2)}, u32[]{:S(2)}) collective-permute-start(bf16[4,96,768]{2,1,0:T(8,128)(2,1)} %pad_maximum_fusion.1.refs_0_), channel_id=1, source_target_pairs={{0,1},{1,0},{2,3},{3,2},{4,5},{5,4},{6,7},{7,6},{8,9},{9,8},{10,11... | collective-permute-start | bytes 1769480 | tf_op jit(solution)/shard_map/ppermute | solution.py:235
  120.2 10.5 %collective-permute-start.21 = (bf16[4,96,768]{2,1,0:T(8,128)(2,1)}, bf16[4,96,768]{2,1,0:T(8,128)(2,1)}, u32[]{:S(2)}, u32[]{:S(2)}) collective-permute-start(bf16[4,96,768]{2,1,0:T(8,128)(2,1)} %pad_maximum_fusion.1.refs_0_), channel_id=1, source_target_pairs={{0,2},{1,5},{2,0},{3,7},{4,6},{5,1},{6,4},{7,3},{8,10},{9,13},{10,... | collective-permute-start | bytes 1769480 | tf_op jit(solution)/shard_map/ppermute | solution.py:235
  128.5 10.3 %collective-permute-start.22 = (bf16[4,96,768]{2,1,0:T(8,128)(2,1)}, bf16[4,96,768]{2,1,0:T(8,128)(2,1)}, u32[]{:S(2)}, u32[]{:S(2)}) collective-permute-start(bf16[4,96,768]{2,1,0:T(8,128)(2,1)} %collective-permute-done.20.refs_1_), channel_id=1, source_target_pairs={{0,2},{1,5},{2,0},{3,7},{4,6},{5,1},{6,4},{7,3},{8,10},{9,13},{10,... | collective-permute-start | bytes 1769480 | tf_op jit(solution)/shard_map/ppermute | solution.py:235
  130.6 19.3 %collective-permute-start.24 = (bf16[4,96,768]{2,1,0:T(8,128)(2,1)}, bf16[4,96,768]{2,1,0:T(8,128)(2,1)}, u32[]{:S(2)}, u32[]{:S(2)}) collective-permute-start(bf16[4,96,768]{2,1,0:T(8,128)(2,1)} %collective-permute-done.20.refs_1_), channel_id=1, source_target_pairs={{0,1},{1,0},{2,3},{3,2},{4,5},{5,4},{6,7},{7,6},{8,9},{9,8},{10,11... | collective-permute-start | bytes 1769480 | tf_op jit(solution)/shard_map/ppermute | solution.py:235
  130.7 19.2 %collective-permute-start.25 = (bf16[4,96,768]{2,1,0:T(8,128)(2,1)}, bf16[4,96,768]{2,1,0:T(8,128)(2,1)}, u32[]{:S(2)}, u32[]{:S(2)}) collective-permute-start(bf16[4,96,768]{2,1,0:T(8,128)(2,1)} %collective-permute-done.21.refs_2_), channel_id=1, source_target_pairs={{0,1},{1,0},{2,3},{3,2},{4,5},{5,4},{6,7},{7,6},{8,9},{9,8},{10,11... | collective-permute-start | bytes 1769480 | tf_op jit(solution)/shard_map/ppermute | solution.py:235
  138.8 11.1 %collective-permute-start.26 = (bf16[4,96,768]{2,1,0:T(8,128)(2,1)}, bf16[4,96,768]{2,1,0:T(8,128)(2,1)}, u32[]{:S(2)}, u32[]{:S(2)}) collective-permute-start(bf16[4,96,768]{2,1,0:T(8,128)(2,1)} %collective-permute-done.22.refs_3_), channel_id=1, source_target_pairs={{0,1},{1,0},{2,3},{3,2},{4,5},{5,4},{6,7},{7,6},{8,9},{9,8},{10,11... | collective-permute-start | bytes 1769480 | tf_op jit(solution)/shard_map/ppermute | solution.py:235
  166.0 16.8 %collective-permute-start.27 = (bf16[768,1536]{1,0:T(8,128)(2,1)}, bf16[768,1536]{1,0:T(8,128)(2,1)}, u32[]{:S(2)}, u32[]{:S(2)}) collective-permute-start(bf16[768,1536]{1,0:T(8,128)(2,1)} %convolution_convert_fusion.6), channel_id=1, source_target_pairs={{0,1},{1,0},{2,3},{3,2},{4,5},{5,4},{6,7},{7,6},{8,9},{9,8},{10,11... | collective-permute-start | bytes 7077896 | tf_op jit(solution)/shard_map/ppermute | solution.py:235
  199.2 13.5 %collective-permute-start.31 = (bf16[768,768]{0,1:T(8,128)(2,1)}, bf16[768,768]{0,1:T(8,128)(2,1)}, u32[]{:S(2)}, u32[]{:S(2)}) collective-permute-start(bf16[768,768]{0,1:T(8,128)(2,1)} %fusion.9), channel_id=1, source_target_pairs={{0,1},{1,0},{2,3},{3,2},{4,5},{5,4},{6,7},{7,6},{8,9},{9,8},{10,11... | collective-permute-start | bytes 3538952 | tf_op jit(solution)/shard_map/ppermute | solution.py:235
  199.3 21.6 %collective-permute-start.28 = (bf16[2,4,48,1536]{3,2,1,0:T(8,128)(2,1)}, bf16[2,4,48,1536]{3,2,1,0:T(8,128)(2,1)}, u32[]{:S(2)}, u32[]{:S(2)}) collective-permute-start(bf16[2,4,48,1536]{3,2,1,0:T(8,128)(2,1)} %get-tuple-element.97), channel_id=1, source_target_pairs={{0,2},{1,5},{2,0},{3,7},{4,6},{5,1},{6,4},{7,3},{8,10},{9,13},{10,... | collective-permute-start | bytes 3538952 | tf_op jit(solution)/shard_map/ppermute | solution.py:235
  202.5 12.7 %collective-permute-start.32 = (bf16[768,384]{1,0:T(8,128)(2,1)}, bf16[768,384]{1,0:T(8,128)(2,1)}, u32[]{:S(2)}, u32[]{:S(2)}) collective-permute-start(bf16[768,384]{1,0:T(8,128)(2,1)} %convolution_convert_fusion.12), channel_id=1, source_target_pairs={{0,1},{1,0},{2,3},{3,2},{4,5},{5,4},{6,7},{7,6},{8,9},{9,8},{10,11... | collective-permute-start | bytes 1769480 | tf_op jit(solution)/shard_map/ppermute | solution.py:235
  203.9 11.2 %collective-permute-start.30 = (bf16[768,384]{1,0:T(8,128)(2,1)}, bf16[768,384]{1,0:T(8,128)(2,1)}, u32[]{:S(2)}, u32[]{:S(2)}) collective-permute-start(bf16[768,384]{1,0:T(8,128)(2,1)} %convolution_convert_fusion.13), channel_id=1, source_target_pairs={{0,1},{1,0},{2,3},{3,2},{4,5},{5,4},{6,7},{7,6},{8,9},{9,8},{10,11... | collective-permute-start | bytes 1769480 | tf_op jit(solution)/shard_map/ppermute | solution.py:235
  219.7 34.6 %collective-permute-start.34 = (bf16[2,4,48,1536]{3,2,1,0:T(8,128)(2,1)}, bf16[2,4,48,1536]{3,2,1,0:T(8,128)(2,1)}, u32[]{:S(2)}, u32[]{:S(2)}) collective-permute-start(bf16[2,4,48,1536]{3,2,1,0:T(8,128)(2,1)} %get-tuple-element.103), channel_id=1, source_target_pairs={{0,2},{1,5},{2,0},{3,7},{4,6},{5,1},{6,4},{7,3},{8,10},{9,13},{10,... | collective-permute-start | bytes 3538952 | tf_op jit(solution)/shard_map/ppermute | solution.py:235
  239.0 12.1 %collective-permute-start.45 = (bf16[4,48,1536]{2,1,0:T(8,128)(2,1)S(1)}, bf16[4,48,1536]{2,1,0:T(8,128)(2,1)S(1)}, u32[]{:S(2)}, u32[]{:S(2)}) collective-permute-start(bf16[4,48,1536]{2,1,0:T(8,128)(2,1)S(1)} %fusion.31), channel_id=1, source_target_pairs={{0,4},{1,3},{2,6},{3,1},{4,0},{5,7},{6,2},{7,5},{8,12},{9,11},{10,... | collective-permute-start | bytes 1769480 | tf_op jit(solution)/shard_map/ppermute | solution.py:235
  243.2 20.0 %collective-permute-start.29 = (bf16[768,384]{1,0:T(8,128)(2,1)}, bf16[768,384]{1,0:T(8,128)(2,1)S(1)}, u32[]{:S(2)}, u32[]{:S(2)}) collective-permute-start(bf16[768,384]{1,0:T(8,128)(2,1)} %convolution_convert_fusion.10), channel_id=1, source_target_pairs={{0,1},{1,0},{2,3},{3,2},{4,5},{5,4},{6,7},{7,6},{8,9},{9,8},{10,11... | collective-permute-start | bytes 1769480 | tf_op jit(solution)/shard_map/ppermute | solution.py:235
  245.7 17.7 %collective-permute-start.33 = (bf16[768,1152]{1,0:T(8,128)(2,1)}, bf16[768,1152]{1,0:T(8,128)(2,1)}, u32[]{:S(2)}, u32[]{:S(2)}) collective-permute-start(bf16[768,1152]{1,0:T(8,128)(2,1)} %convolution_convert_fusion.3), channel_id=1, source_target_pairs={{0,1},{1,0},{2,3},{3,2},{4,5},{5,4},{6,7},{7,6},{8,9},{9,8},{10,11... | collective-permute-start | bytes 5308424 | tf_op jit(solution)/shard_map/ppermute | solution.py:235
  253.2 19.1 %collective-permute-start.46 = (bf16[2,48,1536]{2,1,0:T(8,128)(2,1)}, bf16[2,48,1536]{2,1,0:T(8,128)(2,1)S(1)}, u32[]{:S(2)}, u32[]{:S(2)}) collective-permute-start(bf16[2,48,1536]{2,1,0:T(8,128)(2,1)} %pad_maximum_fusion.7), channel_id=1, source_target_pairs={{0,8},{1,9},{2,10},{3,11},{4,12},{5,13},{6,14},{7,15},{8,0},{9,1},... | collective-permute-start | bytes 884744 | tf_op jit(solution)/shard_map/ppermute | solution.py:235
  256.4 15.9 %collective-permute-start.41 = (bf16[4,48,1536]{2,1,0:T(8,128)(2,1)}, bf16[4,48,1536]{2,1,0:T(8,128)(2,1)}, u32[]{:S(2)}, u32[]{:S(2)}) collective-permute-start(bf16[4,48,1536]{2,1,0:T(8,128)(2,1)} %fusion.30), channel_id=1, source_target_pairs={{0,4},{1,3},{2,6},{3,1},{4,0},{5,7},{6,2},{7,5},{8,12},{9,11},{10,... | collective-permute-start | bytes 1769480 | tf_op jit(solution)/shard_map/ppermute | solution.py:235
  269.0 17.5 %collective-permute-start.36 = (bf16[2,4,48,1664]{3,2,1,0:T(8,128)(2,1)}, bf16[2,4,48,1664]{3,2,1,0:T(8,128)(2,1)S(1)}, u32[]{:S(2)}, u32[]{:S(2)}) collective-permute-start(bf16[2,4,48,1664]{3,2,1,0:T(8,128)(2,1)} %get-tuple-element.106), channel_id=1, source_target_pairs={{0,2},{1,5},{2,0},{3,7},{4,6},{5,1},{6,4},{7,3},{8,10},{9,13},{10,... | collective-permute-start | bytes 3833864 | tf_op jit(solution)/shard_map/ppermute | solution.py:235
  273.5 14.2 %collective-permute-start.47 = (bf16[48,1536]{1,0:T(8,128)(2,1)S(1)}, bf16[48,1536]{1,0:T(8,128)(2,1)S(1)}, u32[]{:S(2)}, u32[]{:S(2)}) collective-permute-start(bf16[48,1536]{1,0:T(8,128)(2,1)S(1)} %fusion.38), channel_id=1, source_target_pairs={{0,16},{1,17},{2,18},{3,19},{4,20},{5,21},{6,22},{7,23},{8,24},{9,... | collective-permute-start | bytes 442376 | tf_op jit(solution)/shard_map/ppermute | solution.py:235
  275.0 12.7 %collective-permute-start.42 = (bf16[2,48,1536]{2,1,0:T(8,128)(2,1)S(1)}, bf16[2,48,1536]{2,1,0:T(8,128)(2,1)S(1)}, u32[]{:S(2)}, u32[]{:S(2)}) collective-permute-start(bf16[2,48,1536]{2,1,0:T(8,128)(2,1)S(1)} %pad_maximum_fusion.6), channel_id=1, source_target_pairs={{0,8},{1,9},{2,10},{3,11},{4,12},{5,13},{6,14},{7,15},{8,0},{9,1},... | collective-permute-start | bytes 884744 | tf_op jit(solution)/shard_map/ppermute | solution.py:235
  287.7 10.7 %collective-permute-start.37 = (bf16[4,48,1664]{2,1,0:T(8,128)(2,1)}, bf16[4,48,1664]{2,1,0:T(8,128)(2,1)}, u32[]{:S(2)}, u32[]{:S(2)}) collective-permute-start(bf16[4,48,1664]{2,1,0:T(8,128)(2,1)} %fusion.29), channel_id=1, source_target_pairs={{0,4},{1,3},{2,6},{3,1},{4,0},{5,7},{6,2},{7,5},{8,12},{9,11},{10,... | collective-permute-start | bytes 1916936 | tf_op jit(solution)/shard_map/ppermute | solution.py:235
  288.8 3.7 %collective-permute-start.48 = (f32[24,1536]{1,0:T(8,128)S(1)}, f32[24,1536]{1,0:T(8,128)}, u32[]{:S(2)}, u32[]{:S(2)}) collective-permute-start(f32[24,1536]{1,0:T(8,128)S(1)} %constant_dynamic-slice_fusion), channel_id=1, source_target_pairs={{0,1},{1,0},{2,3},{3,2},{4,5},{5,4},{6,7},{7,6},{8,9},{9,8},{10,11... | collective-permute-start | bytes 442376 | tf_op jit(solution)/shard_map/ppermute | solution.py:235
  292.5 18.8 %collective-permute-start.43 = (bf16[48,1536]{1,0:T(8,128)(2,1)}, bf16[48,1536]{1,0:T(8,128)(2,1)S(1)}, u32[]{:S(2)}, u32[]{:S(2)}) collective-permute-start(bf16[48,1536]{1,0:T(8,128)(2,1)} %fusion.42), channel_id=1, source_target_pairs={{0,16},{1,17},{2,18},{3,19},{4,20},{5,21},{6,22},{7,23},{8,24},{9,... | collective-permute-start | bytes 442376 | tf_op jit(solution)/shard_map/ppermute | solution.py:235
  299.6 10.3 %collective-permute-start.38 = (bf16[2,48,1664]{2,1,0:T(8,128)(2,1)S(1)}, bf16[2,48,1664]{2,1,0:T(8,128)(2,1)S(1)}, u32[]{:S(2)}, u32[]{:S(2)}) collective-permute-start(bf16[2,48,1664]{2,1,0:T(8,128)(2,1)S(1)} %pad_maximum_fusion.3), channel_id=1, source_target_pairs={{0,8},{1,9},{2,10},{3,11},{4,12},{5,13},{6,14},{7,15},{8,0},{9,1},... | collective-permute-start | bytes 958472 | tf_op jit(solution)/shard_map/ppermute | solution.py:235
  311.3 9.3 %collective-permute-start.39 = (bf16[48,1664]{1,0:T(8,128)(2,1)S(1)}, bf16[48,1664]{1,0:T(8,128)(2,1)S(1)}, u32[]{:S(2)}, u32[]{:S(2)}) collective-permute-start(bf16[48,1664]{1,0:T(8,128)(2,1)S(1)} %get-tuple-element.199), channel_id=1, source_target_pairs={{0,16},{1,17},{2,18},{3,19},{4,20},{5,21},{6,22},{7,23},{8,24},{9,... | collective-permute-start | bytes 479240 | tf_op jit(solution)/shard_map/ppermute | solution.py:235
  (47 other events, 396.4 us)
Sparse Core Ops, SparseCore 0:
  11.5 84.6 all-gather.1
  168.6 112.3 reduce-scatter.1
